TPU v7x, 32 devices: a whole 2x2x4 slice. The times are simulated.
32 devices in a mesh: groups: 2 (over x), patch: 16 (over z, y, core).
Axes of the slice: x: 2, y: 2, z: 4, core: 2. Of those that a mesh axis runs over, the one named last changes fastest.
Arguments:
- tokens: bfloat16 [16384, 1152], P(('groups', 'patch')), parts along dimension 0, may hold values from -6 to 6
- stale_kv: bfloat16 [16384, 1152], P(('groups', 'patch')), parts along dimension 0, may hold values from -40 to 40, as said below
- mod_table: float32 [6, 1152], replicated, may hold values from -2 to 3
- mod_mix: float32 [6, 1152], replicated, may hold values from -3 to 3
- timestep: int32 [2], P('groups'), parts along dimension 0, may hold values from 0 to 999
- frame_order: int32 [8], P('groups'), parts along dimension 0, may hold values from 0 to 3, each once
- spatial_qkv: bfloat16 [3, 1152, 576], replicated, may hold values from -0.1875 to 0.1875
- spatial_out: bfloat16 [576, 1152], replicated, may hold values from -0.25 to 0.25
- temporal_qkv: bfloat16 [3, 1152, 576], replicated, may hold values from -0.1875 to 0.1875
- temporal_out: bfloat16 [576, 1152], replicated, may hold values from -0.25 to 0.25
Outputs:
- block_out: float32 [16384, 1152], P(('groups', 'patch')), parts along dimension 0
There are 2 independent parts, one for each index of `groups`. A program takes and returns all parts, laid end to end along the dimension named above; an argument that names none is the same for every part. Nothing has to cross between parts.
Inputs may be any that keep to these rules, and one draw needn't show every extreme that they name: `frame_order`: a permutation of the 4 time positions. `stale_kv`: previous step's keys and values.
All inputs are finite; a program needn't handle non-finite values.
Results may differ from a plain program's by a relative error of at most 0.013.
The roundings to bfloat16 on the way count: a program that leaves them out, or rounds other values in their place, can miss the bound.
Values may be sent and summed in bfloat16 or wider, within the bound.
No kernel may reach another device: no remote copies, remote signals or barrier semaphores. Data moves between devices by JAX's collectives and lax.ppermute only.
A program may use at most 128 MiB of HBM per device.

v0:
```python
import functools
import math

import jax
import jax.numpy as jnp
from jax import lax
from jax.experimental import pallas as pl
from jax.experimental.pallas import tpu as pltpu
from jax.sharding import PartitionSpec as P


HEADS = 16
LANES = 128
QUERY_ROWS = 128
PAIR_GROUPS = ((0,), (1,), (2,), (3,))
EMIT = (False, False, True, True)
HALVES = 2


epsilon = 1e-06
bf16 = jnp.bfloat16
f32 = jnp.float32
NT = (((1,), (1,)), ((), ()))


def permute(value, target):
    count = lax.axis_size("patch")
    return lax.ppermute(value, "patch", [(source, target(source)) for source in range(count)])


def partner_slot(slot, step, frames):
    if frames & (frames - 1) == 0:
        return slot ^ step
    return (slot + step) % frames


def source_slot(slot, step, frames):
    if frames & (frames - 1) == 0:
        return slot ^ step
    return (slot - step) % frames


def normalize(activations):
    row_mean = jnp.mean(activations, axis=-1, keepdims=True)
    centered = activations - row_mean
    variance = jnp.mean(centered * centered, axis=-1, keepdims=True)
    return centered * lax.rsqrt(variance + epsilon)


def sinusoid(position, feature_width):
    half_width = feature_width // 2
    frequencies = jnp.exp(
        -math.log(10000.0) * jnp.arange(half_width, dtype=jnp.float32) / half_width
    )
    angles = jnp.asarray(position).astype(jnp.float32)[..., None] * frequencies
    return jnp.concatenate([jnp.sin(angles), jnp.cos(angles)], axis=-1)


def column_mask(first, width, dtype):
    column = lax.broadcasted_iota(jnp.int32, (1, 2 * LANES), 1)
    inside = jnp.logical_and(column >= first, column < first + width)
    return jnp.where(inside, 1.0, 0.0).astype(dtype)


def softmax_scale(head_dim):
    return math.log2(math.e) * head_dim ** (-0.5)


def vmem_specs(count):
    return [pl.BlockSpec(memory_space=pltpu.VMEM) for _ in range(count)]


def on_chip_call(kernel, operands, shapes, flops, limit_mib, transcendentals=0, scratch=()):
    operands = [pltpu.with_memory_space_constraint(array, pltpu.VMEM) for array in operands]
    return pl.pallas_call(
        kernel,
        out_shape=[pltpu.VMEM(shape, dtype) for shape, dtype in shapes],
        in_specs=vmem_specs(len(operands)),
        out_specs=vmem_specs(len(shapes)),
        scratch_shapes=list(scratch),
        compiler_params=pltpu.CompilerParams(vmem_limit_bytes=limit_mib * 2**20),
        cost_estimate=pl.CostEstimate(
            flops=flops,
            bytes_accessed=sum(array.size * array.dtype.itemsize for array in operands),
            transcendentals=transcendentals,
        ),
    )(*operands)


def chunk_kernel(kv_ref, *refs, tiles):
    out_refs, sems = refs[:-1], refs[-1]
    copies = []
    for chunk, ref in zip(tiles, out_refs):
        for at, tile in enumerate(chunk):
            copies.append(
                pltpu.make_async_copy(
                    kv_ref.at[:, tile * LANES : (tile + 1) * LANES],
                    ref.at[:, at * LANES : (at + 1) * LANES],
                    sems.at[len(copies)],
                )
            )
            copies[-1].start()
    for copy in copies:
        copy.wait()


def stage_chunks(stale_kv, tiles):
    rows = stale_kv.shape[0]
    return pl.pallas_call(
        functools.partial(chunk_kernel, tiles=tiles),
        out_shape=[pltpu.VMEM((rows, len(chunk) * LANES), bf16) for chunk in tiles],
        in_specs=[pl.BlockSpec(memory_space=pltpu.HBM)],
        out_specs=vmem_specs(len(tiles)),
        scratch_shapes=[pltpu.SemaphoreType.DMA((sum(len(chunk) for chunk in tiles),))],
        compiler_params=pltpu.CompilerParams(vmem_limit_bytes=4 * 2**20),
        name="chunks",
    )(stale_kv)


def piece_kernel(slot_ref, tokens_ref, *refs, frames):
    out_refs, sems = refs[:-1], refs[-1]
    piece = tokens_ref.shape[0] // frames
    copies = []
    for step in range(frames):
        row = partner_slot(slot_ref[0], step, frames) * piece
        copies.append(
            pltpu.make_async_copy(
                tokens_ref.at[pl.ds(row, piece), :], out_refs[step], sems.at[step]
            )
        )
        copies[-1].start()
    for copy in copies:
        copy.wait()


def stage_pieces(slot, tokens, frames):
    rows, feature_width = tokens.shape
    return pl.pallas_call(
        functools.partial(piece_kernel, frames=frames),
        out_shape=[pltpu.VMEM((rows // frames, feature_width), bf16) for _ in range(frames)],
        in_specs=[
            pl.BlockSpec(memory_space=pltpu.SMEM),
            pl.BlockSpec(memory_space=pltpu.HBM),
        ],
        out_specs=vmem_specs(frames),
        scratch_shapes=[pltpu.SemaphoreType.DMA((frames,))],
        compiler_params=pltpu.CompilerParams(vmem_limit_bytes=4 * 2**20),
        name="pieces",
    )(slot, tokens)


def projection_kernel(*refs, frames, width):
    pieces = refs[:frames]
    weight_ref, modulation_ref, query_ref, kv_ref = refs[frames:]
    tokens = jnp.concatenate([ref[...] for ref in pieces], axis=0).astype(f32)
    inputs = normalize(tokens) * (1.0 + modulation_ref[1:2, :]) + modulation_ref[0:1, :]
    inputs = inputs.astype(bf16)
    padded = query_ref.shape[1]
    query_ref[...] = lax.dot_general(
        inputs, weight_ref[:padded, :], NT, preferred_element_type=f32
    ).astype(bf16)
    kv_ref[...] = lax.dot_general(
        inputs, weight_ref[width:, :], NT, preferred_element_type=f32
    ).astype(bf16)


def projections(pieces, weight, modulation, width):
    frames = len(pieces)
    piece, feature_width = pieces[0].shape
    padded = -(-width // LANES) * LANES
    rows = frames * piece
    return on_chip_call(
        functools.partial(projection_kernel, frames=frames, width=width),
        [*pieces, weight, modulation],
        [((rows, padded), bf16), ((rows, 2 * width), bf16)],
        2 * rows * feature_width * 3 * width,
        16,
    )


def pair_plan(width, head_dim):
    plan = []
    for first in range(0, width, 2 * head_dim):
        key_tile = first // LANES
        value_tile = (width + first) // LANES
        plan.append(
            (key_tile, first - key_tile * LANES, value_tile, width + first - value_tile * LANES)
        )
    return plan


def group_tiles(width, head_dim):
    plan = pair_plan(width, head_dim)
    seen, groups = set(), []
    for group in PAIR_GROUPS:
        need = []
        for pair in group:
            key_tile, _, value_tile, _ = plan[pair]
            need += [key_tile, key_tile + 1, value_tile, value_tile + 1]
        fresh = sorted(set(need) - seen)
        seen |= set(fresh)
        groups.append(tuple(fresh))
    return groups


def spatial_kernel(*refs, group, frames, head_dim, width, tiles, held, emitted, kept):
    plan = pair_plan(width, head_dim)
    count = len(tiles)
    position = 0
    query_ref, own_ref, peer_ref = refs[:3]
    near_refs = refs[3 : 3 + count]
    far_refs = refs[3 + count : 3 + 2 * count]
    position = 3 + 2 * count
    held_ref = None
    if held:
        held_ref = refs[position]
        position += 1
    out_count = frames if emitted else 0
    out_refs = refs[position : position + out_count]
    kept_ref = refs[position + out_count] if kept else None

    where = {tile: (c, j) for c, chunk in enumerate(tiles) for j, tile in enumerate(chunk)}

    def from_chunks(chunk_refs):
        def load(tile):
            chunk, at = where[tile]
            return chunk_refs[chunk][:, at * LANES : (at + 1) * LANES]

        return load

    def from_whole(ref):
        return lambda tile: ref[:, tile * LANES : (tile + 1) * LANES]

    blocks = [from_whole(own_ref), from_whole(peer_ref), from_chunks(near_refs), from_chunks(far_refs)]
    rows = query_ref.shape[0]
    scale = softmax_scale(head_dim)
    piece = rows // frames

    def two(block, tile):
        return jnp.concatenate([block(tile), block(tile + 1)], axis=1)

    def scores_of(pair, chunk):
        key_tile, key_lane, _, _ = plan[pair]
        window = query_ref[
            chunk * QUERY_ROWS : (chunk + 1) * QUERY_ROWS, key_tile * LANES : (key_tile + 2) * LANES
        ]
        stacked = jnp.concatenate(
            [
                window * column_mask(key_lane, head_dim, bf16),
                window * column_mask(key_lane + head_dim, head_dim, bf16),
            ],
            axis=0,
        )
        return [
            lax.dot_general(stacked, two(block, key_tile), NT, preferred_element_type=f32)
            for block in blocks
        ]

    def mix(pair, scores):
        _, key_lane, value_tile, value_lane = plan[pair]
        top = functools.reduce(jnp.maximum, [jnp.max(s, axis=-1, keepdims=True) for s in scores])
        top = top * scale
        weights = [jnp.exp2(s * scale - top) for s in scores]
        total = functools.reduce(jnp.add, [jnp.sum(w, axis=-1, keepdims=True) for w in weights])
        mixed = functools.reduce(
            jnp.add,
            [
                jnp.dot(w.astype(bf16), two(block, value_tile), preferred_element_type=f32)
                for w, block in zip(weights, blocks)
            ],
        )
        mixed = mixed / total
        joined = mixed[:QUERY_ROWS] * column_mask(value_lane, head_dim, f32) + mixed[
            QUERY_ROWS:
        ] * column_mask(value_lane + head_dim, head_dim, f32)
        return pltpu.roll(joined, (key_lane - value_lane) % (2 * LANES), 1)

    chunks = rows // QUERY_ROWS
    tasks = [(chunk, pair) for chunk in range(chunks) for pair in group]
    pending = scores_of(tasks[0][1], tasks[0][0])
    parts = {}
    for index, (chunk, pair) in enumerate(tasks):
        scores = pending
        if index + 1 < len(tasks):
            pending = scores_of(tasks[index + 1][1], tasks[index + 1][0])
        joined = mix(pair, scores)
        tile = plan[pair][0]
        for side in range(2):
            half = joined[:, side * LANES : (side + 1) * LANES]
            parts[tile + side] = parts[tile + side] + half if tile + side in parts else half
        if pair != group[-1]:
            continue
        at = chunk * QUERY_ROWS
        for number, tile in enumerate(held):
            old = held_ref[at : at + QUERY_ROWS, number * LANES : (number + 1) * LANES].astype(f32)
            parts[tile] = parts[tile] + old if tile in parts else old
        if kept:
            values = jnp.concatenate([parts[tile] for tile in kept], axis=1)
            kept_ref[at : at + QUERY_ROWS, :] = values.astype(bf16)
        if emitted:
            values = jnp.concatenate([parts[tile] for tile in emitted], axis=1).astype(bf16)
            width_out = out_refs[0].shape[1]
            for sub in range(QUERY_ROWS // piece):
                out_refs[at // piece + sub][...] = values[
                    sub * piece : (sub + 1) * piece, :width_out
                ]
        parts = {}


def tile_flow(width, head_dim):
    plan = pair_plan(width, head_dim)
    flow, held = [], ()
    for number, group in enumerate(PAIR_GROUPS):
        have = sorted({plan[pair][0] + side for pair in group for side in range(2)} | set(held))
        last = number == len(PAIR_GROUPS) - 1
        complete = [tile for tile in have if last or tile <= plan[group[-1]][0]]
        emitted = tuple(complete) if EMIT[number] else ()
        kept = tuple(tile for tile in have if tile not in emitted)
        flow.append((held, emitted, kept))
        held = kept
    return flow


def spatial_group(number, query, own_kv, peer_kv, near, far, carry, frames, head_dim, width):
    group = PAIR_GROUPS[number]
    held, emitted, kept = tile_flow(width, head_dim)[number]
    tiles = tuple(group_tiles(width, head_dim)[: number + 1])
    rows = query.shape[0]
    shapes = []
    if emitted:
        columns = min(width, (emitted[-1] + 1) * LANES) - emitted[0] * LANES
        shapes += [((rows // frames, columns), bf16) for _ in range(frames)]
    if kept:
        shapes.append(((rows, len(kept) * LANES), bf16))
    operands = [query, own_kv, peer_kv, *near[: number + 1], *far[: number + 1]]
    if held:
        operands.append(carry)
    keys = 4 * rows
    results = on_chip_call(
        functools.partial(
            spatial_kernel,
            group=group,
            frames=frames,
            head_dim=head_dim,
            width=width,
            tiles=tiles,
            held=held,
            emitted=emitted,
            kept=kept,
        ),
        operands,
        shapes,
        len(group) * 2 * rows * keys * 256 * 4,
        24,
        len(group) * 2 * rows * keys,
    )
    results = list(results)
    carry = results.pop() if kept else None
    return results, carry


def joined_rows(tokens_refs, mixed_refs):
    groups = len(mixed_refs) // len(tokens_refs)
    tokens = jnp.concatenate([ref[...] for ref in tokens_refs], axis=0).astype(f32)
    mixed = jnp.concatenate(
        [
            jnp.concatenate(
                [ref[...] for ref in mixed_refs[frame * groups : (frame + 1) * groups]], axis=1
            )
            for frame in range(len(tokens_refs))
        ],
        axis=0,
    )
    return tokens, mixed


def temporal_in_kernel(*refs, frames, groups):
    tokens_refs = refs[:frames]
    mixed_refs = refs[frames : frames + frames * groups]
    position = frames + frames * groups
    out_weight, qkv_weight, modulation_ref, place_ref, query_ref, kv_ref = refs[position:]
    width = out_weight.shape[0]
    piece = tokens_refs[0].shape[0]
    tokens, mixed = joined_rows(tokens_refs, mixed_refs)
    after = tokens + modulation_ref[2:3, :] * jnp.dot(
        mixed, out_weight[...], preferred_element_type=f32
    )
    normal = normalize(after) * (1.0 + modulation_ref[4:5, :]) + modulation_ref[3:4, :]
    inputs = jnp.concatenate(
        [
            (normal[frame * piece : (frame + 1) * piece] + place_ref[frame : frame + 1, :]).astype(bf16)
            for frame in range(frames)
        ],
        axis=0,
    )
    query_ref[...] = lax.dot_general(
        inputs, qkv_weight[: query_ref.shape[1], :], NT, preferred_element_type=f32
    ).astype(bf16)
    kv_ref[...] = lax.dot_general(
        inputs, qkv_weight[width:, :], NT, preferred_element_type=f32
    ).astype(bf16)


def temporal_in(tokens, mixed, spatial_out, temporal_qkv, modulation, places):
    frames, groups = len(tokens), len(mixed[0])
    width, feature_width = spatial_out.shape
    padded = -(-width // LANES) * LANES
    rows = frames * tokens[0].shape[0]
    return on_chip_call(
        functools.partial(temporal_in_kernel, frames=frames, groups=groups),
        [
            *tokens,
            *[part for frame in mixed for part in frame],
            spatial_out,
            temporal_qkv,
            modulation,
            places,
        ],
        [((rows, padded), bf16), ((rows, 2 * width), bf16)],
        2 * rows * feature_width * width * 4,
        20,
    )


def temporal_kernel(query_ref, kv_ref, *out_refs, head_dim, first):
    frames = len(out_refs)
    piece, width = out_refs[0].shape
    stride = query_ref.shape[0] // frames
    scale = softmax_scale(head_dim)
    step = max(16, min(piece, LANES // frames))
    block = frames * step
    row_at = lax.broadcasted_iota(jnp.int32, (2 * block, block), 0) % step
    column_at = lax.broadcasted_iota(jnp.int32, (2 * block, block), 1) % step
    same = row_at == column_at
    plan = pair_plan(width, head_dim)

    for start in range(0, piece, step):

        def window(ref, tile):
            return jnp.concatenate(
                [
                    ref[
                        frame * stride + first + start : frame * stride + first + start + step,
                        tile * LANES : (tile + 2) * LANES,
                    ]
                    for frame in range(frames)
                ],
                axis=0,
            )

        parts = {}
        for tile, lane, value_tile, value_lane in plan:
            queries = window(query_ref, tile)
            stacked = jnp.concatenate(
                [
                    queries * column_mask(lane, head_dim, bf16),
                    queries * column_mask(lane + head_dim, head_dim, bf16),
                ],
                axis=0,
            )
            scores = lax.dot_general(stacked, window(kv_ref, tile), NT, preferred_element_type=f32)
            scores = jnp.where(same, scores * scale, -jnp.inf)
            weights = jnp.exp2(scores - jnp.max(scores, axis=-1, keepdims=True))
            weights = (weights / jnp.sum(weights, axis=-1, keepdims=True)).astype(bf16)
            mixed_pair = jnp.dot(weights, window(kv_ref, value_tile), preferred_element_type=f32)
            joined = mixed_pair[:block] * column_mask(value_lane, head_dim, f32) + mixed_pair[
                block:
            ] * column_mask(value_lane + head_dim, head_dim, f32)
            joined = pltpu.roll(joined, (lane - value_lane) % (2 * LANES), 1)
            for side in range(2):
                half = joined[:, side * LANES : (side + 1) * LANES]
                parts[tile + side] = parts[tile + side] + half if tile + side in parts else half
        values = jnp.concatenate([parts[tile] for tile in sorted(parts)], axis=1).astype(bf16)
        for frame in range(frames):
            out_refs[frame][start : start + step, :] = values[
                frame * step : (frame + 1) * step, :width
            ]


def temporal(query, kv, frames, head_dim, first, piece):
    width = kv.shape[1] // 2
    rows = frames * piece
    return on_chip_call(
        functools.partial(temporal_kernel, head_dim=head_dim, first=first),
        [query, kv],
        [((piece, width), bf16) for _ in range(frames)],
        2 * rows * 128 * 256 * 16,
        8,
        rows * 128 * 8,
    )


def after_kernel(*refs, frames, groups):
    weight_ref, modulation_ref, out_ref = refs[frames + frames * groups :]
    tokens, mixed = joined_rows(refs[:frames], refs[frames : frames + frames * groups])
    out_ref[...] = tokens + modulation_ref[2:3, :] * jnp.dot(
        mixed, weight_ref[...], preferred_element_type=f32
    )


def after_spatial(tokens, mixed, weight, modulation):
    frames, groups = len(tokens), len(mixed[0])
    width, feature_width = weight.shape
    rows = frames * tokens[0].shape[0]
    return on_chip_call(
        functools.partial(after_kernel, frames=frames, groups=groups),
        [*tokens, *[part for frame in mixed for part in frame], weight, modulation],
        [((rows, feature_width), f32)],
        2 * rows * feature_width * width,
        16,
    )[0]


def output_kernel(slot_ref, after_ref, weight_ref, modulation_ref, *refs, frames, halves):
    parts, (out_ref, stage_ref, sems) = refs[: frames * halves], refs[frames * halves :]
    piece = after_ref.shape[0] // frames
    copies = []
    for frame in range(frames):
        cut = slice(frame * piece, (frame + 1) * piece)
        mixed = jnp.concatenate([parts[frame * halves + h][...] for h in range(halves)], axis=0)
        stage_ref[cut, :] = after_ref[cut, :] + modulation_ref[5:6, :] * jnp.dot(
            mixed, weight_ref[...], preferred_element_type=f32
        )
        row = partner_slot(slot_ref[0], frame, frames) * piece
        copies.append(
            pltpu.make_async_copy(
                stage_ref.at[cut, :], out_ref.at[pl.ds(row, piece), :], sems.at[frame]
            )
        )
        copies[-1].start()
    for copy in copies:
        copy.wait()


def output(slot, after, weight, modulation, parts, frames):
    rows, feature_width = after.shape
    halves = len(parts[0])
    operands = [after, weight, modulation, *[part for frame in parts for part in frame]]
    return pl.pallas_call(
        functools.partial(output_kernel, frames=frames, halves=halves),
        out_shape=jax.ShapeDtypeStruct((rows, feature_width), f32),
        in_specs=[pl.BlockSpec(memory_space=pltpu.SMEM), *vmem_specs(len(operands))],
        out_specs=pl.BlockSpec(memory_space=pltpu.HBM),
        scratch_shapes=[
            pltpu.VMEM((rows, feature_width), f32),
            pltpu.SemaphoreType.DMA((frames,)),
        ],
        compiler_params=pltpu.CompilerParams(vmem_limit_bytes=16 * 2**20),
        name="block_output",
    )(slot, *[pltpu.with_memory_space_constraint(array, pltpu.VMEM) for array in operands])


def per_device(
    tokens,
    stale_kv,
    mod_table,
    mod_mix,
    timestep,
    frame_order,
    spatial_qkv,
    spatial_out,
    temporal_qkv,
    temporal_out,
):
    devices = lax.axis_size("patch")
    frames = devices // 4
    slot = lax.axis_index("patch") // 4
    rows, feature_width = tokens.shape
    width = spatial_out.shape[0]
    head_dim = feature_width // HEADS
    piece = rows // frames

    def other_core(device):
        return device ^ 1

    def other_chip(device):
        return device ^ 2

    def ahead(step):
        return lambda device: partner_slot(device // 4, step, frames) * 4 + device % 4

    def behind(step):
        return lambda device: source_slot(device // 4, step, frames) * 4 + device % 4

    near, far = [], []
    for chunk in stage_chunks(stale_kv, group_tiles(width, head_dim)):
        near.append(permute(chunk, other_chip))
        far.append(permute(near[-1], other_core))
    peer_kv = permute(stale_kv, other_core)

    slot_word = slot.astype(jnp.int32)[None]
    pieces = stage_pieces(slot_word, tokens, frames)
    there = [pieces[0]]
    there += [permute(pieces[s], ahead(s)) for s in range(1, frames)]

    modulation = mod_table + mod_mix * sinusoid(timestep[0], feature_width)[None, :]
    sources = source_slot(slot, jnp.arange(frames), frames)
    places = sinusoid(frame_order[sources], feature_width)

    query, own_kv = projections(
        pieces,
        jnp.swapaxes(spatial_qkv, 1, 2).reshape(3 * width, feature_width),
        modulation,
        width,
    )

    carry = None
    local = [[] for _ in range(frames)]
    sent = [[] for _ in range(frames)]
    for number in range(len(PAIR_GROUPS)):
        outs, carry = spatial_group(
            number, query, own_kv, peer_kv, near, far, carry, frames, head_dim, width
        )
        for s, out in enumerate(outs):
            local[s].append(out)
            sent[s].append(out if s == 0 else permute(out, ahead(s)))

    after = after_spatial(pieces, local, spatial_out, modulation)
    temporal_query, temporal_kv = temporal_in(
        there,
        sent,
        spatial_out,
        jnp.swapaxes(temporal_qkv, 1, 2).reshape(3 * width, feature_width),
        modulation,
        places,
    )
    half = piece // HALVES
    back = [[] for _ in range(frames)]
    for h in range(HALVES):
        outs = temporal(temporal_query, temporal_kv, frames, head_dim, h * half, half)
        for s, out in enumerate(outs):
            back[s].append(out if s == 0 else permute(out, behind(s)))

    return output(
        slot_word, after, temporal_out, modulation, back, frames
    )


def solution(mesh):
    return jax.shard_map(
        per_device,
        mesh=mesh,
        in_specs=(
            P(("groups", "patch"), None),
            P(("groups", "patch"), None),
            P(),
            P(),
            P("groups"),
            P("groups"),
            P(),
            P(),
            P(),
            P(),
        ),
        out_specs=P(("groups", "patch"), None),
        check_vma=False,
    )
```

profile of v0, /device:TPU:0, one launch (start us, length us, event | category | flops | bytes accessed | tf_op | source)
XLA Modules:
  0.0 99.7 jit_solution(4067728940393016594)
XLA Ops:
  0.0 0.5 collective-permute-start
  0.5 1.3 %copy-done.4 = bf16[512,1152]{1,0:T(8,128)(2,1)S(1)} copy-done((bf16[512,1152]{1,0:T(8,128)(2,1)S(1)}, bf16[512,1152]{1,0:T(8,128)(2,1)}, u32[]{:S(2)}) %copy-start.4) | copy-done | bytes 1179672
  1.8 1.3 %chunks.1 = (bf16[512,512]{1,0:T(8,128)(2,1)}, bf16[512,256]{1,0:T(8,128)(2,1)}, bf16[512,256]{1,0:T(8,128)(2,1)}, bf16[512,128]{1,0:T(8,128)(2,1)S(1)}) custom-call(bf16[512,1152]{1,0:T(8,128)(2,1)S(1)} %copy-done.4), custom_call_target="tpu_custom_call" | custom-call | tf_op jit(solution)/shard_map/chunks/pallas_call | solution.py:109
  3.1 0.6 copy-done.7
  3.7 2.6 %collective-permute-start.1 = (bf16[512,512]{1,0:T(8,128)(2,1)}, bf16[512,512]{1,0:T(8,128)(2,1)}, u32[]{:S(2)}, u32[]{:S(2)}) collective-permute-start(bf16[512,512]{1,0:T(8,128)(2,1)} %get-tuple-element.40), channel_id=1, source_target_pairs={{0,2},{1,3},{2,0},{3,1},{4,6},{5,7},{6,4},{7,5},{8,10},{9,11},{10,... | collective-permute-start | bytes 1572872 | tf_op jit(solution)/shard_map/ppermute | solution.py:28
  6.3 0.0 collective-permute-start.2
  6.3 2.0 %collective-permute-start.3 = (bf16[512,256]{1,0:T(8,128)(2,1)}, bf16[512,256]{1,0:T(8,128)(2,1)}, u32[]{:S(2)}, u32[]{:S(2)}) collective-permute-start(bf16[512,256]{1,0:T(8,128)(2,1)} %get-tuple-element.42), channel_id=1, source_target_pairs={{0,2},{1,3},{2,0},{3,1},{4,6},{5,7},{6,4},{7,5},{8,10},{9,11},{10,... | collective-permute-start | bytes 786440 | tf_op jit(solution)/shard_map/ppermute | solution.py:28
  8.3 0.3 pieces.1
  8.6 2.7 %collective-permute-start.10 = (bf16[128,1152]{1,0:T(8,128)(2,1)S(1)}, bf16[128,1152]{1,0:T(8,128)(2,1)}, u32[]{:S(2)}, u32[]{:S(2)}) collective-permute-start(bf16[128,1152]{1,0:T(8,128)(2,1)S(1)} %get-tuple-element.36.refs_2_), channel_id=1, source_target_pairs={{0,8},{1,9},{2,10},{3,11},{4,12},{5,13},{6,14},{7,15},{8,0},{9,1},... | collective-permute-start | bytes 884744 | tf_op jit(solution)/shard_map/ppermute | solution.py:28
  12.0 0.1 pad_maximum_fusion.1
  12.1 0.8 multiply_add_fusion.refs_5_.refs_13_.refs_14_.modulation_ref
  12.9 6.5 %collective-permute-done.1.refs_3_ = bf16[512,512]{1,0:T(8,128)(2,1)} collective-permute-done((bf16[512,512]{1,0:T(8,128)(2,1)}, bf16[512,512]{1,0:T(8,128)(2,1)}, u32[]{:S(2)}, u32[]{:S(2)}) %collective-permute-start.1) | collective-permute-done | bytes 524320 | tf_op jit(solution)/shard_map/ppermute | solution.py:28
  19.4 0.6 gather_fusion
  20.1 2.1 %copy-done.5 = bf16[3,1152,576]{1,2,0:T(8,128)(2,1)S(1)} copy-done((bf16[3,1152,576]{1,2,0:T(8,128)(2,1)S(1)}, bf16[3,1152,576]{1,2,0:T(8,128)(2,1)}, u32[]{:S(2)}) %copy-start.5) | copy-done | bytes 3981336
  22.2 3.4 %shard_map.100 = (bf16[512,640]{1,0:T(8,128)(2,1)S(1)}, bf16[512,1152]{1,0:T(8,128)(2,1)S(1)}) custom-call(bf16[128,1152]{1,0:T(8,128)(2,1)S(1)} %get-tuple-element.34.refs_0_, bf16[128,1152]{1,0:T(8,128)(2,1)S(1)} %get-tuple-element.35.refs_1_, bf16[128,1152]{1,0:T(8,128)(2,1)S(1)} %get-tuple-element.36.refs_2_, ...), custom_call_target="tpu_custom_call" | custom-call | flops 2038431744 | bytes 5188608 | tf_op jit(solution)/shard_map/pallas_call | solution.py:75
  25.6 0.6 collective-permute-start.5
  26.2 4.2 %collective-permute-done.3.refs_5_ = bf16[512,256]{1,0:T(8,128)(2,1)} collective-permute-done((bf16[512,256]{1,0:T(8,128)(2,1)}, bf16[512,256]{1,0:T(8,128)(2,1)}, u32[]{:S(2)}, u32[]{:S(2)}) %collective-permute-start.3) | collective-permute-done | bytes 262176 | tf_op jit(solution)/shard_map/ppermute | solution.py:28
  30.3 3.8 %collective-permute-start.11 = (bf16[128,1152]{1,0:T(8,128)(2,1)S(1)}, bf16[128,1152]{1,0:T(8,128)(2,1)S(1)}, u32[]{:S(2)}, u32[]{:S(2)}) collective-permute-start(bf16[128,1152]{1,0:T(8,128)(2,1)S(1)} %get-tuple-element.37.refs_3_), channel_id=1, source_target_pairs={{0,12},{1,13},{2,14},{3,15},{4,8},{5,9},{6,10},{7,11},{8,4},{9,5},... | collective-permute-start | bytes 884744 | tf_op jit(solution)/shard_map/ppermute | solution.py:28
  34.2 1.5 %collective-permute-start.7 = (bf16[512,128]{1,0:T(8,128)(2,1)S(1)}, bf16[512,128]{1,0:T(8,128)(2,1)S(1)}, u32[]{:S(2)}, u32[]{:S(2)}) collective-permute-start(bf16[512,128]{1,0:T(8,128)(2,1)S(1)} %copy-done.8), channel_id=1, source_target_pairs={{0,2},{1,3},{2,0},{3,1},{4,6},{5,7},{6,4},{7,5},{8,10},{9,11},{10,... | collective-permute-start | bytes 393224 | tf_op jit(solution)/shard_map/ppermute | solution.py:28
  35.7 4.3 %shard_map.101.refs_7_ = bf16[512,256]{1,0:T(8,128)(2,1)S(1)} custom-call(bf16[512,640]{1,0:T(8,128)(2,1)S(1)} %get-tuple-element.38.refs_0_, bf16[512,1152]{1,0:T(8,128)(2,1)S(1)} %get-tuple-element.39.refs_1_, bf16[512,1152]{1,0:T(8,128)(2,1)S(1)} %collective-permute-done.refs_2_, bf16[512,512]{1,0:T(8,128)(2,1)} %collective-permute-done.1.refs_3_, ...), custom_call_target="tpu_custom_call" | custom-call | flops 2147483648 | bytes 4063232 | tf_op jit(solution)/shard_map/pallas_call | solution.py:75
  40.0 0.1 collective-permute-start.9
  40.1 0.6 collective-permute-start.8
  40.6 4.3 %shard_map.102.refs_9_ = bf16[512,384]{1,0:T(8,128)(2,1)S(1)} custom-call(bf16[512,640]{1,0:T(8,128)(2,1)S(1)} %get-tuple-element.38.refs_0_, bf16[512,1152]{1,0:T(8,128)(2,1)S(1)} %get-tuple-element.39.refs_1_, bf16[512,1152]{1,0:T(8,128)(2,1)S(1)} %collective-permute-done.refs_2_, bf16[512,512]{1,0:T(8,128)(2,1)} %collective-permute-done.1.refs_3_, ...), custom_call_target="tpu_custom_call" | custom-call | flops 2147483648 | bytes 4849664 | tf_op jit(solution)/shard_map/pallas_call | solution.py:75
  44.9 4.6 %shard_map.103 = (bf16[128,384]{1,0:T(8,128)(2,1)S(1)}, bf16[128,384]{1,0:T(8,128)(2,1)S(1)}, bf16[128,384]{1,0:T(8,128)(2,1)S(1)}, bf16[128,384]{1,0:T(8,128)(2,1)S(1)}, bf16[512,128]{1,0:T(8,128)(2,1)S(1)}) custom-call(bf16[512,640]{1,0:T(8,128)(2,1)S(1)} %get-tuple-element.38.refs_0_, bf16[512,1152]{1,0:T(8,128)(2,1)S(1)} %get-tuple-element.39.refs_1_, ...), custom_call_target="tpu_custom_call" | custom-call | flops 2147483648 | bytes 5505024 | tf_op jit(solution)/shard_map/pallas_call | solution.py:75
  49.5 0.0 copy-start.1
  49.5 4.5 %shard_map.104 = (bf16[128,192]{1,0:T(8,128)(2,1)S(1)}, bf16[128,192]{1,0:T(8,128)(2,1)S(1)}, bf16[128,192]{1,0:T(8,128)(2,1)S(1)}, bf16[128,192]{1,0:T(8,128)(2,1)S(1)}) custom-call(bf16[512,640]{1,0:T(8,128)(2,1)S(1)} %get-tuple-element.38.refs_0_, bf16[512,1152]{1,0:T(8,128)(2,1)S(1)} %get-tuple-element.39.refs_1_, ...), custom_call_target="tpu_custom_call" | custom-call | flops 2147483648 | bytes 5505024 | tf_op jit(solution)/shard_map/pallas_call | solution.py:75
  54.0 1.7 %collective-permute-start.13 = (bf16[128,192]{1,0:T(8,128)(2,1)S(1)}, bf16[128,192]{1,0:T(8,128)(2,1)S(1)}, u32[]{:S(2)}, u32[]{:S(2)}) collective-permute-start(bf16[128,192]{1,0:T(8,128)(2,1)S(1)} %get-tuple-element.48.refs_7_), channel_id=1, source_target_pairs={{0,4},{1,5},{2,6},{3,7},{4,0},{5,1},{6,2},{7,3},{8,12},{9,13},{10,... | collective-permute-start | bytes 147464 | tf_op jit(solution)/shard_map/ppermute | solution.py:28
  55.8 0.2 multiply_sine_fusion
  55.9 0.1 collective-permute-start.15
  56.0 2.7 %collective-permute-start.17 = (bf16[128,192]{1,0:T(8,128)(2,1)S(1)}, bf16[128,192]{1,0:T(8,128)(2,1)S(1)}, u32[]{:S(2)}, u32[]{:S(2)}) collective-permute-start(bf16[128,192]{1,0:T(8,128)(2,1)S(1)} %get-tuple-element.52.refs_11_), channel_id=1, source_target_pairs={{0,12},{1,13},{2,14},{3,15},{4,8},{5,9},{6,10},{7,11},{8,4},{9,5},... | collective-permute-start | bytes 147464 | tf_op jit(solution)/shard_map/ppermute | solution.py:28
  58.7 0.8 collective-permute-start.12
  59.5 1.0 collective-permute-start.14
  60.5 2.6 %collective-permute-start.16 = (bf16[128,384]{1,0:T(8,128)(2,1)S(1)}, bf16[128,384]{1,0:T(8,128)(2,1)S(1)}, u32[]{:S(2)}, u32[]{:S(2)}) collective-permute-start(bf16[128,384]{1,0:T(8,128)(2,1)S(1)} %get-tuple-element.51.refs_10_), channel_id=1, source_target_pairs={{0,12},{1,13},{2,14},{3,15},{4,8},{5,9},{6,10},{7,11},{8,4},{9,5},... | collective-permute-start | bytes 294920 | tf_op jit(solution)/shard_map/ppermute | solution.py:28
  63.1 0.1 pad_maximum_fusion.refs_15_
  63.2 0.6 collective-permute-done.15.refs_9_
  63.8 1.4 %collective-permute-done.12.refs_6_ = bf16[128,384]{1,0:T(8,128)(2,1)S(1)} collective-permute-done((bf16[128,384]{1,0:T(8,128)(2,1)S(1)}, bf16[128,384]{1,0:T(8,128)(2,1)S(1)}, u32[]{:S(2)}, u32[]{:S(2)}) %collective-permute-start.12) | collective-permute-done | bytes 98336 | tf_op jit(solution)/shard_map/ppermute | solution.py:28
  65.2 6.4 %collective-permute-done.14.refs_8_ = bf16[128,384]{1,0:T(8,128)(2,1)S(1)} collective-permute-done((bf16[128,384]{1,0:T(8,128)(2,1)S(1)}, bf16[128,384]{1,0:T(8,128)(2,1)S(1)}, u32[]{:S(2)}, u32[]{:S(2)}) %collective-permute-start.14) | collective-permute-done | bytes 98336 | tf_op jit(solution)/shard_map/ppermute | solution.py:28
  71.5 5.4 %shard_map.106 = (bf16[512,640]{1,0:T(8,128)(2,1)S(1)}, bf16[512,1152]{1,0:T(8,128)(2,1)S(1)}) custom-call(bf16[128,1152]{1,0:T(8,128)(2,1)S(1)} %get-tuple-element.34.refs_0_, bf16[128,1152]{1,0:T(8,128)(2,1)S(1)} %collective-permute-done.9.refs_1_, bf16[128,1152]{1,0:T(8,128)(2,1)} %collective-permute-done.10.refs_2_, ...), custom_call_target="tpu_custom_call" | custom-call | flops 2717908992 | bytes 7123968 | tf_op jit(solution)/shard_map/pallas_call | solution.py:75
  76.9 2.4 %shard_map.108 = (bf16[64,576]{1,0:T(8,128)(2,1)S(1)}, bf16[64,576]{1,0:T(8,128)(2,1)S(1)}, bf16[64,576]{1,0:T(8,128)(2,1)S(1)}, bf16[64,576]{1,0:T(8,128)(2,1)S(1)}) custom-call(bf16[512,640]{1,0:T(8,128)(2,1)S(1)} %get-tuple-element.53.query_ref, bf16[512,1152]{1,0:T(8,128)(2,1)S(1)} %get-tuple-element.54.kv_ref), custom_call_target="tpu_custom_call" | custom-call | flops 268435456 | bytes 1835008 | tf_op jit(solution)/shard_map/pallas_call | solution.py:75
  79.3 2.4 %collective-permute-start.19 = (bf16[64,576]{1,0:T(8,128)(2,1)S(1)}, bf16[64,576]{1,0:T(8,128)(2,1)S(1)}, u32[]{:S(2)}, u32[]{:S(2)}) collective-permute-start(bf16[64,576]{1,0:T(8,128)(2,1)S(1)} %get-tuple-element.58), channel_id=1, source_target_pairs={{0,4},{1,5},{2,6},{3,7},{4,0},{5,1},{6,2},{7,3},{8,12},{9,13},{10,... | collective-permute-start | bytes 221192 | tf_op jit(solution)/shard_map/ppermute | solution.py:28
  81.7 2.4 %collective-permute-start.23 = (bf16[64,576]{1,0:T(8,128)(2,1)S(1)}, bf16[64,576]{1,0:T(8,128)(2,1)S(1)}, u32[]{:S(2)}, u32[]{:S(2)}) collective-permute-start(bf16[64,576]{1,0:T(8,128)(2,1)S(1)} %get-tuple-element.62), channel_id=1, source_target_pairs={{0,12},{1,13},{2,14},{3,15},{4,8},{5,9},{6,10},{7,11},{8,4},{9,5},... | collective-permute-start | bytes 221192 | tf_op jit(solution)/shard_map/ppermute | solution.py:28
  84.1 2.4 %shard_map.107 = (bf16[64,576]{1,0:T(8,128)(2,1)S(1)}, bf16[64,576]{1,0:T(8,128)(2,1)S(1)}, bf16[64,576]{1,0:T(8,128)(2,1)S(1)}, bf16[64,576]{1,0:T(8,128)(2,1)S(1)}) custom-call(bf16[512,640]{1,0:T(8,128)(2,1)S(1)} %get-tuple-element.53.query_ref, bf16[512,1152]{1,0:T(8,128)(2,1)S(1)} %get-tuple-element.54.kv_ref), custom_call_target="tpu_custom_call" | custom-call | flops 268435456 | bytes 1835008 | tf_op jit(solution)/shard_map/pallas_call | solution.py:75
  86.5 1.1 %collective-permute-start.18 = (bf16[64,576]{1,0:T(8,128)(2,1)S(1)}, bf16[64,576]{1,0:T(8,128)(2,1)S(1)}, u32[]{:S(2)}, u32[]{:S(2)}) collective-permute-start(bf16[64,576]{1,0:T(8,128)(2,1)S(1)} %get-tuple-element.57), channel_id=1, source_target_pairs={{0,4},{1,5},{2,6},{3,7},{4,0},{5,1},{6,2},{7,3},{8,12},{9,13},{10,... | collective-permute-start | bytes 221192 | tf_op jit(solution)/shard_map/ppermute | solution.py:28
  87.6 0.9 collective-permute-start.20
  88.5 2.4 %collective-permute-start.22 = (bf16[64,576]{1,0:T(8,128)(2,1)S(1)}, bf16[64,576]{1,0:T(8,128)(2,1)S(1)}, u32[]{:S(2)}, u32[]{:S(2)}) collective-permute-start(bf16[64,576]{1,0:T(8,128)(2,1)S(1)} %get-tuple-element.61), channel_id=1, source_target_pairs={{0,12},{1,13},{2,14},{3,15},{4,8},{5,9},{6,10},{7,11},{8,4},{9,5},... | collective-permute-start | bytes 221192 | tf_op jit(solution)/shard_map/ppermute | solution.py:28
  91.0 1.2 %shard_map.105.after_ref = f32[512,1152]{1,0:T(8,128)S(1)} custom-call(bf16[128,1152]{1,0:T(8,128)(2,1)S(1)} %get-tuple-element.34.refs_0_, bf16[128,1152]{1,0:T(8,128)(2,1)S(1)} %get-tuple-element.35.refs_1_, bf16[128,1152]{1,0:T(8,128)(2,1)S(1)} %get-tuple-element.36.refs_2_, bf16[128,1152]{1,0:T(8,128)(2,1)S(1)} %get-tuple-element.37.refs_3_, ...), custom_call_target="tpu_custom_call" | custom-call | flops 679477248 | bytes 3124224 | tf_op jit(solution)/shard_map/pallas_call | solution.py:75
  92.2 5.2 %collective-permute-done.20.refs_4_ = bf16[64,576]{1,0:T(8,128)(2,1)S(1)} collective-permute-done((bf16[64,576]{1,0:T(8,128)(2,1)S(1)}, bf16[64,576]{1,0:T(8,128)(2,1)S(1)}, u32[]{:S(2)}, u32[]{:S(2)}) %collective-permute-start.20) | collective-permute-done | bytes 73760 | tf_op jit(solution)/shard_map/ppermute | solution.py:28
  97.5 2.1 %block_output.1 = f32[512,1152]{1,0:T(8,128)} custom-call(s32[1]{0:T(128)} %bitcast.slot_ref, f32[512,1152]{1,0:T(8,128)S(1)} %shard_map.105.after_ref, bf16[576,1152]{1,0:T(8,128)(2,1)S(1)} %copy-done.2, f32[6,1152]{1,0:T(8,128)S(1)} %multiply_add_fusion.refs_5_.refs_13_.refs_14_.modulation_ref, bf16[64,576]{1,0:T(8,128)(2,1)S(1)} %get-tuple-element.55.refs_0_, ...), custom_call_target="tpu_custom_call" | custom-call | tf_op jit(solution)/shard_map/block_output/pallas_call | solution.py:539
  (40 shorter events, 0.2 us)
Async XLA Ops:
  0.0 19.4 %copy-start = (s32[4]{0:T(128)S(1)}, s32[4]{0:T(128)}, u32[]{:S(2)}) copy-start(s32[4]{0:T(128)} %param.15) | copy-start | bytes 52
  0.0 8.3 %copy-start.3 = (bf16[512,1152]{1,0:T(8,128)(2,1)S(1)}, bf16[512,1152]{1,0:T(8,128)(2,1)}, u32[]{:S(2)}) copy-start(bf16[512,1152]{1,0:T(8,128)(2,1)} %tokens_ref.1) | copy-start | bytes 3538948
  0.0 35.7 %collective-permute-start = (bf16[512,1152]{1,0:T(8,128)(2,1)}, bf16[512,1152]{1,0:T(8,128)(2,1)S(1)}, u32[]{:S(2)}, u32[]{:S(2)}) collective-permute-start(bf16[512,1152]{1,0:T(8,128)(2,1)} %kv_ref.1), channel_id=1, source_target_pairs={{0,1},{1,0},{2,3},{3,2},{4,5},{5,4},{6,7},{7,6},{8,9},{9,8},{10,11... | collective-permute-start | bytes 3538952 | tf_op jit(solution)/shard_map/ppermute | solution.py:28
  0.5 1.3 %copy-start.4 = (bf16[512,1152]{1,0:T(8,128)(2,1)S(1)}, bf16[512,1152]{1,0:T(8,128)(2,1)}, u32[]{:S(2)}) copy-start(bf16[512,1152]{1,0:T(8,128)(2,1)} %kv_ref.1) | copy-start | bytes 3538948
  3.1 0.6 copy-start.7
  3.7 15.7 %collective-permute-start.1 = (bf16[512,512]{1,0:T(8,128)(2,1)}, bf16[512,512]{1,0:T(8,128)(2,1)}, u32[]{:S(2)}, u32[]{:S(2)}) collective-permute-start(bf16[512,512]{1,0:T(8,128)(2,1)} %get-tuple-element.40), channel_id=1, source_target_pairs={{0,2},{1,3},{2,0},{3,1},{4,6},{5,7},{6,4},{7,5},{8,10},{9,11},{10,... | collective-permute-start | bytes 1572872 | tf_op jit(solution)/shard_map/ppermute | solution.py:28
  6.3 19.3 %collective-permute-start.2 = (bf16[512,256]{1,0:T(8,128)(2,1)}, bf16[512,256]{1,0:T(8,128)(2,1)}, u32[]{:S(2)}, u32[]{:S(2)}) collective-permute-start(bf16[512,256]{1,0:T(8,128)(2,1)} %get-tuple-element.41), channel_id=1, source_target_pairs={{0,2},{1,3},{2,0},{3,1},{4,6},{5,7},{6,4},{7,5},{8,10},{9,11},{10,... | collective-permute-start | bytes 786440 | tf_op jit(solution)/shard_map/ppermute | solution.py:28
  6.3 24.0 %collective-permute-start.3 = (bf16[512,256]{1,0:T(8,128)(2,1)}, bf16[512,256]{1,0:T(8,128)(2,1)}, u32[]{:S(2)}, u32[]{:S(2)}) collective-permute-start(bf16[512,256]{1,0:T(8,128)(2,1)} %get-tuple-element.42), channel_id=1, source_target_pairs={{0,2},{1,3},{2,0},{3,1},{4,6},{5,7},{6,4},{7,5},{8,10},{9,11},{10,... | collective-permute-start | bytes 786440 | tf_op jit(solution)/shard_map/ppermute | solution.py:28
  8.6 47.4 %collective-permute-start.10 = (bf16[128,1152]{1,0:T(8,128)(2,1)S(1)}, bf16[128,1152]{1,0:T(8,128)(2,1)}, u32[]{:S(2)}, u32[]{:S(2)}) collective-permute-start(bf16[128,1152]{1,0:T(8,128)(2,1)S(1)} %get-tuple-element.36.refs_2_), channel_id=1, source_target_pairs={{0,8},{1,9},{2,10},{3,11},{4,12},{5,13},{6,14},{7,15},{8,0},{9,1},... | collective-permute-start | bytes 884744 | tf_op jit(solution)/shard_map/ppermute | solution.py:28
  19.4 14.8 %collective-permute-start.4 = (bf16[512,512]{1,0:T(8,128)(2,1)}, bf16[512,512]{1,0:T(8,128)(2,1)S(1)}, u32[]{:S(2)}, u32[]{:S(2)}) collective-permute-start(bf16[512,512]{1,0:T(8,128)(2,1)} %collective-permute-done.1.refs_3_), channel_id=1, source_target_pairs={{0,1},{1,0},{2,3},{3,2},{4,5},{5,4},{6,7},{7,6},{8,9},{9,8},{10,11... | collective-permute-start | bytes 1572872 | tf_op jit(solution)/shard_map/ppermute | solution.py:28
  20.1 2.1 %copy-start.5 = (bf16[3,1152,576]{1,2,0:T(8,128)(2,1)S(1)}, bf16[3,1152,576]{1,2,0:T(8,128)(2,1)}, u32[]{:S(2)}) copy-start(bf16[3,1152,576]{1,2,0:T(8,128)(2,1)} %param.16) | copy-start | bytes 11943940
  22.2 12.0 %copy-start.8 = (bf16[512,128]{1,0:T(8,128)(2,1)S(1)}, bf16[512,128]{1,0:T(8,128)(2,1)}, u32[]{:S(2)}) copy-start(bf16[512,128]{1,0:T(8,128)(2,1)} %copy-done.7) | copy-start | bytes 393220
  25.6 14.5 %collective-permute-start.5 = (bf16[512,256]{1,0:T(8,128)(2,1)}, bf16[512,256]{1,0:T(8,128)(2,1)S(1)}, u32[]{:S(2)}, u32[]{:S(2)}) collective-permute-start(bf16[512,256]{1,0:T(8,128)(2,1)} %collective-permute-done.2.refs_4_), channel_id=1, source_target_pairs={{0,1},{1,0},{2,3},{3,2},{4,5},{5,4},{6,7},{7,6},{8,9},{9,8},{10,11... | collective-permute-start | bytes 786440 | tf_op jit(solution)/shard_map/ppermute | solution.py:28
  30.3 28.4 %collective-permute-start.11 = (bf16[128,1152]{1,0:T(8,128)(2,1)S(1)}, bf16[128,1152]{1,0:T(8,128)(2,1)S(1)}, u32[]{:S(2)}, u32[]{:S(2)}) collective-permute-start(bf16[128,1152]{1,0:T(8,128)(2,1)S(1)} %get-tuple-element.37.refs_3_), channel_id=1, source_target_pairs={{0,12},{1,13},{2,14},{3,15},{4,8},{5,9},{6,10},{7,11},{8,4},{9,5},... | collective-permute-start | bytes 884744 | tf_op jit(solution)/shard_map/ppermute | solution.py:28
  34.2 5.8 %collective-permute-start.7 = (bf16[512,128]{1,0:T(8,128)(2,1)S(1)}, bf16[512,128]{1,0:T(8,128)(2,1)S(1)}, u32[]{:S(2)}, u32[]{:S(2)}) collective-permute-start(bf16[512,128]{1,0:T(8,128)(2,1)S(1)} %copy-done.8), channel_id=1, source_target_pairs={{0,2},{1,3},{2,0},{3,1},{4,6},{5,7},{6,4},{7,5},{8,10},{9,11},{10,... | collective-permute-start | bytes 393224 | tf_op jit(solution)/shard_map/ppermute | solution.py:28
  35.7 9.2 %collective-permute-start.6 = (bf16[512,256]{1,0:T(8,128)(2,1)}, bf16[512,256]{1,0:T(8,128)(2,1)S(1)}, u32[]{:S(2)}, u32[]{:S(2)}) collective-permute-start(bf16[512,256]{1,0:T(8,128)(2,1)} %collective-permute-done.3.refs_5_), channel_id=1, source_target_pairs={{0,1},{1,0},{2,3},{3,2},{4,5},{5,4},{6,7},{7,6},{8,9},{9,8},{10,11... | collective-permute-start | bytes 786440 | tf_op jit(solution)/shard_map/ppermute | solution.py:28
  40.0 19.5 %collective-permute-start.9 = (bf16[128,1152]{1,0:T(8,128)(2,1)S(1)}, bf16[128,1152]{1,0:T(8,128)(2,1)S(1)}, u32[]{:S(2)}, u32[]{:S(2)}) collective-permute-start(bf16[128,1152]{1,0:T(8,128)(2,1)S(1)} %get-tuple-element.35.refs_1_), channel_id=1, source_target_pairs={{0,4},{1,5},{2,6},{3,7},{4,0},{5,1},{6,2},{7,3},{8,12},{9,13},{10,... | collective-permute-start | bytes 884744 | tf_op jit(solution)/shard_map/ppermute | solution.py:28
  40.1 9.4 %collective-permute-start.8 = (bf16[512,128]{1,0:T(8,128)(2,1)S(1)}, bf16[512,128]{1,0:T(8,128)(2,1)S(1)}, u32[]{:S(2)}, u32[]{:S(2)}) collective-permute-start(bf16[512,128]{1,0:T(8,128)(2,1)S(1)} %collective-permute-done.7.refs_6_), channel_id=1, source_target_pairs={{0,1},{1,0},{2,3},{3,2},{4,5},{5,4},{6,7},{7,6},{8,9},{9,8},{10,11... | collective-permute-start | bytes 393224 | tf_op jit(solution)/shard_map/ppermute | solution.py:28
  49.5 22.0 %copy-start.1 = (bf16[576,1152]{1,0:T(8,128)(2,1)S(1)}, bf16[576,1152]{1,0:T(8,128)(2,1)}, u32[]{:S(2)}) copy-start(bf16[576,1152]{1,0:T(8,128)(2,1)} %refs_12_.3) | copy-start | bytes 3981316
  49.5 22.0 %copy-start.6 = (bf16[3,1152,576]{1,2,0:T(8,128)(2,1)S(1)}, bf16[3,1152,576]{1,2,0:T(8,128)(2,1)}, u32[]{:S(2)}) copy-start(bf16[3,1152,576]{1,2,0:T(8,128)(2,1)} %param.18) | copy-start | bytes 11943940
  54.0 6.4 %collective-permute-start.13 = (bf16[128,192]{1,0:T(8,128)(2,1)S(1)}, bf16[128,192]{1,0:T(8,128)(2,1)S(1)}, u32[]{:S(2)}, u32[]{:S(2)}) collective-permute-start(bf16[128,192]{1,0:T(8,128)(2,1)S(1)} %get-tuple-element.48.refs_7_), channel_id=1, source_target_pairs={{0,4},{1,5},{2,6},{3,7},{4,0},{5,1},{6,2},{7,3},{8,12},{9,13},{10,... | collective-permute-start | bytes 147464 | tf_op jit(solution)/shard_map/ppermute | solution.py:28
  55.9 7.9 %collective-permute-start.15 = (bf16[128,192]{1,0:T(8,128)(2,1)S(1)}, bf16[128,192]{1,0:T(8,128)(2,1)S(1)}, u32[]{:S(2)}, u32[]{:S(2)}) collective-permute-start(bf16[128,192]{1,0:T(8,128)(2,1)S(1)} %get-tuple-element.50.refs_9_), channel_id=1, source_target_pairs={{0,8},{1,9},{2,10},{3,11},{4,12},{5,13},{6,14},{7,15},{8,0},{9,1},... | collective-permute-start | bytes 147464 | tf_op jit(solution)/shard_map/ppermute | solution.py:28
  56.0 7.8 %collective-permute-start.17 = (bf16[128,192]{1,0:T(8,128)(2,1)S(1)}, bf16[128,192]{1,0:T(8,128)(2,1)S(1)}, u32[]{:S(2)}, u32[]{:S(2)}) collective-permute-start(bf16[128,192]{1,0:T(8,128)(2,1)S(1)} %get-tuple-element.52.refs_11_), channel_id=1, source_target_pairs={{0,12},{1,13},{2,14},{3,15},{4,8},{5,9},{6,10},{7,11},{8,4},{9,5},... | collective-permute-start | bytes 147464 | tf_op jit(solution)/shard_map/ppermute | solution.py:28
  58.7 6.5 %collective-permute-start.12 = (bf16[128,384]{1,0:T(8,128)(2,1)S(1)}, bf16[128,384]{1,0:T(8,128)(2,1)S(1)}, u32[]{:S(2)}, u32[]{:S(2)}) collective-permute-start(bf16[128,384]{1,0:T(8,128)(2,1)S(1)} %get-tuple-element.47.refs_6_), channel_id=1, source_target_pairs={{0,4},{1,5},{2,6},{3,7},{4,0},{5,1},{6,2},{7,3},{8,12},{9,13},{10,... | collective-permute-start | bytes 294920 | tf_op jit(solution)/shard_map/ppermute | solution.py:28
  59.5 12.0 %collective-permute-start.14 = (bf16[128,384]{1,0:T(8,128)(2,1)S(1)}, bf16[128,384]{1,0:T(8,128)(2,1)S(1)}, u32[]{:S(2)}, u32[]{:S(2)}) collective-permute-start(bf16[128,384]{1,0:T(8,128)(2,1)S(1)} %get-tuple-element.49.refs_8_), channel_id=1, source_target_pairs={{0,8},{1,9},{2,10},{3,11},{4,12},{5,13},{6,14},{7,15},{8,0},{9,1},... | collective-permute-start | bytes 294920 | tf_op jit(solution)/shard_map/ppermute | solution.py:28
  60.5 11.1 %collective-permute-start.16 = (bf16[128,384]{1,0:T(8,128)(2,1)S(1)}, bf16[128,384]{1,0:T(8,128)(2,1)S(1)}, u32[]{:S(2)}, u32[]{:S(2)}) collective-permute-start(bf16[128,384]{1,0:T(8,128)(2,1)S(1)} %get-tuple-element.51.refs_10_), channel_id=1, source_target_pairs={{0,12},{1,13},{2,14},{3,15},{4,8},{5,9},{6,10},{7,11},{8,4},{9,5},... | collective-permute-start | bytes 294920 | tf_op jit(solution)/shard_map/ppermute | solution.py:28
  79.3 9.2 %collective-permute-start.19 = (bf16[64,576]{1,0:T(8,128)(2,1)S(1)}, bf16[64,576]{1,0:T(8,128)(2,1)S(1)}, u32[]{:S(2)}, u32[]{:S(2)}) collective-permute-start(bf16[64,576]{1,0:T(8,128)(2,1)S(1)} %get-tuple-element.58), channel_id=1, source_target_pairs={{0,4},{1,5},{2,6},{3,7},{4,0},{5,1},{6,2},{7,3},{8,12},{9,13},{10,... | collective-permute-start | bytes 221192 | tf_op jit(solution)/shard_map/ppermute | solution.py:28
  81.7 10.5 %collective-permute-start.21 = (bf16[64,576]{1,0:T(8,128)(2,1)S(1)}, bf16[64,576]{1,0:T(8,128)(2,1)S(1)}, u32[]{:S(2)}, u32[]{:S(2)}) collective-permute-start(bf16[64,576]{1,0:T(8,128)(2,1)S(1)} %get-tuple-element.60), channel_id=1, source_target_pairs={{0,8},{1,9},{2,10},{3,11},{4,12},{5,13},{6,14},{7,15},{8,0},{9,1},... | collective-permute-start | bytes 221192 | tf_op jit(solution)/shard_map/ppermute | solution.py:28
  81.7 10.5 %collective-permute-start.23 = (bf16[64,576]{1,0:T(8,128)(2,1)S(1)}, bf16[64,576]{1,0:T(8,128)(2,1)S(1)}, u32[]{:S(2)}, u32[]{:S(2)}) collective-permute-start(bf16[64,576]{1,0:T(8,128)(2,1)S(1)} %get-tuple-element.62), channel_id=1, source_target_pairs={{0,12},{1,13},{2,14},{3,15},{4,8},{5,9},{6,10},{7,11},{8,4},{9,5},... | collective-permute-start | bytes 221192 | tf_op jit(solution)/shard_map/ppermute | solution.py:28
  86.5 5.7 %collective-permute-start.18 = (bf16[64,576]{1,0:T(8,128)(2,1)S(1)}, bf16[64,576]{1,0:T(8,128)(2,1)S(1)}, u32[]{:S(2)}, u32[]{:S(2)}) collective-permute-start(bf16[64,576]{1,0:T(8,128)(2,1)S(1)} %get-tuple-element.57), channel_id=1, source_target_pairs={{0,4},{1,5},{2,6},{3,7},{4,0},{5,1},{6,2},{7,3},{8,12},{9,13},{10,... | collective-permute-start | bytes 221192 | tf_op jit(solution)/shard_map/ppermute | solution.py:28
  87.6 9.8 %collective-permute-start.20 = (bf16[64,576]{1,0:T(8,128)(2,1)S(1)}, bf16[64,576]{1,0:T(8,128)(2,1)S(1)}, u32[]{:S(2)}, u32[]{:S(2)}) collective-permute-start(bf16[64,576]{1,0:T(8,128)(2,1)S(1)} %get-tuple-element.59), channel_id=1, source_target_pairs={{0,8},{1,9},{2,10},{3,11},{4,12},{5,13},{6,14},{7,15},{8,0},{9,1},... | collective-permute-start | bytes 221192 | tf_op jit(solution)/shard_map/ppermute | solution.py:28
  88.5 8.9 %copy-start.2 = (bf16[576,1152]{1,0:T(8,128)(2,1)S(1)}, bf16[576,1152]{1,0:T(8,128)(2,1)}, u32[]{:S(2)}) copy-start(bf16[576,1152]{1,0:T(8,128)(2,1)} %weight_ref.1) | copy-start | bytes 3981316
  88.5 8.9 %collective-permute-start.22 = (bf16[64,576]{1,0:T(8,128)(2,1)S(1)}, bf16[64,576]{1,0:T(8,128)(2,1)S(1)}, u32[]{:S(2)}, u32[]{:S(2)}) collective-permute-start(bf16[64,576]{1,0:T(8,128)(2,1)S(1)} %get-tuple-element.61), channel_id=1, source_target_pairs={{0,12},{1,13},{2,14},{3,15},{4,8},{5,9},{6,10},{7,11},{8,4},{9,5},... | collective-permute-start | bytes 221192 | tf_op jit(solution)/shard_map/ppermute | solution.py:28
where the time goes:
time: 100 us; the launch traced here: 99.7 us
  Pallas kernels  35.9 us (36%)
  starting transfers between devices  32.5 us (32%)
  waiting for transfers between devices  24.3 us (24%)
  local copies, waits for them, and re-layouts  4.71 us (5%)
  other arithmetic  1.19 us (1%)
  between operations  1.05 us (1%)
    ppermute x24, starting transfers between devices, permute(): lax.ppermute(value, 'patch', [(source, target(source)) for source in rang...  32.5 us
    pallas_call x9, Pallas kernels, on_chip_call(): pl.pallas_call(kernel, out_shape=[pltpu.VMEM(shape, dtype) for shape, dty...  32.3 us
    ppermute x24, waiting for transfers between devices, permute(): lax.ppermute(value, 'patch', [(source, target(source)) for source in rang...  24.3 us
    unnamed x18, local copies, waits for them, and re-layouts  4.07 us
    pallas_call x1, Pallas kernels, output(): pl.pallas_call(functools.partial(output_kernel, frames=frames, halves=hal...  2.06 us
  transfers between devices with their start and end apart: 24, of which 6 were waited for; matrix products, arithmetic and copies ran while one was open for 2% of the time, Pallas kernels for 26%

commit v1 on v0

--- a/solution.py
+++ b/solution.py
@@ -3,6 +3,7 @@
 
 import jax
 import jax.numpy as jnp
+import numpy as np
 from jax import lax
 from jax.experimental import pallas as pl
 from jax.experimental.pallas import tpu as pltpu
@@ -45,15 +46,6 @@
     centered = activations - row_mean
     variance = jnp.mean(centered * centered, axis=-1, keepdims=True)
     return centered * lax.rsqrt(variance + epsilon)
-
-
-def sinusoid(position, feature_width):
-    half_width = feature_width // 2
-    frequencies = jnp.exp(
-        -math.log(10000.0) * jnp.arange(half_width, dtype=jnp.float32) / half_width
-    )
-    angles = jnp.asarray(position).astype(jnp.float32)[..., None] * frequencies
-    return jnp.concatenate([jnp.sin(angles), jnp.cos(angles)], axis=-1)
 
 
 def column_mask(first, width, dtype):
@@ -112,9 +104,9 @@
         in_specs=[pl.BlockSpec(memory_space=pltpu.HBM)],
         out_specs=vmem_specs(len(tiles)),
         scratch_shapes=[pltpu.SemaphoreType.DMA((sum(len(chunk) for chunk in tiles),))],
-        compiler_params=pltpu.CompilerParams(vmem_limit_bytes=4 * 2**20),
+        compiler_params=pltpu.CompilerParams(vmem_limit_bytes=2**20),
         name="chunks",
-    )(stale_kv)
+    )(pltpu.with_memory_space_constraint(stale_kv, pltpu.HBM))
 
 
 def piece_kernel(slot_ref, tokens_ref, *refs, frames):
@@ -144,9 +136,40 @@
         ],
         out_specs=vmem_specs(frames),
         scratch_shapes=[pltpu.SemaphoreType.DMA((frames,))],
-        compiler_params=pltpu.CompilerParams(vmem_limit_bytes=4 * 2**20),
+        compiler_params=pltpu.CompilerParams(vmem_limit_bytes=2**20),
         name="pieces",
-    )(slot, tokens)
+    )(slot, pltpu.with_memory_space_constraint(tokens, pltpu.HBM))
+
+
+def modulation_kernel(slot_ref, time_ref, order_ref, rate_ref, table_ref, mix_ref, out_ref, place_ref):
+    frames, feature_width = place_ref.shape
+    rows = -(-(frames + 1) // 8) * 8
+    row = lax.broadcasted_iota(jnp.int32, (rows, 1), 0)
+    position = jnp.where(row == frames, time_ref[0], 0)
+    for step in range(frames):
+        frame = order_ref[source_slot(slot_ref[0], step, frames)]
+        position = jnp.where(row == step, frame, position)
+    angles = position.astype(f32) * rate_ref[...]
+    column = lax.broadcasted_iota(jnp.int32, (rows, feature_width), 1)
+    waves = jnp.where(column < feature_width // 2, jnp.sin(angles), jnp.cos(angles))
+    place_ref[...] = waves[:frames]
+    out_ref[...] = table_ref[...] + mix_ref[...] * waves[frames : frames + 1]
+
+
+def modulate(slot, timestep, frame_order, mod_table, mod_mix):
+    frames, feature_width = frame_order.shape[0], mod_table.shape[1]
+    half = feature_width // 2
+    rates = np.exp(-math.log(10000.0) * np.arange(half) / half).astype(np.float32)
+    operands = [jnp.asarray(np.concatenate([rates, rates])[None]), mod_table, mod_mix]
+    operands = [pltpu.with_memory_space_constraint(array, pltpu.VMEM) for array in operands]
+    return pl.pallas_call(
+        modulation_kernel,
+        out_shape=[pltpu.VMEM(mod_table.shape, f32), pltpu.VMEM((frames, feature_width), f32)],
+        in_specs=[pl.BlockSpec(memory_space=pltpu.SMEM) for _ in range(3)] + vmem_specs(3),
+        out_specs=vmem_specs(2),
+        compiler_params=pltpu.CompilerParams(vmem_limit_bytes=2**20),
+        name="modulation",
+    )(slot, timestep, frame_order, *operands)
 
 
 def projection_kernel(*refs, frames, width):
@@ -174,7 +197,7 @@
         [*pieces, weight, modulation],
         [((rows, padded), bf16), ((rows, 2 * width), bf16)],
         2 * rows * feature_width * 3 * width,
-        16,
+        4,
     )
 
 
@@ -207,6 +230,7 @@
     plan = pair_plan(width, head_dim)
     count = len(tiles)
     position = 0
+    refs, (scores_ref, weights_ref) = refs[:-2], refs[-2:]
     query_ref, own_ref, peer_ref = refs[:3]
     near_refs = refs[3 : 3 + count]
     far_refs = refs[3 + count : 3 + 2 * count]
@@ -239,7 +263,8 @@
     def two(block, tile):
         return jnp.concatenate([block(tile), block(tile + 1)], axis=1)
 
-    def scores_of(pair, chunk):
+    def score(index):
+        chunk, pair = tasks[index]
         key_tile, key_lane, _, _ = plan[pair]
         window = query_ref[
             chunk * QUERY_ROWS : (chunk + 1) * QUERY_ROWS, key_tile * LANES : (key_tile + 2) * LANES
@@ -251,22 +276,32 @@
             ],
             axis=0,
         )
-        return [
-            lax.dot_general(stacked, two(block, key_tile), NT, preferred_element_type=f32)
-            for block in blocks
-        ]
-
-    def mix(pair, scores):
-        _, key_lane, value_tile, value_lane = plan[pair]
-        top = functools.reduce(jnp.maximum, [jnp.max(s, axis=-1, keepdims=True) for s in scores])
-        top = top * scale
-        weights = [jnp.exp2(s * scale - top) for s in scores]
-        total = functools.reduce(jnp.add, [jnp.sum(w, axis=-1, keepdims=True) for w in weights])
+        for number, block in enumerate(blocks):
+            scores_ref[index % 2, :, number * rows : (number + 1) * rows] = lax.dot_general(
+                stacked, two(block, key_tile), NT, preferred_element_type=f32
+            )
+
+    def weigh(index):
+        totals = []
+        for row in range(0, 2 * QUERY_ROWS, 16):
+            scores = scores_ref[index % 2, row : row + 16, :]
+            top = jnp.max(scores, axis=-1, keepdims=True) * scale
+            weights = jnp.exp2(scores * scale - top)
+            totals.append(jnp.sum(weights, axis=-1, keepdims=True))
+            weights_ref[index % 2, row : row + 16, :] = weights.astype(bf16)
+        return jnp.concatenate(totals, axis=0)
+
+    def mix(index, total):
+        _, key_lane, value_tile, value_lane = plan[tasks[index][1]]
         mixed = functools.reduce(
             jnp.add,
             [
-                jnp.dot(w.astype(bf16), two(block, value_tile), preferred_element_type=f32)
-                for w, block in zip(weights, blocks)
+                jnp.dot(
+                    weights_ref[index % 2, :, number * rows : (number + 1) * rows],
+                    two(block, value_tile),
+                    preferred_element_type=f32,
+                )
+                for number, block in enumerate(blocks)
             ],
         )
         mixed = mixed / total
@@ -275,21 +310,18 @@
         ] * column_mask(value_lane + head_dim, head_dim, f32)
         return pltpu.roll(joined, (key_lane - value_lane) % (2 * LANES), 1)
 
-    chunks = rows // QUERY_ROWS
-    tasks = [(chunk, pair) for chunk in range(chunks) for pair in group]
-    pending = scores_of(tasks[0][1], tasks[0][0])
+    tasks = [(chunk, pair) for chunk in range(rows // QUERY_ROWS) for pair in group]
     parts = {}
-    for index, (chunk, pair) in enumerate(tasks):
-        scores = pending
-        if index + 1 < len(tasks):
-            pending = scores_of(tasks[index + 1][1], tasks[index + 1][0])
-        joined = mix(pair, scores)
+
+    def finish(index, total):
+        chunk, pair = tasks[index]
+        joined = mix(index, total)
         tile = plan[pair][0]
         for side in range(2):
             half = joined[:, side * LANES : (side + 1) * LANES]
             parts[tile + side] = parts[tile + side] + half if tile + side in parts else half
         if pair != group[-1]:
-            continue
+            return
         at = chunk * QUERY_ROWS
         for number, tile in enumerate(held):
             old = held_ref[at : at + QUERY_ROWS, number * LANES : (number + 1) * LANES].astype(f32)
@@ -304,7 +336,17 @@
                 out_refs[at // piece + sub][...] = values[
                     sub * piece : (sub + 1) * piece, :width_out
                 ]
-        parts = {}
+        parts.clear()
+
+    score(0)
+    total = None
+    for index in range(len(tasks)):
+        if index + 1 < len(tasks):
+            score(index + 1)
+        if index > 0:
+            finish(index - 1, total)
+        total = weigh(index)
+    finish(len(tasks) - 1, total)
 
 
 def tile_flow(width, head_dim):
@@ -351,8 +393,12 @@
         operands,
         shapes,
         len(group) * 2 * rows * keys * 256 * 4,
-        24,
+        8,
         len(group) * 2 * rows * keys,
+        [
+            pltpu.VMEM((2, 2 * QUERY_ROWS, keys), f32),
+            pltpu.VMEM((2, 2 * QUERY_ROWS, keys), bf16),
+        ],
     )
     results = list(results)
     carry = results.pop() if kept else None
@@ -418,7 +464,7 @@
         ],
         [((rows, padded), bf16), ((rows, 2 * width), bf16)],
         2 * rows * feature_width * width * 4,
-        20,
+        6,
     )
 
 
@@ -485,7 +531,7 @@
         [query, kv],
         [((piece, width), bf16) for _ in range(frames)],
         2 * rows * 128 * 256 * 16,
-        8,
+        2,
         rows * 128 * 8,
     )
 
@@ -507,7 +553,7 @@
         [*tokens, *[part for frame in mixed for part in frame], weight, modulation],
         [((rows, feature_width), f32)],
         2 * rows * feature_width * width,
-        16,
+        4,
     )[0]
 
 
@@ -545,7 +591,7 @@
             pltpu.VMEM((rows, feature_width), f32),
             pltpu.SemaphoreType.DMA((frames,)),
         ],
-        compiler_params=pltpu.CompilerParams(vmem_limit_bytes=16 * 2**20),
+        compiler_params=pltpu.CompilerParams(vmem_limit_bytes=4 * 2**20),
         name="block_output",
     )(slot, *[pltpu.with_memory_space_constraint(array, pltpu.VMEM) for array in operands])
 
@@ -593,10 +639,7 @@
     there = [pieces[0]]
     there += [permute(pieces[s], ahead(s)) for s in range(1, frames)]
 
-    modulation = mod_table + mod_mix * sinusoid(timestep[0], feature_width)[None, :]
-    sources = source_slot(slot, jnp.arange(frames), frames)
-    places = sinusoid(frame_order[sources], feature_width)
-
+    modulation, places = modulate(slot_word, timestep, frame_order, mod_table, mod_mix)
     query, own_kv = projections(
         pieces,
         jnp.swapaxes(spatial_qkv, 1, 2).reshape(3 * width, feature_width),

time: 100 us -> 97.5 us (0.975)
  waiting for transfers between devices: 24.3 us -> 29.5 us
  local copies, waits for them, and re-layouts: 4.71 us -> 2.16 us
  Pallas kernels: 35.9 us -> 34 us
  starting transfers between devices: 32.5 us -> 30.6 us
  other arithmetic: 1.19 us -> 0 us
    ppermute x24, waiting for transfers between devices: 24.3 us -> 29.5 us  [permute(): lax.ppermute(value, 'patch', [(source, target(source)) for source in rang...]
    pallas_call x9, Pallas kernels: 32.3 us -> 28.5 us  [on_chip_call(): pl.pallas_call(kernel, out_shape=[pltpu.VMEM(shape, dtype) for shape, dty...]
    ppermute x24, starting transfers between devices: 32.5 us -> 30.6 us  [permute(): lax.ppermute(value, 'patch', [(source, target(source)) for source in rang...]
    unnamed x18 -> x16, local copies, waits for them, and re-layouts: 4.07 us -> 2.16 us
  transfers between devices with their start and end apart: 24 -> 24, of which waited for: 6 -> 6; matrix products, arithmetic and copies ran while one was open for 2% -> 0% of each run, Pallas kernels for 26% -> 26%
where the time goes in v1:
time: 97.5 us; the launch traced here: 97.3 us
  Pallas kernels  34 us (35%)
  starting transfers between devices  30.6 us (31%)
  waiting for transfers between devices  29.5 us (30%)
  local copies, waits for them, and re-layouts  2.16 us (2%)
  between operations  1.06 us (1%)
    ppermute x24, starting transfers between devices, permute(): lax.ppermute(value, 'patch', [(source, target(source)) for source in rang...  30.6 us
    ppermute x24, waiting for transfers between devices, permute(): lax.ppermute(value, 'patch', [(source, target(source)) for source in rang...  29.5 us
    pallas_call x9, Pallas kernels, on_chip_call(): pl.pallas_call(kernel, out_shape=[pltpu.VMEM(shape, dtype) for shape, dty...  28.5 us
    unnamed x16, local copies, waits for them, and re-layouts  2.16 us
    pallas_call x1, Pallas kernels, output(): pl.pallas_call(functools.partial(output_kernel, frames=frames, halves=hal...  2.06 us
  transfers between devices with their start and end apart: 24, of which 6 were waited for; matrix products, arithmetic and copies ran while one was open for 0% of the time, Pallas kernels for 26%

profile of v1, /device:TPU:0, one launch (start us, length us, event | category | flops | bytes accessed | tf_op | source)
XLA Modules:
  0.0 97.3 jit_solution(4828373215958450090)
XLA Ops:
  0.0 0.6 collective-permute-start
  0.6 1.4 %chunks.1 = (bf16[512,512]{1,0:T(8,128)(2,1)S(1)}, bf16[512,256]{1,0:T(8,128)(2,1)S(1)}, bf16[512,256]{1,0:T(8,128)(2,1)S(1)}, bf16[512,128]{1,0:T(8,128)(2,1)S(1)}) custom-call(bf16[512,1152]{1,0:T(8,128)(2,1)} %kv_ref.1), custom_call_target="tpu_custom_call" | custom-call | tf_op jit(solution)/shard_map/chunks/pallas_call | solution.py:101
  2.0 2.6 %collective-permute-start.1 = (bf16[512,512]{1,0:T(8,128)(2,1)S(1)}, bf16[512,512]{1,0:T(8,128)(2,1)S(1)}, u32[]{:S(2)}, u32[]{:S(2)}) collective-permute-start(bf16[512,512]{1,0:T(8,128)(2,1)S(1)} %get-tuple-element.43), channel_id=1, source_target_pairs={{0,2},{1,3},{2,0},{3,1},{4,6},{5,7},{6,4},{7,5},{8,10},{9,11},{10,... | collective-permute-start | bytes 1572872 | tf_op jit(solution)/shard_map/ppermute | solution.py:29
  4.6 12.6 %collective-permute-done.1.refs_3_ = bf16[512,512]{1,0:T(8,128)(2,1)S(1)} collective-permute-done((bf16[512,512]{1,0:T(8,128)(2,1)S(1)}, bf16[512,512]{1,0:T(8,128)(2,1)S(1)}, u32[]{:S(2)}, u32[]{:S(2)}) %collective-permute-start.1) | collective-permute-done | bytes 524320 | tf_op jit(solution)/shard_map/ppermute | solution.py:29
  17.2 0.0 collective-permute-start.4
  17.2 1.7 %collective-permute-start.2 = (bf16[512,256]{1,0:T(8,128)(2,1)S(1)}, bf16[512,256]{1,0:T(8,128)(2,1)S(1)}, u32[]{:S(2)}, u32[]{:S(2)}) collective-permute-start(bf16[512,256]{1,0:T(8,128)(2,1)S(1)} %get-tuple-element.44), channel_id=1, source_target_pairs={{0,2},{1,3},{2,0},{3,1},{4,6},{5,7},{6,4},{7,5},{8,10},{9,11},{10,... | collective-permute-start | bytes 786440 | tf_op jit(solution)/shard_map/ppermute | solution.py:29
  18.9 0.3 collective-permute-start.3
  19.2 1.3 %pieces.1 = (bf16[128,1152]{1,0:T(8,128)(2,1)S(1)}, bf16[128,1152]{1,0:T(8,128)(2,1)S(1)}, bf16[128,1152]{1,0:T(8,128)(2,1)S(1)}, bf16[128,1152]{1,0:T(8,128)(2,1)S(1)}) custom-call(s32[1]{0:T(128)} %bitcast.slot_ref, bf16[512,1152]{1,0:T(8,128)(2,1)} %tokens_ref.1), custom_call_target="tpu_custom_call" | custom-call | tf_op jit(solution)/shard_map/pieces/pallas_call | solution.py:130
  20.5 2.9 %collective-permute-start.10 = (bf16[128,1152]{1,0:T(8,128)(2,1)S(1)}, bf16[128,1152]{1,0:T(8,128)(2,1)S(1)}, u32[]{:S(2)}, u32[]{:S(2)}) collective-permute-start(bf16[128,1152]{1,0:T(8,128)(2,1)S(1)} %get-tuple-element.38.refs_2_), channel_id=1, source_target_pairs={{0,8},{1,9},{2,10},{3,11},{4,12},{5,13},{6,14},{7,15},{8,0},{9,1},... | collective-permute-start | bytes 884744 | tf_op jit(solution)/shard_map/ppermute | solution.py:29
  24.0 0.7 modulation.1
  24.7 1.6 %collective-permute-done.2.refs_4_ = bf16[512,256]{1,0:T(8,128)(2,1)S(1)} collective-permute-done((bf16[512,256]{1,0:T(8,128)(2,1)S(1)}, bf16[512,256]{1,0:T(8,128)(2,1)S(1)}, u32[]{:S(2)}, u32[]{:S(2)}) %collective-permute-start.2) | collective-permute-done | bytes 262176 | tf_op jit(solution)/shard_map/ppermute | solution.py:29
  26.4 0.0 collective-permute-start.5
  26.4 2.1 %copy-done.6 = bf16[3,1152,576]{1,2,0:T(8,128)(2,1)S(1)} copy-done((bf16[3,1152,576]{1,2,0:T(8,128)(2,1)S(1)}, bf16[3,1152,576]{1,2,0:T(8,128)(2,1)}, u32[]{:S(2)}) %copy-start.6) | copy-done | bytes 3981336
  28.5 3.4 %shard_map.109 = (bf16[512,640]{1,0:T(8,128)(2,1)S(1)}, bf16[512,1152]{1,0:T(8,128)(2,1)S(1)}) custom-call(bf16[128,1152]{1,0:T(8,128)(2,1)S(1)} %get-tuple-element.36.refs_0_, bf16[128,1152]{1,0:T(8,128)(2,1)S(1)} %get-tuple-element.37.refs_1_, bf16[128,1152]{1,0:T(8,128)(2,1)S(1)} %get-tuple-element.38.refs_2_, ...), custom_call_target="tpu_custom_call" | custom-call | flops 2038431744 | bytes 5188608 | tf_op jit(solution)/shard_map/pallas_call | solution.py:67
  31.9 3.9 %collective-permute-start.11 = (bf16[128,1152]{1,0:T(8,128)(2,1)S(1)}, bf16[128,1152]{1,0:T(8,128)(2,1)S(1)}, u32[]{:S(2)}, u32[]{:S(2)}) collective-permute-start(bf16[128,1152]{1,0:T(8,128)(2,1)S(1)} %get-tuple-element.39.refs_3_), channel_id=1, source_target_pairs={{0,12},{1,13},{2,14},{3,15},{4,8},{5,9},{6,10},{7,11},{8,4},{9,5},... | collective-permute-start | bytes 884744 | tf_op jit(solution)/shard_map/ppermute | solution.py:29
  35.8 1.5 %collective-permute-start.7 = (bf16[512,128]{1,0:T(8,128)(2,1)S(1)}, bf16[512,128]{1,0:T(8,128)(2,1)S(1)}, u32[]{:S(2)}, u32[]{:S(2)}) collective-permute-start(bf16[512,128]{1,0:T(8,128)(2,1)S(1)} %get-tuple-element.47), channel_id=1, source_target_pairs={{0,2},{1,3},{2,0},{3,1},{4,6},{5,7},{6,4},{7,5},{8,10},{9,11},{10,... | collective-permute-start | bytes 393224 | tf_op jit(solution)/shard_map/ppermute | solution.py:29
  37.3 0.0 collective-permute-done.refs_2_
  37.3 0.0 collective-permute-start.6
  37.3 3.7 %shard_map.110.refs_7_ = bf16[512,256]{1,0:T(8,128)(2,1)S(1)} custom-call(bf16[512,640]{1,0:T(8,128)(2,1)S(1)} %get-tuple-element.41.refs_0_, bf16[512,1152]{1,0:T(8,128)(2,1)S(1)} %get-tuple-element.42.refs_1_, bf16[512,1152]{1,0:T(8,128)(2,1)S(1)} %collective-permute-done.refs_2_, bf16[512,512]{1,0:T(8,128)(2,1)S(1)} %collective-permute-done.1.refs_3_, ...), custom_call_target="tpu_custom_call" | custom-call | flops 2147483648 | bytes 4063232 | tf_op jit(solution)/shard_map/pallas_call | solution.py:67
  41.0 0.4 collective-permute-done.7.refs_6_
  41.4 0.0 collective-permute-start.9
  41.4 0.0 collective-permute-done.5.refs_6_.refs_7_.refs_8_
  41.4 0.2 collective-permute-start.8
  41.6 3.6 %shard_map.111.refs_9_ = bf16[512,384]{1,0:T(8,128)(2,1)S(1)} custom-call(bf16[512,640]{1,0:T(8,128)(2,1)S(1)} %get-tuple-element.41.refs_0_, bf16[512,1152]{1,0:T(8,128)(2,1)S(1)} %get-tuple-element.42.refs_1_, bf16[512,1152]{1,0:T(8,128)(2,1)S(1)} %collective-permute-done.refs_2_, bf16[512,512]{1,0:T(8,128)(2,1)S(1)} %collective-permute-done.1.refs_3_, ...), custom_call_target="tpu_custom_call" | custom-call | flops 2147483648 | bytes 4849664 | tf_op jit(solution)/shard_map/pallas_call | solution.py:67
  45.3 0.0 collective-permute-done.6.refs_8_.refs_9_
  45.3 3.8 %shard_map.112 = (bf16[128,384]{1,0:T(8,128)(2,1)S(1)}, bf16[128,384]{1,0:T(8,128)(2,1)S(1)}, bf16[128,384]{1,0:T(8,128)(2,1)S(1)}, bf16[128,384]{1,0:T(8,128)(2,1)S(1)}, bf16[512,128]{1,0:T(8,128)(2,1)S(1)}) custom-call(bf16[512,640]{1,0:T(8,128)(2,1)S(1)} %get-tuple-element.41.refs_0_, bf16[512,1152]{1,0:T(8,128)(2,1)S(1)} %get-tuple-element.42.refs_1_, ...), custom_call_target="tpu_custom_call" | custom-call | flops 2147483648 | bytes 5505024 | tf_op jit(solution)/shard_map/pallas_call | solution.py:67
  49.0 0.0 copy-start
  49.1 0.0 copy-start.7
  49.1 3.5 %shard_map.113 = (bf16[128,192]{1,0:T(8,128)(2,1)S(1)}, bf16[128,192]{1,0:T(8,128)(2,1)S(1)}, bf16[128,192]{1,0:T(8,128)(2,1)S(1)}, bf16[128,192]{1,0:T(8,128)(2,1)S(1)}) custom-call(bf16[512,640]{1,0:T(8,128)(2,1)S(1)} %get-tuple-element.41.refs_0_, bf16[512,1152]{1,0:T(8,128)(2,1)S(1)} %get-tuple-element.42.refs_1_, ...), custom_call_target="tpu_custom_call" | custom-call | flops 2147483648 | bytes 5505024 | tf_op jit(solution)/shard_map/pallas_call | solution.py:67
  52.6 1.9 %collective-permute-start.13 = (bf16[128,192]{1,0:T(8,128)(2,1)S(1)}, bf16[128,192]{1,0:T(8,128)(2,1)S(1)}, u32[]{:S(2)}, u32[]{:S(2)}) collective-permute-start(bf16[128,192]{1,0:T(8,128)(2,1)S(1)} %get-tuple-element.51.refs_7_), channel_id=1, source_target_pairs={{0,4},{1,5},{2,6},{3,7},{4,0},{5,1},{6,2},{7,3},{8,12},{9,13},{10,... | collective-permute-start | bytes 147464 | tf_op jit(solution)/shard_map/ppermute | solution.py:29
  54.5 0.2 collective-permute-start.12
  54.7 0.7 collective-permute-start.14
  55.4 3.5 %collective-permute-start.16 = (bf16[128,384]{1,0:T(8,128)(2,1)S(1)}, bf16[128,384]{1,0:T(8,128)(2,1)S(1)}, u32[]{:S(2)}, u32[]{:S(2)}) collective-permute-start(bf16[128,384]{1,0:T(8,128)(2,1)S(1)} %get-tuple-element.54.refs_10_), channel_id=1, source_target_pairs={{0,12},{1,13},{2,14},{3,15},{4,8},{5,9},{6,10},{7,11},{8,4},{9,5},... | collective-permute-start | bytes 294920 | tf_op jit(solution)/shard_map/ppermute | solution.py:29
  58.9 1.7 %collective-permute-start.17 = (bf16[128,192]{1,0:T(8,128)(2,1)S(1)}, bf16[128,192]{1,0:T(8,128)(2,1)S(1)}, u32[]{:S(2)}, u32[]{:S(2)}) collective-permute-start(bf16[128,192]{1,0:T(8,128)(2,1)S(1)} %get-tuple-element.55.refs_11_), channel_id=1, source_target_pairs={{0,12},{1,13},{2,14},{3,15},{4,8},{5,9},{6,10},{7,11},{8,4},{9,5},... | collective-permute-start | bytes 147464 | tf_op jit(solution)/shard_map/ppermute | solution.py:29
  60.6 11.1 %collective-permute-done.15.refs_9_ = bf16[128,192]{1,0:T(8,128)(2,1)S(1)} collective-permute-done((bf16[128,192]{1,0:T(8,128)(2,1)S(1)}, bf16[128,192]{1,0:T(8,128)(2,1)S(1)}, u32[]{:S(2)}, u32[]{:S(2)}) %collective-permute-start.15) | collective-permute-done | bytes 49184 | tf_op jit(solution)/shard_map/ppermute | solution.py:29
  71.7 4.5 %shard_map.115 = (bf16[512,640]{1,0:T(8,128)(2,1)S(1)}, bf16[512,1152]{1,0:T(8,128)(2,1)S(1)}) custom-call(bf16[128,1152]{1,0:T(8,128)(2,1)S(1)} %get-tuple-element.36.refs_0_, bf16[128,1152]{1,0:T(8,128)(2,1)S(1)} %collective-permute-done.9.refs_1_, bf16[128,1152]{1,0:T(8,128)(2,1)S(1)} %collective-permute-done.10.refs_2_, ...), custom_call_target="tpu_custom_call" | custom-call | flops 2717908992 | bytes 7123968 | tf_op jit(solution)/shard_map/pallas_call | solution.py:67
  76.2 2.4 %shard_map.117 = (bf16[64,576]{1,0:T(8,128)(2,1)S(1)}, bf16[64,576]{1,0:T(8,128)(2,1)S(1)}, bf16[64,576]{1,0:T(8,128)(2,1)S(1)}, bf16[64,576]{1,0:T(8,128)(2,1)S(1)}) custom-call(bf16[512,640]{1,0:T(8,128)(2,1)S(1)} %get-tuple-element.57.query_ref, bf16[512,1152]{1,0:T(8,128)(2,1)S(1)} %get-tuple-element.58.kv_ref), custom_call_target="tpu_custom_call" | custom-call | flops 268435456 | bytes 1835008 | tf_op jit(solution)/shard_map/pallas_call | solution.py:67
  78.5 1.3 %collective-permute-start.19 = (bf16[64,576]{1,0:T(8,128)(2,1)S(1)}, bf16[64,576]{1,0:T(8,128)(2,1)S(1)}, u32[]{:S(2)}, u32[]{:S(2)}) collective-permute-start(bf16[64,576]{1,0:T(8,128)(2,1)S(1)} %get-tuple-element.62), channel_id=1, source_target_pairs={{0,4},{1,5},{2,6},{3,7},{4,0},{5,1},{6,2},{7,3},{8,12},{9,13},{10,... | collective-permute-start | bytes 221192 | tf_op jit(solution)/shard_map/ppermute | solution.py:29
  79.9 0.7 collective-permute-start.21
  80.6 2.4 %collective-permute-start.23 = (bf16[64,576]{1,0:T(8,128)(2,1)S(1)}, bf16[64,576]{1,0:T(8,128)(2,1)S(1)}, u32[]{:S(2)}, u32[]{:S(2)}) collective-permute-start(bf16[64,576]{1,0:T(8,128)(2,1)S(1)} %get-tuple-element.66), channel_id=1, source_target_pairs={{0,12},{1,13},{2,14},{3,15},{4,8},{5,9},{6,10},{7,11},{8,4},{9,5},... | collective-permute-start | bytes 221192 | tf_op jit(solution)/shard_map/ppermute | solution.py:29
  83.0 2.6 %shard_map.116 = (bf16[64,576]{1,0:T(8,128)(2,1)S(1)}, bf16[64,576]{1,0:T(8,128)(2,1)S(1)}, bf16[64,576]{1,0:T(8,128)(2,1)S(1)}, bf16[64,576]{1,0:T(8,128)(2,1)S(1)}) custom-call(bf16[512,640]{1,0:T(8,128)(2,1)S(1)} %get-tuple-element.57.query_ref, bf16[512,1152]{1,0:T(8,128)(2,1)S(1)} %get-tuple-element.58.kv_ref), custom_call_target="tpu_custom_call" | custom-call | flops 268435456 | bytes 1835008 | tf_op jit(solution)/shard_map/pallas_call | solution.py:67
  85.6 0.4 collective-permute-start.18
  86.0 1.6 %collective-permute-start.20 = (bf16[64,576]{1,0:T(8,128)(2,1)S(1)}, bf16[64,576]{1,0:T(8,128)(2,1)S(1)}, u32[]{:S(2)}, u32[]{:S(2)}) collective-permute-start(bf16[64,576]{1,0:T(8,128)(2,1)S(1)} %get-tuple-element.63), channel_id=1, source_target_pairs={{0,8},{1,9},{2,10},{3,11},{4,12},{5,13},{6,14},{7,15},{8,0},{9,1},... | collective-permute-start | bytes 221192 | tf_op jit(solution)/shard_map/ppermute | solution.py:29
  87.6 2.4 %collective-permute-start.22 = (bf16[64,576]{1,0:T(8,128)(2,1)S(1)}, bf16[64,576]{1,0:T(8,128)(2,1)S(1)}, u32[]{:S(2)}, u32[]{:S(2)}) collective-permute-start(bf16[64,576]{1,0:T(8,128)(2,1)S(1)} %get-tuple-element.65), channel_id=1, source_target_pairs={{0,12},{1,13},{2,14},{3,15},{4,8},{5,9},{6,10},{7,11},{8,4},{9,5},... | collective-permute-start | bytes 221192 | tf_op jit(solution)/shard_map/ppermute | solution.py:29
  90.0 1.2 %shard_map.114.after_ref = f32[512,1152]{1,0:T(8,128)S(1)} custom-call(bf16[128,1152]{1,0:T(8,128)(2,1)S(1)} %get-tuple-element.36.refs_0_, bf16[128,1152]{1,0:T(8,128)(2,1)S(1)} %get-tuple-element.37.refs_1_, bf16[128,1152]{1,0:T(8,128)(2,1)S(1)} %get-tuple-element.38.refs_2_, bf16[128,1152]{1,0:T(8,128)(2,1)S(1)} %get-tuple-element.39.refs_3_, ...), custom_call_target="tpu_custom_call" | custom-call | flops 679477248 | bytes 3124224 | tf_op jit(solution)/shard_map/pallas_call | solution.py:67
  91.3 0.4 collective-permute-done.18.refs_2_
  91.7 3.3 %collective-permute-done.20.refs_4_ = bf16[64,576]{1,0:T(8,128)(2,1)S(1)} collective-permute-done((bf16[64,576]{1,0:T(8,128)(2,1)S(1)}, bf16[64,576]{1,0:T(8,128)(2,1)S(1)}, u32[]{:S(2)}, u32[]{:S(2)}) %collective-permute-start.20) | collective-permute-done | bytes 73760 | tf_op jit(solution)/shard_map/ppermute | solution.py:29
  95.0 2.1 %block_output.1 = f32[512,1152]{1,0:T(8,128)} custom-call(s32[1]{0:T(128)} %bitcast.slot_ref, f32[512,1152]{1,0:T(8,128)S(1)} %shard_map.114.after_ref, bf16[576,1152]{1,0:T(8,128)(2,1)S(1)} %copy-done.1, f32[6,1152]{1,0:T(8,128)S(1)} %get-tuple-element.40.refs_5_.refs_13_.refs_14_.modulation_ref, bf16[64,576]{1,0:T(8,128)(2,1)S(1)} %get-tuple-element.59.refs_0_, ...), custom_call_target="tpu_custom_call" | custom-call | tf_op jit(solution)/shard_map/block_output/pallas_call | solution.py:585
  (29 shorter events, 0.1 us)
Async XLA Ops:
  0.0 24.0 %copy-start.4 = (f32[1,1152]{1,0:T(1,128)S(1)}, f32[1,1152]{1,0:T(1,128)}, u32[]{:S(2)}) copy-start(f32[1,1152]{1,0:T(1,128)} %constant.22.clone.rate_ref) | copy-start | bytes 13828
  0.0 24.0 %copy-start.2 = (f32[6,1152]{1,0:T(8,128)S(1)}, f32[6,1152]{1,0:T(8,128)}, u32[]{:S(2)}) copy-start(f32[6,1152]{1,0:T(8,128)} %table_ref.1) | copy-start | bytes 82948
  0.0 24.0 %copy-start.3 = (f32[6,1152]{1,0:T(8,128)S(1)}, f32[6,1152]{1,0:T(8,128)}, u32[]{:S(2)}) copy-start(f32[6,1152]{1,0:T(8,128)} %mix_ref.1) | copy-start | bytes 82948
  0.0 24.0 %copy-start.5 = (s32[4]{0:T(128)S(1)}, s32[4]{0:T(128)}, u32[]{:S(2)}) copy-start(s32[4]{0:T(128)} %order_ref.1) | copy-start | bytes 52
  0.0 37.3 %collective-permute-start = (bf16[512,1152]{1,0:T(8,128)(2,1)}, bf16[512,1152]{1,0:T(8,128)(2,1)S(1)}, u32[]{:S(2)}, u32[]{:S(2)}) collective-permute-start(bf16[512,1152]{1,0:T(8,128)(2,1)} %kv_ref.1), channel_id=1, source_target_pairs={{0,1},{1,0},{2,3},{3,2},{4,5},{5,4},{6,7},{7,6},{8,9},{9,8},{10,11... | collective-permute-start | bytes 3538952 | tf_op jit(solution)/shard_map/ppermute | solution.py:29
  2.0 15.2 %collective-permute-start.1 = (bf16[512,512]{1,0:T(8,128)(2,1)S(1)}, bf16[512,512]{1,0:T(8,128)(2,1)S(1)}, u32[]{:S(2)}, u32[]{:S(2)}) collective-permute-start(bf16[512,512]{1,0:T(8,128)(2,1)S(1)} %get-tuple-element.43), channel_id=1, source_target_pairs={{0,2},{1,3},{2,0},{3,1},{4,6},{5,7},{6,4},{7,5},{8,10},{9,11},{10,... | collective-permute-start | bytes 1572872 | tf_op jit(solution)/shard_map/ppermute | solution.py:29
  17.2 18.6 %collective-permute-start.4 = (bf16[512,512]{1,0:T(8,128)(2,1)S(1)}, bf16[512,512]{1,0:T(8,128)(2,1)S(1)}, u32[]{:S(2)}, u32[]{:S(2)}) collective-permute-start(bf16[512,512]{1,0:T(8,128)(2,1)S(1)} %collective-permute-done.1.refs_3_), channel_id=1, source_target_pairs={{0,1},{1,0},{2,3},{3,2},{4,5},{5,4},{6,7},{7,6},{8,9},{9,8},{10,11... | collective-permute-start | bytes 1572872 | tf_op jit(solution)/shard_map/ppermute | solution.py:29
  17.2 9.2 %collective-permute-start.2 = (bf16[512,256]{1,0:T(8,128)(2,1)S(1)}, bf16[512,256]{1,0:T(8,128)(2,1)S(1)}, u32[]{:S(2)}, u32[]{:S(2)}) collective-permute-start(bf16[512,256]{1,0:T(8,128)(2,1)S(1)} %get-tuple-element.44), channel_id=1, source_target_pairs={{0,2},{1,3},{2,0},{3,1},{4,6},{5,7},{6,4},{7,5},{8,10},{9,11},{10,... | collective-permute-start | bytes 786440 | tf_op jit(solution)/shard_map/ppermute | solution.py:29
  18.9 12.9 %collective-permute-start.3 = (bf16[512,256]{1,0:T(8,128)(2,1)S(1)}, bf16[512,256]{1,0:T(8,128)(2,1)S(1)}, u32[]{:S(2)}, u32[]{:S(2)}) collective-permute-start(bf16[512,256]{1,0:T(8,128)(2,1)S(1)} %get-tuple-element.45), channel_id=1, source_target_pairs={{0,2},{1,3},{2,0},{3,1},{4,6},{5,7},{6,4},{7,5},{8,10},{9,11},{10,... | collective-permute-start | bytes 786440 | tf_op jit(solution)/shard_map/ppermute | solution.py:29
  20.5 34.2 %collective-permute-start.10 = (bf16[128,1152]{1,0:T(8,128)(2,1)S(1)}, bf16[128,1152]{1,0:T(8,128)(2,1)S(1)}, u32[]{:S(2)}, u32[]{:S(2)}) collective-permute-start(bf16[128,1152]{1,0:T(8,128)(2,1)S(1)} %get-tuple-element.38.refs_2_), channel_id=1, source_target_pairs={{0,8},{1,9},{2,10},{3,11},{4,12},{5,13},{6,14},{7,15},{8,0},{9,1},... | collective-permute-start | bytes 884744 | tf_op jit(solution)/shard_map/ppermute | solution.py:29
  26.4 15.0 %collective-permute-start.5 = (bf16[512,256]{1,0:T(8,128)(2,1)S(1)}, bf16[512,256]{1,0:T(8,128)(2,1)S(1)}, u32[]{:S(2)}, u32[]{:S(2)}) collective-permute-start(bf16[512,256]{1,0:T(8,128)(2,1)S(1)} %collective-permute-done.2.refs_4_), channel_id=1, source_target_pairs={{0,1},{1,0},{2,3},{3,2},{4,5},{5,4},{6,7},{7,6},{8,9},{9,8},{10,11... | collective-permute-start | bytes 786440 | tf_op jit(solution)/shard_map/ppermute | solution.py:29
  26.4 2.1 %copy-start.6 = (bf16[3,1152,576]{1,2,0:T(8,128)(2,1)S(1)}, bf16[3,1152,576]{1,2,0:T(8,128)(2,1)}, u32[]{:S(2)}) copy-start(bf16[3,1152,576]{1,2,0:T(8,128)(2,1)} %param.17) | copy-start | bytes 11943940
  31.9 23.5 %collective-permute-start.11 = (bf16[128,1152]{1,0:T(8,128)(2,1)S(1)}, bf16[128,1152]{1,0:T(8,128)(2,1)S(1)}, u32[]{:S(2)}, u32[]{:S(2)}) collective-permute-start(bf16[128,1152]{1,0:T(8,128)(2,1)S(1)} %get-tuple-element.39.refs_3_), channel_id=1, source_target_pairs={{0,12},{1,13},{2,14},{3,15},{4,8},{5,9},{6,10},{7,11},{8,4},{9,5},... | collective-permute-start | bytes 884744 | tf_op jit(solution)/shard_map/ppermute | solution.py:29
  35.8 5.6 %collective-permute-start.7 = (bf16[512,128]{1,0:T(8,128)(2,1)S(1)}, bf16[512,128]{1,0:T(8,128)(2,1)S(1)}, u32[]{:S(2)}, u32[]{:S(2)}) collective-permute-start(bf16[512,128]{1,0:T(8,128)(2,1)S(1)} %get-tuple-element.47), channel_id=1, source_target_pairs={{0,2},{1,3},{2,0},{3,1},{4,6},{5,7},{6,4},{7,5},{8,10},{9,11},{10,... | collective-permute-start | bytes 393224 | tf_op jit(solution)/shard_map/ppermute | solution.py:29
  37.3 8.0 %collective-permute-start.6 = (bf16[512,256]{1,0:T(8,128)(2,1)S(1)}, bf16[512,256]{1,0:T(8,128)(2,1)S(1)}, u32[]{:S(2)}, u32[]{:S(2)}) collective-permute-start(bf16[512,256]{1,0:T(8,128)(2,1)S(1)} %collective-permute-done.3.refs_5_), channel_id=1, source_target_pairs={{0,1},{1,0},{2,3},{3,2},{4,5},{5,4},{6,7},{7,6},{8,9},{9,8},{10,11... | collective-permute-start | bytes 786440 | tf_op jit(solution)/shard_map/ppermute | solution.py:29
  41.4 17.5 %collective-permute-start.9 = (bf16[128,1152]{1,0:T(8,128)(2,1)S(1)}, bf16[128,1152]{1,0:T(8,128)(2,1)S(1)}, u32[]{:S(2)}, u32[]{:S(2)}) collective-permute-start(bf16[128,1152]{1,0:T(8,128)(2,1)S(1)} %get-tuple-element.37.refs_1_), channel_id=1, source_target_pairs={{0,4},{1,5},{2,6},{3,7},{4,0},{5,1},{6,2},{7,3},{8,12},{9,13},{10,... | collective-permute-start | bytes 884744 | tf_op jit(solution)/shard_map/ppermute | solution.py:29
  41.4 7.6 %collective-permute-start.8 = (bf16[512,128]{1,0:T(8,128)(2,1)S(1)}, bf16[512,128]{1,0:T(8,128)(2,1)S(1)}, u32[]{:S(2)}, u32[]{:S(2)}) collective-permute-start(bf16[512,128]{1,0:T(8,128)(2,1)S(1)} %collective-permute-done.7.refs_6_), channel_id=1, source_target_pairs={{0,1},{1,0},{2,3},{3,2},{4,5},{5,4},{6,7},{7,6},{8,9},{9,8},{10,11... | collective-permute-start | bytes 393224 | tf_op jit(solution)/shard_map/ppermute | solution.py:29
  49.0 22.6 %copy-start = (bf16[576,1152]{1,0:T(8,128)(2,1)S(1)}, bf16[576,1152]{1,0:T(8,128)(2,1)}, u32[]{:S(2)}) copy-start(bf16[576,1152]{1,0:T(8,128)(2,1)} %refs_12_.3) | copy-start | bytes 3981316
  49.1 22.6 %copy-start.7 = (bf16[3,1152,576]{1,2,0:T(8,128)(2,1)S(1)}, bf16[3,1152,576]{1,2,0:T(8,128)(2,1)}, u32[]{:S(2)}) copy-start(bf16[3,1152,576]{1,2,0:T(8,128)(2,1)} %param.19) | copy-start | bytes 11943940
  52.6 6.3 %collective-permute-start.13 = (bf16[128,192]{1,0:T(8,128)(2,1)S(1)}, bf16[128,192]{1,0:T(8,128)(2,1)S(1)}, u32[]{:S(2)}, u32[]{:S(2)}) collective-permute-start(bf16[128,192]{1,0:T(8,128)(2,1)S(1)} %get-tuple-element.51.refs_7_), channel_id=1, source_target_pairs={{0,4},{1,5},{2,6},{3,7},{4,0},{5,1},{6,2},{7,3},{8,12},{9,13},{10,... | collective-permute-start | bytes 147464 | tf_op jit(solution)/shard_map/ppermute | solution.py:29
  54.5 17.2 %collective-permute-start.12 = (bf16[128,384]{1,0:T(8,128)(2,1)S(1)}, bf16[128,384]{1,0:T(8,128)(2,1)S(1)}, u32[]{:S(2)}, u32[]{:S(2)}) collective-permute-start(bf16[128,384]{1,0:T(8,128)(2,1)S(1)} %get-tuple-element.50.refs_6_), channel_id=1, source_target_pairs={{0,4},{1,5},{2,6},{3,7},{4,0},{5,1},{6,2},{7,3},{8,12},{9,13},{10,... | collective-permute-start | bytes 294920 | tf_op jit(solution)/shard_map/ppermute | solution.py:29
  54.7 17.0 %collective-permute-start.14 = (bf16[128,384]{1,0:T(8,128)(2,1)S(1)}, bf16[128,384]{1,0:T(8,128)(2,1)S(1)}, u32[]{:S(2)}, u32[]{:S(2)}) collective-permute-start(bf16[128,384]{1,0:T(8,128)(2,1)S(1)} %get-tuple-element.52.refs_8_), channel_id=1, source_target_pairs={{0,8},{1,9},{2,10},{3,11},{4,12},{5,13},{6,14},{7,15},{8,0},{9,1},... | collective-permute-start | bytes 294920 | tf_op jit(solution)/shard_map/ppermute | solution.py:29
  55.4 16.3 %collective-permute-start.16 = (bf16[128,384]{1,0:T(8,128)(2,1)S(1)}, bf16[128,384]{1,0:T(8,128)(2,1)S(1)}, u32[]{:S(2)}, u32[]{:S(2)}) collective-permute-start(bf16[128,384]{1,0:T(8,128)(2,1)S(1)} %get-tuple-element.54.refs_10_), channel_id=1, source_target_pairs={{0,12},{1,13},{2,14},{3,15},{4,8},{5,9},{6,10},{7,11},{8,4},{9,5},... | collective-permute-start | bytes 294920 | tf_op jit(solution)/shard_map/ppermute | solution.py:29
  58.9 12.8 %collective-permute-start.15 = (bf16[128,192]{1,0:T(8,128)(2,1)S(1)}, bf16[128,192]{1,0:T(8,128)(2,1)S(1)}, u32[]{:S(2)}, u32[]{:S(2)}) collective-permute-start(bf16[128,192]{1,0:T(8,128)(2,1)S(1)} %get-tuple-element.53.refs_9_), channel_id=1, source_target_pairs={{0,8},{1,9},{2,10},{3,11},{4,12},{5,13},{6,14},{7,15},{8,0},{9,1},... | collective-permute-start | bytes 147464 | tf_op jit(solution)/shard_map/ppermute | solution.py:29
  58.9 12.8 %collective-permute-start.17 = (bf16[128,192]{1,0:T(8,128)(2,1)S(1)}, bf16[128,192]{1,0:T(8,128)(2,1)S(1)}, u32[]{:S(2)}, u32[]{:S(2)}) collective-permute-start(bf16[128,192]{1,0:T(8,128)(2,1)S(1)} %get-tuple-element.55.refs_11_), channel_id=1, source_target_pairs={{0,12},{1,13},{2,14},{3,15},{4,8},{5,9},{6,10},{7,11},{8,4},{9,5},... | collective-permute-start | bytes 147464 | tf_op jit(solution)/shard_map/ppermute | solution.py:29
  78.5 9.1 %collective-permute-start.19 = (bf16[64,576]{1,0:T(8,128)(2,1)S(1)}, bf16[64,576]{1,0:T(8,128)(2,1)S(1)}, u32[]{:S(2)}, u32[]{:S(2)}) collective-permute-start(bf16[64,576]{1,0:T(8,128)(2,1)S(1)} %get-tuple-element.62), channel_id=1, source_target_pairs={{0,4},{1,5},{2,6},{3,7},{4,0},{5,1},{6,2},{7,3},{8,12},{9,13},{10,... | collective-permute-start | bytes 221192 | tf_op jit(solution)/shard_map/ppermute | solution.py:29
  79.9 11.4 %collective-permute-start.21 = (bf16[64,576]{1,0:T(8,128)(2,1)S(1)}, bf16[64,576]{1,0:T(8,128)(2,1)S(1)}, u32[]{:S(2)}, u32[]{:S(2)}) collective-permute-start(bf16[64,576]{1,0:T(8,128)(2,1)S(1)} %get-tuple-element.64), channel_id=1, source_target_pairs={{0,8},{1,9},{2,10},{3,11},{4,12},{5,13},{6,14},{7,15},{8,0},{9,1},... | collective-permute-start | bytes 221192 | tf_op jit(solution)/shard_map/ppermute | solution.py:29
  80.6 10.7 %collective-permute-start.23 = (bf16[64,576]{1,0:T(8,128)(2,1)S(1)}, bf16[64,576]{1,0:T(8,128)(2,1)S(1)}, u32[]{:S(2)}, u32[]{:S(2)}) collective-permute-start(bf16[64,576]{1,0:T(8,128)(2,1)S(1)} %get-tuple-element.66), channel_id=1, source_target_pairs={{0,12},{1,13},{2,14},{3,15},{4,8},{5,9},{6,10},{7,11},{8,4},{9,5},... | collective-permute-start | bytes 221192 | tf_op jit(solution)/shard_map/ppermute | solution.py:29
  85.6 6.1 %collective-permute-start.18 = (bf16[64,576]{1,0:T(8,128)(2,1)S(1)}, bf16[64,576]{1,0:T(8,128)(2,1)S(1)}, u32[]{:S(2)}, u32[]{:S(2)}) collective-permute-start(bf16[64,576]{1,0:T(8,128)(2,1)S(1)} %get-tuple-element.61), channel_id=1, source_target_pairs={{0,4},{1,5},{2,6},{3,7},{4,0},{5,1},{6,2},{7,3},{8,12},{9,13},{10,... | collective-permute-start | bytes 221192 | tf_op jit(solution)/shard_map/ppermute | solution.py:29
  86.0 9.0 %collective-permute-start.20 = (bf16[64,576]{1,0:T(8,128)(2,1)S(1)}, bf16[64,576]{1,0:T(8,128)(2,1)S(1)}, u32[]{:S(2)}, u32[]{:S(2)}) collective-permute-start(bf16[64,576]{1,0:T(8,128)(2,1)S(1)} %get-tuple-element.63), channel_id=1, source_target_pairs={{0,8},{1,9},{2,10},{3,11},{4,12},{5,13},{6,14},{7,15},{8,0},{9,1},... | collective-permute-start | bytes 221192 | tf_op jit(solution)/shard_map/ppermute | solution.py:29
  87.6 7.4 %copy-start.1 = (bf16[576,1152]{1,0:T(8,128)(2,1)S(1)}, bf16[576,1152]{1,0:T(8,128)(2,1)}, u32[]{:S(2)}) copy-start(bf16[576,1152]{1,0:T(8,128)(2,1)} %weight_ref.1) | copy-start | bytes 3981316
  87.6 7.4 %collective-permute-start.22 = (bf16[64,576]{1,0:T(8,128)(2,1)S(1)}, bf16[64,576]{1,0:T(8,128)(2,1)S(1)}, u32[]{:S(2)}, u32[]{:S(2)}) collective-permute-start(bf16[64,576]{1,0:T(8,128)(2,1)S(1)} %get-tuple-element.65), channel_id=1, source_target_pairs={{0,12},{1,13},{2,14},{3,15},{4,8},{5,9},{6,10},{7,11},{8,4},{9,5},... | collective-permute-start | bytes 221192 | tf_op jit(solution)/shard_map/ppermute | solution.py:29

commit v2 on v1

--- a/solution.py
+++ b/solution.py
@@ -14,7 +14,7 @@
 LANES = 128
 QUERY_ROWS = 128
 PAIR_GROUPS = ((0,), (1,), (2,), (3,))
-EMIT = (False, False, True, True)
+EMIT = (False, True, False, True)
 HALVES = 2
 
 
@@ -172,16 +172,25 @@
     )(slot, timestep, frame_order, *operands)
 
 
-def projection_kernel(*refs, frames, width):
+def projection_kernel(weight_hbm, *refs, frames, width):
     pieces = refs[:frames]
-    weight_ref, modulation_ref, query_ref, kv_ref = refs[frames:]
+    modulation_ref, query_ref, kv_ref, weight_ref, sems = refs[frames:]
+    padded = query_ref.shape[1]
+    parts = (slice(0, padded), slice(padded, weight_ref.shape[0]))
+    copies = [
+        pltpu.make_async_copy(weight_hbm.at[part, :], weight_ref.at[part, :], sems.at[number])
+        for number, part in enumerate(parts)
+    ]
+    for copy in copies:
+        copy.start()
     tokens = jnp.concatenate([ref[...] for ref in pieces], axis=0).astype(f32)
     inputs = normalize(tokens) * (1.0 + modulation_ref[1:2, :]) + modulation_ref[0:1, :]
     inputs = inputs.astype(bf16)
-    padded = query_ref.shape[1]
+    copies[0].wait()
     query_ref[...] = lax.dot_general(
         inputs, weight_ref[:padded, :], NT, preferred_element_type=f32
     ).astype(bf16)
+    copies[1].wait()
     kv_ref[...] = lax.dot_general(
         inputs, weight_ref[width:, :], NT, preferred_element_type=f32
     ).astype(bf16)
@@ -192,13 +201,55 @@
     piece, feature_width = pieces[0].shape
     padded = -(-width // LANES) * LANES
     rows = frames * piece
-    return on_chip_call(
+    operands = [pltpu.with_memory_space_constraint(weight, pltpu.HBM)]
+    operands += [pltpu.with_memory_space_constraint(x, pltpu.VMEM) for x in (*pieces, modulation)]
+    return pl.pallas_call(
         functools.partial(projection_kernel, frames=frames, width=width),
-        [*pieces, weight, modulation],
-        [((rows, padded), bf16), ((rows, 2 * width), bf16)],
-        2 * rows * feature_width * 3 * width,
-        4,
-    )
+        out_shape=[pltpu.VMEM((rows, padded), bf16), pltpu.VMEM((rows, 2 * width), bf16)],
+        in_specs=[pl.BlockSpec(memory_space=pltpu.HBM), *vmem_specs(frames + 1)],
+        out_specs=vmem_specs(2),
+        scratch_shapes=[pltpu.VMEM(weight.shape, bf16), pltpu.SemaphoreType.DMA((2,))],
+        compiler_params=pltpu.CompilerParams(vmem_limit_bytes=8 * 2**20),
+        cost_estimate=pl.CostEstimate(
+            flops=2 * rows * feature_width * 3 * width,
+            bytes_accessed=2 * weight.size,
+            transcendentals=0,
+        ),
+        name="projections",
+    )(*operands)
+
+
+def stack_rows(rows, width):
+    return rows * width // LANES
+
+
+def stack(tiles, width):
+    rows = tiles[0].shape[0]
+    whole = width // LANES
+    stacked = list(tiles[:whole])
+    if width % LANES:
+        fold = tiles[whole]
+        lane = lax.broadcasted_iota(jnp.int32, (1, LANES), 1)
+        low = jnp.where(lane < LANES // 2, fold[: rows // 2], 0.0)
+        high = jnp.where(lane < LANES // 2, fold[rows // 2 :], 0.0)
+        stacked.append(low + pltpu.roll(high, LANES // 2, 1))
+    return jnp.concatenate(stacked, axis=0).astype(bf16)
+
+
+def unstack(stacked, rows, width, first, count):
+    whole = width // LANES
+    tiles = [stacked[t * rows + first : t * rows + first + count, :] for t in range(whole)]
+    if width % LANES:
+        half = rows // 2
+        fold = stacked[whole * rows :, :]
+        turned = pltpu.roll(fold.astype(f32), LANES // 2, 1).astype(stacked.dtype)
+        both = jnp.concatenate([fold, turned], axis=0)
+        if first % half == 0 and count == half:
+            both = turned if first else fold
+        else:
+            both = both[first : first + count]
+        tiles.append(both[:, : LANES // 2])
+    return jnp.concatenate(tiles, axis=1)
 
 
 def pair_plan(width, head_dim):
@@ -226,7 +277,7 @@
     return groups
 
 
-def spatial_kernel(*refs, group, frames, head_dim, width, tiles, held, emitted, kept):
+def spatial_kernel(*refs, group, frames, head_dim, width, tiles, held, emitted, kept, columns):
     plan = pair_plan(width, head_dim)
     count = len(tiles)
     position = 0
@@ -330,12 +381,11 @@
             values = jnp.concatenate([parts[tile] for tile in kept], axis=1)
             kept_ref[at : at + QUERY_ROWS, :] = values.astype(bf16)
         if emitted:
-            values = jnp.concatenate([parts[tile] for tile in emitted], axis=1).astype(bf16)
-            width_out = out_refs[0].shape[1]
             for sub in range(QUERY_ROWS // piece):
-                out_refs[at // piece + sub][...] = values[
-                    sub * piece : (sub + 1) * piece, :width_out
-                ]
+                cut = slice(sub * piece, (sub + 1) * piece)
+                out_refs[at // piece + sub][...] = stack(
+                    [parts[tile][cut] for tile in emitted], columns
+                )
         parts.clear()
 
     score(0)
@@ -363,15 +413,24 @@
     return flow
 
 
+def emitted_columns(emitted, width):
+    return min(width, (emitted[-1] + 1) * LANES) - emitted[0] * LANES if emitted else 0
+
+
+def group_columns(width, head_dim):
+    flow = tile_flow(width, head_dim)
+    return tuple(emitted_columns(emitted, width) for _, emitted, _ in flow if emitted)
+
+
 def spatial_group(number, query, own_kv, peer_kv, near, far, carry, frames, head_dim, width):
     group = PAIR_GROUPS[number]
     held, emitted, kept = tile_flow(width, head_dim)[number]
     tiles = tuple(group_tiles(width, head_dim)[: number + 1])
     rows = query.shape[0]
     shapes = []
+    columns = emitted_columns(emitted, width)
     if emitted:
-        columns = min(width, (emitted[-1] + 1) * LANES) - emitted[0] * LANES
-        shapes += [((rows // frames, columns), bf16) for _ in range(frames)]
+        shapes += [((stack_rows(rows // frames, columns), LANES), bf16) for _ in range(frames)]
     if kept:
         shapes.append(((rows, len(kept) * LANES), bf16))
     operands = [query, own_kv, peer_kv, *near[: number + 1], *far[: number + 1]]
@@ -389,6 +448,7 @@
             held=held,
             emitted=emitted,
             kept=kept,
+            columns=columns,
         ),
         operands,
         shapes,
@@ -405,13 +465,19 @@
     return results, carry
 
 
-def joined_rows(tokens_refs, mixed_refs):
-    groups = len(mixed_refs) // len(tokens_refs)
-    tokens = jnp.concatenate([ref[...] for ref in tokens_refs], axis=0).astype(f32)
+def joined_rows(tokens_refs, mixed_refs, columns, first, count):
+    groups = len(columns)
+    piece = tokens_refs[0].shape[0]
+    cut = slice(first, first + count)
+    tokens = jnp.concatenate([ref[cut, :] for ref in tokens_refs], axis=0).astype(f32)
     mixed = jnp.concatenate(
         [
             jnp.concatenate(
-                [ref[...] for ref in mixed_refs[frame * groups : (frame + 1) * groups]], axis=1
+                [
+                    unstack(mixed_refs[frame * groups + g][...], piece, columns[g], first, count)
+                    for g in range(groups)
+                ],
+                axis=1,
             )
             for frame in range(len(tokens_refs))
         ],
@@ -420,14 +486,16 @@
     return tokens, mixed
 
 
-def temporal_in_kernel(*refs, frames, groups):
+def temporal_kernel(*refs, frames, head_dim, columns, first, piece):
+    groups = len(columns)
     tokens_refs = refs[:frames]
     mixed_refs = refs[frames : frames + frames * groups]
     position = frames + frames * groups
-    out_weight, qkv_weight, modulation_ref, place_ref, query_ref, kv_ref = refs[position:]
+    out_weight, qkv_weight, modulation_ref, place_ref = refs[position : position + 4]
+    out_refs = refs[position + 4 : position + 4 + frames]
+    query_ref, kv_ref = refs[position + 4 + frames :]
     width = out_weight.shape[0]
-    piece = tokens_refs[0].shape[0]
-    tokens, mixed = joined_rows(tokens_refs, mixed_refs)
+    tokens, mixed = joined_rows(tokens_refs, mixed_refs, columns, first, piece)
     after = tokens + modulation_ref[2:3, :] * jnp.dot(
         mixed, out_weight[...], preferred_element_type=f32
     )
@@ -446,14 +514,88 @@
         inputs, qkv_weight[width:, :], NT, preferred_element_type=f32
     ).astype(bf16)
 
-
-def temporal_in(tokens, mixed, spatial_out, temporal_qkv, modulation, places):
-    frames, groups = len(tokens), len(mixed[0])
+    scale = softmax_scale(head_dim)
+    step = max(16, min(piece, LANES // frames))
+    block = frames * step
+    row_at = lax.broadcasted_iota(jnp.int32, (2 * block, block), 0) % step
+    column_at = lax.broadcasted_iota(jnp.int32, (2 * block, block), 1) % step
+    same = row_at == column_at
+    plan = pair_plan(width, head_dim)
+
+    def window(ref, start, tile):
+        return jnp.concatenate(
+            [
+                ref[
+                    frame * piece + start : frame * piece + start + step,
+                    tile * LANES : (tile + 2) * LANES,
+                ]
+                for frame in range(frames)
+            ],
+            axis=0,
+        )
+
+    def score(start, tile, lane):
+        queries = window(query_ref, start, tile)
+        stacked = jnp.concatenate(
+            [
+                queries * column_mask(lane, head_dim, bf16),
+                queries * column_mask(lane + head_dim, head_dim, bf16),
+            ],
+            axis=0,
+        )
+        scores = lax.dot_general(
+            stacked, window(kv_ref, start, tile), NT, preferred_element_type=f32
+        )
+        return jnp.where(same, scores * scale, -jnp.inf)
+
+    def weigh(scores):
+        weights = jnp.exp2(scores - jnp.max(scores, axis=-1, keepdims=True))
+        return (weights / jnp.sum(weights, axis=-1, keepdims=True)).astype(bf16)
+
+    starts = range(0, piece, step)
+    tasks = [(start, *entry) for start in starts for entry in plan]
+    scores = [score(start, tile, lane) for start, tile, lane, _, _ in tasks]
+    weights = [weigh(value) for value in scores]
+    mixed_pairs = [
+        jnp.dot(value, window(kv_ref, start, value_tile), preferred_element_type=f32)
+        for value, (start, _, _, value_tile, _) in zip(weights, tasks)
+    ]
+    parts = {start: {} for start in starts}
+    for pair, (start, tile, lane, _, value_lane) in zip(mixed_pairs, tasks):
+        joined = pair[:block] * column_mask(value_lane, head_dim, f32) + pair[
+            block:
+        ] * column_mask(value_lane + head_dim, head_dim, f32)
+        joined = pltpu.roll(joined, (lane - value_lane) % (2 * LANES), 1)
+        have = parts[start]
+        for side in range(2):
+            half = joined[:, side * LANES : (side + 1) * LANES]
+            have[tile + side] = have[tile + side] + half if tile + side in have else half
+    for frame in range(frames):
+        cut = slice(frame * step, (frame + 1) * step)
+        out_refs[frame][...] = stack(
+            [
+                jnp.concatenate([parts[start][tile][cut] for start in starts], axis=0)
+                for tile in sorted(parts[0])
+            ],
+            width,
+        )
+
+
+def temporal(tokens, mixed, columns, weights, modulation, places, head_dim, first, piece):
+    frames = len(tokens)
+    spatial_out, temporal_qkv = weights
     width, feature_width = spatial_out.shape
     padded = -(-width // LANES) * LANES
-    rows = frames * tokens[0].shape[0]
+    rows = frames * piece
     return on_chip_call(
-        functools.partial(temporal_in_kernel, frames=frames, groups=groups),
+        functools.partial(
+            temporal_kernel,
+            frames=frames,
+            head_dim=head_dim,
+            columns=columns,
+            first=first,
+            piece=piece,
+        ),
         [
             *tokens,
             *[part for frame in mixed for part in frame],
@@ -462,115 +604,62 @@
             modulation,
             places,
         ],
-        [((rows, padded), bf16), ((rows, 2 * width), bf16)],
-        2 * rows * feature_width * width * 4,
+        [((stack_rows(piece, width), LANES), bf16) for _ in range(frames)],
+        2 * rows * feature_width * width * 5,
         6,
-    )
-
-
-def temporal_kernel(query_ref, kv_ref, *out_refs, head_dim, first):
-    frames = len(out_refs)
-    piece, width = out_refs[0].shape
-    stride = query_ref.shape[0] // frames
-    scale = softmax_scale(head_dim)
-    step = max(16, min(piece, LANES // frames))
-    block = frames * step
-    row_at = lax.broadcasted_iota(jnp.int32, (2 * block, block), 0) % step
-    column_at = lax.broadcasted_iota(jnp.int32, (2 * block, block), 1) % step
-    same = row_at == column_at
-    plan = pair_plan(width, head_dim)
-
-    for start in range(0, piece, step):
-
-        def window(ref, tile):
-            return jnp.concatenate(
-                [
-                    ref[
-                        frame * stride + first + start : frame * stride + first + start + step,
-                        tile * LANES : (tile + 2) * LANES,
-                    ]
-                    for frame in range(frames)
-                ],
-                axis=0,
-            )
-
-        parts = {}
-        for tile, lane, value_tile, value_lane in plan:
-            queries = window(query_ref, tile)
-            stacked = jnp.concatenate(
-                [
-                    queries * column_mask(lane, head_dim, bf16),
-                    queries * column_mask(lane + head_dim, head_dim, bf16),
-                ],
-                axis=0,
-            )
-            scores = lax.dot_general(stacked, window(kv_ref, tile), NT, preferred_element_type=f32)
-            scores = jnp.where(same, scores * scale, -jnp.inf)
-            weights = jnp.exp2(scores - jnp.max(scores, axis=-1, keepdims=True))
-            weights = (weights / jnp.sum(weights, axis=-1, keepdims=True)).astype(bf16)
-            mixed_pair = jnp.dot(weights, window(kv_ref, value_tile), preferred_element_type=f32)
-            joined = mixed_pair[:block] * column_mask(value_lane, head_dim, f32) + mixed_pair[
-                block:
-            ] * column_mask(value_lane + head_dim, head_dim, f32)
-            joined = pltpu.roll(joined, (lane - value_lane) % (2 * LANES), 1)
-            for side in range(2):
-                half = joined[:, side * LANES : (side + 1) * LANES]
-                parts[tile + side] = parts[tile + side] + half if tile + side in parts else half
-        values = jnp.concatenate([parts[tile] for tile in sorted(parts)], axis=1).astype(bf16)
-        for frame in range(frames):
-            out_refs[frame][start : start + step, :] = values[
-                frame * step : (frame + 1) * step, :width
-            ]
-
-
-def temporal(query, kv, frames, head_dim, first, piece):
-    width = kv.shape[1] // 2
-    rows = frames * piece
-    return on_chip_call(
-        functools.partial(temporal_kernel, head_dim=head_dim, first=first),
-        [query, kv],
-        [((piece, width), bf16) for _ in range(frames)],
-        2 * rows * 128 * 256 * 16,
-        2,
         rows * 128 * 8,
-    )
-
-
-def after_kernel(*refs, frames, groups):
-    weight_ref, modulation_ref, out_ref = refs[frames + frames * groups :]
-    tokens, mixed = joined_rows(refs[:frames], refs[frames : frames + frames * groups])
+        [pltpu.VMEM((rows, padded), bf16), pltpu.VMEM((rows, 2 * width), bf16)],
+    )
+
+
+def after_kernel(*refs, frames, columns):
+    mixed_end = frames * (1 + len(columns))
+    weight_ref, modulation_ref, out_ref = refs[mixed_end:]
+    piece = refs[0].shape[0]
+    tokens, mixed = joined_rows(refs[:frames], refs[frames:mixed_end], columns, 0, piece)
     out_ref[...] = tokens + modulation_ref[2:3, :] * jnp.dot(
         mixed, weight_ref[...], preferred_element_type=f32
     )
 
 
-def after_spatial(tokens, mixed, weight, modulation):
-    frames, groups = len(tokens), len(mixed[0])
+def after_spatial(tokens, mixed, columns, weight, modulation):
+    frames = len(tokens)
     width, feature_width = weight.shape
     rows = frames * tokens[0].shape[0]
     return on_chip_call(
-        functools.partial(after_kernel, frames=frames, groups=groups),
+        functools.partial(after_kernel, frames=frames, columns=columns),
         [*tokens, *[part for frame in mixed for part in frame], weight, modulation],
         [((rows, feature_width), f32)],
         2 * rows * feature_width * width,
-        4,
+        6,
     )[0]
 
 
-def output_kernel(slot_ref, after_ref, weight_ref, modulation_ref, *refs, frames, halves):
-    parts, (out_ref, stage_ref, sems) = refs[: frames * halves], refs[frames * halves :]
+def output_kernel(slot_ref, after_ref, weight_ref, modulation_ref, *refs, frames, number):
+    parts = refs[:frames]
+    out_ref, stage_ref, sems = refs[-3:]
     piece = after_ref.shape[0] // frames
+    half = piece // HALVES
+    first = number * half
+    width = weight_ref.shape[0]
+    mixed = jnp.concatenate(
+        [unstack(ref[...].astype(f32), half, width, 0, half).astype(bf16) for ref in parts], axis=0
+    )
+    after = jnp.concatenate(
+        [after_ref[frame * piece + first : frame * piece + first + half, :] for frame in range(frames)],
+        axis=0,
+    )
+    stage_ref[...] = after + modulation_ref[5:6, :] * jnp.dot(
+        mixed, weight_ref[...], preferred_element_type=f32
+    )
     copies = []
     for frame in range(frames):
-        cut = slice(frame * piece, (frame + 1) * piece)
-        mixed = jnp.concatenate([parts[frame * halves + h][...] for h in range(halves)], axis=0)
-        stage_ref[cut, :] = after_ref[cut, :] + modulation_ref[5:6, :] * jnp.dot(
-            mixed, weight_ref[...], preferred_element_type=f32
-        )
-        row = partner_slot(slot_ref[0], frame, frames) * piece
+        row = partner_slot(slot_ref[0], frame, frames) * piece + first
         copies.append(
             pltpu.make_async_copy(
-                stage_ref.at[cut, :], out_ref.at[pl.ds(row, piece), :], sems.at[frame]
+                stage_ref.at[frame * half : (frame + 1) * half, :],
+                out_ref.at[pl.ds(row, half), :],
+                sems.at[frame],
             )
         )
         copies[-1].start()
@@ -578,22 +667,29 @@
         copy.wait()
 
 
-def output(slot, after, weight, modulation, parts, frames):
+def output(number, slot, after, weight, modulation, parts, result):
+    frames = len(parts)
     rows, feature_width = after.shape
-    halves = len(parts[0])
-    operands = [after, weight, modulation, *[part for frame in parts for part in frame]]
+    operands = [after, weight, modulation, *parts]
+    specs = [pl.BlockSpec(memory_space=pltpu.SMEM), *vmem_specs(len(operands))]
+    operands = [pltpu.with_memory_space_constraint(array, pltpu.VMEM) for array in operands]
+    aliases = {}
+    if result is not None:
+        aliases = {len(specs): 0}
+        specs.append(pl.BlockSpec(memory_space=pltpu.HBM))
+        operands.append(result)
     return pl.pallas_call(
-        functools.partial(output_kernel, frames=frames, halves=halves),
+        functools.partial(output_kernel, frames=frames, number=number),
         out_shape=jax.ShapeDtypeStruct((rows, feature_width), f32),
-        in_specs=[pl.BlockSpec(memory_space=pltpu.SMEM), *vmem_specs(len(operands))],
+        in_specs=specs,
         out_specs=pl.BlockSpec(memory_space=pltpu.HBM),
         scratch_shapes=[
-            pltpu.VMEM((rows, feature_width), f32),
+            pltpu.VMEM((rows // HALVES, feature_width), f32),
             pltpu.SemaphoreType.DMA((frames,)),
         ],
+        input_output_aliases=aliases,
         compiler_params=pltpu.CompilerParams(vmem_limit_bytes=4 * 2**20),
-        name="block_output",
-    )(slot, *[pltpu.with_memory_space_constraint(array, pltpu.VMEM) for array in operands])
+    )(slot, *operands)
 
 
 def per_device(
@@ -658,25 +754,18 @@
             local[s].append(out)
             sent[s].append(out if s == 0 else permute(out, ahead(s)))
 
-    after = after_spatial(pieces, local, spatial_out, modulation)
-    temporal_query, temporal_kv = temporal_in(
-        there,
-        sent,
-        spatial_out,
-        jnp.swapaxes(temporal_qkv, 1, 2).reshape(3 * width, feature_width),
-        modulation,
-        places,
-    )
+    columns = group_columns(width, head_dim)
+    after = after_spatial(pieces, local, columns, spatial_out, modulation)
+    weights = (spatial_out, jnp.swapaxes(temporal_qkv, 1, 2).reshape(3 * width, feature_width))
     half = piece // HALVES
-    back = [[] for _ in range(frames)]
+    back = []
     for h in range(HALVES):
-        outs = temporal(temporal_query, temporal_kv, frames, head_dim, h * half, half)
-        for s, out in enumerate(outs):
-            back[s].append(out if s == 0 else permute(out, behind(s)))
-
-    return output(
-        slot_word, after, temporal_out, modulation, back, frames
-    )
+        outs = temporal(there, sent, columns, weights, modulation, places, head_dim, h * half, half)
+        back.append([out if s == 0 else permute(out, behind(s)) for s, out in enumerate(outs)])
+    result = None
+    for h in range(HALVES):
+        result = output(h, slot_word, after, temporal_out, modulation, back[h], result)
+    return result
 
 
 def solution(mesh):

time: 97.5 us -> 92.7 us (0.951)
  waiting for transfers between devices: 29.5 us -> 25 us
  local copies, waits for them, and re-layouts: 2.16 us -> 0.03 us
  Pallas kernels: 34 us -> 35.8 us
    pallas_call x1 -> x3, Pallas kernels: 2.06 us -> 8.4 us  [the longest x1 4.91 us: projections(): pl.pallas_call(functools.partial(projection_kernel, frames=frames, width=...]
    ppermute x24, waiting for transfers between devices: 29.5 us -> 25 us  [permute(): lax.ppermute(value, 'patch', [(source, target(source)) for source in rang...]
    pallas_call x9 -> x7, Pallas kernels: 28.5 us -> 24 us  [on_chip_call(): pl.pallas_call(kernel, out_shape=[pltpu.VMEM(shape, dtype) for shape, dty...]
    unnamed x16 -> x14, local copies, waits for them, and re-layouts: 2.16 us -> 0.03 us
  transfers between devices with their start and end apart: 24 -> 24, of which waited for: 6 -> 6; matrix products, arithmetic and copies ran while one was open for 0% -> 0% of each run, Pallas kernels for 26% -> 32%
where the time goes in v2:
time: 92.7 us; the launch traced here: 92.5 us
  Pallas kernels  35.8 us (39%)
  starting transfers between devices  30.6 us (33%)
  waiting for transfers between devices  25 us (27%)
  between operations  1.05 us (1%)
    ppermute x24, starting transfers between devices, permute(): lax.ppermute(value, 'patch', [(source, target(source)) for source in rang...  30.6 us
    ppermute x24, waiting for transfers between devices, permute(): lax.ppermute(value, 'patch', [(source, target(source)) for source in rang...  25 us
    pallas_call x7, Pallas kernels, on_chip_call(): pl.pallas_call(kernel, out_shape=[pltpu.VMEM(shape, dtype) for shape, dty...  24 us
    pallas_call x1, Pallas kernels, projections(): pl.pallas_call(functools.partial(projection_kernel, frames=frames, width=...  4.91 us
    pallas_call x2, Pallas kernels, output(): pl.pallas_call(functools.partial(output_kernel, frames=frames, number=num...  3.49 us
  transfers between devices with their start and end apart: 24, of which 6 were waited for; matrix products, arithmetic and copies ran while one was open for 0% of the time, Pallas kernels for 32%

profile of v2, /device:TPU:0, one launch (start us, length us, event | category | flops | bytes accessed | tf_op | source)
XLA Modules:
  0.0 92.5 jit_solution(10609351197191363907)
XLA Ops:
  0.0 0.6 collective-permute-start
  0.6 1.4 %chunks.1 = (bf16[512,512]{1,0:T(8,128)(2,1)S(1)}, bf16[512,256]{1,0:T(8,128)(2,1)S(1)}, bf16[512,256]{1,0:T(8,128)(2,1)S(1)}, bf16[512,128]{1,0:T(8,128)(2,1)S(1)}) custom-call(bf16[512,1152]{1,0:T(8,128)(2,1)} %kv_ref.1), custom_call_target="tpu_custom_call" | custom-call | tf_op jit(solution)/shard_map/chunks/pallas_call | solution.py:101
  2.0 2.6 %collective-permute-start.1 = (bf16[512,512]{1,0:T(8,128)(2,1)S(1)}, bf16[512,512]{1,0:T(8,128)(2,1)S(1)}, u32[]{:S(2)}, u32[]{:S(2)}) collective-permute-start(bf16[512,512]{1,0:T(8,128)(2,1)S(1)} %get-tuple-element.41), channel_id=1, source_target_pairs={{0,2},{1,3},{2,0},{3,1},{4,6},{5,7},{6,4},{7,5},{8,10},{9,11},{10,... | collective-permute-start | bytes 1572872 | tf_op jit(solution)/shard_map/ppermute | solution.py:29
  4.6 12.6 %collective-permute-done.1.refs_3_ = bf16[512,512]{1,0:T(8,128)(2,1)S(1)} collective-permute-done((bf16[512,512]{1,0:T(8,128)(2,1)S(1)}, bf16[512,512]{1,0:T(8,128)(2,1)S(1)}, u32[]{:S(2)}, u32[]{:S(2)}) %collective-permute-start.1) | collective-permute-done | bytes 524320 | tf_op jit(solution)/shard_map/ppermute | solution.py:29
  17.2 0.0 collective-permute-start.3
  17.2 1.7 %collective-permute-start.2 = (bf16[512,256]{1,0:T(8,128)(2,1)S(1)}, bf16[512,256]{1,0:T(8,128)(2,1)S(1)}, u32[]{:S(2)}, u32[]{:S(2)}) collective-permute-start(bf16[512,256]{1,0:T(8,128)(2,1)S(1)} %get-tuple-element.42), channel_id=1, source_target_pairs={{0,2},{1,3},{2,0},{3,1},{4,6},{5,7},{6,4},{7,5},{8,10},{9,11},{10,... | collective-permute-start | bytes 786440 | tf_op jit(solution)/shard_map/ppermute | solution.py:29
  18.9 0.3 collective-permute-start.5
  19.2 1.3 %pieces.1 = (bf16[128,1152]{1,0:T(8,128)(2,1)S(1)}, bf16[128,1152]{1,0:T(8,128)(2,1)S(1)}, bf16[128,1152]{1,0:T(8,128)(2,1)S(1)}, bf16[128,1152]{1,0:T(8,128)(2,1)S(1)}) custom-call(s32[1]{0:T(128)} %bitcast.slot_ref, bf16[512,1152]{1,0:T(8,128)(2,1)} %tokens_ref.1), custom_call_target="tpu_custom_call" | custom-call | tf_op jit(solution)/shard_map/pieces/pallas_call | solution.py:130
  20.5 2.9 %collective-permute-start.10 = (bf16[128,1152]{1,0:T(8,128)(2,1)S(1)}, bf16[128,1152]{1,0:T(8,128)(2,1)S(1)}, u32[]{:S(2)}, u32[]{:S(2)}) collective-permute-start(bf16[128,1152]{1,0:T(8,128)(2,1)S(1)} %get-tuple-element.36.refs_2_), channel_id=1, source_target_pairs={{0,8},{1,9},{2,10},{3,11},{4,12},{5,13},{6,14},{7,15},{8,0},{9,1},... | collective-permute-start | bytes 884744 | tf_op jit(solution)/shard_map/ppermute | solution.py:29
  24.0 0.7 modulation.1
  24.7 1.6 %collective-permute-done.2.refs_4_ = bf16[512,256]{1,0:T(8,128)(2,1)S(1)} collective-permute-done((bf16[512,256]{1,0:T(8,128)(2,1)S(1)}, bf16[512,256]{1,0:T(8,128)(2,1)S(1)}, u32[]{:S(2)}, u32[]{:S(2)}) %collective-permute-start.2) | collective-permute-done | bytes 262176 | tf_op jit(solution)/shard_map/ppermute | solution.py:29
  26.4 0.0 collective-permute-start.4
  26.4 4.9 %projections.1 = (bf16[512,640]{1,0:T(8,128)(2,1)S(1)}, bf16[512,1152]{1,0:T(8,128)(2,1)S(1)}) custom-call(bf16[1728,1152]{1,0:T(8,128)(2,1)} %bitcast.9, bf16[128,1152]{1,0:T(8,128)(2,1)S(1)} %get-tuple-element.34.refs_0_, bf16[128,1152]{1,0:T(8,128)(2,1)S(1)} %get-tuple-element.35.refs_1_, bf16[128,1152]{1,0:T(8,128)(2,1)S(1)} %get-tuple-element.36.refs_2_, ...), custom_call_target="tpu_custom_call" | custom-call | flops 2038431744 | bytes 3981312 | tf_op jit(solution)/shard_map/projections/pallas_call | solution.py:206
  31.3 0.2 collective-permute-done.5.refs_5_
  31.5 3.8 %collective-permute-start.11 = (bf16[128,1152]{1,0:T(8,128)(2,1)S(1)}, bf16[128,1152]{1,0:T(8,128)(2,1)S(1)}, u32[]{:S(2)}, u32[]{:S(2)}) collective-permute-start(bf16[128,1152]{1,0:T(8,128)(2,1)S(1)} %get-tuple-element.37.refs_3_), channel_id=1, source_target_pairs={{0,12},{1,13},{2,14},{3,15},{4,8},{5,9},{6,10},{7,11},{8,4},{9,5},... | collective-permute-start | bytes 884744 | tf_op jit(solution)/shard_map/ppermute | solution.py:29
  35.3 1.5 %collective-permute-start.6 = (bf16[512,128]{1,0:T(8,128)(2,1)S(1)}, bf16[512,128]{1,0:T(8,128)(2,1)S(1)}, u32[]{:S(2)}, u32[]{:S(2)}) collective-permute-start(bf16[512,128]{1,0:T(8,128)(2,1)S(1)} %get-tuple-element.45), channel_id=1, source_target_pairs={{0,2},{1,3},{2,0},{3,1},{4,6},{5,7},{6,4},{7,5},{8,10},{9,11},{10,... | collective-permute-start | bytes 393224 | tf_op jit(solution)/shard_map/ppermute | solution.py:29
  36.9 0.0 collective-permute-done.refs_2_
  36.9 0.0 collective-permute-start.7
  36.9 3.7 %shard_map.109.refs_7_ = bf16[512,256]{1,0:T(8,128)(2,1)S(1)} custom-call(bf16[512,640]{1,0:T(8,128)(2,1)S(1)} %get-tuple-element.39.refs_0_, bf16[512,1152]{1,0:T(8,128)(2,1)S(1)} %get-tuple-element.40.refs_1_, bf16[512,1152]{1,0:T(8,128)(2,1)S(1)} %collective-permute-done.refs_2_, bf16[512,512]{1,0:T(8,128)(2,1)S(1)} %collective-permute-done.1.refs_3_, ...), custom_call_target="tpu_custom_call" | custom-call | flops 2147483648 | bytes 4063232 | tf_op jit(solution)/shard_map/pallas_call | solution.py:67
  40.5 0.3 collective-permute-done.6.refs_6_
  40.8 0.0 collective-permute-start.9
  40.8 0.0 collective-permute-done.4.refs_6_.refs_7_.refs_8_
  40.8 0.4 collective-permute-start.8
  41.2 3.6 %shard_map.110 = (bf16[256,128]{1,0:T(8,128)(2,1)S(1)}, bf16[256,128]{1,0:T(8,128)(2,1)S(1)}, bf16[256,128]{1,0:T(8,128)(2,1)S(1)}, bf16[256,128]{1,0:T(8,128)(2,1)S(1)}, bf16[512,128]{1,0:T(8,128)(2,1)S(1)}) custom-call(bf16[512,640]{1,0:T(8,128)(2,1)S(1)} %get-tuple-element.39.refs_0_, bf16[512,1152]{1,0:T(8,128)(2,1)S(1)} %get-tuple-element.40.refs_1_, ...), custom_call_target="tpu_custom_call" | custom-call | flops 2147483648 | bytes 4849664 | tf_op jit(solution)/shard_map/pallas_call | solution.py:67
  44.8 0.0 collective-permute-done.7.refs_8_.refs_9_
  44.9 1.7 %collective-permute-start.12 = (bf16[256,128]{1,0:T(8,128)(2,1)S(1)}, bf16[256,128]{1,0:T(8,128)(2,1)S(1)}, u32[]{:S(2)}, u32[]{:S(2)}) collective-permute-start(bf16[256,128]{1,0:T(8,128)(2,1)S(1)} %get-tuple-element.48.refs_6_), channel_id=1, source_target_pairs={{0,4},{1,5},{2,6},{3,7},{4,0},{5,1},{6,2},{7,3},{8,12},{9,13},{10,... | collective-permute-start | bytes 196616 | tf_op jit(solution)/shard_map/ppermute | solution.py:29
  46.6 3.8 %shard_map.111.refs_11_ = bf16[512,256]{1,0:T(8,128)(2,1)S(1)} custom-call(bf16[512,640]{1,0:T(8,128)(2,1)S(1)} %get-tuple-element.39.refs_0_, bf16[512,1152]{1,0:T(8,128)(2,1)S(1)} %get-tuple-element.40.refs_1_, bf16[512,1152]{1,0:T(8,128)(2,1)S(1)} %collective-permute-done.refs_2_, bf16[512,512]{1,0:T(8,128)(2,1)S(1)} %collective-permute-done.1.refs_3_, ...), custom_call_target="tpu_custom_call" | custom-call | flops 2147483648 | bytes 5242880 | tf_op jit(solution)/shard_map/pallas_call | solution.py:67
  50.3 0.0 copy-start
  50.4 0.0 copy-start.1
  50.4 0.0 collective-permute-done.8.refs_10_
  50.4 3.7 %shard_map.112 = (bf16[320,128]{1,0:T(8,128)(2,1)S(1)}, bf16[320,128]{1,0:T(8,128)(2,1)S(1)}, bf16[320,128]{1,0:T(8,128)(2,1)S(1)}, bf16[320,128]{1,0:T(8,128)(2,1)S(1)}) custom-call(bf16[512,640]{1,0:T(8,128)(2,1)S(1)} %get-tuple-element.39.refs_0_, bf16[512,1152]{1,0:T(8,128)(2,1)S(1)} %get-tuple-element.40.refs_1_, ...), custom_call_target="tpu_custom_call" | custom-call | flops 2147483648 | bytes 5636096 | tf_op jit(solution)/shard_map/pallas_call | solution.py:67
  54.1 0.4 collective-permute-start.13
  54.5 0.6 collective-permute-start.15
  55.1 3.5 %collective-permute-start.17 = (bf16[320,128]{1,0:T(8,128)(2,1)S(1)}, bf16[320,128]{1,0:T(8,128)(2,1)S(1)}, u32[]{:S(2)}, u32[]{:S(2)}) collective-permute-start(bf16[320,128]{1,0:T(8,128)(2,1)S(1)} %get-tuple-element.53.refs_11_), channel_id=1, source_target_pairs={{0,12},{1,13},{2,14},{3,15},{4,8},{5,9},{6,10},{7,11},{8,4},{9,5},... | collective-permute-start | bytes 245768 | tf_op jit(solution)/shard_map/ppermute | solution.py:29
  58.5 1.8 %collective-permute-start.16 = (bf16[256,128]{1,0:T(8,128)(2,1)S(1)}, bf16[256,128]{1,0:T(8,128)(2,1)S(1)}, u32[]{:S(2)}, u32[]{:S(2)}) collective-permute-start(bf16[256,128]{1,0:T(8,128)(2,1)S(1)} %get-tuple-element.52.refs_10_), channel_id=1, source_target_pairs={{0,12},{1,13},{2,14},{3,15},{4,8},{5,9},{6,10},{7,11},{8,4},{9,5},... | collective-permute-start | bytes 196616 | tf_op jit(solution)/shard_map/ppermute | solution.py:29
  60.4 9.5 %collective-permute-done.14.refs_8_ = bf16[256,128]{1,0:T(8,128)(2,1)S(1)} collective-permute-done((bf16[256,128]{1,0:T(8,128)(2,1)S(1)}, bf16[256,128]{1,0:T(8,128)(2,1)S(1)}, u32[]{:S(2)}, u32[]{:S(2)}) %collective-permute-start.14) | collective-permute-done | bytes 65568 | tf_op jit(solution)/shard_map/ppermute | solution.py:29
  69.9 4.0 %shard_map.115 = (bf16[288,128]{1,0:T(8,128)(2,1)S(1)}, bf16[288,128]{1,0:T(8,128)(2,1)S(1)}, bf16[288,128]{1,0:T(8,128)(2,1)S(1)}, bf16[288,128]{1,0:T(8,128)(2,1)S(1)}) custom-call(bf16[128,1152]{1,0:T(8,128)(2,1)S(1)} %get-tuple-element.34.refs_0_, bf16[128,1152]{1,0:T(8,128)(2,1)S(1)} %collective-permute-done.9.refs_1_, ...), custom_call_target="tpu_custom_call" | custom-call | flops 1698693120 | bytes 7123968 | tf_op jit(solution)/shard_map/pallas_call | solution.py:67
  73.9 1.3 %collective-permute-start.21 = (bf16[288,128]{1,0:T(8,128)(2,1)S(1)}, bf16[288,128]{1,0:T(8,128)(2,1)S(1)}, u32[]{:S(2)}, u32[]{:S(2)}) collective-permute-start(bf16[288,128]{1,0:T(8,128)(2,1)S(1)} %get-tuple-element.60), channel_id=1, source_target_pairs={{0,4},{1,5},{2,6},{3,7},{4,0},{5,1},{6,2},{7,3},{8,12},{9,13},{10,... | collective-permute-start | bytes 221192 | tf_op jit(solution)/shard_map/ppermute | solution.py:29
  75.2 0.7 collective-permute-start.22
  75.9 2.4 %collective-permute-start.23 = (bf16[288,128]{1,0:T(8,128)(2,1)S(1)}, bf16[288,128]{1,0:T(8,128)(2,1)S(1)}, u32[]{:S(2)}, u32[]{:S(2)}) collective-permute-start(bf16[288,128]{1,0:T(8,128)(2,1)S(1)} %get-tuple-element.62), channel_id=1, source_target_pairs={{0,12},{1,13},{2,14},{3,15},{4,8},{5,9},{6,10},{7,11},{8,4},{9,5},... | collective-permute-start | bytes 221192 | tf_op jit(solution)/shard_map/ppermute | solution.py:29
  78.4 4.1 %shard_map.114 = (bf16[288,128]{1,0:T(8,128)(2,1)S(1)}, bf16[288,128]{1,0:T(8,128)(2,1)S(1)}, bf16[288,128]{1,0:T(8,128)(2,1)S(1)}, bf16[288,128]{1,0:T(8,128)(2,1)S(1)}) custom-call(bf16[128,1152]{1,0:T(8,128)(2,1)S(1)} %get-tuple-element.34.refs_0_, bf16[128,1152]{1,0:T(8,128)(2,1)S(1)} %collective-permute-done.9.refs_1_, ...), custom_call_target="tpu_custom_call" | custom-call | flops 1698693120 | bytes 7123968 | tf_op jit(solution)/shard_map/pallas_call | solution.py:67
  82.5 0.4 collective-permute-start.18
  82.9 1.6 %collective-permute-start.19 = (bf16[288,128]{1,0:T(8,128)(2,1)S(1)}, bf16[288,128]{1,0:T(8,128)(2,1)S(1)}, u32[]{:S(2)}, u32[]{:S(2)}) collective-permute-start(bf16[288,128]{1,0:T(8,128)(2,1)S(1)} %get-tuple-element.57), channel_id=1, source_target_pairs={{0,8},{1,9},{2,10},{3,11},{4,12},{5,13},{6,14},{7,15},{8,0},{9,1},... | collective-permute-start | bytes 221192 | tf_op jit(solution)/shard_map/ppermute | solution.py:29
  84.4 2.5 %collective-permute-start.20 = (bf16[288,128]{1,0:T(8,128)(2,1)S(1)}, bf16[288,128]{1,0:T(8,128)(2,1)S(1)}, u32[]{:S(2)}, u32[]{:S(2)}) collective-permute-start(bf16[288,128]{1,0:T(8,128)(2,1)S(1)} %get-tuple-element.58), channel_id=1, source_target_pairs={{0,12},{1,13},{2,14},{3,15},{4,8},{5,9},{6,10},{7,11},{8,4},{9,5},... | collective-permute-start | bytes 221192 | tf_op jit(solution)/shard_map/ppermute | solution.py:29
  86.9 1.2 %shard_map.113.after_ref = f32[512,1152]{1,0:T(8,128)S(1)} custom-call(bf16[128,1152]{1,0:T(8,128)(2,1)S(1)} %get-tuple-element.34.refs_0_, bf16[128,1152]{1,0:T(8,128)(2,1)S(1)} %get-tuple-element.35.refs_1_, bf16[128,1152]{1,0:T(8,128)(2,1)S(1)} %get-tuple-element.36.refs_2_, bf16[128,1152]{1,0:T(8,128)(2,1)S(1)} %get-tuple-element.37.refs_3_, ...), custom_call_target="tpu_custom_call" | custom-call | flops 679477248 | bytes 3124224 | tf_op jit(solution)/shard_map/pallas_call | solution.py:67
  88.1 1.7 %shard_map.116.refs_4_ = f32[512,1152]{1,0:T(8,128)} custom-call(s32[1]{0:T(128)} %bitcast.slot_ref, f32[512,1152]{1,0:T(8,128)S(1)} %shard_map.113.after_ref, bf16[576,1152]{1,0:T(8,128)(2,1)S(1)} %copy-done.2, f32[6,1152]{1,0:T(8,128)S(1)} %get-tuple-element.38.refs_4_.refs_13_.refs_14_.modulation_ref, bf16[288,128]{1,0:T(8,128)(2,1)S(1)} %get-tuple-element.59.refs_0_, ...), custom_call_target="tpu_custom_call" | custom-call | tf_op jit(solution)/shard_map/pallas_call | solution.py:681
  89.9 0.7 collective-permute-done.20.refs_3_
  90.6 1.7 %shard_map.117 = f32[512,1152]{1,0:T(8,128)} custom-call(s32[1]{0:T(128)} %bitcast.slot_ref, f32[512,1152]{1,0:T(8,128)S(1)} %shard_map.113.after_ref, bf16[576,1152]{1,0:T(8,128)(2,1)S(1)} %copy-done.2, f32[6,1152]{1,0:T(8,128)S(1)} %get-tuple-element.38.refs_4_.refs_13_.refs_14_.modulation_ref, ...), custom_call_target="tpu_custom_call", output_to_operand_aliasing={{}: (8, {})} | custom-call | tf_op jit(solution)/shard_map/pallas_call | solution.py:681
  (27 shorter events, 0.1 us)
Async XLA Ops:
  0.0 24.0 %copy-start.5 = (f32[1,1152]{1,0:T(1,128)S(1)}, f32[1,1152]{1,0:T(1,128)}, u32[]{:S(2)}) copy-start(f32[1,1152]{1,0:T(1,128)} %constant.22.clone.rate_ref) | copy-start | bytes 13828
  0.0 24.0 %copy-start.3 = (f32[6,1152]{1,0:T(8,128)S(1)}, f32[6,1152]{1,0:T(8,128)}, u32[]{:S(2)}) copy-start(f32[6,1152]{1,0:T(8,128)} %table_ref.1) | copy-start | bytes 82948
  0.0 24.0 %copy-start.4 = (f32[6,1152]{1,0:T(8,128)S(1)}, f32[6,1152]{1,0:T(8,128)}, u32[]{:S(2)}) copy-start(f32[6,1152]{1,0:T(8,128)} %mix_ref.1) | copy-start | bytes 82948
  0.0 24.0 %copy-start.6 = (s32[4]{0:T(128)S(1)}, s32[4]{0:T(128)}, u32[]{:S(2)}) copy-start(s32[4]{0:T(128)} %order_ref.1) | copy-start | bytes 52
  0.0 36.9 %collective-permute-start = (bf16[512,1152]{1,0:T(8,128)(2,1)}, bf16[512,1152]{1,0:T(8,128)(2,1)S(1)}, u32[]{:S(2)}, u32[]{:S(2)}) collective-permute-start(bf16[512,1152]{1,0:T(8,128)(2,1)} %kv_ref.1), channel_id=1, source_target_pairs={{0,1},{1,0},{2,3},{3,2},{4,5},{5,4},{6,7},{7,6},{8,9},{9,8},{10,11... | collective-permute-start | bytes 3538952 | tf_op jit(solution)/shard_map/ppermute | solution.py:29
  2.0 15.2 %collective-permute-start.1 = (bf16[512,512]{1,0:T(8,128)(2,1)S(1)}, bf16[512,512]{1,0:T(8,128)(2,1)S(1)}, u32[]{:S(2)}, u32[]{:S(2)}) collective-permute-start(bf16[512,512]{1,0:T(8,128)(2,1)S(1)} %get-tuple-element.41), channel_id=1, source_target_pairs={{0,2},{1,3},{2,0},{3,1},{4,6},{5,7},{6,4},{7,5},{8,10},{9,11},{10,... | collective-permute-start | bytes 1572872 | tf_op jit(solution)/shard_map/ppermute | solution.py:29
  17.2 18.2 %collective-permute-start.3 = (bf16[512,512]{1,0:T(8,128)(2,1)S(1)}, bf16[512,512]{1,0:T(8,128)(2,1)S(1)}, u32[]{:S(2)}, u32[]{:S(2)}) collective-permute-start(bf16[512,512]{1,0:T(8,128)(2,1)S(1)} %collective-permute-done.1.refs_3_), channel_id=1, source_target_pairs={{0,1},{1,0},{2,3},{3,2},{4,5},{5,4},{6,7},{7,6},{8,9},{9,8},{10,11... | collective-permute-start | bytes 1572872 | tf_op jit(solution)/shard_map/ppermute | solution.py:29
  17.2 9.2 %collective-permute-start.2 = (bf16[512,256]{1,0:T(8,128)(2,1)S(1)}, bf16[512,256]{1,0:T(8,128)(2,1)S(1)}, u32[]{:S(2)}, u32[]{:S(2)}) collective-permute-start(bf16[512,256]{1,0:T(8,128)(2,1)S(1)} %get-tuple-element.42), channel_id=1, source_target_pairs={{0,2},{1,3},{2,0},{3,1},{4,6},{5,7},{6,4},{7,5},{8,10},{9,11},{10,... | collective-permute-start | bytes 786440 | tf_op jit(solution)/shard_map/ppermute | solution.py:29
  18.9 12.6 %collective-permute-start.5 = (bf16[512,256]{1,0:T(8,128)(2,1)S(1)}, bf16[512,256]{1,0:T(8,128)(2,1)S(1)}, u32[]{:S(2)}, u32[]{:S(2)}) collective-permute-start(bf16[512,256]{1,0:T(8,128)(2,1)S(1)} %get-tuple-element.44), channel_id=1, source_target_pairs={{0,2},{1,3},{2,0},{3,1},{4,6},{5,7},{6,4},{7,5},{8,10},{9,11},{10,... | collective-permute-start | bytes 786440 | tf_op jit(solution)/shard_map/ppermute | solution.py:29
  20.5 34.0 %collective-permute-start.10 = (bf16[128,1152]{1,0:T(8,128)(2,1)S(1)}, bf16[128,1152]{1,0:T(8,128)(2,1)S(1)}, u32[]{:S(2)}, u32[]{:S(2)}) collective-permute-start(bf16[128,1152]{1,0:T(8,128)(2,1)S(1)} %get-tuple-element.36.refs_2_), channel_id=1, source_target_pairs={{0,8},{1,9},{2,10},{3,11},{4,12},{5,13},{6,14},{7,15},{8,0},{9,1},... | collective-permute-start | bytes 884744 | tf_op jit(solution)/shard_map/ppermute | solution.py:29
  26.4 14.5 %collective-permute-start.4 = (bf16[512,256]{1,0:T(8,128)(2,1)S(1)}, bf16[512,256]{1,0:T(8,128)(2,1)S(1)}, u32[]{:S(2)}, u32[]{:S(2)}) collective-permute-start(bf16[512,256]{1,0:T(8,128)(2,1)S(1)} %collective-permute-done.2.refs_4_), channel_id=1, source_target_pairs={{0,1},{1,0},{2,3},{3,2},{4,5},{5,4},{6,7},{7,6},{8,9},{9,8},{10,11... | collective-permute-start | bytes 786440 | tf_op jit(solution)/shard_map/ppermute | solution.py:29
  31.5 23.5 %collective-permute-start.11 = (bf16[128,1152]{1,0:T(8,128)(2,1)S(1)}, bf16[128,1152]{1,0:T(8,128)(2,1)S(1)}, u32[]{:S(2)}, u32[]{:S(2)}) collective-permute-start(bf16[128,1152]{1,0:T(8,128)(2,1)S(1)} %get-tuple-element.37.refs_3_), channel_id=1, source_target_pairs={{0,12},{1,13},{2,14},{3,15},{4,8},{5,9},{6,10},{7,11},{8,4},{9,5},... | collective-permute-start | bytes 884744 | tf_op jit(solution)/shard_map/ppermute | solution.py:29
  35.3 5.5 %collective-permute-start.6 = (bf16[512,128]{1,0:T(8,128)(2,1)S(1)}, bf16[512,128]{1,0:T(8,128)(2,1)S(1)}, u32[]{:S(2)}, u32[]{:S(2)}) collective-permute-start(bf16[512,128]{1,0:T(8,128)(2,1)S(1)} %get-tuple-element.45), channel_id=1, source_target_pairs={{0,2},{1,3},{2,0},{3,1},{4,6},{5,7},{6,4},{7,5},{8,10},{9,11},{10,... | collective-permute-start | bytes 393224 | tf_op jit(solution)/shard_map/ppermute | solution.py:29
  36.9 8.0 %collective-permute-start.7 = (bf16[512,256]{1,0:T(8,128)(2,1)S(1)}, bf16[512,256]{1,0:T(8,128)(2,1)S(1)}, u32[]{:S(2)}, u32[]{:S(2)}) collective-permute-start(bf16[512,256]{1,0:T(8,128)(2,1)S(1)} %collective-permute-done.5.refs_5_), channel_id=1, source_target_pairs={{0,1},{1,0},{2,3},{3,2},{4,5},{5,4},{6,7},{7,6},{8,9},{9,8},{10,11... | collective-permute-start | bytes 786440 | tf_op jit(solution)/shard_map/ppermute | solution.py:29
  40.8 17.7 %collective-permute-start.9 = (bf16[128,1152]{1,0:T(8,128)(2,1)S(1)}, bf16[128,1152]{1,0:T(8,128)(2,1)S(1)}, u32[]{:S(2)}, u32[]{:S(2)}) collective-permute-start(bf16[128,1152]{1,0:T(8,128)(2,1)S(1)} %get-tuple-element.35.refs_1_), channel_id=1, source_target_pairs={{0,4},{1,5},{2,6},{3,7},{4,0},{5,1},{6,2},{7,3},{8,12},{9,13},{10,... | collective-permute-start | bytes 884744 | tf_op jit(solution)/shard_map/ppermute | solution.py:29
  40.8 9.5 %collective-permute-start.8 = (bf16[512,128]{1,0:T(8,128)(2,1)S(1)}, bf16[512,128]{1,0:T(8,128)(2,1)S(1)}, u32[]{:S(2)}, u32[]{:S(2)}) collective-permute-start(bf16[512,128]{1,0:T(8,128)(2,1)S(1)} %collective-permute-done.6.refs_6_), channel_id=1, source_target_pairs={{0,1},{1,0},{2,3},{3,2},{4,5},{5,4},{6,7},{7,6},{8,9},{9,8},{10,11... | collective-permute-start | bytes 393224 | tf_op jit(solution)/shard_map/ppermute | solution.py:29
  44.9 13.7 %collective-permute-start.12 = (bf16[256,128]{1,0:T(8,128)(2,1)S(1)}, bf16[256,128]{1,0:T(8,128)(2,1)S(1)}, u32[]{:S(2)}, u32[]{:S(2)}) collective-permute-start(bf16[256,128]{1,0:T(8,128)(2,1)S(1)} %get-tuple-element.48.refs_6_), channel_id=1, source_target_pairs={{0,4},{1,5},{2,6},{3,7},{4,0},{5,1},{6,2},{7,3},{8,12},{9,13},{10,... | collective-permute-start | bytes 196616 | tf_op jit(solution)/shard_map/ppermute | solution.py:29
  50.3 19.6 %copy-start = (bf16[3,1152,576]{1,2,0:T(8,128)(2,1)S(1)}, bf16[3,1152,576]{1,2,0:T(8,128)(2,1)}, u32[]{:S(2)}) copy-start(bf16[3,1152,576]{1,2,0:T(8,128)(2,1)} %param.19) | copy-start | bytes 11943940
  50.4 19.5 %copy-start.1 = (bf16[576,1152]{1,0:T(8,128)(2,1)S(1)}, bf16[576,1152]{1,0:T(8,128)(2,1)}, u32[]{:S(2)}) copy-start(bf16[576,1152]{1,0:T(8,128)(2,1)} %refs_12_.5) | copy-start | bytes 3981316
  54.1 15.8 %collective-permute-start.13 = (bf16[320,128]{1,0:T(8,128)(2,1)S(1)}, bf16[320,128]{1,0:T(8,128)(2,1)S(1)}, u32[]{:S(2)}, u32[]{:S(2)}) collective-permute-start(bf16[320,128]{1,0:T(8,128)(2,1)S(1)} %get-tuple-element.49.refs_7_), channel_id=1, source_target_pairs={{0,4},{1,5},{2,6},{3,7},{4,0},{5,1},{6,2},{7,3},{8,12},{9,13},{10,... | collective-permute-start | bytes 245768 | tf_op jit(solution)/shard_map/ppermute | solution.py:29
  54.5 15.4 %collective-permute-start.15 = (bf16[320,128]{1,0:T(8,128)(2,1)S(1)}, bf16[320,128]{1,0:T(8,128)(2,1)S(1)}, u32[]{:S(2)}, u32[]{:S(2)}) collective-permute-start(bf16[320,128]{1,0:T(8,128)(2,1)S(1)} %get-tuple-element.51.refs_9_), channel_id=1, source_target_pairs={{0,8},{1,9},{2,10},{3,11},{4,12},{5,13},{6,14},{7,15},{8,0},{9,1},... | collective-permute-start | bytes 245768 | tf_op jit(solution)/shard_map/ppermute | solution.py:29
  55.1 14.8 %collective-permute-start.17 = (bf16[320,128]{1,0:T(8,128)(2,1)S(1)}, bf16[320,128]{1,0:T(8,128)(2,1)S(1)}, u32[]{:S(2)}, u32[]{:S(2)}) collective-permute-start(bf16[320,128]{1,0:T(8,128)(2,1)S(1)} %get-tuple-element.53.refs_11_), channel_id=1, source_target_pairs={{0,12},{1,13},{2,14},{3,15},{4,8},{5,9},{6,10},{7,11},{8,4},{9,5},... | collective-permute-start | bytes 245768 | tf_op jit(solution)/shard_map/ppermute | solution.py:29
  58.5 11.3 %collective-permute-start.14 = (bf16[256,128]{1,0:T(8,128)(2,1)S(1)}, bf16[256,128]{1,0:T(8,128)(2,1)S(1)}, u32[]{:S(2)}, u32[]{:S(2)}) collective-permute-start(bf16[256,128]{1,0:T(8,128)(2,1)S(1)} %get-tuple-element.50.refs_8_), channel_id=1, source_target_pairs={{0,8},{1,9},{2,10},{3,11},{4,12},{5,13},{6,14},{7,15},{8,0},{9,1},... | collective-permute-start | bytes 196616 | tf_op jit(solution)/shard_map/ppermute | solution.py:29
  58.5 11.3 %collective-permute-start.16 = (bf16[256,128]{1,0:T(8,128)(2,1)S(1)}, bf16[256,128]{1,0:T(8,128)(2,1)S(1)}, u32[]{:S(2)}, u32[]{:S(2)}) collective-permute-start(bf16[256,128]{1,0:T(8,128)(2,1)S(1)} %get-tuple-element.52.refs_10_), channel_id=1, source_target_pairs={{0,12},{1,13},{2,14},{3,15},{4,8},{5,9},{6,10},{7,11},{8,4},{9,5},... | collective-permute-start | bytes 196616 | tf_op jit(solution)/shard_map/ppermute | solution.py:29
  73.9 10.5 %collective-permute-start.21 = (bf16[288,128]{1,0:T(8,128)(2,1)S(1)}, bf16[288,128]{1,0:T(8,128)(2,1)S(1)}, u32[]{:S(2)}, u32[]{:S(2)}) collective-permute-start(bf16[288,128]{1,0:T(8,128)(2,1)S(1)} %get-tuple-element.60), channel_id=1, source_target_pairs={{0,4},{1,5},{2,6},{3,7},{4,0},{5,1},{6,2},{7,3},{8,12},{9,13},{10,... | collective-permute-start | bytes 221192 | tf_op jit(solution)/shard_map/ppermute | solution.py:29
  75.2 12.9 %collective-permute-start.22 = (bf16[288,128]{1,0:T(8,128)(2,1)S(1)}, bf16[288,128]{1,0:T(8,128)(2,1)S(1)}, u32[]{:S(2)}, u32[]{:S(2)}) collective-permute-start(bf16[288,128]{1,0:T(8,128)(2,1)S(1)} %get-tuple-element.61), channel_id=1, source_target_pairs={{0,8},{1,9},{2,10},{3,11},{4,12},{5,13},{6,14},{7,15},{8,0},{9,1},... | collective-permute-start | bytes 221192 | tf_op jit(solution)/shard_map/ppermute | solution.py:29
  75.9 12.2 %collective-permute-start.23 = (bf16[288,128]{1,0:T(8,128)(2,1)S(1)}, bf16[288,128]{1,0:T(8,128)(2,1)S(1)}, u32[]{:S(2)}, u32[]{:S(2)}) collective-permute-start(bf16[288,128]{1,0:T(8,128)(2,1)S(1)} %get-tuple-element.62), channel_id=1, source_target_pairs={{0,12},{1,13},{2,14},{3,15},{4,8},{5,9},{6,10},{7,11},{8,4},{9,5},... | collective-permute-start | bytes 221192 | tf_op jit(solution)/shard_map/ppermute | solution.py:29
  82.5 7.4 %collective-permute-start.18 = (bf16[288,128]{1,0:T(8,128)(2,1)S(1)}, bf16[288,128]{1,0:T(8,128)(2,1)S(1)}, u32[]{:S(2)}, u32[]{:S(2)}) collective-permute-start(bf16[288,128]{1,0:T(8,128)(2,1)S(1)} %get-tuple-element.56), channel_id=1, source_target_pairs={{0,4},{1,5},{2,6},{3,7},{4,0},{5,1},{6,2},{7,3},{8,12},{9,13},{10,... | collective-permute-start | bytes 221192 | tf_op jit(solution)/shard_map/ppermute | solution.py:29
  82.9 7.0 %collective-permute-start.19 = (bf16[288,128]{1,0:T(8,128)(2,1)S(1)}, bf16[288,128]{1,0:T(8,128)(2,1)S(1)}, u32[]{:S(2)}, u32[]{:S(2)}) collective-permute-start(bf16[288,128]{1,0:T(8,128)(2,1)S(1)} %get-tuple-element.57), channel_id=1, source_target_pairs={{0,8},{1,9},{2,10},{3,11},{4,12},{5,13},{6,14},{7,15},{8,0},{9,1},... | collective-permute-start | bytes 221192 | tf_op jit(solution)/shard_map/ppermute | solution.py:29
  84.4 3.7 %copy-start.2 = (bf16[576,1152]{1,0:T(8,128)(2,1)S(1)}, bf16[576,1152]{1,0:T(8,128)(2,1)}, u32[]{:S(2)}) copy-start(bf16[576,1152]{1,0:T(8,128)(2,1)} %weight_ref.3) | copy-start | bytes 3981316
  84.4 6.2 %collective-permute-start.20 = (bf16[288,128]{1,0:T(8,128)(2,1)S(1)}, bf16[288,128]{1,0:T(8,128)(2,1)S(1)}, u32[]{:S(2)}, u32[]{:S(2)}) collective-permute-start(bf16[288,128]{1,0:T(8,128)(2,1)S(1)} %get-tuple-element.58), channel_id=1, source_target_pairs={{0,12},{1,13},{2,14},{3,15},{4,8},{5,9},{6,10},{7,11},{8,4},{9,5},... | collective-permute-start | bytes 221192 | tf_op jit(solution)/shard_map/ppermute | solution.py:29

commit v3 on v2

--- a/solution.py
+++ b/solution.py
@@ -14,7 +14,7 @@
 LANES = 128
 QUERY_ROWS = 128
 PAIR_GROUPS = ((0,), (1,), (2,), (3,))
-EMIT = (False, True, False, True)
+EMIT = (False, False, True, True)
 HALVES = 2
 
 
@@ -141,8 +141,21 @@
     )(slot, pltpu.with_memory_space_constraint(tokens, pltpu.HBM))
 
 
-def modulation_kernel(slot_ref, time_ref, order_ref, rate_ref, table_ref, mix_ref, out_ref, place_ref):
-    frames, feature_width = place_ref.shape
+def projection_kernel(slot_ref, time_ref, order_ref, weight_hbm, *refs, frames, width):
+    rate_ref, table_ref, mix_ref = refs[:3]
+    pieces = refs[3 : 3 + frames]
+    query_ref, kv_ref, modulation_ref, place_ref, weight_ref, sems = refs[3 + frames :]
+    padded = query_ref.shape[1]
+    feature_width = place_ref.shape[1]
+    middle = width + padded
+    parts = (slice(0, padded), slice(padded, middle), slice(middle, weight_ref.shape[0]))
+    copies = [
+        pltpu.make_async_copy(weight_hbm.at[part, :], weight_ref.at[part, :], sems.at[number])
+        for number, part in enumerate(parts)
+    ]
+    for copy in copies:
+        copy.start()
+
     rows = -(-(frames + 1) // 8) * 8
     row = lax.broadcasted_iota(jnp.int32, (rows, 1), 0)
     position = jnp.where(row == frames, time_ref[0], 0)
@@ -153,62 +166,54 @@
     column = lax.broadcasted_iota(jnp.int32, (rows, feature_width), 1)
     waves = jnp.where(column < feature_width // 2, jnp.sin(angles), jnp.cos(angles))
     place_ref[...] = waves[:frames]
-    out_ref[...] = table_ref[...] + mix_ref[...] * waves[frames : frames + 1]
-
-
-def modulate(slot, timestep, frame_order, mod_table, mod_mix):
-    frames, feature_width = frame_order.shape[0], mod_table.shape[1]
-    half = feature_width // 2
-    rates = np.exp(-math.log(10000.0) * np.arange(half) / half).astype(np.float32)
-    operands = [jnp.asarray(np.concatenate([rates, rates])[None]), mod_table, mod_mix]
-    operands = [pltpu.with_memory_space_constraint(array, pltpu.VMEM) for array in operands]
-    return pl.pallas_call(
-        modulation_kernel,
-        out_shape=[pltpu.VMEM(mod_table.shape, f32), pltpu.VMEM((frames, feature_width), f32)],
-        in_specs=[pl.BlockSpec(memory_space=pltpu.SMEM) for _ in range(3)] + vmem_specs(3),
-        out_specs=vmem_specs(2),
-        compiler_params=pltpu.CompilerParams(vmem_limit_bytes=2**20),
-        name="modulation",
-    )(slot, timestep, frame_order, *operands)
-
-
-def projection_kernel(weight_hbm, *refs, frames, width):
-    pieces = refs[:frames]
-    modulation_ref, query_ref, kv_ref, weight_ref, sems = refs[frames:]
-    padded = query_ref.shape[1]
-    parts = (slice(0, padded), slice(padded, weight_ref.shape[0]))
-    copies = [
-        pltpu.make_async_copy(weight_hbm.at[part, :], weight_ref.at[part, :], sems.at[number])
-        for number, part in enumerate(parts)
-    ]
-    for copy in copies:
-        copy.start()
+    modulation = table_ref[...] + mix_ref[...] * waves[frames : frames + 1]
+    modulation_ref[...] = modulation
+
     tokens = jnp.concatenate([ref[...] for ref in pieces], axis=0).astype(f32)
-    inputs = normalize(tokens) * (1.0 + modulation_ref[1:2, :]) + modulation_ref[0:1, :]
+    inputs = normalize(tokens) * (1.0 + modulation[1:2, :]) + modulation[0:1, :]
     inputs = inputs.astype(bf16)
+
+    def project(first, last):
+        return lax.dot_general(
+            inputs, weight_ref[first:last, :], NT, preferred_element_type=f32
+        ).astype(bf16)
+
     copies[0].wait()
-    query_ref[...] = lax.dot_general(
-        inputs, weight_ref[:padded, :], NT, preferred_element_type=f32
-    ).astype(bf16)
+    query_ref[...] = project(0, padded)
     copies[1].wait()
-    kv_ref[...] = lax.dot_general(
-        inputs, weight_ref[width:, :], NT, preferred_element_type=f32
-    ).astype(bf16)
-
-
-def projections(pieces, weight, modulation, width):
+    kv_ref[:, :padded] = project(width, middle)
+    copies[2].wait()
+    kv_ref[:, padded:] = project(middle, weight_ref.shape[0])
+
+
+def projections(slot, timestep, frame_order, weight, mod_table, mod_mix, pieces, width):
     frames = len(pieces)
     piece, feature_width = pieces[0].shape
     padded = -(-width // LANES) * LANES
     rows = frames * piece
+    half = feature_width // 2
+    rates = np.exp(-math.log(10000.0) * np.arange(half) / half).astype(np.float32)
+    rates = jnp.asarray(np.concatenate([rates, rates])[None])
     operands = [pltpu.with_memory_space_constraint(weight, pltpu.HBM)]
-    operands += [pltpu.with_memory_space_constraint(x, pltpu.VMEM) for x in (*pieces, modulation)]
+    operands += [
+        pltpu.with_memory_space_constraint(x, pltpu.VMEM)
+        for x in (rates, mod_table, mod_mix, *pieces)
+    ]
     return pl.pallas_call(
         functools.partial(projection_kernel, frames=frames, width=width),
-        out_shape=[pltpu.VMEM((rows, padded), bf16), pltpu.VMEM((rows, 2 * width), bf16)],
-        in_specs=[pl.BlockSpec(memory_space=pltpu.HBM), *vmem_specs(frames + 1)],
-        out_specs=vmem_specs(2),
-        scratch_shapes=[pltpu.VMEM(weight.shape, bf16), pltpu.SemaphoreType.DMA((2,))],
+        out_shape=[
+            pltpu.VMEM((rows, padded), bf16),
+            pltpu.VMEM((rows, 2 * width), bf16),
+            pltpu.VMEM(mod_table.shape, f32),
+            pltpu.VMEM((frames, feature_width), f32),
+        ],
+        in_specs=[
+            *[pl.BlockSpec(memory_space=pltpu.SMEM) for _ in range(3)],
+            pl.BlockSpec(memory_space=pltpu.HBM),
+            *vmem_specs(3 + frames),
+        ],
+        out_specs=vmem_specs(4),
+        scratch_shapes=[pltpu.VMEM(weight.shape, bf16), pltpu.SemaphoreType.DMA((3,))],
         compiler_params=pltpu.CompilerParams(vmem_limit_bytes=8 * 2**20),
         cost_estimate=pl.CostEstimate(
             flops=2 * rows * feature_width * 3 * width,
@@ -216,7 +221,7 @@
             transcendentals=0,
         ),
         name="projections",
-    )(*operands)
+    )(slot, timestep, frame_order, *operands)
 
 
 def stack_rows(rows, width):
@@ -735,11 +740,14 @@
     there = [pieces[0]]
     there += [permute(pieces[s], ahead(s)) for s in range(1, frames)]
 
-    modulation, places = modulate(slot_word, timestep, frame_order, mod_table, mod_mix)
-    query, own_kv = projections(
+    query, own_kv, modulation, places = projections(
+        slot_word,
+        timestep,
+        frame_order,
+        jnp.swapaxes(spatial_qkv, 1, 2).reshape(3 * width, feature_width),
+        mod_table,
+        mod_mix,
         pieces,
-        jnp.swapaxes(spatial_qkv, 1, 2).reshape(3 * width, feature_width),
-        modulation,
         width,
     )
 

time: 92.7 us -> 94 us (1.014)
  waiting for transfers between devices: 25 us -> 26.4 us
    pallas_call x1, Pallas kernels: 4.91 us -> 6.35 us  [projections(): pl.pallas_call(functools.partial(projection_kernel, frames=frames, width=...]
    ppermute x24, waiting for transfers between devices: 25 us -> 26.4 us  [permute(): lax.ppermute(value, 'patch', [(source, target(source)) for source in rang...]
  transfers between devices with their start and end apart: 24 -> 24, of which waited for: 6 -> 5; matrix products, arithmetic and copies ran while one was open for 0% -> 0% of each run, Pallas kernels for 32% -> 32%
where the time goes in v3:
time: 94 us; the launch traced here: 93.8 us
  Pallas kernels  36 us (38%)
  starting transfers between devices  30.3 us (32%)
  waiting for transfers between devices  26.4 us (28%)
  between operations  1.05 us (1%)
    ppermute x24, starting transfers between devices, permute(): lax.ppermute(value, 'patch', [(source, target(source)) for source in rang...  30.3 us
    ppermute x24, waiting for transfers between devices, permute(): lax.ppermute(value, 'patch', [(source, target(source)) for source in rang...  26.4 us
    pallas_call x7, Pallas kernels, on_chip_call(): pl.pallas_call(kernel, out_shape=[pltpu.VMEM(shape, dtype) for shape, dty...  23.4 us
    pallas_call x1, Pallas kernels, projections(): pl.pallas_call(functools.partial(projection_kernel, frames=frames, width=...  6.35 us
    pallas_call x2, Pallas kernels, output(): pl.pallas_call(functools.partial(output_kernel, frames=frames, number=num...  3.49 us
  transfers between devices with their start and end apart: 24, of which 5 were waited for; matrix products, arithmetic and copies ran while one was open for 0% of the time, Pallas kernels for 32%

profile of v3, /device:TPU:0, one launch (start us, length us, event | category | flops | bytes accessed | tf_op | source)
XLA Modules:
  0.0 93.8 jit_solution(10009931923997172540)
XLA Ops:
  0.0 0.6 collective-permute-start
  0.6 1.4 %chunks.1 = (bf16[512,512]{1,0:T(8,128)(2,1)S(1)}, bf16[512,256]{1,0:T(8,128)(2,1)S(1)}, bf16[512,256]{1,0:T(8,128)(2,1)S(1)}, bf16[512,128]{1,0:T(8,128)(2,1)S(1)}) custom-call(bf16[512,1152]{1,0:T(8,128)(2,1)} %kv_ref.1), custom_call_target="tpu_custom_call" | custom-call | tf_op jit(solution)/shard_map/chunks/pallas_call | solution.py:101
  2.0 2.6 %collective-permute-start.1 = (bf16[512,512]{1,0:T(8,128)(2,1)S(1)}, bf16[512,512]{1,0:T(8,128)(2,1)S(1)}, u32[]{:S(2)}, u32[]{:S(2)}) collective-permute-start(bf16[512,512]{1,0:T(8,128)(2,1)S(1)} %get-tuple-element.40), channel_id=1, source_target_pairs={{0,2},{1,3},{2,0},{3,1},{4,6},{5,7},{6,4},{7,5},{8,10},{9,11},{10,... | collective-permute-start | bytes 1572872 | tf_op jit(solution)/shard_map/ppermute | solution.py:29
  4.6 12.6 %collective-permute-done.1.refs_3_ = bf16[512,512]{1,0:T(8,128)(2,1)S(1)} collective-permute-done((bf16[512,512]{1,0:T(8,128)(2,1)S(1)}, bf16[512,512]{1,0:T(8,128)(2,1)S(1)}, u32[]{:S(2)}, u32[]{:S(2)}) %collective-permute-start.1) | collective-permute-done | bytes 524320 | tf_op jit(solution)/shard_map/ppermute | solution.py:29
  17.2 0.0 collective-permute-start.4
  17.2 1.7 %collective-permute-start.2 = (bf16[512,256]{1,0:T(8,128)(2,1)S(1)}, bf16[512,256]{1,0:T(8,128)(2,1)S(1)}, u32[]{:S(2)}, u32[]{:S(2)}) collective-permute-start(bf16[512,256]{1,0:T(8,128)(2,1)S(1)} %get-tuple-element.41), channel_id=1, source_target_pairs={{0,2},{1,3},{2,0},{3,1},{4,6},{5,7},{6,4},{7,5},{8,10},{9,11},{10,... | collective-permute-start | bytes 786440 | tf_op jit(solution)/shard_map/ppermute | solution.py:29
  18.9 0.3 collective-permute-start.3
  19.2 1.3 %pieces.1 = (bf16[128,1152]{1,0:T(8,128)(2,1)S(1)}, bf16[128,1152]{1,0:T(8,128)(2,1)S(1)}, bf16[128,1152]{1,0:T(8,128)(2,1)S(1)}, bf16[128,1152]{1,0:T(8,128)(2,1)S(1)}) custom-call(s32[1]{0:T(128)} %bitcast.slot_ref, bf16[512,1152]{1,0:T(8,128)(2,1)} %tokens_ref.1), custom_call_target="tpu_custom_call" | custom-call | tf_op jit(solution)/shard_map/pieces/pallas_call | solution.py:130
  20.5 2.9 %collective-permute-start.10 = (bf16[128,1152]{1,0:T(8,128)(2,1)S(1)}, bf16[128,1152]{1,0:T(8,128)(2,1)S(1)}, u32[]{:S(2)}, u32[]{:S(2)}) collective-permute-start(bf16[128,1152]{1,0:T(8,128)(2,1)S(1)} %get-tuple-element.36.refs_5_.refs_2_), channel_id=1, source_target_pairs={{0,8},{1,9},{2,10},{3,11},{4,12},{5,13},{6,14},{7,15},{8,0},{9,1},... | collective-permute-start | bytes 884744 | tf_op jit(solution)/shard_map/ppermute | solution.py:29
  24.0 2.4 %collective-permute-done.2.refs_4_ = bf16[512,256]{1,0:T(8,128)(2,1)S(1)} collective-permute-done((bf16[512,256]{1,0:T(8,128)(2,1)S(1)}, bf16[512,256]{1,0:T(8,128)(2,1)S(1)}, u32[]{:S(2)}, u32[]{:S(2)}) %collective-permute-start.2) | collective-permute-done | bytes 262176 | tf_op jit(solution)/shard_map/ppermute | solution.py:29
  26.4 0.0 collective-permute-start.5
  26.4 6.3 %projections.1 = (bf16[512,640]{1,0:T(8,128)(2,1)S(1)}, bf16[512,1152]{1,0:T(8,128)(2,1)S(1)}, f32[6,1152]{1,0:T(8,128)S(1)}, f32[4,1152]{1,0:T(4,128)S(1)}) custom-call(s32[1]{0:T(128)} %bitcast.slot_ref, s32[1]{0:T(128)S(6)} %copy.14.time_ref, s32[4]{0:T(128)S(1)} %copy-done.5, bf16[1728,1152]{1,0:T(8,128)(2,1)} %bitcast.9, f32[1,1152]{1,0:T(1,128)S(1)} %copy-done.6, ...), custom_call_target="tpu_custom_call" | custom-call | flops 2038431744 | bytes 3981312 | tf_op jit(solution)/shard_map/projections/pallas_call | solution.py:202
  32.8 0.0 collective-permute-done.3.refs_5_
  32.8 3.9 %collective-permute-start.11 = (bf16[128,1152]{1,0:T(8,128)(2,1)S(1)}, bf16[128,1152]{1,0:T(8,128)(2,1)S(1)}, u32[]{:S(2)}, u32[]{:S(2)}) collective-permute-start(bf16[128,1152]{1,0:T(8,128)(2,1)S(1)} %get-tuple-element.37.refs_6_.refs_3_), channel_id=1, source_target_pairs={{0,12},{1,13},{2,14},{3,15},{4,8},{5,9},{6,10},{7,11},{8,4},{9,5},... | collective-permute-start | bytes 884744 | tf_op jit(solution)/shard_map/ppermute | solution.py:29
  36.7 0.0 collective-permute-done.4.refs_4_.refs_5_.refs_6_.refs_7_
  36.7 1.5 %collective-permute-start.7 = (bf16[512,128]{1,0:T(8,128)(2,1)S(1)}, bf16[512,128]{1,0:T(8,128)(2,1)S(1)}, u32[]{:S(2)}, u32[]{:S(2)}) collective-permute-start(bf16[512,128]{1,0:T(8,128)(2,1)S(1)} %get-tuple-element.44), channel_id=1, source_target_pairs={{0,2},{1,3},{2,0},{3,1},{4,6},{5,7},{6,4},{7,5},{8,10},{9,11},{10,... | collective-permute-start | bytes 393224 | tf_op jit(solution)/shard_map/ppermute | solution.py:29
  38.2 0.0 collective-permute-done.refs_2_
  38.2 0.0 collective-permute-start.6
  38.2 3.4 %shard_map.109.refs_7_ = bf16[512,256]{1,0:T(8,128)(2,1)S(1)} custom-call(bf16[512,640]{1,0:T(8,128)(2,1)S(1)} %get-tuple-element.38.refs_0_, bf16[512,1152]{1,0:T(8,128)(2,1)S(1)} %get-tuple-element.39.refs_1_, bf16[512,1152]{1,0:T(8,128)(2,1)S(1)} %collective-permute-done.refs_2_, bf16[512,512]{1,0:T(8,128)(2,1)S(1)} %collective-permute-done.1.refs_3_, ...), custom_call_target="tpu_custom_call" | custom-call | flops 2147483648 | bytes 4063232 | tf_op jit(solution)/shard_map/pallas_call | solution.py:67
  41.6 0.7 collective-permute-done.7.refs_6_
  42.3 3.5 %shard_map.110.refs_9_ = bf16[512,384]{1,0:T(8,128)(2,1)S(1)} custom-call(bf16[512,640]{1,0:T(8,128)(2,1)S(1)} %get-tuple-element.38.refs_0_, bf16[512,1152]{1,0:T(8,128)(2,1)S(1)} %get-tuple-element.39.refs_1_, bf16[512,1152]{1,0:T(8,128)(2,1)S(1)} %collective-permute-done.refs_2_, bf16[512,512]{1,0:T(8,128)(2,1)S(1)} %collective-permute-done.1.refs_3_, ...), custom_call_target="tpu_custom_call" | custom-call | flops 2147483648 | bytes 4849664 | tf_op jit(solution)/shard_map/pallas_call | solution.py:67
  45.8 0.0 collective-permute-done.6.refs_8_.refs_9_
  45.8 3.7 %shard_map.111 = (bf16[384,128]{1,0:T(8,128)(2,1)S(1)}, bf16[384,128]{1,0:T(8,128)(2,1)S(1)}, bf16[384,128]{1,0:T(8,128)(2,1)S(1)}, bf16[384,128]{1,0:T(8,128)(2,1)S(1)}, bf16[512,128]{1,0:T(8,128)(2,1)S(1)}) custom-call(bf16[512,640]{1,0:T(8,128)(2,1)S(1)} %get-tuple-element.38.refs_0_, bf16[512,1152]{1,0:T(8,128)(2,1)S(1)} %get-tuple-element.39.refs_1_, ...), custom_call_target="tpu_custom_call" | custom-call | flops 2147483648 | bytes 5505024 | tf_op jit(solution)/shard_map/pallas_call | solution.py:67
  49.5 0.0 collective-permute-done.8.refs_10_
  49.5 0.0 copy-start
  49.5 0.0 copy-start.1
  49.5 3.5 %shard_map.112 = (bf16[192,128]{1,0:T(8,128)(2,1)S(1)}, bf16[192,128]{1,0:T(8,128)(2,1)S(1)}, bf16[192,128]{1,0:T(8,128)(2,1)S(1)}, bf16[192,128]{1,0:T(8,128)(2,1)S(1)}) custom-call(bf16[512,640]{1,0:T(8,128)(2,1)S(1)} %get-tuple-element.38.refs_0_, bf16[512,1152]{1,0:T(8,128)(2,1)S(1)} %get-tuple-element.39.refs_1_, ...), custom_call_target="tpu_custom_call" | custom-call | flops 2147483648 | bytes 5505024 | tf_op jit(solution)/shard_map/pallas_call | solution.py:67
  53.1 2.1 %collective-permute-start.13 = (bf16[192,128]{1,0:T(8,128)(2,1)S(1)}, bf16[192,128]{1,0:T(8,128)(2,1)S(1)}, u32[]{:S(2)}, u32[]{:S(2)}) collective-permute-start(bf16[192,128]{1,0:T(8,128)(2,1)S(1)} %get-tuple-element.48.refs_7_), channel_id=1, source_target_pairs={{0,4},{1,5},{2,6},{3,7},{4,0},{5,1},{6,2},{7,3},{8,12},{9,13},{10,... | collective-permute-start | bytes 147464 | tf_op jit(solution)/shard_map/ppermute | solution.py:29
  55.2 0.1 collective-permute-start.12
  55.2 0.9 collective-permute-start.14
  56.1 3.5 %collective-permute-start.16 = (bf16[384,128]{1,0:T(8,128)(2,1)S(1)}, bf16[384,128]{1,0:T(8,128)(2,1)S(1)}, u32[]{:S(2)}, u32[]{:S(2)}) collective-permute-start(bf16[384,128]{1,0:T(8,128)(2,1)S(1)} %get-tuple-element.51.refs_10_), channel_id=1, source_target_pairs={{0,12},{1,13},{2,14},{3,15},{4,8},{5,9},{6,10},{7,11},{8,4},{9,5},... | collective-permute-start | bytes 294920 | tf_op jit(solution)/shard_map/ppermute | solution.py:29
  59.6 0.0 collective-permute-done.9.refs_1_
  59.6 1.5 %collective-permute-start.17 = (bf16[192,128]{1,0:T(8,128)(2,1)S(1)}, bf16[192,128]{1,0:T(8,128)(2,1)S(1)}, u32[]{:S(2)}, u32[]{:S(2)}) collective-permute-start(bf16[192,128]{1,0:T(8,128)(2,1)S(1)} %get-tuple-element.52.refs_11_), channel_id=1, source_target_pairs={{0,12},{1,13},{2,14},{3,15},{4,8},{5,9},{6,10},{7,11},{8,4},{9,5},... | collective-permute-start | bytes 147464 | tf_op jit(solution)/shard_map/ppermute | solution.py:29
  61.1 10.0 %collective-permute-done.15.refs_9_ = bf16[192,128]{1,0:T(8,128)(2,1)S(1)} collective-permute-done((bf16[192,128]{1,0:T(8,128)(2,1)S(1)}, bf16[192,128]{1,0:T(8,128)(2,1)S(1)}, u32[]{:S(2)}, u32[]{:S(2)}) %collective-permute-start.15) | collective-permute-done | bytes 49184 | tf_op jit(solution)/shard_map/ppermute | solution.py:29
  71.1 0.0 collective-permute-done.16.refs_10_
  71.2 4.0 %shard_map.115 = (bf16[288,128]{1,0:T(8,128)(2,1)S(1)}, bf16[288,128]{1,0:T(8,128)(2,1)S(1)}, bf16[288,128]{1,0:T(8,128)(2,1)S(1)}, bf16[288,128]{1,0:T(8,128)(2,1)S(1)}) custom-call(bf16[128,1152]{1,0:T(8,128)(2,1)S(1)} %get-tuple-element.34.refs_3_.refs_0_, bf16[128,1152]{1,0:T(8,128)(2,1)S(1)} %collective-permute-done.9.refs_1_, ...), custom_call_target="tpu_custom_call" | custom-call | flops 1698693120 | bytes 7123968 | tf_op jit(solution)/shard_map/pallas_call | solution.py:67
  75.2 1.1 %collective-permute-start.21 = (bf16[288,128]{1,0:T(8,128)(2,1)S(1)}, bf16[288,128]{1,0:T(8,128)(2,1)S(1)}, u32[]{:S(2)}, u32[]{:S(2)}) collective-permute-start(bf16[288,128]{1,0:T(8,128)(2,1)S(1)} %get-tuple-element.60), channel_id=1, source_target_pairs={{0,4},{1,5},{2,6},{3,7},{4,0},{5,1},{6,2},{7,3},{8,12},{9,13},{10,... | collective-permute-start | bytes 221192 | tf_op jit(solution)/shard_map/ppermute | solution.py:29
  76.3 0.9 collective-permute-start.22
  77.2 2.4 %collective-permute-start.23 = (bf16[288,128]{1,0:T(8,128)(2,1)S(1)}, bf16[288,128]{1,0:T(8,128)(2,1)S(1)}, u32[]{:S(2)}, u32[]{:S(2)}) collective-permute-start(bf16[288,128]{1,0:T(8,128)(2,1)S(1)} %get-tuple-element.62), channel_id=1, source_target_pairs={{0,12},{1,13},{2,14},{3,15},{4,8},{5,9},{6,10},{7,11},{8,4},{9,5},... | collective-permute-start | bytes 221192 | tf_op jit(solution)/shard_map/ppermute | solution.py:29
  79.6 4.1 %shard_map.114 = (bf16[288,128]{1,0:T(8,128)(2,1)S(1)}, bf16[288,128]{1,0:T(8,128)(2,1)S(1)}, bf16[288,128]{1,0:T(8,128)(2,1)S(1)}, bf16[288,128]{1,0:T(8,128)(2,1)S(1)}) custom-call(bf16[128,1152]{1,0:T(8,128)(2,1)S(1)} %get-tuple-element.34.refs_3_.refs_0_, bf16[128,1152]{1,0:T(8,128)(2,1)S(1)} %collective-permute-done.9.refs_1_, ...), custom_call_target="tpu_custom_call" | custom-call | flops 1698693120 | bytes 7123968 | tf_op jit(solution)/shard_map/pallas_call | solution.py:67
  83.7 0.2 collective-permute-start.18
  83.9 1.8 %collective-permute-start.19 = (bf16[288,128]{1,0:T(8,128)(2,1)S(1)}, bf16[288,128]{1,0:T(8,128)(2,1)S(1)}, u32[]{:S(2)}, u32[]{:S(2)}) collective-permute-start(bf16[288,128]{1,0:T(8,128)(2,1)S(1)} %get-tuple-element.57), channel_id=1, source_target_pairs={{0,8},{1,9},{2,10},{3,11},{4,12},{5,13},{6,14},{7,15},{8,0},{9,1},... | collective-permute-start | bytes 221192 | tf_op jit(solution)/shard_map/ppermute | solution.py:29
  85.7 2.4 %collective-permute-start.20 = (bf16[288,128]{1,0:T(8,128)(2,1)S(1)}, bf16[288,128]{1,0:T(8,128)(2,1)S(1)}, u32[]{:S(2)}, u32[]{:S(2)}) collective-permute-start(bf16[288,128]{1,0:T(8,128)(2,1)S(1)} %get-tuple-element.58), channel_id=1, source_target_pairs={{0,12},{1,13},{2,14},{3,15},{4,8},{5,9},{6,10},{7,11},{8,4},{9,5},... | collective-permute-start | bytes 221192 | tf_op jit(solution)/shard_map/ppermute | solution.py:29
  88.1 1.2 %shard_map.113.after_ref = f32[512,1152]{1,0:T(8,128)S(1)} custom-call(bf16[128,1152]{1,0:T(8,128)(2,1)S(1)} %get-tuple-element.34.refs_3_.refs_0_, bf16[128,1152]{1,0:T(8,128)(2,1)S(1)} %get-tuple-element.35.refs_4_.refs_1_, bf16[128,1152]{1,0:T(8,128)(2,1)S(1)} %get-tuple-element.36.refs_5_.refs_2_, ...), custom_call_target="tpu_custom_call" | custom-call | flops 679477248 | bytes 3124224 | tf_op jit(solution)/shard_map/pallas_call | solution.py:67
  89.3 0.0 collective-permute-done.22.refs_2_
  89.4 1.7 %shard_map.116.refs_4_ = f32[512,1152]{1,0:T(8,128)} custom-call(s32[1]{0:T(128)} %bitcast.slot_ref, f32[512,1152]{1,0:T(8,128)S(1)} %shard_map.113.after_ref, bf16[576,1152]{1,0:T(8,128)(2,1)S(1)} %copy-done.2, f32[6,1152]{1,0:T(8,128)S(1)} %get-tuple-element.53.refs_13_.refs_14_.modulation_ref, bf16[288,128]{1,0:T(8,128)(2,1)S(1)} %get-tuple-element.59.refs_0_, ...), custom_call_target="tpu_custom_call" | custom-call | tf_op jit(solution)/shard_map/pallas_call | solution.py:686
  91.1 0.7 collective-permute-done.20.refs_3_
  91.9 1.7 %shard_map.117 = f32[512,1152]{1,0:T(8,128)} custom-call(s32[1]{0:T(128)} %bitcast.slot_ref, f32[512,1152]{1,0:T(8,128)S(1)} %shard_map.113.after_ref, bf16[576,1152]{1,0:T(8,128)(2,1)S(1)} %copy-done.2, f32[6,1152]{1,0:T(8,128)S(1)} %get-tuple-element.53.refs_13_.refs_14_.modulation_ref, ...), custom_call_target="tpu_custom_call", output_to_operand_aliasing={{}: (8, {})} | custom-call | tf_op jit(solution)/shard_map/pallas_call | solution.py:686
  (26 shorter events, 0.1 us)
Async XLA Ops:
  0.0 26.4 %copy-start.6 = (f32[1,1152]{1,0:T(1,128)S(1)}, f32[1,1152]{1,0:T(1,128)}, u32[]{:S(2)}) copy-start(f32[1,1152]{1,0:T(1,128)} %constant.22.clone.refs_0_) | copy-start | bytes 13828
  0.0 26.4 %copy-start.3 = (f32[6,1152]{1,0:T(8,128)S(1)}, f32[6,1152]{1,0:T(8,128)}, u32[]{:S(2)}) copy-start(f32[6,1152]{1,0:T(8,128)} %refs_1_.1) | copy-start | bytes 82948
  0.0 26.4 %copy-start.4 = (f32[6,1152]{1,0:T(8,128)S(1)}, f32[6,1152]{1,0:T(8,128)}, u32[]{:S(2)}) copy-start(f32[6,1152]{1,0:T(8,128)} %refs_2_.1) | copy-start | bytes 82948
  0.0 26.4 %copy-start.5 = (s32[4]{0:T(128)S(1)}, s32[4]{0:T(128)}, u32[]{:S(2)}) copy-start(s32[4]{0:T(128)} %order_ref.1) | copy-start | bytes 52
  0.0 38.2 %collective-permute-start = (bf16[512,1152]{1,0:T(8,128)(2,1)}, bf16[512,1152]{1,0:T(8,128)(2,1)S(1)}, u32[]{:S(2)}, u32[]{:S(2)}) collective-permute-start(bf16[512,1152]{1,0:T(8,128)(2,1)} %kv_ref.1), channel_id=1, source_target_pairs={{0,1},{1,0},{2,3},{3,2},{4,5},{5,4},{6,7},{7,6},{8,9},{9,8},{10,11... | collective-permute-start | bytes 3538952 | tf_op jit(solution)/shard_map/ppermute | solution.py:29
  2.0 15.2 %collective-permute-start.1 = (bf16[512,512]{1,0:T(8,128)(2,1)S(1)}, bf16[512,512]{1,0:T(8,128)(2,1)S(1)}, u32[]{:S(2)}, u32[]{:S(2)}) collective-permute-start(bf16[512,512]{1,0:T(8,128)(2,1)S(1)} %get-tuple-element.40), channel_id=1, source_target_pairs={{0,2},{1,3},{2,0},{3,1},{4,6},{5,7},{6,4},{7,5},{8,10},{9,11},{10,... | collective-permute-start | bytes 1572872 | tf_op jit(solution)/shard_map/ppermute | solution.py:29
  17.2 19.5 %collective-permute-start.4 = (bf16[512,512]{1,0:T(8,128)(2,1)S(1)}, bf16[512,512]{1,0:T(8,128)(2,1)S(1)}, u32[]{:S(2)}, u32[]{:S(2)}) collective-permute-start(bf16[512,512]{1,0:T(8,128)(2,1)S(1)} %collective-permute-done.1.refs_3_), channel_id=1, source_target_pairs={{0,1},{1,0},{2,3},{3,2},{4,5},{5,4},{6,7},{7,6},{8,9},{9,8},{10,11... | collective-permute-start | bytes 1572872 | tf_op jit(solution)/shard_map/ppermute | solution.py:29
  17.2 9.2 %collective-permute-start.2 = (bf16[512,256]{1,0:T(8,128)(2,1)S(1)}, bf16[512,256]{1,0:T(8,128)(2,1)S(1)}, u32[]{:S(2)}, u32[]{:S(2)}) collective-permute-start(bf16[512,256]{1,0:T(8,128)(2,1)S(1)} %get-tuple-element.41), channel_id=1, source_target_pairs={{0,2},{1,3},{2,0},{3,1},{4,6},{5,7},{6,4},{7,5},{8,10},{9,11},{10,... | collective-permute-start | bytes 786440 | tf_op jit(solution)/shard_map/ppermute | solution.py:29
  18.9 13.8 %collective-permute-start.3 = (bf16[512,256]{1,0:T(8,128)(2,1)S(1)}, bf16[512,256]{1,0:T(8,128)(2,1)S(1)}, u32[]{:S(2)}, u32[]{:S(2)}) collective-permute-start(bf16[512,256]{1,0:T(8,128)(2,1)S(1)} %get-tuple-element.42), channel_id=1, source_target_pairs={{0,2},{1,3},{2,0},{3,1},{4,6},{5,7},{6,4},{7,5},{8,10},{9,11},{10,... | collective-permute-start | bytes 786440 | tf_op jit(solution)/shard_map/ppermute | solution.py:29
  20.5 34.8 %collective-permute-start.10 = (bf16[128,1152]{1,0:T(8,128)(2,1)S(1)}, bf16[128,1152]{1,0:T(8,128)(2,1)S(1)}, u32[]{:S(2)}, u32[]{:S(2)}) collective-permute-start(bf16[128,1152]{1,0:T(8,128)(2,1)S(1)} %get-tuple-element.36.refs_5_.refs_2_), channel_id=1, source_target_pairs={{0,8},{1,9},{2,10},{3,11},{4,12},{5,13},{6,14},{7,15},{8,0},{9,1},... | collective-permute-start | bytes 884744 | tf_op jit(solution)/shard_map/ppermute | solution.py:29
  26.4 15.9 %collective-permute-start.5 = (bf16[512,256]{1,0:T(8,128)(2,1)S(1)}, bf16[512,256]{1,0:T(8,128)(2,1)S(1)}, u32[]{:S(2)}, u32[]{:S(2)}) collective-permute-start(bf16[512,256]{1,0:T(8,128)(2,1)S(1)} %collective-permute-done.2.refs_4_), channel_id=1, source_target_pairs={{0,1},{1,0},{2,3},{3,2},{4,5},{5,4},{6,7},{7,6},{8,9},{9,8},{10,11... | collective-permute-start | bytes 786440 | tf_op jit(solution)/shard_map/ppermute | solution.py:29
  32.8 23.3 %collective-permute-start.11 = (bf16[128,1152]{1,0:T(8,128)(2,1)S(1)}, bf16[128,1152]{1,0:T(8,128)(2,1)S(1)}, u32[]{:S(2)}, u32[]{:S(2)}) collective-permute-start(bf16[128,1152]{1,0:T(8,128)(2,1)S(1)} %get-tuple-element.37.refs_6_.refs_3_), channel_id=1, source_target_pairs={{0,12},{1,13},{2,14},{3,15},{4,8},{5,9},{6,10},{7,11},{8,4},{9,5},... | collective-permute-start | bytes 884744 | tf_op jit(solution)/shard_map/ppermute | solution.py:29
  36.7 5.6 %collective-permute-start.7 = (bf16[512,128]{1,0:T(8,128)(2,1)S(1)}, bf16[512,128]{1,0:T(8,128)(2,1)S(1)}, u32[]{:S(2)}, u32[]{:S(2)}) collective-permute-start(bf16[512,128]{1,0:T(8,128)(2,1)S(1)} %get-tuple-element.44), channel_id=1, source_target_pairs={{0,2},{1,3},{2,0},{3,1},{4,6},{5,7},{6,4},{7,5},{8,10},{9,11},{10,... | collective-permute-start | bytes 393224 | tf_op jit(solution)/shard_map/ppermute | solution.py:29
  38.2 7.6 %collective-permute-start.6 = (bf16[512,256]{1,0:T(8,128)(2,1)S(1)}, bf16[512,256]{1,0:T(8,128)(2,1)S(1)}, u32[]{:S(2)}, u32[]{:S(2)}) collective-permute-start(bf16[512,256]{1,0:T(8,128)(2,1)S(1)} %collective-permute-done.3.refs_5_), channel_id=1, source_target_pairs={{0,1},{1,0},{2,3},{3,2},{4,5},{5,4},{6,7},{7,6},{8,9},{9,8},{10,11... | collective-permute-start | bytes 786440 | tf_op jit(solution)/shard_map/ppermute | solution.py:29
  42.3 17.3 %collective-permute-start.9 = (bf16[128,1152]{1,0:T(8,128)(2,1)S(1)}, bf16[128,1152]{1,0:T(8,128)(2,1)S(1)}, u32[]{:S(2)}, u32[]{:S(2)}) collective-permute-start(bf16[128,1152]{1,0:T(8,128)(2,1)S(1)} %get-tuple-element.35.refs_4_.refs_1_), channel_id=1, source_target_pairs={{0,4},{1,5},{2,6},{3,7},{4,0},{5,1},{6,2},{7,3},{8,12},{9,13},{10,... | collective-permute-start | bytes 884744 | tf_op jit(solution)/shard_map/ppermute | solution.py:29
  42.3 7.2 %collective-permute-start.8 = (bf16[512,128]{1,0:T(8,128)(2,1)S(1)}, bf16[512,128]{1,0:T(8,128)(2,1)S(1)}, u32[]{:S(2)}, u32[]{:S(2)}) collective-permute-start(bf16[512,128]{1,0:T(8,128)(2,1)S(1)} %collective-permute-done.7.refs_6_), channel_id=1, source_target_pairs={{0,1},{1,0},{2,3},{3,2},{4,5},{5,4},{6,7},{7,6},{8,9},{9,8},{10,11... | collective-permute-start | bytes 393224 | tf_op jit(solution)/shard_map/ppermute | solution.py:29
  49.5 21.6 %copy-start = (bf16[3,1152,576]{1,2,0:T(8,128)(2,1)S(1)}, bf16[3,1152,576]{1,2,0:T(8,128)(2,1)}, u32[]{:S(2)}) copy-start(bf16[3,1152,576]{1,2,0:T(8,128)(2,1)} %param.19) | copy-start | bytes 11943940
  49.5 21.6 %copy-start.1 = (bf16[576,1152]{1,0:T(8,128)(2,1)S(1)}, bf16[576,1152]{1,0:T(8,128)(2,1)}, u32[]{:S(2)}) copy-start(bf16[576,1152]{1,0:T(8,128)(2,1)} %refs_12_.5) | copy-start | bytes 3981316
  53.1 6.5 %collective-permute-start.13 = (bf16[192,128]{1,0:T(8,128)(2,1)S(1)}, bf16[192,128]{1,0:T(8,128)(2,1)S(1)}, u32[]{:S(2)}, u32[]{:S(2)}) collective-permute-start(bf16[192,128]{1,0:T(8,128)(2,1)S(1)} %get-tuple-element.48.refs_7_), channel_id=1, source_target_pairs={{0,4},{1,5},{2,6},{3,7},{4,0},{5,1},{6,2},{7,3},{8,12},{9,13},{10,... | collective-permute-start | bytes 147464 | tf_op jit(solution)/shard_map/ppermute | solution.py:29
  55.2 16.0 %collective-permute-start.12 = (bf16[384,128]{1,0:T(8,128)(2,1)S(1)}, bf16[384,128]{1,0:T(8,128)(2,1)S(1)}, u32[]{:S(2)}, u32[]{:S(2)}) collective-permute-start(bf16[384,128]{1,0:T(8,128)(2,1)S(1)} %get-tuple-element.47.refs_6_), channel_id=1, source_target_pairs={{0,4},{1,5},{2,6},{3,7},{4,0},{5,1},{6,2},{7,3},{8,12},{9,13},{10,... | collective-permute-start | bytes 294920 | tf_op jit(solution)/shard_map/ppermute | solution.py:29
  55.2 15.9 %collective-permute-start.14 = (bf16[384,128]{1,0:T(8,128)(2,1)S(1)}, bf16[384,128]{1,0:T(8,128)(2,1)S(1)}, u32[]{:S(2)}, u32[]{:S(2)}) collective-permute-start(bf16[384,128]{1,0:T(8,128)(2,1)S(1)} %get-tuple-element.49.refs_8_), channel_id=1, source_target_pairs={{0,8},{1,9},{2,10},{3,11},{4,12},{5,13},{6,14},{7,15},{8,0},{9,1},... | collective-permute-start | bytes 294920 | tf_op jit(solution)/shard_map/ppermute | solution.py:29
  56.1 15.0 %collective-permute-start.16 = (bf16[384,128]{1,0:T(8,128)(2,1)S(1)}, bf16[384,128]{1,0:T(8,128)(2,1)S(1)}, u32[]{:S(2)}, u32[]{:S(2)}) collective-permute-start(bf16[384,128]{1,0:T(8,128)(2,1)S(1)} %get-tuple-element.51.refs_10_), channel_id=1, source_target_pairs={{0,12},{1,13},{2,14},{3,15},{4,8},{5,9},{6,10},{7,11},{8,4},{9,5},... | collective-permute-start | bytes 294920 | tf_op jit(solution)/shard_map/ppermute | solution.py:29
  59.6 11.6 %collective-permute-start.15 = (bf16[192,128]{1,0:T(8,128)(2,1)S(1)}, bf16[192,128]{1,0:T(8,128)(2,1)S(1)}, u32[]{:S(2)}, u32[]{:S(2)}) collective-permute-start(bf16[192,128]{1,0:T(8,128)(2,1)S(1)} %get-tuple-element.50.refs_9_), channel_id=1, source_target_pairs={{0,8},{1,9},{2,10},{3,11},{4,12},{5,13},{6,14},{7,15},{8,0},{9,1},... | collective-permute-start | bytes 147464 | tf_op jit(solution)/shard_map/ppermute | solution.py:29
  59.6 11.6 %collective-permute-start.17 = (bf16[192,128]{1,0:T(8,128)(2,1)S(1)}, bf16[192,128]{1,0:T(8,128)(2,1)S(1)}, u32[]{:S(2)}, u32[]{:S(2)}) collective-permute-start(bf16[192,128]{1,0:T(8,128)(2,1)S(1)} %get-tuple-element.52.refs_11_), channel_id=1, source_target_pairs={{0,12},{1,13},{2,14},{3,15},{4,8},{5,9},{6,10},{7,11},{8,4},{9,5},... | collective-permute-start | bytes 147464 | tf_op jit(solution)/shard_map/ppermute | solution.py:29
  75.2 10.5 %collective-permute-start.21 = (bf16[288,128]{1,0:T(8,128)(2,1)S(1)}, bf16[288,128]{1,0:T(8,128)(2,1)S(1)}, u32[]{:S(2)}, u32[]{:S(2)}) collective-permute-start(bf16[288,128]{1,0:T(8,128)(2,1)S(1)} %get-tuple-element.60), channel_id=1, source_target_pairs={{0,4},{1,5},{2,6},{3,7},{4,0},{5,1},{6,2},{7,3},{8,12},{9,13},{10,... | collective-permute-start | bytes 221192 | tf_op jit(solution)/shard_map/ppermute | solution.py:29
  76.3 13.0 %collective-permute-start.22 = (bf16[288,128]{1,0:T(8,128)(2,1)S(1)}, bf16[288,128]{1,0:T(8,128)(2,1)S(1)}, u32[]{:S(2)}, u32[]{:S(2)}) collective-permute-start(bf16[288,128]{1,0:T(8,128)(2,1)S(1)} %get-tuple-element.61), channel_id=1, source_target_pairs={{0,8},{1,9},{2,10},{3,11},{4,12},{5,13},{6,14},{7,15},{8,0},{9,1},... | collective-permute-start | bytes 221192 | tf_op jit(solution)/shard_map/ppermute | solution.py:29
  77.2 12.2 %collective-permute-start.23 = (bf16[288,128]{1,0:T(8,128)(2,1)S(1)}, bf16[288,128]{1,0:T(8,128)(2,1)S(1)}, u32[]{:S(2)}, u32[]{:S(2)}) collective-permute-start(bf16[288,128]{1,0:T(8,128)(2,1)S(1)} %get-tuple-element.62), channel_id=1, source_target_pairs={{0,12},{1,13},{2,14},{3,15},{4,8},{5,9},{6,10},{7,11},{8,4},{9,5},... | collective-permute-start | bytes 221192 | tf_op jit(solution)/shard_map/ppermute | solution.py:29
  83.7 7.4 %collective-permute-start.18 = (bf16[288,128]{1,0:T(8,128)(2,1)S(1)}, bf16[288,128]{1,0:T(8,128)(2,1)S(1)}, u32[]{:S(2)}, u32[]{:S(2)}) collective-permute-start(bf16[288,128]{1,0:T(8,128)(2,1)S(1)} %get-tuple-element.56), channel_id=1, source_target_pairs={{0,4},{1,5},{2,6},{3,7},{4,0},{5,1},{6,2},{7,3},{8,12},{9,13},{10,... | collective-permute-start | bytes 221192 | tf_op jit(solution)/shard_map/ppermute | solution.py:29
  83.9 7.2 %collective-permute-start.19 = (bf16[288,128]{1,0:T(8,128)(2,1)S(1)}, bf16[288,128]{1,0:T(8,128)(2,1)S(1)}, u32[]{:S(2)}, u32[]{:S(2)}) collective-permute-start(bf16[288,128]{1,0:T(8,128)(2,1)S(1)} %get-tuple-element.57), channel_id=1, source_target_pairs={{0,8},{1,9},{2,10},{3,11},{4,12},{5,13},{6,14},{7,15},{8,0},{9,1},... | collective-permute-start | bytes 221192 | tf_op jit(solution)/shard_map/ppermute | solution.py:29
  85.7 3.7 %copy-start.2 = (bf16[576,1152]{1,0:T(8,128)(2,1)S(1)}, bf16[576,1152]{1,0:T(8,128)(2,1)}, u32[]{:S(2)}) copy-start(bf16[576,1152]{1,0:T(8,128)(2,1)} %weight_ref.3) | copy-start | bytes 3981316
  85.7 6.2 %collective-permute-start.20 = (bf16[288,128]{1,0:T(8,128)(2,1)S(1)}, bf16[288,128]{1,0:T(8,128)(2,1)S(1)}, u32[]{:S(2)}, u32[]{:S(2)}) collective-permute-start(bf16[288,128]{1,0:T(8,128)(2,1)S(1)} %get-tuple-element.58), channel_id=1, source_target_pairs={{0,12},{1,13},{2,14},{3,15},{4,8},{5,9},{6,10},{7,11},{8,4},{9,5},... | collective-permute-start | bytes 221192 | tf_op jit(solution)/shard_map/ppermute | solution.py:29

commit v4 on v3

--- a/solution.py
+++ b/solution.py
@@ -13,8 +13,9 @@
 HEADS = 16
 LANES = 128
 QUERY_ROWS = 128
-PAIR_GROUPS = ((0,), (1,), (2,), (3,))
-EMIT = (False, False, True, True)
+STRIP = 16
+PAIR_GROUPS = ((0,), (1,), (2, 3))
+EMIT = (False, True, True)
 HALVES = 2
 
 
@@ -144,9 +145,9 @@
 def projection_kernel(slot_ref, time_ref, order_ref, weight_hbm, *refs, frames, width):
     rate_ref, table_ref, mix_ref = refs[:3]
     pieces = refs[3 : 3 + frames]
-    query_ref, kv_ref, modulation_ref, place_ref, weight_ref, sems = refs[3 + frames :]
+    query_ref, kv_ref, modulation_ref, place_ref = refs[3 + frames : 7 + frames]
+    weight_ref, inputs_ref, sems = refs[7 + frames :]
     padded = query_ref.shape[1]
-    feature_width = place_ref.shape[1]
     middle = width + padded
     parts = (slice(0, padded), slice(padded, middle), slice(middle, weight_ref.shape[0]))
     copies = [
@@ -163,15 +164,18 @@
         frame = order_ref[source_slot(slot_ref[0], step, frames)]
         position = jnp.where(row == step, frame, position)
     angles = position.astype(f32) * rate_ref[...]
-    column = lax.broadcasted_iota(jnp.int32, (rows, feature_width), 1)
-    waves = jnp.where(column < feature_width // 2, jnp.sin(angles), jnp.cos(angles))
+    waves = jnp.concatenate([jnp.sin(angles), jnp.cos(angles)], axis=1)
     place_ref[...] = waves[:frames]
     modulation = table_ref[...] + mix_ref[...] * waves[frames : frames + 1]
     modulation_ref[...] = modulation
 
-    tokens = jnp.concatenate([ref[...] for ref in pieces], axis=0).astype(f32)
-    inputs = normalize(tokens) * (1.0 + modulation[1:2, :]) + modulation[0:1, :]
-    inputs = inputs.astype(bf16)
+    piece = pieces[0].shape[0]
+    gain, shift = 1.0 + modulation[1:2, :], modulation[0:1, :]
+    for row in range(0, inputs_ref.shape[0], STRIP):
+        at = row % piece
+        tokens = pieces[row // piece][at : at + STRIP, :].astype(f32)
+        inputs_ref[row : row + STRIP, :] = (normalize(tokens) * gain + shift).astype(bf16)
+    inputs = inputs_ref[...]
 
     def project(first, last):
         return lax.dot_general(
@@ -193,7 +197,7 @@
     rows = frames * piece
     half = feature_width // 2
     rates = np.exp(-math.log(10000.0) * np.arange(half) / half).astype(np.float32)
-    rates = jnp.asarray(np.concatenate([rates, rates])[None])
+    rates = jnp.asarray(rates[None])
     operands = [pltpu.with_memory_space_constraint(weight, pltpu.HBM)]
     operands += [
         pltpu.with_memory_space_constraint(x, pltpu.VMEM)
@@ -213,7 +217,11 @@
             *vmem_specs(3 + frames),
         ],
         out_specs=vmem_specs(4),
-        scratch_shapes=[pltpu.VMEM(weight.shape, bf16), pltpu.SemaphoreType.DMA((3,))],
+        scratch_shapes=[
+            pltpu.VMEM(weight.shape, bf16),
+            pltpu.VMEM((rows, feature_width), bf16),
+            pltpu.SemaphoreType.DMA((3,)),
+        ],
         compiler_params=pltpu.CompilerParams(vmem_limit_bytes=8 * 2**20),
         cost_estimate=pl.CostEstimate(
             flops=2 * rows * feature_width * 3 * width,
@@ -282,7 +290,7 @@
     return groups
 
 
-def spatial_kernel(*refs, group, frames, head_dim, width, tiles, held, emitted, kept, columns):
+def spatial_kernel(*refs, group, frames, head_dim, width, tiles, held, emitted, kept, columns, chunks):
     plan = pair_plan(width, head_dim)
     count = len(tiles)
     position = 0
@@ -295,8 +303,11 @@
     if held:
         held_ref = refs[position]
         position += 1
-    out_count = frames if emitted else 0
-    out_refs = refs[position : position + out_count]
+    rows = query_ref.shape[0]
+    piece = rows // frames
+    covered = part_pieces(chunks, piece)
+    out_count = len(covered) if emitted else 0
+    out_refs = dict(zip(covered, refs[position : position + out_count]))
     kept_ref = refs[position + out_count] if kept else None
 
     where = {tile: (c, j) for c, chunk in enumerate(tiles) for j, tile in enumerate(chunk)}
@@ -312,9 +323,7 @@
         return lambda tile: ref[:, tile * LANES : (tile + 1) * LANES]
 
     blocks = [from_whole(own_ref), from_whole(peer_ref), from_chunks(near_refs), from_chunks(far_refs)]
-    rows = query_ref.shape[0]
     scale = softmax_scale(head_dim)
-    piece = rows // frames
 
     def two(block, tile):
         return jnp.concatenate([block(tile), block(tile + 1)], axis=1)
@@ -339,12 +348,12 @@
 
     def weigh(index):
         totals = []
-        for row in range(0, 2 * QUERY_ROWS, 16):
-            scores = scores_ref[index % 2, row : row + 16, :]
+        for row in range(0, 2 * QUERY_ROWS, STRIP):
+            scores = scores_ref[index % 2, row : row + STRIP, :]
             top = jnp.max(scores, axis=-1, keepdims=True) * scale
             weights = jnp.exp2(scores * scale - top)
             totals.append(jnp.sum(weights, axis=-1, keepdims=True))
-            weights_ref[index % 2, row : row + 16, :] = weights.astype(bf16)
+            weights_ref[index % 2, row : row + STRIP, :] = weights.astype(bf16)
         return jnp.concatenate(totals, axis=0)
 
     def mix(index, total):
@@ -366,7 +375,7 @@
         ] * column_mask(value_lane + head_dim, head_dim, f32)
         return pltpu.roll(joined, (key_lane - value_lane) % (2 * LANES), 1)
 
-    tasks = [(chunk, pair) for chunk in range(rows // QUERY_ROWS) for pair in group]
+    tasks = [(chunk, pair) for chunk in chunks for pair in group]
     parts = {}
 
     def finish(index, total):
@@ -388,7 +397,7 @@
         if emitted:
             for sub in range(QUERY_ROWS // piece):
                 cut = slice(sub * piece, (sub + 1) * piece)
-                out_refs[at // piece + sub][...] = stack(
+                out_refs[(at + sub * piece) // piece][...] = stack(
                     [parts[tile][cut] for tile in emitted], columns
                 )
         parts.clear()
@@ -427,15 +436,31 @@
     return tuple(emitted_columns(emitted, width) for _, emitted, _ in flow if emitted)
 
 
-def spatial_group(number, query, own_kv, peer_kv, near, far, carry, frames, head_dim, width):
+def part_pieces(chunks, piece):
+    per = QUERY_ROWS // piece
+    return [chunk * per + sub for chunk in chunks for sub in range(per)]
+
+
+def row_parts(number, rows):
+    chunks = list(range(rows // QUERY_ROWS))
+    if number < len(PAIR_GROUPS) - 1 or len(chunks) < 3:
+        return [chunks]
+    return [[chunk] for chunk in chunks[:1:-1]] + [chunks[1::-1]]
+
+
+def spatial_group(
+    number, part, query, own_kv, peer_kv, near, far, carry, frames, head_dim, width
+):
     group = PAIR_GROUPS[number]
     held, emitted, kept = tile_flow(width, head_dim)[number]
     tiles = tuple(group_tiles(width, head_dim)[: number + 1])
     rows = query.shape[0]
+    chunks = row_parts(number, rows)[part]
     shapes = []
     columns = emitted_columns(emitted, width)
     if emitted:
-        shapes += [((stack_rows(rows // frames, columns), LANES), bf16) for _ in range(frames)]
+        count = len(chunks) * QUERY_ROWS // (rows // frames)
+        shapes += [((stack_rows(rows // frames, columns), LANES), bf16) for _ in range(count)]
     if kept:
         shapes.append(((rows, len(kept) * LANES), bf16))
     operands = [query, own_kv, peer_kv, *near[: number + 1], *far[: number + 1]]
@@ -454,10 +479,11 @@
             emitted=emitted,
             kept=kept,
             columns=columns,
+            chunks=chunks,
         ),
         operands,
         shapes,
-        len(group) * 2 * rows * keys * 256 * 4,
+        len(group) * 2 * len(chunks) * QUERY_ROWS * keys * 256 * 4,
         8,
         len(group) * 2 * rows * keys,
         [
@@ -755,12 +781,15 @@
     local = [[] for _ in range(frames)]
     sent = [[] for _ in range(frames)]
     for number in range(len(PAIR_GROUPS)):
-        outs, carry = spatial_group(
-            number, query, own_kv, peer_kv, near, far, carry, frames, head_dim, width
-        )
-        for s, out in enumerate(outs):
-            local[s].append(out)
-            sent[s].append(out if s == 0 else permute(out, ahead(s)))
+        handed = carry
+        for part, chunks in enumerate(row_parts(number, rows)):
+            outs, carry = spatial_group(
+                number, part, query, own_kv, peer_kv, near, far, handed, frames, head_dim, width
+            )
+            covered = part_pieces(chunks, piece)
+            for s, out in zip(covered, outs):
+                local[s].append(out)
+                sent[s].append(out if s == 0 else permute(out, ahead(s)))
 
     columns = group_columns(width, head_dim)
     after = after_spatial(pieces, local, columns, spatial_out, modulation)
@@ -777,21 +806,11 @@
 
 
 def solution(mesh):
+    split = P(("groups", "patch"), None)
     return jax.shard_map(
         per_device,
         mesh=mesh,
-        in_specs=(
-            P(("groups", "patch"), None),
-            P(("groups", "patch"), None),
-            P(),
-            P(),
-            P("groups"),
-            P("groups"),
-            P(),
-            P(),
-            P(),
-            P(),
-        ),
-        out_specs=P(("groups", "patch"), None),
+        in_specs=(split, split, P(), P(), P("groups"), P("groups"), P(), P(), P(), P()),
+        out_specs=split,
         check_vma=False,
     )

time: 94 us -> 99.9 us (1.063)
  starting transfers between devices: 30.3 us -> 36.7 us
  waiting for transfers between devices: 26.4 us -> 24.4 us
  local copies, waits for them, and re-layouts: 0.03 us -> 1.55 us
    ppermute x24 -> x22, starting transfers between devices: 30.3 us -> 36.7 us  [permute(): lax.ppermute(value, 'patch', [(source, target(source)) for source in rang...]
    ppermute x24 -> x22, waiting for transfers between devices: 26.4 us -> 24.4 us  [permute(): lax.ppermute(value, 'patch', [(source, target(source)) for source in rang...]
    unnamed x14, local copies, waits for them, and re-layouts: 0.03 us -> 1.55 us
    pallas_call x7 -> x8, Pallas kernels: 23.4 us -> 23.9 us  [on_chip_call(): pl.pallas_call(kernel, out_shape=[pltpu.VMEM(shape, dtype) for shape, dty...]
  transfers between devices with their start and end apart: 24 -> 22, of which waited for: 5 -> 8; matrix products, arithmetic and copies ran while one was open for 0% -> 0% of each run, Pallas kernels for 32% -> 30%
where the time goes in v4:
time: 99.9 us; the launch traced here: 99.6 us
  starting transfers between devices  36.7 us (37%)
  Pallas kernels  36 us (36%)
  waiting for transfers between devices  24.4 us (24%)
  local copies, waits for them, and re-layouts  1.55 us (2%)
  between operations  1.02 us (1%)
    ppermute x22, starting transfers between devices, permute(): lax.ppermute(value, 'patch', [(source, target(source)) for source in rang...  36.7 us
    ppermute x22, waiting for transfers between devices, permute(): lax.ppermute(value, 'patch', [(source, target(source)) for source in rang...  24.4 us
    pallas_call x8, Pallas kernels, on_chip_call(): pl.pallas_call(kernel, out_shape=[pltpu.VMEM(shape, dtype) for shape, dty...  23.9 us
    pallas_call x1, Pallas kernels, projections(): pl.pallas_call(functools.partial(projection_kernel, frames=frames, width=...  6 us
    pallas_call x2, Pallas kernels, output(): pl.pallas_call(functools.partial(output_kernel, frames=frames, number=num...  3.49 us
  transfers between devices with their start and end apart: 22, of which 8 were waited for; matrix products, arithmetic and copies ran while one was open for 0% of the time, Pallas kernels for 30%

profile of v4, /device:TPU:0, one launch (start us, length us, event | category | flops | bytes accessed | tf_op | source)
XLA Modules:
  0.0 99.6 jit_solution(17652645097586564102)
XLA Ops:
  0.0 0.5 collective-permute-start
  0.5 1.4 %chunks.1 = (bf16[512,512]{1,0:T(8,128)(2,1)S(1)}, bf16[512,256]{1,0:T(8,128)(2,1)S(1)}, bf16[512,384]{1,0:T(8,128)(2,1)S(1)}) custom-call(bf16[512,1152]{1,0:T(8,128)(2,1)} %kv_ref.1), custom_call_target="tpu_custom_call" | custom-call | tf_op jit(solution)/shard_map/chunks/pallas_call | solution.py:102
  1.9 2.6 %collective-permute-start.1 = (bf16[512,512]{1,0:T(8,128)(2,1)S(1)}, bf16[512,512]{1,0:T(8,128)(2,1)S(1)}, u32[]{:S(2)}, u32[]{:S(2)}) collective-permute-start(bf16[512,512]{1,0:T(8,128)(2,1)S(1)} %get-tuple-element.37), channel_id=1, source_target_pairs={{0,2},{1,3},{2,0},{3,1},{4,6},{5,7},{6,4},{7,5},{8,10},{9,11},{10,... | collective-permute-start | bytes 1572872 | tf_op jit(solution)/shard_map/ppermute | solution.py:30
  4.5 12.6 %collective-permute-done.1.refs_3_ = bf16[512,512]{1,0:T(8,128)(2,1)S(1)} collective-permute-done((bf16[512,512]{1,0:T(8,128)(2,1)S(1)}, bf16[512,512]{1,0:T(8,128)(2,1)S(1)}, u32[]{:S(2)}, u32[]{:S(2)}) %collective-permute-start.1) | collective-permute-done | bytes 524320 | tf_op jit(solution)/shard_map/ppermute | solution.py:30
  17.1 0.0 collective-permute-start.3
  17.1 1.7 %collective-permute-start.2 = (bf16[512,256]{1,0:T(8,128)(2,1)S(1)}, bf16[512,256]{1,0:T(8,128)(2,1)S(1)}, u32[]{:S(2)}, u32[]{:S(2)}) collective-permute-start(bf16[512,256]{1,0:T(8,128)(2,1)S(1)} %get-tuple-element.38), channel_id=1, source_target_pairs={{0,2},{1,3},{2,0},{3,1},{4,6},{5,7},{6,4},{7,5},{8,10},{9,11},{10,... | collective-permute-start | bytes 786440 | tf_op jit(solution)/shard_map/ppermute | solution.py:30
  18.8 0.3 collective-permute-start.5
  19.1 1.3 %pieces.1 = (bf16[128,1152]{1,0:T(8,128)(2,1)S(1)}, bf16[128,1152]{1,0:T(8,128)(2,1)S(1)}, bf16[128,1152]{1,0:T(8,128)(2,1)S(1)}, bf16[128,1152]{1,0:T(8,128)(2,1)S(1)}) custom-call(s32[1]{0:T(128)} %bitcast.slot_ref, bf16[512,1152]{1,0:T(8,128)(2,1)} %tokens_ref.1), custom_call_target="tpu_custom_call" | custom-call | tf_op jit(solution)/shard_map/pieces/pallas_call | solution.py:131
  20.4 1.9 %collective-permute-start.7 = (bf16[128,1152]{1,0:T(8,128)(2,1)S(1)}, bf16[128,1152]{1,0:T(8,128)(2,1)S(1)}, u32[]{:S(2)}, u32[]{:S(2)}) collective-permute-start(bf16[128,1152]{1,0:T(8,128)(2,1)S(1)} %get-tuple-element.32.refs_4_.refs_1_), channel_id=1, source_target_pairs={{0,4},{1,5},{2,6},{3,7},{4,0},{5,1},{6,2},{7,3},{8,12},{9,13},{10,... | collective-permute-start | bytes 884744 | tf_op jit(solution)/shard_map/ppermute | solution.py:30
  22.9 3.4 %collective-permute-done.2.refs_4_ = bf16[512,256]{1,0:T(8,128)(2,1)S(1)} collective-permute-done((bf16[512,256]{1,0:T(8,128)(2,1)S(1)}, bf16[512,256]{1,0:T(8,128)(2,1)S(1)}, u32[]{:S(2)}, u32[]{:S(2)}) %collective-permute-start.2) | collective-permute-done | bytes 262176 | tf_op jit(solution)/shard_map/ppermute | solution.py:30
  26.3 0.0 collective-permute-start.4
  26.3 0.0 copy-start.3
  26.3 0.8 copy-done.3
  27.1 0.8 copy-done.4
  27.8 6.0 %projections.1 = (bf16[512,640]{1,0:T(8,128)(2,1)S(1)}, bf16[512,1152]{1,0:T(8,128)(2,1)S(1)}, f32[6,1152]{1,0:T(8,128)S(1)}, f32[4,1152]{1,0:T(4,128)S(1)}) custom-call(s32[1]{0:T(128)} %bitcast.slot_ref, s32[1]{0:T(128)S(6)} %copy.14.time_ref, s32[4]{0:T(128)S(1)} %copy-done.5, bf16[1728,1152]{1,0:T(8,128)(2,1)} %bitcast.9, f32[1,576]{1,0:T(1,128)S(1)} %copy-done.6, ...), custom_call_target="tpu_custom_call" | custom-call | flops 2038431744 | bytes 3981312 | tf_op jit(solution)/shard_map/projections/pallas_call | solution.py:206
  33.8 0.4 collective-permute-done.5.refs_5_
  34.3 2.8 %collective-permute-start.8 = (bf16[128,1152]{1,0:T(8,128)(2,1)S(1)}, bf16[128,1152]{1,0:T(8,128)(2,1)S(1)}, u32[]{:S(2)}, u32[]{:S(2)}) collective-permute-start(bf16[128,1152]{1,0:T(8,128)(2,1)S(1)} %get-tuple-element.33.refs_5_.refs_2_), channel_id=1, source_target_pairs={{0,8},{1,9},{2,10},{3,11},{4,12},{5,13},{6,14},{7,15},{8,0},{9,1},... | collective-permute-start | bytes 884744 | tf_op jit(solution)/shard_map/ppermute | solution.py:30
  37.1 1.3 %collective-permute-start.9 = (bf16[128,1152]{1,0:T(8,128)(2,1)S(1)}, bf16[128,1152]{1,0:T(8,128)(2,1)S(1)}, u32[]{:S(2)}, u32[]{:S(2)}) collective-permute-start(bf16[128,1152]{1,0:T(8,128)(2,1)S(1)} %get-tuple-element.34.refs_6_.refs_3_), channel_id=1, source_target_pairs={{0,12},{1,13},{2,14},{3,15},{4,8},{5,9},{6,10},{7,11},{8,4},{9,5},... | collective-permute-start | bytes 884744 | tf_op jit(solution)/shard_map/ppermute | solution.py:30
  38.4 0.0 collective-permute-done.refs_2_
  38.4 3.3 %shard_map.109.refs_7_ = bf16[512,256]{1,0:T(8,128)(2,1)S(1)} custom-call(bf16[512,640]{1,0:T(8,128)(2,1)S(1)} %get-tuple-element.35.refs_0_, bf16[512,1152]{1,0:T(8,128)(2,1)S(1)} %get-tuple-element.36.refs_1_, bf16[512,1152]{1,0:T(8,128)(2,1)S(1)} %collective-permute-done.refs_2_, bf16[512,512]{1,0:T(8,128)(2,1)S(1)} %collective-permute-done.1.refs_3_, ...), custom_call_target="tpu_custom_call" | custom-call | flops 2147483648 | bytes 4063232 | tf_op jit(solution)/shard_map/pallas_call | solution.py:68
  41.8 3.3 %shard_map.110 = (bf16[256,128]{1,0:T(8,128)(2,1)S(1)}, bf16[256,128]{1,0:T(8,128)(2,1)S(1)}, bf16[256,128]{1,0:T(8,128)(2,1)S(1)}, bf16[256,128]{1,0:T(8,128)(2,1)S(1)}, bf16[512,128]{1,0:T(8,128)(2,1)S(1)}) custom-call(bf16[512,640]{1,0:T(8,128)(2,1)S(1)} %get-tuple-element.35.refs_0_, bf16[512,1152]{1,0:T(8,128)(2,1)S(1)} %get-tuple-element.36.refs_1_, ...), custom_call_target="tpu_custom_call" | custom-call | flops 2147483648 | bytes 4849664 | tf_op jit(solution)/shard_map/pallas_call | solution.py:68
  45.1 0.4 collective-permute-start.10
  45.5 3.6 %shard_map.111 = (bf16[320,128]{1,0:T(8,128)(2,1)S(1)}, bf16[320,128]{1,0:T(8,128)(2,1)S(1)}) custom-call(bf16[512,640]{1,0:T(8,128)(2,1)S(1)} %get-tuple-element.35.refs_0_, bf16[512,1152]{1,0:T(8,128)(2,1)S(1)} %get-tuple-element.36.refs_1_, bf16[512,1152]{1,0:T(8,128)(2,1)S(1)} %collective-permute-done.refs_2_, ...), custom_call_target="tpu_custom_call" | custom-call | flops 2147483648 | bytes 5505024 | tf_op jit(solution)/shard_map/pallas_call | solution.py:68
  49.1 1.8 %collective-permute-start.11 = (bf16[320,128]{1,0:T(8,128)(2,1)S(1)}, bf16[320,128]{1,0:T(8,128)(2,1)S(1)}, u32[]{:S(2)}, u32[]{:S(2)}) collective-permute-start(bf16[320,128]{1,0:T(8,128)(2,1)S(1)} %get-tuple-element.44.refs_7_), channel_id=1, source_target_pairs={{0,4},{1,5},{2,6},{3,7},{4,0},{5,1},{6,2},{7,3},{8,12},{9,13},{10,... | collective-permute-start | bytes 245768 | tf_op jit(solution)/shard_map/ppermute | solution.py:30
  50.9 2.1 %shard_map.112.refs_9_ = bf16[320,128]{1,0:T(8,128)(2,1)S(1)} custom-call(bf16[512,640]{1,0:T(8,128)(2,1)S(1)} %get-tuple-element.35.refs_0_, bf16[512,1152]{1,0:T(8,128)(2,1)S(1)} %get-tuple-element.36.refs_1_, bf16[512,1152]{1,0:T(8,128)(2,1)S(1)} %collective-permute-done.refs_2_, bf16[512,512]{1,0:T(8,128)(2,1)S(1)} %collective-permute-done.1.refs_3_, ...), custom_call_target="tpu_custom_call" | custom-call | flops 1073741824 | bytes 5505024 | tf_op jit(solution)/shard_map/pallas_call | solution.py:68
  53.0 0.0 copy-start
  53.0 0.0 copy-start.1
  53.1 2.1 %shard_map.113.refs_11_ = bf16[320,128]{1,0:T(8,128)(2,1)S(1)} custom-call(bf16[512,640]{1,0:T(8,128)(2,1)S(1)} %get-tuple-element.35.refs_0_, bf16[512,1152]{1,0:T(8,128)(2,1)S(1)} %get-tuple-element.36.refs_1_, bf16[512,1152]{1,0:T(8,128)(2,1)S(1)} %collective-permute-done.refs_2_, bf16[512,512]{1,0:T(8,128)(2,1)S(1)} %collective-permute-done.1.refs_3_, ...), custom_call_target="tpu_custom_call" | custom-call | flops 1073741824 | bytes 5505024 | tf_op jit(solution)/shard_map/pallas_call | solution.py:68
  55.2 1.8 %collective-permute-start.13 = (bf16[320,128]{1,0:T(8,128)(2,1)S(1)}, bf16[320,128]{1,0:T(8,128)(2,1)S(1)}, u32[]{:S(2)}, u32[]{:S(2)}) collective-permute-start(bf16[320,128]{1,0:T(8,128)(2,1)S(1)} %shard_map.112.refs_9_), channel_id=1, source_target_pairs={{0,8},{1,9},{2,10},{3,11},{4,12},{5,13},{6,14},{7,15},{8,0},{9,1},... | collective-permute-start | bytes 245768 | tf_op jit(solution)/shard_map/ppermute | solution.py:30
  56.9 0.8 collective-permute-done.8.refs_2_
  57.7 3.0 %collective-permute-start.15 = (bf16[320,128]{1,0:T(8,128)(2,1)S(1)}, bf16[320,128]{1,0:T(8,128)(2,1)S(1)}, u32[]{:S(2)}, u32[]{:S(2)}) collective-permute-start(bf16[320,128]{1,0:T(8,128)(2,1)S(1)} %shard_map.113.refs_11_), channel_id=1, source_target_pairs={{0,12},{1,13},{2,14},{3,15},{4,8},{5,9},{6,10},{7,11},{8,4},{9,5},... | collective-permute-start | bytes 245768 | tf_op jit(solution)/shard_map/ppermute | solution.py:30
  60.7 8.9 %collective-permute-start.12 = (bf16[256,128]{1,0:T(8,128)(2,1)S(1)}, bf16[256,128]{1,0:T(8,128)(2,1)S(1)}, u32[]{:S(2)}, u32[]{:S(2)}) collective-permute-start(bf16[256,128]{1,0:T(8,128)(2,1)S(1)} %get-tuple-element.45.refs_8_), channel_id=1, source_target_pairs={{0,8},{1,9},{2,10},{3,11},{4,12},{5,13},{6,14},{7,15},{8,0},{9,1},... | collective-permute-start | bytes 196616 | tf_op jit(solution)/shard_map/ppermute | solution.py:30
  69.6 0.8 collective-permute-start.14
  70.5 3.0 %collective-permute-done.12.refs_8_ = bf16[256,128]{1,0:T(8,128)(2,1)S(1)} collective-permute-done((bf16[256,128]{1,0:T(8,128)(2,1)S(1)}, bf16[256,128]{1,0:T(8,128)(2,1)S(1)}, u32[]{:S(2)}, u32[]{:S(2)}) %collective-permute-start.12) | collective-permute-done | bytes 65568 | tf_op jit(solution)/shard_map/ppermute | solution.py:30
  73.5 2.3 %collective-permute-done.14.refs_10_ = bf16[256,128]{1,0:T(8,128)(2,1)S(1)} collective-permute-done((bf16[256,128]{1,0:T(8,128)(2,1)S(1)}, bf16[256,128]{1,0:T(8,128)(2,1)S(1)}, u32[]{:S(2)}, u32[]{:S(2)}) %collective-permute-start.14) | collective-permute-done | bytes 65568 | tf_op jit(solution)/shard_map/ppermute | solution.py:30
  75.8 4.0 %shard_map.116 = (bf16[288,128]{1,0:T(8,128)(2,1)S(1)}, bf16[288,128]{1,0:T(8,128)(2,1)S(1)}, bf16[288,128]{1,0:T(8,128)(2,1)S(1)}, bf16[288,128]{1,0:T(8,128)(2,1)S(1)}) custom-call(bf16[128,1152]{1,0:T(8,128)(2,1)S(1)} %get-tuple-element.31.refs_3_.refs_0_, bf16[128,1152]{1,0:T(8,128)(2,1)S(1)} %collective-permute-done.7.refs_1_, ...), custom_call_target="tpu_custom_call" | custom-call | flops 1698693120 | bytes 7123968 | tf_op jit(solution)/shard_map/pallas_call | solution.py:68
  79.9 1.0 %collective-permute-start.19 = (bf16[288,128]{1,0:T(8,128)(2,1)S(1)}, bf16[288,128]{1,0:T(8,128)(2,1)S(1)}, u32[]{:S(2)}, u32[]{:S(2)}) collective-permute-start(bf16[288,128]{1,0:T(8,128)(2,1)S(1)} %get-tuple-element.54), channel_id=1, source_target_pairs={{0,4},{1,5},{2,6},{3,7},{4,0},{5,1},{6,2},{7,3},{8,12},{9,13},{10,... | collective-permute-start | bytes 221192 | tf_op jit(solution)/shard_map/ppermute | solution.py:30
  80.9 2.0 %collective-permute-start.20 = (bf16[288,128]{1,0:T(8,128)(2,1)S(1)}, bf16[288,128]{1,0:T(8,128)(2,1)S(1)}, u32[]{:S(2)}, u32[]{:S(2)}) collective-permute-start(bf16[288,128]{1,0:T(8,128)(2,1)S(1)} %get-tuple-element.55), channel_id=1, source_target_pairs={{0,8},{1,9},{2,10},{3,11},{4,12},{5,13},{6,14},{7,15},{8,0},{9,1},... | collective-permute-start | bytes 221192 | tf_op jit(solution)/shard_map/ppermute | solution.py:30
  82.9 1.4 %collective-permute-start.21 = (bf16[288,128]{1,0:T(8,128)(2,1)S(1)}, bf16[288,128]{1,0:T(8,128)(2,1)S(1)}, u32[]{:S(2)}, u32[]{:S(2)}) collective-permute-start(bf16[288,128]{1,0:T(8,128)(2,1)S(1)} %get-tuple-element.56), channel_id=1, source_target_pairs={{0,12},{1,13},{2,14},{3,15},{4,8},{5,9},{6,10},{7,11},{8,4},{9,5},... | collective-permute-start | bytes 221192 | tf_op jit(solution)/shard_map/ppermute | solution.py:30
  84.3 4.1 %shard_map.115 = (bf16[288,128]{1,0:T(8,128)(2,1)S(1)}, bf16[288,128]{1,0:T(8,128)(2,1)S(1)}, bf16[288,128]{1,0:T(8,128)(2,1)S(1)}, bf16[288,128]{1,0:T(8,128)(2,1)S(1)}) custom-call(bf16[128,1152]{1,0:T(8,128)(2,1)S(1)} %get-tuple-element.31.refs_3_.refs_0_, bf16[128,1152]{1,0:T(8,128)(2,1)S(1)} %collective-permute-done.7.refs_1_, ...), custom_call_target="tpu_custom_call" | custom-call | flops 1698693120 | bytes 7123968 | tf_op jit(solution)/shard_map/pallas_call | solution.py:68
  88.4 0.6 collective-permute-start.16
  89.0 2.5 %collective-permute-start.17 = (bf16[288,128]{1,0:T(8,128)(2,1)S(1)}, bf16[288,128]{1,0:T(8,128)(2,1)S(1)}, u32[]{:S(2)}, u32[]{:S(2)}) collective-permute-start(bf16[288,128]{1,0:T(8,128)(2,1)S(1)} %get-tuple-element.51), channel_id=1, source_target_pairs={{0,8},{1,9},{2,10},{3,11},{4,12},{5,13},{6,14},{7,15},{8,0},{9,1},... | collective-permute-start | bytes 221192 | tf_op jit(solution)/shard_map/ppermute | solution.py:30
  91.5 1.4 %collective-permute-start.18 = (bf16[288,128]{1,0:T(8,128)(2,1)S(1)}, bf16[288,128]{1,0:T(8,128)(2,1)S(1)}, u32[]{:S(2)}, u32[]{:S(2)}) collective-permute-start(bf16[288,128]{1,0:T(8,128)(2,1)S(1)} %get-tuple-element.52), channel_id=1, source_target_pairs={{0,12},{1,13},{2,14},{3,15},{4,8},{5,9},{6,10},{7,11},{8,4},{9,5},... | collective-permute-start | bytes 221192 | tf_op jit(solution)/shard_map/ppermute | solution.py:30
  92.8 1.2 %shard_map.114.after_ref = f32[512,1152]{1,0:T(8,128)S(1)} custom-call(bf16[128,1152]{1,0:T(8,128)(2,1)S(1)} %get-tuple-element.31.refs_3_.refs_0_, bf16[128,1152]{1,0:T(8,128)(2,1)S(1)} %get-tuple-element.32.refs_4_.refs_1_, bf16[128,1152]{1,0:T(8,128)(2,1)S(1)} %get-tuple-element.33.refs_5_.refs_2_, ...), custom_call_target="tpu_custom_call" | custom-call | flops 679477248 | bytes 3124224 | tf_op jit(solution)/shard_map/pallas_call | solution.py:68
  94.1 1.8 %shard_map.117.refs_4_ = f32[512,1152]{1,0:T(8,128)} custom-call(s32[1]{0:T(128)} %bitcast.slot_ref, f32[512,1152]{1,0:T(8,128)S(1)} %shard_map.114.after_ref, bf16[576,1152]{1,0:T(8,128)(2,1)S(1)} %copy-done.2, f32[6,1152]{1,0:T(8,128)S(1)} %get-tuple-element.47.refs_13_.refs_14_.modulation_ref, bf16[288,128]{1,0:T(8,128)(2,1)S(1)} %get-tuple-element.53.refs_0_, ...), custom_call_target="tpu_custom_call" | custom-call | tf_op jit(solution)/shard_map/pallas_call | solution.py:712
  95.8 0.7 collective-permute-done.17.refs_2_
  96.5 1.2 %collective-permute-done.18.refs_3_ = bf16[288,128]{1,0:T(8,128)(2,1)S(1)} collective-permute-done((bf16[288,128]{1,0:T(8,128)(2,1)S(1)}, bf16[288,128]{1,0:T(8,128)(2,1)S(1)}, u32[]{:S(2)}, u32[]{:S(2)}) %collective-permute-start.18) | collective-permute-done | bytes 73760 | tf_op jit(solution)/shard_map/ppermute | solution.py:30
  97.7 1.7 %shard_map.118 = f32[512,1152]{1,0:T(8,128)} custom-call(s32[1]{0:T(128)} %bitcast.slot_ref, f32[512,1152]{1,0:T(8,128)S(1)} %shard_map.114.after_ref, bf16[576,1152]{1,0:T(8,128)(2,1)S(1)} %copy-done.2, f32[6,1152]{1,0:T(8,128)S(1)} %get-tuple-element.47.refs_13_.refs_14_.modulation_ref, ...), custom_call_target="tpu_custom_call", output_to_operand_aliasing={{}: (8, {})} | custom-call | tf_op jit(solution)/shard_map/pallas_call | solution.py:712
  (23 shorter events, 0.1 us)
Async XLA Ops:
  0.0 26.3 %copy-start.6 = (f32[1,576]{1,0:T(1,128)S(1)}, f32[1,576]{1,0:T(1,128)}, u32[]{:S(2)}) copy-start(f32[1,576]{1,0:T(1,128)} %constant.22.clone.refs_0_) | copy-start | bytes 6916
  0.0 26.3 %copy-start.5 = (s32[4]{0:T(128)S(1)}, s32[4]{0:T(128)}, u32[]{:S(2)}) copy-start(s32[4]{0:T(128)} %order_ref.1) | copy-start | bytes 52
  0.0 38.4 %collective-permute-start = (bf16[512,1152]{1,0:T(8,128)(2,1)}, bf16[512,1152]{1,0:T(8,128)(2,1)S(1)}, u32[]{:S(2)}, u32[]{:S(2)}) collective-permute-start(bf16[512,1152]{1,0:T(8,128)(2,1)} %kv_ref.1), channel_id=1, source_target_pairs={{0,1},{1,0},{2,3},{3,2},{4,5},{5,4},{6,7},{7,6},{8,9},{9,8},{10,11... | collective-permute-start | bytes 3538952 | tf_op jit(solution)/shard_map/ppermute | solution.py:30
  1.9 15.2 %collective-permute-start.1 = (bf16[512,512]{1,0:T(8,128)(2,1)S(1)}, bf16[512,512]{1,0:T(8,128)(2,1)S(1)}, u32[]{:S(2)}, u32[]{:S(2)}) collective-permute-start(bf16[512,512]{1,0:T(8,128)(2,1)S(1)} %get-tuple-element.37), channel_id=1, source_target_pairs={{0,2},{1,3},{2,0},{3,1},{4,6},{5,7},{6,4},{7,5},{8,10},{9,11},{10,... | collective-permute-start | bytes 1572872 | tf_op jit(solution)/shard_map/ppermute | solution.py:30
  17.1 20.0 %collective-permute-start.3 = (bf16[512,512]{1,0:T(8,128)(2,1)S(1)}, bf16[512,512]{1,0:T(8,128)(2,1)S(1)}, u32[]{:S(2)}, u32[]{:S(2)}) collective-permute-start(bf16[512,512]{1,0:T(8,128)(2,1)S(1)} %collective-permute-done.1.refs_3_), channel_id=1, source_target_pairs={{0,1},{1,0},{2,3},{3,2},{4,5},{5,4},{6,7},{7,6},{8,9},{9,8},{10,11... | collective-permute-start | bytes 1572872 | tf_op jit(solution)/shard_map/ppermute | solution.py:30
  17.1 9.2 %collective-permute-start.2 = (bf16[512,256]{1,0:T(8,128)(2,1)S(1)}, bf16[512,256]{1,0:T(8,128)(2,1)S(1)}, u32[]{:S(2)}, u32[]{:S(2)}) collective-permute-start(bf16[512,256]{1,0:T(8,128)(2,1)S(1)} %get-tuple-element.38), channel_id=1, source_target_pairs={{0,2},{1,3},{2,0},{3,1},{4,6},{5,7},{6,4},{7,5},{8,10},{9,11},{10,... | collective-permute-start | bytes 786440 | tf_op jit(solution)/shard_map/ppermute | solution.py:30
  18.8 15.4 %collective-permute-start.5 = (bf16[512,384]{1,0:T(8,128)(2,1)S(1)}, bf16[512,384]{1,0:T(8,128)(2,1)S(1)}, u32[]{:S(2)}, u32[]{:S(2)}) collective-permute-start(bf16[512,384]{1,0:T(8,128)(2,1)S(1)} %get-tuple-element.40), channel_id=1, source_target_pairs={{0,2},{1,3},{2,0},{3,1},{4,6},{5,7},{6,4},{7,5},{8,10},{9,11},{10,... | collective-permute-start | bytes 1179656 | tf_op jit(solution)/shard_map/ppermute | solution.py:30
  20.4 34.8 %collective-permute-start.7 = (bf16[128,1152]{1,0:T(8,128)(2,1)S(1)}, bf16[128,1152]{1,0:T(8,128)(2,1)S(1)}, u32[]{:S(2)}, u32[]{:S(2)}) collective-permute-start(bf16[128,1152]{1,0:T(8,128)(2,1)S(1)} %get-tuple-element.32.refs_4_.refs_1_), channel_id=1, source_target_pairs={{0,4},{1,5},{2,6},{3,7},{4,0},{5,1},{6,2},{7,3},{8,12},{9,13},{10,... | collective-permute-start | bytes 884744 | tf_op jit(solution)/shard_map/ppermute | solution.py:30
  26.3 15.5 %collective-permute-start.4 = (bf16[512,256]{1,0:T(8,128)(2,1)S(1)}, bf16[512,256]{1,0:T(8,128)(2,1)S(1)}, u32[]{:S(2)}, u32[]{:S(2)}) collective-permute-start(bf16[512,256]{1,0:T(8,128)(2,1)S(1)} %collective-permute-done.2.refs_4_), channel_id=1, source_target_pairs={{0,1},{1,0},{2,3},{3,2},{4,5},{5,4},{6,7},{7,6},{8,9},{9,8},{10,11... | collective-permute-start | bytes 786440 | tf_op jit(solution)/shard_map/ppermute | solution.py:30
  26.3 0.8 copy-start.3
  27.1 0.8 copy-start.4
  34.3 23.5 %collective-permute-start.8 = (bf16[128,1152]{1,0:T(8,128)(2,1)S(1)}, bf16[128,1152]{1,0:T(8,128)(2,1)S(1)}, u32[]{:S(2)}, u32[]{:S(2)}) collective-permute-start(bf16[128,1152]{1,0:T(8,128)(2,1)S(1)} %get-tuple-element.33.refs_5_.refs_2_), channel_id=1, source_target_pairs={{0,8},{1,9},{2,10},{3,11},{4,12},{5,13},{6,14},{7,15},{8,0},{9,1},... | collective-permute-start | bytes 884744 | tf_op jit(solution)/shard_map/ppermute | solution.py:30
  37.1 23.6 %collective-permute-start.9 = (bf16[128,1152]{1,0:T(8,128)(2,1)S(1)}, bf16[128,1152]{1,0:T(8,128)(2,1)S(1)}, u32[]{:S(2)}, u32[]{:S(2)}) collective-permute-start(bf16[128,1152]{1,0:T(8,128)(2,1)S(1)} %get-tuple-element.34.refs_6_.refs_3_), channel_id=1, source_target_pairs={{0,12},{1,13},{2,14},{3,15},{4,8},{5,9},{6,10},{7,11},{8,4},{9,5},... | collective-permute-start | bytes 884744 | tf_op jit(solution)/shard_map/ppermute | solution.py:30
  38.4 7.1 %collective-permute-start.6 = (bf16[512,384]{1,0:T(8,128)(2,1)S(1)}, bf16[512,384]{1,0:T(8,128)(2,1)S(1)}, u32[]{:S(2)}, u32[]{:S(2)}) collective-permute-start(bf16[512,384]{1,0:T(8,128)(2,1)S(1)} %collective-permute-done.5.refs_5_), channel_id=1, source_target_pairs={{0,1},{1,0},{2,3},{3,2},{4,5},{5,4},{6,7},{7,6},{8,9},{9,8},{10,11... | collective-permute-start | bytes 1179656 | tf_op jit(solution)/shard_map/ppermute | solution.py:30
  45.1 24.5 %collective-permute-start.10 = (bf16[256,128]{1,0:T(8,128)(2,1)S(1)}, bf16[256,128]{1,0:T(8,128)(2,1)S(1)}, u32[]{:S(2)}, u32[]{:S(2)}) collective-permute-start(bf16[256,128]{1,0:T(8,128)(2,1)S(1)} %get-tuple-element.43.refs_6_), channel_id=1, source_target_pairs={{0,4},{1,5},{2,6},{3,7},{4,0},{5,1},{6,2},{7,3},{8,12},{9,13},{10,... | collective-permute-start | bytes 196616 | tf_op jit(solution)/shard_map/ppermute | solution.py:30
  49.1 26.7 %collective-permute-start.11 = (bf16[320,128]{1,0:T(8,128)(2,1)S(1)}, bf16[320,128]{1,0:T(8,128)(2,1)S(1)}, u32[]{:S(2)}, u32[]{:S(2)}) collective-permute-start(bf16[320,128]{1,0:T(8,128)(2,1)S(1)} %get-tuple-element.44.refs_7_), channel_id=1, source_target_pairs={{0,4},{1,5},{2,6},{3,7},{4,0},{5,1},{6,2},{7,3},{8,12},{9,13},{10,... | collective-permute-start | bytes 245768 | tf_op jit(solution)/shard_map/ppermute | solution.py:30
  53.0 22.8 %copy-start = (bf16[3,1152,576]{1,2,0:T(8,128)(2,1)S(1)}, bf16[3,1152,576]{1,2,0:T(8,128)(2,1)}, u32[]{:S(2)}) copy-start(bf16[3,1152,576]{1,2,0:T(8,128)(2,1)} %param.19) | copy-start | bytes 11943940
  53.0 22.8 %copy-start.1 = (bf16[576,1152]{1,0:T(8,128)(2,1)S(1)}, bf16[576,1152]{1,0:T(8,128)(2,1)}, u32[]{:S(2)}) copy-start(bf16[576,1152]{1,0:T(8,128)(2,1)} %refs_12_.5) | copy-start | bytes 3981316
  55.2 20.6 %collective-permute-start.13 = (bf16[320,128]{1,0:T(8,128)(2,1)S(1)}, bf16[320,128]{1,0:T(8,128)(2,1)S(1)}, u32[]{:S(2)}, u32[]{:S(2)}) collective-permute-start(bf16[320,128]{1,0:T(8,128)(2,1)S(1)} %shard_map.112.refs_9_), channel_id=1, source_target_pairs={{0,8},{1,9},{2,10},{3,11},{4,12},{5,13},{6,14},{7,15},{8,0},{9,1},... | collective-permute-start | bytes 245768 | tf_op jit(solution)/shard_map/ppermute | solution.py:30
  57.7 18.1 %collective-permute-start.15 = (bf16[320,128]{1,0:T(8,128)(2,1)S(1)}, bf16[320,128]{1,0:T(8,128)(2,1)S(1)}, u32[]{:S(2)}, u32[]{:S(2)}) collective-permute-start(bf16[320,128]{1,0:T(8,128)(2,1)S(1)} %shard_map.113.refs_11_), channel_id=1, source_target_pairs={{0,12},{1,13},{2,14},{3,15},{4,8},{5,9},{6,10},{7,11},{8,4},{9,5},... | collective-permute-start | bytes 245768 | tf_op jit(solution)/shard_map/ppermute | solution.py:30
  60.7 12.8 %collective-permute-start.12 = (bf16[256,128]{1,0:T(8,128)(2,1)S(1)}, bf16[256,128]{1,0:T(8,128)(2,1)S(1)}, u32[]{:S(2)}, u32[]{:S(2)}) collective-permute-start(bf16[256,128]{1,0:T(8,128)(2,1)S(1)} %get-tuple-element.45.refs_8_), channel_id=1, source_target_pairs={{0,8},{1,9},{2,10},{3,11},{4,12},{5,13},{6,14},{7,15},{8,0},{9,1},... | collective-permute-start | bytes 196616 | tf_op jit(solution)/shard_map/ppermute | solution.py:30
  69.6 6.2 %collective-permute-start.14 = (bf16[256,128]{1,0:T(8,128)(2,1)S(1)}, bf16[256,128]{1,0:T(8,128)(2,1)S(1)}, u32[]{:S(2)}, u32[]{:S(2)}) collective-permute-start(bf16[256,128]{1,0:T(8,128)(2,1)S(1)} %get-tuple-element.46.refs_10_), channel_id=1, source_target_pairs={{0,12},{1,13},{2,14},{3,15},{4,8},{5,9},{6,10},{7,11},{8,4},{9,5},... | collective-permute-start | bytes 196616 | tf_op jit(solution)/shard_map/ppermute | solution.py:30
  79.9 11.6 %collective-permute-start.19 = (bf16[288,128]{1,0:T(8,128)(2,1)S(1)}, bf16[288,128]{1,0:T(8,128)(2,1)S(1)}, u32[]{:S(2)}, u32[]{:S(2)}) collective-permute-start(bf16[288,128]{1,0:T(8,128)(2,1)S(1)} %get-tuple-element.54), channel_id=1, source_target_pairs={{0,4},{1,5},{2,6},{3,7},{4,0},{5,1},{6,2},{7,3},{8,12},{9,13},{10,... | collective-permute-start | bytes 221192 | tf_op jit(solution)/shard_map/ppermute | solution.py:30
  80.9 13.2 %collective-permute-start.20 = (bf16[288,128]{1,0:T(8,128)(2,1)S(1)}, bf16[288,128]{1,0:T(8,128)(2,1)S(1)}, u32[]{:S(2)}, u32[]{:S(2)}) collective-permute-start(bf16[288,128]{1,0:T(8,128)(2,1)S(1)} %get-tuple-element.55), channel_id=1, source_target_pairs={{0,8},{1,9},{2,10},{3,11},{4,12},{5,13},{6,14},{7,15},{8,0},{9,1},... | collective-permute-start | bytes 221192 | tf_op jit(solution)/shard_map/ppermute | solution.py:30
  82.9 11.1 %collective-permute-start.21 = (bf16[288,128]{1,0:T(8,128)(2,1)S(1)}, bf16[288,128]{1,0:T(8,128)(2,1)S(1)}, u32[]{:S(2)}, u32[]{:S(2)}) collective-permute-start(bf16[288,128]{1,0:T(8,128)(2,1)S(1)} %get-tuple-element.56), channel_id=1, source_target_pairs={{0,12},{1,13},{2,14},{3,15},{4,8},{5,9},{6,10},{7,11},{8,4},{9,5},... | collective-permute-start | bytes 221192 | tf_op jit(solution)/shard_map/ppermute | solution.py:30
  88.4 7.4 %collective-permute-start.16 = (bf16[288,128]{1,0:T(8,128)(2,1)S(1)}, bf16[288,128]{1,0:T(8,128)(2,1)S(1)}, u32[]{:S(2)}, u32[]{:S(2)}) collective-permute-start(bf16[288,128]{1,0:T(8,128)(2,1)S(1)} %get-tuple-element.50), channel_id=1, source_target_pairs={{0,4},{1,5},{2,6},{3,7},{4,0},{5,1},{6,2},{7,3},{8,12},{9,13},{10,... | collective-permute-start | bytes 221192 | tf_op jit(solution)/shard_map/ppermute | solution.py:30
  89.0 7.5 %collective-permute-start.17 = (bf16[288,128]{1,0:T(8,128)(2,1)S(1)}, bf16[288,128]{1,0:T(8,128)(2,1)S(1)}, u32[]{:S(2)}, u32[]{:S(2)}) collective-permute-start(bf16[288,128]{1,0:T(8,128)(2,1)S(1)} %get-tuple-element.51), channel_id=1, source_target_pairs={{0,8},{1,9},{2,10},{3,11},{4,12},{5,13},{6,14},{7,15},{8,0},{9,1},... | collective-permute-start | bytes 221192 | tf_op jit(solution)/shard_map/ppermute | solution.py:30
  91.5 2.6 %copy-start.2 = (bf16[576,1152]{1,0:T(8,128)(2,1)S(1)}, bf16[576,1152]{1,0:T(8,128)(2,1)}, u32[]{:S(2)}) copy-start(bf16[576,1152]{1,0:T(8,128)(2,1)} %weight_ref.3) | copy-start | bytes 3981316
  91.5 6.3 %collective-permute-start.18 = (bf16[288,128]{1,0:T(8,128)(2,1)S(1)}, bf16[288,128]{1,0:T(8,128)(2,1)S(1)}, u32[]{:S(2)}, u32[]{:S(2)}) collective-permute-start(bf16[288,128]{1,0:T(8,128)(2,1)S(1)} %get-tuple-element.52), channel_id=1, source_target_pairs={{0,12},{1,13},{2,14},{3,15},{4,8},{5,9},{6,10},{7,11},{8,4},{9,5},... | collective-permute-start | bytes 221192 | tf_op jit(solution)/shard_map/ppermute | solution.py:30

commit v5 on v4

--- a/solution.py
+++ b/solution.py
@@ -17,6 +17,7 @@
 PAIR_GROUPS = ((0,), (1,), (2, 3))
 EMIT = (False, True, True)
 HALVES = 2
+STAGING_FLOPS = 4 * 10**9
 
 
 epsilon = 1e-06
@@ -138,24 +139,18 @@
         out_specs=vmem_specs(frames),
         scratch_shapes=[pltpu.SemaphoreType.DMA((frames,))],
         compiler_params=pltpu.CompilerParams(vmem_limit_bytes=2**20),
+        cost_estimate=pl.CostEstimate(
+            flops=STAGING_FLOPS, bytes_accessed=4 * tokens.size, transcendentals=0
+        ),
         name="pieces",
     )(slot, pltpu.with_memory_space_constraint(tokens, pltpu.HBM))
 
 
-def projection_kernel(slot_ref, time_ref, order_ref, weight_hbm, *refs, frames, width):
+def projection_kernel(slot_ref, time_ref, order_ref, weight_ref, *refs, frames, width):
     rate_ref, table_ref, mix_ref = refs[:3]
     pieces = refs[3 : 3 + frames]
-    query_ref, kv_ref, modulation_ref, place_ref = refs[3 + frames : 7 + frames]
-    weight_ref, inputs_ref, sems = refs[7 + frames :]
+    query_ref, kv_ref, modulation_ref, place_ref = refs[3 + frames :]
     padded = query_ref.shape[1]
-    middle = width + padded
-    parts = (slice(0, padded), slice(padded, middle), slice(middle, weight_ref.shape[0]))
-    copies = [
-        pltpu.make_async_copy(weight_hbm.at[part, :], weight_ref.at[part, :], sems.at[number])
-        for number, part in enumerate(parts)
-    ]
-    for copy in copies:
-        copy.start()
 
     rows = -(-(frames + 1) // 8) * 8
     row = lax.broadcasted_iota(jnp.int32, (rows, 1), 0)
@@ -169,25 +164,15 @@
     modulation = table_ref[...] + mix_ref[...] * waves[frames : frames + 1]
     modulation_ref[...] = modulation
 
-    piece = pieces[0].shape[0]
-    gain, shift = 1.0 + modulation[1:2, :], modulation[0:1, :]
-    for row in range(0, inputs_ref.shape[0], STRIP):
-        at = row % piece
-        tokens = pieces[row // piece][at : at + STRIP, :].astype(f32)
-        inputs_ref[row : row + STRIP, :] = (normalize(tokens) * gain + shift).astype(bf16)
-    inputs = inputs_ref[...]
-
-    def project(first, last):
-        return lax.dot_general(
-            inputs, weight_ref[first:last, :], NT, preferred_element_type=f32
-        ).astype(bf16)
-
-    copies[0].wait()
-    query_ref[...] = project(0, padded)
-    copies[1].wait()
-    kv_ref[:, :padded] = project(width, middle)
-    copies[2].wait()
-    kv_ref[:, padded:] = project(middle, weight_ref.shape[0])
+    tokens = jnp.concatenate([ref[...] for ref in pieces], axis=0).astype(f32)
+    inputs = normalize(tokens) * (1.0 + modulation[1:2, :]) + modulation[0:1, :]
+    inputs = inputs.astype(bf16)
+    query_ref[...] = lax.dot_general(
+        inputs, weight_ref[:padded, :], NT, preferred_element_type=f32
+    ).astype(bf16)
+    kv_ref[...] = lax.dot_general(
+        inputs, weight_ref[width:, :], NT, preferred_element_type=f32
+    ).astype(bf16)
 
 
 def projections(slot, timestep, frame_order, weight, mod_table, mod_mix, pieces, width):
@@ -198,10 +183,9 @@
     half = feature_width // 2
     rates = np.exp(-math.log(10000.0) * np.arange(half) / half).astype(np.float32)
     rates = jnp.asarray(rates[None])
-    operands = [pltpu.with_memory_space_constraint(weight, pltpu.HBM)]
-    operands += [
+    operands = [
         pltpu.with_memory_space_constraint(x, pltpu.VMEM)
-        for x in (rates, mod_table, mod_mix, *pieces)
+        for x in (weight, rates, mod_table, mod_mix, *pieces)
     ]
     return pl.pallas_call(
         functools.partial(projection_kernel, frames=frames, width=width),
@@ -213,16 +197,10 @@
         ],
         in_specs=[
             *[pl.BlockSpec(memory_space=pltpu.SMEM) for _ in range(3)],
-            pl.BlockSpec(memory_space=pltpu.HBM),
-            *vmem_specs(3 + frames),
+            *vmem_specs(4 + frames),
         ],
         out_specs=vmem_specs(4),
-        scratch_shapes=[
-            pltpu.VMEM(weight.shape, bf16),
-            pltpu.VMEM((rows, feature_width), bf16),
-            pltpu.SemaphoreType.DMA((3,)),
-        ],
-        compiler_params=pltpu.CompilerParams(vmem_limit_bytes=8 * 2**20),
+        compiler_params=pltpu.CompilerParams(vmem_limit_bytes=4 * 2**20),
         cost_estimate=pl.CostEstimate(
             flops=2 * rows * feature_width * 3 * width,
             bytes_accessed=2 * weight.size,
@@ -443,9 +421,9 @@
 
 def row_parts(number, rows):
     chunks = list(range(rows // QUERY_ROWS))
-    if number < len(PAIR_GROUPS) - 1 or len(chunks) < 3:
+    if number < len(PAIR_GROUPS) - 1:
         return [chunks]
-    return [[chunk] for chunk in chunks[:1:-1]] + [chunks[1::-1]]
+    return [[chunk] for chunk in reversed(chunks)]
 
 
 def spatial_group(
@@ -762,6 +740,7 @@
     peer_kv = permute(stale_kv, other_core)
 
     slot_word = slot.astype(jnp.int32)[None]
+    spatial_weight = jnp.swapaxes(spatial_qkv, 1, 2).reshape(3 * width, feature_width)
     pieces = stage_pieces(slot_word, tokens, frames)
     there = [pieces[0]]
     there += [permute(pieces[s], ahead(s)) for s in range(1, frames)]
@@ -770,7 +749,7 @@
         slot_word,
         timestep,
         frame_order,
-        jnp.swapaxes(spatial_qkv, 1, 2).reshape(3 * width, feature_width),
+        spatial_weight,
         mod_table,
         mod_mix,
         pieces,

time: 99.9 us -> 96.1 us (0.962)
  starting transfers between devices: 36.7 us -> 30.8 us
  waiting for transfers between devices: 24.4 us -> 28.8 us
  local copies, waits for them, and re-layouts: 1.55 us -> 0.04 us
    ppermute x22, starting transfers between devices: 36.7 us -> 30.8 us  [permute(): lax.ppermute(value, 'patch', [(source, target(source)) for source in rang...]
    ppermute x22, waiting for transfers between devices: 24.4 us -> 28.8 us  [permute(): lax.ppermute(value, 'patch', [(source, target(source)) for source in rang...]
    pallas_call x1, Pallas kernels: 6 us -> 3.95 us  [projections(): pl.pallas_call(functools.partial(projection_kernel, frames=frames, width=...]
    unnamed x14 -> x16, local copies, waits for them, and re-layouts: 1.55 us -> 0.04 us
    pallas_call x8 -> x9, Pallas kernels: 23.9 us -> 25 us  [on_chip_call(): pl.pallas_call(kernel, out_shape=[pltpu.VMEM(shape, dtype) for shape, dty...]
  transfers between devices with their start and end apart: 22 -> 22, of which waited for: 8 -> 8; matrix products, arithmetic and copies ran while one was open for 0% -> 0% of each run, Pallas kernels for 30% -> 31%
where the time goes in v5:
time: 96.1 us; the launch traced here: 95.9 us
  Pallas kernels  35.2 us (37%)
  starting transfers between devices  30.8 us (32%)
  waiting for transfers between devices  28.8 us (30%)
  between operations  1.04 us (1%)
    ppermute x22, starting transfers between devices, permute(): lax.ppermute(value, 'patch', [(source, target(source)) for source in rang...  30.8 us
    ppermute x22, waiting for transfers between devices, permute(): lax.ppermute(value, 'patch', [(source, target(source)) for source in rang...  28.8 us
    pallas_call x9, Pallas kernels, on_chip_call(): pl.pallas_call(kernel, out_shape=[pltpu.VMEM(shape, dtype) for shape, dty...  25 us
    pallas_call x1, Pallas kernels, projections(): pl.pallas_call(functools.partial(projection_kernel, frames=frames, width=...  3.95 us
    pallas_call x2, Pallas kernels, output(): pl.pallas_call(functools.partial(output_kernel, frames=frames, number=num...  3.49 us
  transfers between devices with their start and end apart: 22, of which 8 were waited for; matrix products, arithmetic and copies ran while one was open for 0% of the time, Pallas kernels for 31%

profile of v5, /device:TPU:0, one launch (start us, length us, event | category | flops | bytes accessed | tf_op | source)
XLA Modules:
  0.0 95.9 jit_solution(8245248396432876507)
XLA Ops:
  0.0 0.5 collective-permute-start
  0.5 1.4 %chunks.1 = (bf16[512,512]{1,0:T(8,128)(2,1)S(1)}, bf16[512,256]{1,0:T(8,128)(2,1)S(1)}, bf16[512,384]{1,0:T(8,128)(2,1)S(1)}) custom-call(bf16[512,1152]{1,0:T(8,128)(2,1)} %kv_ref.1), custom_call_target="tpu_custom_call" | custom-call | tf_op jit(solution)/shard_map/chunks/pallas_call | solution.py:103
  1.9 2.6 %collective-permute-start.1 = (bf16[512,512]{1,0:T(8,128)(2,1)S(1)}, bf16[512,512]{1,0:T(8,128)(2,1)S(1)}, u32[]{:S(2)}, u32[]{:S(2)}) collective-permute-start(bf16[512,512]{1,0:T(8,128)(2,1)S(1)} %get-tuple-element.35), channel_id=1, source_target_pairs={{0,2},{1,3},{2,0},{3,1},{4,6},{5,7},{6,4},{7,5},{8,10},{9,11},{10,... | collective-permute-start | bytes 1572872 | tf_op jit(solution)/shard_map/ppermute | solution.py:31
  4.5 0.1 collective-permute-start.2
  4.6 1.9 %collective-permute-start.5 = (bf16[512,384]{1,0:T(8,128)(2,1)S(1)}, bf16[512,384]{1,0:T(8,128)(2,1)S(1)}, u32[]{:S(2)}, u32[]{:S(2)}) collective-permute-start(bf16[512,384]{1,0:T(8,128)(2,1)S(1)} %get-tuple-element.38), channel_id=1, source_target_pairs={{0,2},{1,3},{2,0},{3,1},{4,6},{5,7},{6,4},{7,5},{8,10},{9,11},{10,... | collective-permute-start | bytes 1179656 | tf_op jit(solution)/shard_map/ppermute | solution.py:31
  6.5 10.7 %collective-permute-done.1.refs_3_ = bf16[512,512]{1,0:T(8,128)(2,1)S(1)} collective-permute-done((bf16[512,512]{1,0:T(8,128)(2,1)S(1)}, bf16[512,512]{1,0:T(8,128)(2,1)S(1)}, u32[]{:S(2)}, u32[]{:S(2)}) %collective-permute-start.1) | collective-permute-done | bytes 524320 | tf_op jit(solution)/shard_map/ppermute | solution.py:31
  17.3 0.0 collective-permute-start.3
  17.3 0.0 copy-start.6
  17.3 0.0 copy-start.7
  17.3 1.4 %pieces.1 = (bf16[128,1152]{1,0:T(8,128)(2,1)S(1)}, bf16[128,1152]{1,0:T(8,128)(2,1)S(1)}, bf16[128,1152]{1,0:T(8,128)(2,1)S(1)}, bf16[128,1152]{1,0:T(8,128)(2,1)S(1)}) custom-call(s32[1]{0:T(128)} %bitcast.slot_ref, bf16[512,1152]{1,0:T(8,128)(2,1)} %tokens_ref.1), custom_call_target="tpu_custom_call" | custom-call | flops 4000000000 | bytes 2359296 | tf_op jit(solution)/shard_map/pieces/pallas_call | solution.py:132
  18.7 2.1 %collective-permute-start.7 = (bf16[128,1152]{1,0:T(8,128)(2,1)S(1)}, bf16[128,1152]{1,0:T(8,128)(2,1)S(1)}, u32[]{:S(2)}, u32[]{:S(2)}) collective-permute-start(bf16[128,1152]{1,0:T(8,128)(2,1)S(1)} %get-tuple-element.30.refs_4_.refs_1_), channel_id=1, source_target_pairs={{0,4},{1,5},{2,6},{3,7},{4,0},{5,1},{6,2},{7,3},{8,12},{9,13},{10,... | collective-permute-start | bytes 884744 | tf_op jit(solution)/shard_map/ppermute | solution.py:31
  21.5 1.4 %collective-permute-done.2.refs_4_ = bf16[512,256]{1,0:T(8,128)(2,1)S(1)} collective-permute-done((bf16[512,256]{1,0:T(8,128)(2,1)S(1)}, bf16[512,256]{1,0:T(8,128)(2,1)S(1)}, u32[]{:S(2)}, u32[]{:S(2)}) %collective-permute-start.2) | collective-permute-done | bytes 262176 | tf_op jit(solution)/shard_map/ppermute | solution.py:31
  22.9 4.0 %projections.1 = (bf16[512,640]{1,0:T(8,128)(2,1)S(1)}, bf16[512,1152]{1,0:T(8,128)(2,1)S(1)}, f32[6,1152]{1,0:T(8,128)S(1)}, f32[4,1152]{1,0:T(4,128)S(1)}) custom-call(s32[1]{0:T(128)} %bitcast.slot_ref, s32[1]{0:T(128)S(6)} %copy.14.time_ref, s32[4]{0:T(128)S(1)} %copy-done.6, bf16[1728,1152]{1,0:T(8,128)(2,1)S(1)} %bitcast.9, f32[1,576]{1,0:T(1,128)S(1)} %copy-done.7, ...), custom_call_target="tpu_custom_call" | custom-call | flops 2038431744 | bytes 3981312 | tf_op jit(solution)/shard_map/projections/pallas_call | solution.py:190
  26.9 4.2 %collective-permute-done.5.refs_5_ = bf16[512,384]{1,0:T(8,128)(2,1)S(1)} collective-permute-done((bf16[512,384]{1,0:T(8,128)(2,1)S(1)}, bf16[512,384]{1,0:T(8,128)(2,1)S(1)}, u32[]{:S(2)}, u32[]{:S(2)}) %collective-permute-start.5) | collective-permute-done | bytes 393248 | tf_op jit(solution)/shard_map/ppermute | solution.py:31
  31.1 2.8 %collective-permute-start.8 = (bf16[128,1152]{1,0:T(8,128)(2,1)S(1)}, bf16[128,1152]{1,0:T(8,128)(2,1)S(1)}, u32[]{:S(2)}, u32[]{:S(2)}) collective-permute-start(bf16[128,1152]{1,0:T(8,128)(2,1)S(1)} %get-tuple-element.31.refs_5_.refs_2_), channel_id=1, source_target_pairs={{0,8},{1,9},{2,10},{3,11},{4,12},{5,13},{6,14},{7,15},{8,0},{9,1},... | collective-permute-start | bytes 884744 | tf_op jit(solution)/shard_map/ppermute | solution.py:31
  34.0 0.0 collective-permute-done.3.refs_4_.refs_5_.refs_6_
  34.0 1.3 %collective-permute-start.9 = (bf16[128,1152]{1,0:T(8,128)(2,1)S(1)}, bf16[128,1152]{1,0:T(8,128)(2,1)S(1)}, u32[]{:S(2)}, u32[]{:S(2)}) collective-permute-start(bf16[128,1152]{1,0:T(8,128)(2,1)S(1)} %get-tuple-element.32.refs_6_.refs_3_), channel_id=1, source_target_pairs={{0,12},{1,13},{2,14},{3,15},{4,8},{5,9},{6,10},{7,11},{8,4},{9,5},... | collective-permute-start | bytes 884744 | tf_op jit(solution)/shard_map/ppermute | solution.py:31
  35.3 3.4 %shard_map.109.refs_7_ = bf16[512,256]{1,0:T(8,128)(2,1)S(1)} custom-call(bf16[512,640]{1,0:T(8,128)(2,1)S(1)} %get-tuple-element.33.refs_0_, bf16[512,1152]{1,0:T(8,128)(2,1)S(1)} %get-tuple-element.34.refs_1_, bf16[512,1152]{1,0:T(8,128)(2,1)S(1)} %collective-permute-done.refs_2_, bf16[512,512]{1,0:T(8,128)(2,1)S(1)} %collective-permute-done.1.refs_3_, ...), custom_call_target="tpu_custom_call" | custom-call | flops 2147483648 | bytes 4063232 | tf_op jit(solution)/shard_map/pallas_call | solution.py:69
  38.7 3.5 %shard_map.110 = (bf16[256,128]{1,0:T(8,128)(2,1)S(1)}, bf16[256,128]{1,0:T(8,128)(2,1)S(1)}, bf16[256,128]{1,0:T(8,128)(2,1)S(1)}, bf16[256,128]{1,0:T(8,128)(2,1)S(1)}, bf16[512,128]{1,0:T(8,128)(2,1)S(1)}) custom-call(bf16[512,640]{1,0:T(8,128)(2,1)S(1)} %get-tuple-element.33.refs_0_, bf16[512,1152]{1,0:T(8,128)(2,1)S(1)} %get-tuple-element.34.refs_1_, ...), custom_call_target="tpu_custom_call" | custom-call | flops 2147483648 | bytes 4849664 | tf_op jit(solution)/shard_map/pallas_call | solution.py:69
  42.2 0.4 collective-permute-start.10
  42.6 2.3 %shard_map.112.refs_7_ = bf16[320,128]{1,0:T(8,128)(2,1)S(1)} custom-call(bf16[512,640]{1,0:T(8,128)(2,1)S(1)} %get-tuple-element.33.refs_0_, bf16[512,1152]{1,0:T(8,128)(2,1)S(1)} %get-tuple-element.34.refs_1_, bf16[512,1152]{1,0:T(8,128)(2,1)S(1)} %collective-permute-done.refs_2_, bf16[512,512]{1,0:T(8,128)(2,1)S(1)} %collective-permute-done.1.refs_3_, ...), custom_call_target="tpu_custom_call" | custom-call | flops 1073741824 | bytes 5505024 | tf_op jit(solution)/shard_map/pallas_call | solution.py:69
  44.9 1.8 %collective-permute-start.11 = (bf16[320,128]{1,0:T(8,128)(2,1)S(1)}, bf16[320,128]{1,0:T(8,128)(2,1)S(1)}, u32[]{:S(2)}, u32[]{:S(2)}) collective-permute-start(bf16[320,128]{1,0:T(8,128)(2,1)S(1)} %shard_map.112.refs_7_), channel_id=1, source_target_pairs={{0,4},{1,5},{2,6},{3,7},{4,0},{5,1},{6,2},{7,3},{8,12},{9,13},{10,... | collective-permute-start | bytes 245768 | tf_op jit(solution)/shard_map/ppermute | solution.py:31
  46.7 2.1 %shard_map.113.refs_9_ = bf16[320,128]{1,0:T(8,128)(2,1)S(1)} custom-call(bf16[512,640]{1,0:T(8,128)(2,1)S(1)} %get-tuple-element.33.refs_0_, bf16[512,1152]{1,0:T(8,128)(2,1)S(1)} %get-tuple-element.34.refs_1_, bf16[512,1152]{1,0:T(8,128)(2,1)S(1)} %collective-permute-done.refs_2_, bf16[512,512]{1,0:T(8,128)(2,1)S(1)} %collective-permute-done.1.refs_3_, ...), custom_call_target="tpu_custom_call" | custom-call | flops 1073741824 | bytes 5505024 | tf_op jit(solution)/shard_map/pallas_call | solution.py:69
  48.9 2.1 %shard_map.114.refs_11_ = bf16[320,128]{1,0:T(8,128)(2,1)S(1)} custom-call(bf16[512,640]{1,0:T(8,128)(2,1)S(1)} %get-tuple-element.33.refs_0_, bf16[512,1152]{1,0:T(8,128)(2,1)S(1)} %get-tuple-element.34.refs_1_, bf16[512,1152]{1,0:T(8,128)(2,1)S(1)} %collective-permute-done.refs_2_, bf16[512,512]{1,0:T(8,128)(2,1)S(1)} %collective-permute-done.1.refs_3_, ...), custom_call_target="tpu_custom_call" | custom-call | flops 1073741824 | bytes 5505024 | tf_op jit(solution)/shard_map/pallas_call | solution.py:69
  51.0 0.0 collective-permute-done.7.refs_1_
  51.0 1.8 %collective-permute-start.12 = (bf16[256,128]{1,0:T(8,128)(2,1)S(1)}, bf16[256,128]{1,0:T(8,128)(2,1)S(1)}, u32[]{:S(2)}, u32[]{:S(2)}) collective-permute-start(bf16[256,128]{1,0:T(8,128)(2,1)S(1)} %get-tuple-element.41.refs_8_), channel_id=1, source_target_pairs={{0,8},{1,9},{2,10},{3,11},{4,12},{5,13},{6,14},{7,15},{8,0},{9,1},... | collective-permute-start | bytes 196616 | tf_op jit(solution)/shard_map/ppermute | solution.py:31
  52.8 2.5 %collective-permute-done.8.refs_2_ = bf16[128,1152]{1,0:T(8,128)(2,1)S(1)} collective-permute-done((bf16[128,1152]{1,0:T(8,128)(2,1)S(1)}, bf16[128,1152]{1,0:T(8,128)(2,1)S(1)}, u32[]{:S(2)}, u32[]{:S(2)}) %collective-permute-start.8) | collective-permute-done | bytes 294944 | tf_op jit(solution)/shard_map/ppermute | solution.py:31
  55.3 0.0 collective-permute-start.13
  55.3 0.0 collective-permute-done.9.refs_3_
  55.3 0.0 copy-start.1
  55.3 1.9 %collective-permute-start.14 = (bf16[256,128]{1,0:T(8,128)(2,1)S(1)}, bf16[256,128]{1,0:T(8,128)(2,1)S(1)}, u32[]{:S(2)}, u32[]{:S(2)}) collective-permute-start(bf16[256,128]{1,0:T(8,128)(2,1)S(1)} %get-tuple-element.42.refs_10_), channel_id=1, source_target_pairs={{0,12},{1,13},{2,14},{3,15},{4,8},{5,9},{6,10},{7,11},{8,4},{9,5},... | collective-permute-start | bytes 196616 | tf_op jit(solution)/shard_map/ppermute | solution.py:31
  57.2 2.0 %collective-permute-start.15 = (bf16[320,128]{1,0:T(8,128)(2,1)S(1)}, bf16[320,128]{1,0:T(8,128)(2,1)S(1)}, u32[]{:S(2)}, u32[]{:S(2)}) collective-permute-start(bf16[320,128]{1,0:T(8,128)(2,1)S(1)} %shard_map.114.refs_11_), channel_id=1, source_target_pairs={{0,12},{1,13},{2,14},{3,15},{4,8},{5,9},{6,10},{7,11},{8,4},{9,5},... | collective-permute-start | bytes 245768 | tf_op jit(solution)/shard_map/ppermute | solution.py:31
  59.2 2.1 %shard_map.111.refs_5_ = bf16[320,128]{1,0:T(8,128)(2,1)S(1)} custom-call(bf16[512,640]{1,0:T(8,128)(2,1)S(1)} %get-tuple-element.33.refs_0_, bf16[512,1152]{1,0:T(8,128)(2,1)S(1)} %get-tuple-element.34.refs_1_, bf16[512,1152]{1,0:T(8,128)(2,1)S(1)} %collective-permute-done.refs_2_, bf16[512,512]{1,0:T(8,128)(2,1)S(1)} %collective-permute-done.1.refs_3_, ...), custom_call_target="tpu_custom_call" | custom-call | flops 1073741824 | bytes 5505024 | tf_op jit(solution)/shard_map/pallas_call | solution.py:69
  61.4 7.1 %collective-permute-done.12.refs_8_ = bf16[256,128]{1,0:T(8,128)(2,1)S(1)} collective-permute-done((bf16[256,128]{1,0:T(8,128)(2,1)S(1)}, bf16[256,128]{1,0:T(8,128)(2,1)S(1)}, u32[]{:S(2)}, u32[]{:S(2)}) %collective-permute-start.12) | collective-permute-done | bytes 65568 | tf_op jit(solution)/shard_map/ppermute | solution.py:31
  68.5 0.9 collective-permute-done.13.refs_9_
  69.4 4.0 %shard_map.117 = (bf16[288,128]{1,0:T(8,128)(2,1)S(1)}, bf16[288,128]{1,0:T(8,128)(2,1)S(1)}, bf16[288,128]{1,0:T(8,128)(2,1)S(1)}, bf16[288,128]{1,0:T(8,128)(2,1)S(1)}) custom-call(bf16[128,1152]{1,0:T(8,128)(2,1)S(1)} %get-tuple-element.29.refs_3_.refs_0_, bf16[128,1152]{1,0:T(8,128)(2,1)S(1)} %collective-permute-done.7.refs_1_, ...), custom_call_target="tpu_custom_call" | custom-call | flops 1698693120 | bytes 7123968 | tf_op jit(solution)/shard_map/pallas_call | solution.py:69
  73.4 4.5 %collective-permute-start.19 = (bf16[288,128]{1,0:T(8,128)(2,1)S(1)}, bf16[288,128]{1,0:T(8,128)(2,1)S(1)}, u32[]{:S(2)}, u32[]{:S(2)}) collective-permute-start(bf16[288,128]{1,0:T(8,128)(2,1)S(1)} %get-tuple-element.50), channel_id=1, source_target_pairs={{0,4},{1,5},{2,6},{3,7},{4,0},{5,1},{6,2},{7,3},{8,12},{9,13},{10,... | collective-permute-start | bytes 221192 | tf_op jit(solution)/shard_map/ppermute | solution.py:31
  77.9 1.3 %collective-permute-start.20 = (bf16[288,128]{1,0:T(8,128)(2,1)S(1)}, bf16[288,128]{1,0:T(8,128)(2,1)S(1)}, u32[]{:S(2)}, u32[]{:S(2)}) collective-permute-start(bf16[288,128]{1,0:T(8,128)(2,1)S(1)} %get-tuple-element.51), channel_id=1, source_target_pairs={{0,8},{1,9},{2,10},{3,11},{4,12},{5,13},{6,14},{7,15},{8,0},{9,1},... | collective-permute-start | bytes 221192 | tf_op jit(solution)/shard_map/ppermute | solution.py:31
  79.2 1.4 %collective-permute-start.21 = (bf16[288,128]{1,0:T(8,128)(2,1)S(1)}, bf16[288,128]{1,0:T(8,128)(2,1)S(1)}, u32[]{:S(2)}, u32[]{:S(2)}) collective-permute-start(bf16[288,128]{1,0:T(8,128)(2,1)S(1)} %get-tuple-element.52), channel_id=1, source_target_pairs={{0,12},{1,13},{2,14},{3,15},{4,8},{5,9},{6,10},{7,11},{8,4},{9,5},... | collective-permute-start | bytes 221192 | tf_op jit(solution)/shard_map/ppermute | solution.py:31
  80.6 4.1 %shard_map.116 = (bf16[288,128]{1,0:T(8,128)(2,1)S(1)}, bf16[288,128]{1,0:T(8,128)(2,1)S(1)}, bf16[288,128]{1,0:T(8,128)(2,1)S(1)}, bf16[288,128]{1,0:T(8,128)(2,1)S(1)}) custom-call(bf16[128,1152]{1,0:T(8,128)(2,1)S(1)} %get-tuple-element.29.refs_3_.refs_0_, bf16[128,1152]{1,0:T(8,128)(2,1)S(1)} %collective-permute-done.7.refs_1_, ...), custom_call_target="tpu_custom_call" | custom-call | flops 1698693120 | bytes 7123968 | tf_op jit(solution)/shard_map/pallas_call | solution.py:69
  84.7 0.9 collective-permute-start.16
  85.5 2.2 %collective-permute-start.17 = (bf16[288,128]{1,0:T(8,128)(2,1)S(1)}, bf16[288,128]{1,0:T(8,128)(2,1)S(1)}, u32[]{:S(2)}, u32[]{:S(2)}) collective-permute-start(bf16[288,128]{1,0:T(8,128)(2,1)S(1)} %get-tuple-element.47), channel_id=1, source_target_pairs={{0,8},{1,9},{2,10},{3,11},{4,12},{5,13},{6,14},{7,15},{8,0},{9,1},... | collective-permute-start | bytes 221192 | tf_op jit(solution)/shard_map/ppermute | solution.py:31
  87.7 1.4 %collective-permute-start.18 = (bf16[288,128]{1,0:T(8,128)(2,1)S(1)}, bf16[288,128]{1,0:T(8,128)(2,1)S(1)}, u32[]{:S(2)}, u32[]{:S(2)}) collective-permute-start(bf16[288,128]{1,0:T(8,128)(2,1)S(1)} %get-tuple-element.48), channel_id=1, source_target_pairs={{0,12},{1,13},{2,14},{3,15},{4,8},{5,9},{6,10},{7,11},{8,4},{9,5},... | collective-permute-start | bytes 221192 | tf_op jit(solution)/shard_map/ppermute | solution.py:31
  89.1 1.2 %shard_map.115.after_ref = f32[512,1152]{1,0:T(8,128)S(1)} custom-call(bf16[128,1152]{1,0:T(8,128)(2,1)S(1)} %get-tuple-element.29.refs_3_.refs_0_, bf16[128,1152]{1,0:T(8,128)(2,1)S(1)} %get-tuple-element.30.refs_4_.refs_1_, bf16[128,1152]{1,0:T(8,128)(2,1)S(1)} %get-tuple-element.31.refs_5_.refs_2_, ...), custom_call_target="tpu_custom_call" | custom-call | flops 679477248 | bytes 3124224 | tf_op jit(solution)/shard_map/pallas_call | solution.py:69
  90.3 1.8 %shard_map.118.refs_4_ = f32[512,1152]{1,0:T(8,128)} custom-call(s32[1]{0:T(128)} %bitcast.slot_ref, f32[512,1152]{1,0:T(8,128)S(1)} %shard_map.115.after_ref, bf16[576,1152]{1,0:T(8,128)(2,1)S(1)} %copy-done.2, f32[6,1152]{1,0:T(8,128)S(1)} %get-tuple-element.43.refs_13_.refs_14_.modulation_ref, bf16[288,128]{1,0:T(8,128)(2,1)S(1)} %get-tuple-element.49.refs_0_, ...), custom_call_target="tpu_custom_call" | custom-call | tf_op jit(solution)/shard_map/pallas_call | solution.py:690
  92.1 0.3 collective-permute-done.17.refs_2_
  92.4 1.6 %collective-permute-done.18.refs_3_ = bf16[288,128]{1,0:T(8,128)(2,1)S(1)} collective-permute-done((bf16[288,128]{1,0:T(8,128)(2,1)S(1)}, bf16[288,128]{1,0:T(8,128)(2,1)S(1)}, u32[]{:S(2)}, u32[]{:S(2)}) %collective-permute-start.18) | collective-permute-done | bytes 73760 | tf_op jit(solution)/shard_map/ppermute | solution.py:31
  94.0 1.7 %shard_map.119 = f32[512,1152]{1,0:T(8,128)} custom-call(s32[1]{0:T(128)} %bitcast.slot_ref, f32[512,1152]{1,0:T(8,128)S(1)} %shard_map.115.after_ref, bf16[576,1152]{1,0:T(8,128)(2,1)S(1)} %copy-done.2, f32[6,1152]{1,0:T(8,128)S(1)} %get-tuple-element.43.refs_13_.refs_14_.modulation_ref, ...), custom_call_target="tpu_custom_call", output_to_operand_aliasing={{}: (8, {})} | custom-call | tf_op jit(solution)/shard_map/pallas_call | solution.py:690
  (26 shorter events, 0.1 us)
Async XLA Ops:
  0.0 35.3 %collective-permute-start = (bf16[512,1152]{1,0:T(8,128)(2,1)}, bf16[512,1152]{1,0:T(8,128)(2,1)S(1)}, u32[]{:S(2)}, u32[]{:S(2)}) collective-permute-start(bf16[512,1152]{1,0:T(8,128)(2,1)} %kv_ref.1), channel_id=1, source_target_pairs={{0,1},{1,0},{2,3},{3,2},{4,5},{5,4},{6,7},{7,6},{8,9},{9,8},{10,11... | collective-permute-start | bytes 3538952 | tf_op jit(solution)/shard_map/ppermute | solution.py:31
  1.9 15.3 %collective-permute-start.1 = (bf16[512,512]{1,0:T(8,128)(2,1)S(1)}, bf16[512,512]{1,0:T(8,128)(2,1)S(1)}, u32[]{:S(2)}, u32[]{:S(2)}) collective-permute-start(bf16[512,512]{1,0:T(8,128)(2,1)S(1)} %get-tuple-element.35), channel_id=1, source_target_pairs={{0,2},{1,3},{2,0},{3,1},{4,6},{5,7},{6,4},{7,5},{8,10},{9,11},{10,... | collective-permute-start | bytes 1572872 | tf_op jit(solution)/shard_map/ppermute | solution.py:31
  4.5 18.4 %collective-permute-start.2 = (bf16[512,256]{1,0:T(8,128)(2,1)S(1)}, bf16[512,256]{1,0:T(8,128)(2,1)S(1)}, u32[]{:S(2)}, u32[]{:S(2)}) collective-permute-start(bf16[512,256]{1,0:T(8,128)(2,1)S(1)} %get-tuple-element.36), channel_id=1, source_target_pairs={{0,2},{1,3},{2,0},{3,1},{4,6},{5,7},{6,4},{7,5},{8,10},{9,11},{10,... | collective-permute-start | bytes 786440 | tf_op jit(solution)/shard_map/ppermute | solution.py:31
  4.6 26.6 %collective-permute-start.5 = (bf16[512,384]{1,0:T(8,128)(2,1)S(1)}, bf16[512,384]{1,0:T(8,128)(2,1)S(1)}, u32[]{:S(2)}, u32[]{:S(2)}) collective-permute-start(bf16[512,384]{1,0:T(8,128)(2,1)S(1)} %get-tuple-element.38), channel_id=1, source_target_pairs={{0,2},{1,3},{2,0},{3,1},{4,6},{5,7},{6,4},{7,5},{8,10},{9,11},{10,... | collective-permute-start | bytes 1179656 | tf_op jit(solution)/shard_map/ppermute | solution.py:31
  17.3 16.7 %collective-permute-start.3 = (bf16[512,512]{1,0:T(8,128)(2,1)S(1)}, bf16[512,512]{1,0:T(8,128)(2,1)S(1)}, u32[]{:S(2)}, u32[]{:S(2)}) collective-permute-start(bf16[512,512]{1,0:T(8,128)(2,1)S(1)} %collective-permute-done.1.refs_3_), channel_id=1, source_target_pairs={{0,1},{1,0},{2,3},{3,2},{4,5},{5,4},{6,7},{7,6},{8,9},{9,8},{10,11... | collective-permute-start | bytes 1572872 | tf_op jit(solution)/shard_map/ppermute | solution.py:31
  17.3 5.6 %copy-start.3 = (bf16[3,1152,576]{1,2,0:T(8,128)(2,1)S(1)}, bf16[3,1152,576]{1,2,0:T(8,128)(2,1)}, u32[]{:S(2)}) copy-start(bf16[3,1152,576]{1,2,0:T(8,128)(2,1)} %param.17) | copy-start | bytes 11943940
  17.3 5.6 %copy-start.4 = (f32[6,1152]{1,0:T(8,128)S(1)}, f32[6,1152]{1,0:T(8,128)}, u32[]{:S(2)}) copy-start(f32[6,1152]{1,0:T(8,128)} %refs_1_.1) | copy-start | bytes 82948
  17.3 5.6 %copy-start.5 = (f32[6,1152]{1,0:T(8,128)S(1)}, f32[6,1152]{1,0:T(8,128)}, u32[]{:S(2)}) copy-start(f32[6,1152]{1,0:T(8,128)} %refs_2_.1) | copy-start | bytes 82948
  17.3 5.6 %copy-start.6 = (s32[4]{0:T(128)S(1)}, s32[4]{0:T(128)}, u32[]{:S(2)}) copy-start(s32[4]{0:T(128)} %order_ref.1) | copy-start | bytes 52
  17.3 5.6 %copy-start.7 = (f32[1,576]{1,0:T(1,128)S(1)}, f32[1,576]{1,0:T(1,128)}, u32[]{:S(2)}) copy-start(f32[1,576]{1,0:T(1,128)} %constant.22.clone.refs_0_) | copy-start | bytes 6916
  18.7 32.3 %collective-permute-start.7 = (bf16[128,1152]{1,0:T(8,128)(2,1)S(1)}, bf16[128,1152]{1,0:T(8,128)(2,1)S(1)}, u32[]{:S(2)}, u32[]{:S(2)}) collective-permute-start(bf16[128,1152]{1,0:T(8,128)(2,1)S(1)} %get-tuple-element.30.refs_4_.refs_1_), channel_id=1, source_target_pairs={{0,4},{1,5},{2,6},{3,7},{4,0},{5,1},{6,2},{7,3},{8,12},{9,13},{10,... | collective-permute-start | bytes 884744 | tf_op jit(solution)/shard_map/ppermute | solution.py:31
  22.9 15.8 %collective-permute-start.4 = (bf16[512,256]{1,0:T(8,128)(2,1)S(1)}, bf16[512,256]{1,0:T(8,128)(2,1)S(1)}, u32[]{:S(2)}, u32[]{:S(2)}) collective-permute-start(bf16[512,256]{1,0:T(8,128)(2,1)S(1)} %collective-permute-done.2.refs_4_), channel_id=1, source_target_pairs={{0,1},{1,0},{2,3},{3,2},{4,5},{5,4},{6,7},{7,6},{8,9},{9,8},{10,11... | collective-permute-start | bytes 786440 | tf_op jit(solution)/shard_map/ppermute | solution.py:31
  31.1 24.2 %collective-permute-start.8 = (bf16[128,1152]{1,0:T(8,128)(2,1)S(1)}, bf16[128,1152]{1,0:T(8,128)(2,1)S(1)}, u32[]{:S(2)}, u32[]{:S(2)}) collective-permute-start(bf16[128,1152]{1,0:T(8,128)(2,1)S(1)} %get-tuple-element.31.refs_5_.refs_2_), channel_id=1, source_target_pairs={{0,8},{1,9},{2,10},{3,11},{4,12},{5,13},{6,14},{7,15},{8,0},{9,1},... | collective-permute-start | bytes 884744 | tf_op jit(solution)/shard_map/ppermute | solution.py:31
  34.0 21.3 %collective-permute-start.9 = (bf16[128,1152]{1,0:T(8,128)(2,1)S(1)}, bf16[128,1152]{1,0:T(8,128)(2,1)S(1)}, u32[]{:S(2)}, u32[]{:S(2)}) collective-permute-start(bf16[128,1152]{1,0:T(8,128)(2,1)S(1)} %get-tuple-element.32.refs_6_.refs_3_), channel_id=1, source_target_pairs={{0,12},{1,13},{2,14},{3,15},{4,8},{5,9},{6,10},{7,11},{8,4},{9,5},... | collective-permute-start | bytes 884744 | tf_op jit(solution)/shard_map/ppermute | solution.py:31
  35.3 7.3 %collective-permute-start.6 = (bf16[512,384]{1,0:T(8,128)(2,1)S(1)}, bf16[512,384]{1,0:T(8,128)(2,1)S(1)}, u32[]{:S(2)}, u32[]{:S(2)}) collective-permute-start(bf16[512,384]{1,0:T(8,128)(2,1)S(1)} %collective-permute-done.5.refs_5_), channel_id=1, source_target_pairs={{0,1},{1,0},{2,3},{3,2},{4,5},{5,4},{6,7},{7,6},{8,9},{9,8},{10,11... | collective-permute-start | bytes 1179656 | tf_op jit(solution)/shard_map/ppermute | solution.py:31
  42.2 15.0 %collective-permute-start.10 = (bf16[256,128]{1,0:T(8,128)(2,1)S(1)}, bf16[256,128]{1,0:T(8,128)(2,1)S(1)}, u32[]{:S(2)}, u32[]{:S(2)}) collective-permute-start(bf16[256,128]{1,0:T(8,128)(2,1)S(1)} %get-tuple-element.40.refs_6_), channel_id=1, source_target_pairs={{0,4},{1,5},{2,6},{3,7},{4,0},{5,1},{6,2},{7,3},{8,12},{9,13},{10,... | collective-permute-start | bytes 196616 | tf_op jit(solution)/shard_map/ppermute | solution.py:31
  44.9 23.5 %collective-permute-start.11 = (bf16[320,128]{1,0:T(8,128)(2,1)S(1)}, bf16[320,128]{1,0:T(8,128)(2,1)S(1)}, u32[]{:S(2)}, u32[]{:S(2)}) collective-permute-start(bf16[320,128]{1,0:T(8,128)(2,1)S(1)} %shard_map.112.refs_7_), channel_id=1, source_target_pairs={{0,4},{1,5},{2,6},{3,7},{4,0},{5,1},{6,2},{7,3},{8,12},{9,13},{10,... | collective-permute-start | bytes 245768 | tf_op jit(solution)/shard_map/ppermute | solution.py:31
  51.0 17.5 %collective-permute-start.12 = (bf16[256,128]{1,0:T(8,128)(2,1)S(1)}, bf16[256,128]{1,0:T(8,128)(2,1)S(1)}, u32[]{:S(2)}, u32[]{:S(2)}) collective-permute-start(bf16[256,128]{1,0:T(8,128)(2,1)S(1)} %get-tuple-element.41.refs_8_), channel_id=1, source_target_pairs={{0,8},{1,9},{2,10},{3,11},{4,12},{5,13},{6,14},{7,15},{8,0},{9,1},... | collective-permute-start | bytes 196616 | tf_op jit(solution)/shard_map/ppermute | solution.py:31
  55.3 14.1 %collective-permute-start.13 = (bf16[320,128]{1,0:T(8,128)(2,1)S(1)}, bf16[320,128]{1,0:T(8,128)(2,1)S(1)}, u32[]{:S(2)}, u32[]{:S(2)}) collective-permute-start(bf16[320,128]{1,0:T(8,128)(2,1)S(1)} %shard_map.113.refs_9_), channel_id=1, source_target_pairs={{0,8},{1,9},{2,10},{3,11},{4,12},{5,13},{6,14},{7,15},{8,0},{9,1},... | collective-permute-start | bytes 245768 | tf_op jit(solution)/shard_map/ppermute | solution.py:31
  55.3 14.1 %copy-start = (bf16[3,1152,576]{1,2,0:T(8,128)(2,1)S(1)}, bf16[3,1152,576]{1,2,0:T(8,128)(2,1)}, u32[]{:S(2)}) copy-start(bf16[3,1152,576]{1,2,0:T(8,128)(2,1)} %param.19) | copy-start | bytes 11943940
  55.3 14.1 %copy-start.1 = (bf16[576,1152]{1,0:T(8,128)(2,1)S(1)}, bf16[576,1152]{1,0:T(8,128)(2,1)}, u32[]{:S(2)}) copy-start(bf16[576,1152]{1,0:T(8,128)(2,1)} %refs_12_.5) | copy-start | bytes 3981316
  55.3 13.2 %collective-permute-start.14 = (bf16[256,128]{1,0:T(8,128)(2,1)S(1)}, bf16[256,128]{1,0:T(8,128)(2,1)S(1)}, u32[]{:S(2)}, u32[]{:S(2)}) collective-permute-start(bf16[256,128]{1,0:T(8,128)(2,1)S(1)} %get-tuple-element.42.refs_10_), channel_id=1, source_target_pairs={{0,12},{1,13},{2,14},{3,15},{4,8},{5,9},{6,10},{7,11},{8,4},{9,5},... | collective-permute-start | bytes 196616 | tf_op jit(solution)/shard_map/ppermute | solution.py:31
  57.2 12.2 %collective-permute-start.15 = (bf16[320,128]{1,0:T(8,128)(2,1)S(1)}, bf16[320,128]{1,0:T(8,128)(2,1)S(1)}, u32[]{:S(2)}, u32[]{:S(2)}) collective-permute-start(bf16[320,128]{1,0:T(8,128)(2,1)S(1)} %shard_map.114.refs_11_), channel_id=1, source_target_pairs={{0,12},{1,13},{2,14},{3,15},{4,8},{5,9},{6,10},{7,11},{8,4},{9,5},... | collective-permute-start | bytes 245768 | tf_op jit(solution)/shard_map/ppermute | solution.py:31
  73.4 14.3 %collective-permute-start.19 = (bf16[288,128]{1,0:T(8,128)(2,1)S(1)}, bf16[288,128]{1,0:T(8,128)(2,1)S(1)}, u32[]{:S(2)}, u32[]{:S(2)}) collective-permute-start(bf16[288,128]{1,0:T(8,128)(2,1)S(1)} %get-tuple-element.50), channel_id=1, source_target_pairs={{0,4},{1,5},{2,6},{3,7},{4,0},{5,1},{6,2},{7,3},{8,12},{9,13},{10,... | collective-permute-start | bytes 221192 | tf_op jit(solution)/shard_map/ppermute | solution.py:31
  77.9 12.4 %collective-permute-start.20 = (bf16[288,128]{1,0:T(8,128)(2,1)S(1)}, bf16[288,128]{1,0:T(8,128)(2,1)S(1)}, u32[]{:S(2)}, u32[]{:S(2)}) collective-permute-start(bf16[288,128]{1,0:T(8,128)(2,1)S(1)} %get-tuple-element.51), channel_id=1, source_target_pairs={{0,8},{1,9},{2,10},{3,11},{4,12},{5,13},{6,14},{7,15},{8,0},{9,1},... | collective-permute-start | bytes 221192 | tf_op jit(solution)/shard_map/ppermute | solution.py:31
  79.2 11.1 %collective-permute-start.21 = (bf16[288,128]{1,0:T(8,128)(2,1)S(1)}, bf16[288,128]{1,0:T(8,128)(2,1)S(1)}, u32[]{:S(2)}, u32[]{:S(2)}) collective-permute-start(bf16[288,128]{1,0:T(8,128)(2,1)S(1)} %get-tuple-element.52), channel_id=1, source_target_pairs={{0,12},{1,13},{2,14},{3,15},{4,8},{5,9},{6,10},{7,11},{8,4},{9,5},... | collective-permute-start | bytes 221192 | tf_op jit(solution)/shard_map/ppermute | solution.py:31
  84.7 7.4 %collective-permute-start.16 = (bf16[288,128]{1,0:T(8,128)(2,1)S(1)}, bf16[288,128]{1,0:T(8,128)(2,1)S(1)}, u32[]{:S(2)}, u32[]{:S(2)}) collective-permute-start(bf16[288,128]{1,0:T(8,128)(2,1)S(1)} %get-tuple-element.46), channel_id=1, source_target_pairs={{0,4},{1,5},{2,6},{3,7},{4,0},{5,1},{6,2},{7,3},{8,12},{9,13},{10,... | collective-permute-start | bytes 221192 | tf_op jit(solution)/shard_map/ppermute | solution.py:31
  85.5 6.9 %collective-permute-start.17 = (bf16[288,128]{1,0:T(8,128)(2,1)S(1)}, bf16[288,128]{1,0:T(8,128)(2,1)S(1)}, u32[]{:S(2)}, u32[]{:S(2)}) collective-permute-start(bf16[288,128]{1,0:T(8,128)(2,1)S(1)} %get-tuple-element.47), channel_id=1, source_target_pairs={{0,8},{1,9},{2,10},{3,11},{4,12},{5,13},{6,14},{7,15},{8,0},{9,1},... | collective-permute-start | bytes 221192 | tf_op jit(solution)/shard_map/ppermute | solution.py:31
  87.7 2.6 %copy-start.2 = (bf16[576,1152]{1,0:T(8,128)(2,1)S(1)}, bf16[576,1152]{1,0:T(8,128)(2,1)}, u32[]{:S(2)}) copy-start(bf16[576,1152]{1,0:T(8,128)(2,1)} %weight_ref.3) | copy-start | bytes 3981316
  87.7 6.3 %collective-permute-start.18 = (bf16[288,128]{1,0:T(8,128)(2,1)S(1)}, bf16[288,128]{1,0:T(8,128)(2,1)S(1)}, u32[]{:S(2)}, u32[]{:S(2)}) collective-permute-start(bf16[288,128]{1,0:T(8,128)(2,1)S(1)} %get-tuple-element.48), channel_id=1, source_target_pairs={{0,12},{1,13},{2,14},{3,15},{4,8},{5,9},{6,10},{7,11},{8,4},{9,5},... | collective-permute-start | bytes 221192 | tf_op jit(solution)/shard_map/ppermute | solution.py:31

commit v6 on v5

--- a/solution.py
+++ b/solution.py
@@ -16,7 +16,7 @@
 STRIP = 16
 PAIR_GROUPS = ((0,), (1,), (2, 3))
 EMIT = (False, True, True)
-HALVES = 2
+NEAR_GROUPS = ((0,), (1,), (2,), (3,))
 STAGING_FLOPS = 4 * 10**9
 
 
@@ -81,8 +81,7 @@
     )(*operands)
 
 
-def chunk_kernel(kv_ref, *refs, tiles):
-    out_refs, sems = refs[:-1], refs[-1]
+def tile_copies(kv_ref, out_refs, tiles, sems):
     copies = []
     for chunk, ref in zip(tiles, out_refs):
         for at, tile in enumerate(chunk):
@@ -93,57 +92,75 @@
                     sems.at[len(copies)],
                 )
             )
-            copies[-1].start()
+    return copies
+
+
+def first_kernel(kv_ref, out_ref, sems, *, tiles):
+    copies = tile_copies(kv_ref, [out_ref], tiles, sems)
+    for copy in copies:
+        copy.start()
     for copy in copies:
         copy.wait()
 
 
-def stage_chunks(stale_kv, tiles):
-    rows = stale_kv.shape[0]
+def stage_first(stale_kv, tiles):
     return pl.pallas_call(
-        functools.partial(chunk_kernel, tiles=tiles),
-        out_shape=[pltpu.VMEM((rows, len(chunk) * LANES), bf16) for chunk in tiles],
+        functools.partial(first_kernel, tiles=[tiles]),
+        out_shape=pltpu.VMEM((stale_kv.shape[0], len(tiles) * LANES), bf16),
         in_specs=[pl.BlockSpec(memory_space=pltpu.HBM)],
-        out_specs=vmem_specs(len(tiles)),
-        scratch_shapes=[pltpu.SemaphoreType.DMA((sum(len(chunk) for chunk in tiles),))],
+        out_specs=pl.BlockSpec(memory_space=pltpu.VMEM),
+        scratch_shapes=[pltpu.SemaphoreType.DMA((len(tiles),))],
         compiler_params=pltpu.CompilerParams(vmem_limit_bytes=2**20),
-        name="chunks",
+        name="first",
     )(pltpu.with_memory_space_constraint(stale_kv, pltpu.HBM))
 
 
-def piece_kernel(slot_ref, tokens_ref, *refs, frames):
-    out_refs, sems = refs[:-1], refs[-1]
+def piece_kernel(slot_ref, tokens_ref, kv_ref, *refs, frames, tiles):
+    out_refs, piece_sems, tile_sems = refs[:-2], refs[-2], refs[-1]
     piece = tokens_ref.shape[0] // frames
     copies = []
     for step in range(frames):
         row = partner_slot(slot_ref[0], step, frames) * piece
         copies.append(
             pltpu.make_async_copy(
-                tokens_ref.at[pl.ds(row, piece), :], out_refs[step], sems.at[step]
+                tokens_ref.at[pl.ds(row, piece), :], out_refs[step], piece_sems.at[step]
             )
         )
-        copies[-1].start()
+    copies += tile_copies(kv_ref, out_refs[frames:], tiles, tile_sems)
+    for copy in copies:
+        copy.start()
     for copy in copies:
         copy.wait()
 
 
-def stage_pieces(slot, tokens, frames):
+def stage_pieces(slot, tokens, stale_kv, tiles, frames):
     rows, feature_width = tokens.shape
-    return pl.pallas_call(
-        functools.partial(piece_kernel, frames=frames),
-        out_shape=[pltpu.VMEM((rows // frames, feature_width), bf16) for _ in range(frames)],
+    shapes = [(rows // frames, feature_width) for _ in range(frames)]
+    shapes += [(rows, len(chunk) * LANES) for chunk in tiles]
+    outs = pl.pallas_call(
+        functools.partial(piece_kernel, frames=frames, tiles=tiles),
+        out_shape=[pltpu.VMEM(shape, bf16) for shape in shapes],
         in_specs=[
             pl.BlockSpec(memory_space=pltpu.SMEM),
             pl.BlockSpec(memory_space=pltpu.HBM),
+            pl.BlockSpec(memory_space=pltpu.HBM),
         ],
-        out_specs=vmem_specs(frames),
-        scratch_shapes=[pltpu.SemaphoreType.DMA((frames,))],
+        out_specs=vmem_specs(len(shapes)),
+        scratch_shapes=[
+            pltpu.SemaphoreType.DMA((frames,)),
+            pltpu.SemaphoreType.DMA((sum(len(chunk) for chunk in tiles),)),
+        ],
         compiler_params=pltpu.CompilerParams(vmem_limit_bytes=2**20),
         cost_estimate=pl.CostEstimate(
             flops=STAGING_FLOPS, bytes_accessed=4 * tokens.size, transcendentals=0
         ),
         name="pieces",
-    )(slot, pltpu.with_memory_space_constraint(tokens, pltpu.HBM))
+    )(
+        slot,
+        pltpu.with_memory_space_constraint(tokens, pltpu.HBM),
+        pltpu.with_memory_space_constraint(stale_kv, pltpu.HBM),
+    )
+    return outs[:frames], outs[frames:]
 
 
 def projection_kernel(slot_ref, time_ref, order_ref, weight_ref, *refs, frames, width):
@@ -257,7 +274,7 @@
 def group_tiles(width, head_dim):
     plan = pair_plan(width, head_dim)
     seen, groups = set(), []
-    for group in PAIR_GROUPS:
+    for group in NEAR_GROUPS:
         need = []
         for pair in group:
             key_tile, _, value_tile, _ = plan[pair]
@@ -391,6 +408,11 @@
     finish(len(tasks) - 1, total)
 
 
+def near_needed(number):
+    last = PAIR_GROUPS[number][-1]
+    return next(n for n, group in enumerate(NEAR_GROUPS) if last in group) + 1
+
+
 def tile_flow(width, head_dim):
     plan = pair_plan(width, head_dim)
     flow, held = [], ()
@@ -414,6 +436,17 @@
     return tuple(emitted_columns(emitted, width) for _, emitted, _ in flow if emitted)
 
 
+def target_parts(rows):
+    return row_parts(len(PAIR_GROUPS) - 1, rows)
+
+
+def output_parts(rows, piece):
+    parts = [part_pieces(chunks, piece) for chunks in target_parts(rows)]
+    if len(parts) < 2:
+        return parts
+    return [[s for part in parts[:1] + parts[2:] for s in part], parts[1]]
+
+
 def part_pieces(chunks, piece):
     per = QUERY_ROWS // piece
     return [chunk * per + sub for chunk in chunks for sub in range(per)]
@@ -431,7 +464,8 @@
 ):
     group = PAIR_GROUPS[number]
     held, emitted, kept = tile_flow(width, head_dim)[number]
-    tiles = tuple(group_tiles(width, head_dim)[: number + 1])
+    arrived = near_needed(number)
+    tiles = tuple(group_tiles(width, head_dim)[:arrived])
     rows = query.shape[0]
     chunks = row_parts(number, rows)[part]
     shapes = []
@@ -441,7 +475,7 @@
         shapes += [((stack_rows(rows // frames, columns), LANES), bf16) for _ in range(count)]
     if kept:
         shapes.append(((rows, len(kept) * LANES), bf16))
-    operands = [query, own_kv, peer_kv, *near[: number + 1], *far[: number + 1]]
+    operands = [query, own_kv, peer_kv, *near[:arrived], *far[:arrived]]
     if held:
         operands.append(carry)
     keys = 4 * rows
@@ -495,23 +529,26 @@
     return tokens, mixed
 
 
-def temporal_kernel(*refs, frames, head_dim, columns, first, piece):
+def temporal_in_kernel(*refs, frames, columns):
     groups = len(columns)
     tokens_refs = refs[:frames]
     mixed_refs = refs[frames : frames + frames * groups]
-    position = frames + frames * groups
-    out_weight, qkv_weight, modulation_ref, place_ref = refs[position : position + 4]
-    out_refs = refs[position + 4 : position + 4 + frames]
-    query_ref, kv_ref = refs[position + 4 + frames :]
+    out_weight, qkv_weight, modulation_ref, place_ref, query_ref, kv_ref = refs[
+        frames + frames * groups :
+    ]
     width = out_weight.shape[0]
-    tokens, mixed = joined_rows(tokens_refs, mixed_refs, columns, first, piece)
+    piece = tokens_refs[0].shape[0]
+    tokens, mixed = joined_rows(tokens_refs, mixed_refs, columns, 0, piece)
     after = tokens + modulation_ref[2:3, :] * jnp.dot(
         mixed, out_weight[...], preferred_element_type=f32
     )
-    normal = normalize(after) * (1.0 + modulation_ref[4:5, :]) + modulation_ref[3:4, :]
+    normal = normalize(after) * (1.0 + modulation_ref[4:5, :])
     inputs = jnp.concatenate(
         [
-            (normal[frame * piece : (frame + 1) * piece] + place_ref[frame : frame + 1, :]).astype(bf16)
+            (
+                normal[frame * piece : (frame + 1) * piece]
+                + (modulation_ref[3:4, :] + place_ref[frame : frame + 1, :])
+            ).astype(bf16)
             for frame in range(frames)
         ],
         axis=0,
@@ -523,28 +560,46 @@
         inputs, qkv_weight[width:, :], NT, preferred_element_type=f32
     ).astype(bf16)
 
+
+def temporal_in(tokens, mixed, columns, weights, modulation, places):
+    frames = len(tokens)
+    width, feature_width = weights[0].shape
+    padded = -(-width // LANES) * LANES
+    rows = frames * tokens[0].shape[0]
+    return on_chip_call(
+        functools.partial(temporal_in_kernel, frames=frames, columns=columns),
+        [*tokens, *[part for frame in mixed for part in frame], *weights, modulation, places],
+        [((rows, padded), bf16), ((rows, 2 * width), bf16)],
+        2 * rows * feature_width * width * 4,
+        8,
+    )
+
+
+def temporal_kernel(query_ref, kv_ref, *out_refs, frames, head_dim, targets):
+    piece = query_ref.shape[0] // frames
+    width = kv_ref.shape[1] // 2
     scale = softmax_scale(head_dim)
     step = max(16, min(piece, LANES // frames))
-    block = frames * step
-    row_at = lax.broadcasted_iota(jnp.int32, (2 * block, block), 0) % step
-    column_at = lax.broadcasted_iota(jnp.int32, (2 * block, block), 1) % step
+    block = len(targets) * step
+    row_at = lax.broadcasted_iota(jnp.int32, (2 * block, frames * step), 0) % step
+    column_at = lax.broadcasted_iota(jnp.int32, (2 * block, frames * step), 1) % step
     same = row_at == column_at
     plan = pair_plan(width, head_dim)
 
-    def window(ref, start, tile):
+    def window(ref, members, start, tile):
         return jnp.concatenate(
             [
                 ref[
                     frame * piece + start : frame * piece + start + step,
                     tile * LANES : (tile + 2) * LANES,
                 ]
-                for frame in range(frames)
+                for frame in members
             ],
             axis=0,
         )
 
     def score(start, tile, lane):
-        queries = window(query_ref, start, tile)
+        queries = window(query_ref, targets, start, tile)
         stacked = jnp.concatenate(
             [
                 queries * column_mask(lane, head_dim, bf16),
@@ -553,7 +608,7 @@
             axis=0,
         )
         scores = lax.dot_general(
-            stacked, window(kv_ref, start, tile), NT, preferred_element_type=f32
+            stacked, window(kv_ref, range(frames), start, tile), NT, preferred_element_type=f32
         )
         return jnp.where(same, scores * scale, -jnp.inf)
 
@@ -566,7 +621,9 @@
     scores = [score(start, tile, lane) for start, tile, lane, _, _ in tasks]
     weights = [weigh(value) for value in scores]
     mixed_pairs = [
-        jnp.dot(value, window(kv_ref, start, value_tile), preferred_element_type=f32)
+        jnp.dot(
+            value, window(kv_ref, range(frames), start, value_tile), preferred_element_type=f32
+        )
         for value, (start, _, _, value_tile, _) in zip(weights, tasks)
     ]
     parts = {start: {} for start in starts}
@@ -579,9 +636,9 @@
         for side in range(2):
             half = joined[:, side * LANES : (side + 1) * LANES]
             have[tile + side] = have[tile + side] + half if tile + side in have else half
-    for frame in range(frames):
-        cut = slice(frame * step, (frame + 1) * step)
-        out_refs[frame][...] = stack(
+    for number in range(len(targets)):
+        cut = slice(number * step, (number + 1) * step)
+        out_refs[number][...] = stack(
             [
                 jnp.concatenate([parts[start][tile][cut] for start in starts], axis=0)
                 for tile in sorted(parts[0])
@@ -590,34 +647,17 @@
         )
 
 
-def temporal(tokens, mixed, columns, weights, modulation, places, head_dim, first, piece):
-    frames = len(tokens)
-    spatial_out, temporal_qkv = weights
-    width, feature_width = spatial_out.shape
-    padded = -(-width // LANES) * LANES
-    rows = frames * piece
+def temporal(query, kv, frames, head_dim, targets):
+    width = kv.shape[1] // 2
+    rows = query.shape[0]
+    shape = (stack_rows(rows // frames, width), LANES)
     return on_chip_call(
-        functools.partial(
-            temporal_kernel,
-            frames=frames,
-            head_dim=head_dim,
-            columns=columns,
-            first=first,
-            piece=piece,
-        ),
-        [
-            *tokens,
-            *[part for frame in mixed for part in frame],
-            spatial_out,
-            temporal_qkv,
-            modulation,
-            places,
-        ],
-        [((stack_rows(piece, width), LANES), bf16) for _ in range(frames)],
-        2 * rows * feature_width * width * 5,
-        6,
+        functools.partial(temporal_kernel, frames=frames, head_dim=head_dim, targets=targets),
+        [query, kv],
+        [(shape, bf16) for _ in targets],
+        2 * rows * 128 * 256 * 8,
+        4,
         rows * 128 * 8,
-        [pltpu.VMEM((rows, padded), bf16), pltpu.VMEM((rows, 2 * width), bf16)],
     )
 
 
@@ -644,31 +684,28 @@
     )[0]
 
 
-def output_kernel(slot_ref, after_ref, weight_ref, modulation_ref, *refs, frames, number):
-    parts = refs[:frames]
+def output_kernel(slot_ref, after_ref, weight_ref, modulation_ref, *refs, frames, members):
+    parts = refs[: len(members)]
     out_ref, stage_ref, sems = refs[-3:]
     piece = after_ref.shape[0] // frames
-    half = piece // HALVES
-    first = number * half
     width = weight_ref.shape[0]
     mixed = jnp.concatenate(
-        [unstack(ref[...].astype(f32), half, width, 0, half).astype(bf16) for ref in parts], axis=0
+        [unstack(ref[...].astype(f32), piece, width, 0, piece).astype(bf16) for ref in parts], axis=0
     )
     after = jnp.concatenate(
-        [after_ref[frame * piece + first : frame * piece + first + half, :] for frame in range(frames)],
-        axis=0,
+        [after_ref[frame * piece : (frame + 1) * piece, :] for frame in members], axis=0
     )
     stage_ref[...] = after + modulation_ref[5:6, :] * jnp.dot(
         mixed, weight_ref[...], preferred_element_type=f32
     )
     copies = []
-    for frame in range(frames):
-        row = partner_slot(slot_ref[0], frame, frames) * piece + first
+    for number, frame in enumerate(members):
+        row = partner_slot(slot_ref[0], frame, frames) * piece
         copies.append(
             pltpu.make_async_copy(
-                stage_ref.at[frame * half : (frame + 1) * half, :],
-                out_ref.at[pl.ds(row, half), :],
-                sems.at[frame],
+                stage_ref.at[number * piece : (number + 1) * piece, :],
+                out_ref.at[pl.ds(row, piece), :],
+                sems.at[number],
             )
         )
         copies[-1].start()
@@ -676,8 +713,7 @@
         copy.wait()
 
 
-def output(number, slot, after, weight, modulation, parts, result):
-    frames = len(parts)
+def output(slot, after, weight, modulation, parts, members, frames, result):
     rows, feature_width = after.shape
     operands = [after, weight, modulation, *parts]
     specs = [pl.BlockSpec(memory_space=pltpu.SMEM), *vmem_specs(len(operands))]
@@ -688,16 +724,16 @@
         specs.append(pl.BlockSpec(memory_space=pltpu.HBM))
         operands.append(result)
     return pl.pallas_call(
-        functools.partial(output_kernel, frames=frames, number=number),
+        functools.partial(output_kernel, frames=frames, members=members),
         out_shape=jax.ShapeDtypeStruct((rows, feature_width), f32),
         in_specs=specs,
         out_specs=pl.BlockSpec(memory_space=pltpu.HBM),
         scratch_shapes=[
-            pltpu.VMEM((rows // HALVES, feature_width), f32),
-            pltpu.SemaphoreType.DMA((frames,)),
+            pltpu.VMEM((rows // frames * len(members), feature_width), f32),
+            pltpu.SemaphoreType.DMA((len(members),)),
         ],
         input_output_aliases=aliases,
-        compiler_params=pltpu.CompilerParams(vmem_limit_bytes=4 * 2**20),
+        compiler_params=pltpu.CompilerParams(vmem_limit_bytes=6 * 2**20),
     )(slot, *operands)
 
 
@@ -733,15 +769,17 @@
     def behind(step):
         return lambda device: source_slot(device // 4, step, frames) * 4 + device % 4
 
+    slot_word = slot.astype(jnp.int32)[None]
+    tiles = group_tiles(width, head_dim)
+    chunks = [stage_first(stale_kv, tiles[0])]
+    pieces, others = stage_pieces(slot_word, tokens, stale_kv, tiles[1:], frames)
     near, far = [], []
-    for chunk in stage_chunks(stale_kv, group_tiles(width, head_dim)):
+    for chunk in [*chunks, *others]:
         near.append(permute(chunk, other_chip))
         far.append(permute(near[-1], other_core))
     peer_kv = permute(stale_kv, other_core)
 
-    slot_word = slot.astype(jnp.int32)[None]
     spatial_weight = jnp.swapaxes(spatial_qkv, 1, 2).reshape(3 * width, feature_width)
-    pieces = stage_pieces(slot_word, tokens, frames)
     there = [pieces[0]]
     there += [permute(pieces[s], ahead(s)) for s in range(1, frames)]
 
@@ -773,14 +811,17 @@
     columns = group_columns(width, head_dim)
     after = after_spatial(pieces, local, columns, spatial_out, modulation)
     weights = (spatial_out, jnp.swapaxes(temporal_qkv, 1, 2).reshape(3 * width, feature_width))
-    half = piece // HALVES
-    back = []
-    for h in range(HALVES):
-        outs = temporal(there, sent, columns, weights, modulation, places, head_dim, h * half, half)
-        back.append([out if s == 0 else permute(out, behind(s)) for s, out in enumerate(outs)])
+    temporal_query, temporal_kv = temporal_in(there, sent, columns, weights, modulation, places)
+    back = {}
+    for chunks in target_parts(rows):
+        targets = part_pieces(chunks, piece)
+        outs = temporal(temporal_query, temporal_kv, frames, head_dim, targets)
+        for s, out in zip(targets, outs):
+            back[s] = out if s == 0 else permute(out, behind(s))
     result = None
-    for h in range(HALVES):
-        result = output(h, slot_word, after, temporal_out, modulation, back[h], result)
+    for members in output_parts(rows, piece):
+        parts = [back[s] for s in members]
+        result = output(slot_word, after, temporal_out, modulation, parts, members, frames, result)
     return result
 
 

time: 96.1 us -> 95.7 us (level)
  starting transfers between devices: 30.8 us -> 28.4 us
  waiting for transfers between devices: 28.8 us -> 30 us
    ppermute x22 -> x21, starting transfers between devices: 30.8 us -> 28.4 us  [permute(): lax.ppermute(value, 'patch', [(source, target(source)) for source in rang...]
    ppermute x22 -> x21, waiting for transfers between devices: 28.8 us -> 30 us  [permute(): lax.ppermute(value, 'patch', [(source, target(source)) for source in rang...]
    pallas_call x9 -> x12, Pallas kernels: 25 us -> 25.6 us  [on_chip_call(): pl.pallas_call(kernel, out_shape=[pltpu.VMEM(shape, dtype) for shape, dty...]
  transfers between devices with their start and end apart: 22 -> 21, of which waited for: 8 -> 7; matrix products, arithmetic and copies ran while one was open for 0% -> 0% of each run, Pallas kernels for 31% -> 28%
where the time goes in v6:
time: 95.7 us; the launch traced here: 95.5 us
  Pallas kernels  36 us (38%)
  waiting for transfers between devices  30 us (31%)
  starting transfers between devices  28.4 us (30%)
  between operations  1.06 us (1%)
    ppermute x21, waiting for transfers between devices, permute(): lax.ppermute(value, 'patch', [(source, target(source)) for source in rang...  30 us
    ppermute x21, starting transfers between devices, permute(): lax.ppermute(value, 'patch', [(source, target(source)) for source in rang...  28.4 us
    pallas_call x12, Pallas kernels, on_chip_call(): pl.pallas_call(kernel, out_shape=[pltpu.VMEM(shape, dtype) for shape, dty...  25.6 us
    pallas_call x1, Pallas kernels, projections(): pl.pallas_call(functools.partial(projection_kernel, frames=frames, width=...  3.95 us
    pallas_call x2, Pallas kernels, output(): pl.pallas_call(functools.partial(output_kernel, frames=frames, members=me...  3.44 us
  transfers between devices with their start and end apart: 21, of which 7 were waited for; matrix products, arithmetic and copies ran while one was open for 0% of the time, Pallas kernels for 28%

profile of v6, /device:TPU:0, one launch (start us, length us, event | category | flops | bytes accessed | tf_op | source)
XLA Modules:
  0.0 95.5 jit_solution(3831527394245042095)
XLA Ops:
  0.0 1.2 %first.1 = bf16[512,512]{1,0:T(8,128)(2,1)S(1)} custom-call(bf16[512,1152]{1,0:T(8,128)(2,1)} %kv_ref.3), custom_call_target="tpu_custom_call" | custom-call | tf_op jit(solution)/shard_map/first/pallas_call | solution.py:107
  1.2 3.1 %collective-permute-start.1 = (bf16[512,512]{1,0:T(8,128)(2,1)S(1)}, bf16[512,512]{1,0:T(8,128)(2,1)S(1)}, u32[]{:S(2)}, u32[]{:S(2)}) collective-permute-start(bf16[512,512]{1,0:T(8,128)(2,1)S(1)} %first.1), channel_id=1, source_target_pairs={{0,2},{1,3},{2,0},{3,1},{4,6},{5,7},{6,4},{7,5},{8,10},{9,11},{10,... | collective-permute-start | bytes 1572872 | tf_op jit(solution)/shard_map/ppermute | solution.py:31
  4.3 0.0 collective-permute-start
  4.3 11.9 %collective-permute-done.1.refs_3_ = bf16[512,512]{1,0:T(8,128)(2,1)S(1)} collective-permute-done((bf16[512,512]{1,0:T(8,128)(2,1)S(1)}, bf16[512,512]{1,0:T(8,128)(2,1)S(1)}, u32[]{:S(2)}, u32[]{:S(2)}) %collective-permute-start.1) | collective-permute-done | bytes 524320 | tf_op jit(solution)/shard_map/ppermute | solution.py:31
  16.2 0.0 copy-start.6
  16.3 0.0 copy-start.7
  16.3 1.7 %pieces.1 = (bf16[128,1152]{1,0:T(8,128)(2,1)S(1)}, bf16[128,1152]{1,0:T(8,128)(2,1)S(1)}, bf16[128,1152]{1,0:T(8,128)(2,1)S(1)}, bf16[128,1152]{1,0:T(8,128)(2,...) custom-call(s32[1]{0:T(128)} %bitcast.slot_ref, ...), custom_call_target="tpu_custom_call" | custom-call | flops 4000000000 | bytes 2359296 | tf_op jit(solution)/shard_map/pieces/pallas_call | solution.py:140
  18.0 1.8 %collective-permute-start.2 = (bf16[512,256]{1,0:T(8,128)(2,1)S(1)}, bf16[512,256]{1,0:T(8,128)(2,1)S(1)}, u32[]{:S(2)}, u32[]{:S(2)}) collective-permute-start(bf16[512,256]{1,0:T(8,128)(2,1)S(1)} %get-tuple-element.29), channel_id=1, source_target_pairs={{0,2},{1,3},{2,0},{3,1},{4,6},{5,7},{6,4},{7,5},{8,10},{9,11},{10,... | collective-permute-start | bytes 786440 | tf_op jit(solution)/shard_map/ppermute | solution.py:31
  19.8 0.3 collective-permute-start.5
  20.1 1.8 %collective-permute-start.9 = (bf16[128,1152]{1,0:T(8,128)(2,1)S(1)}, bf16[128,1152]{1,0:T(8,128)(2,1)S(1)}, u32[]{:S(2)}, u32[]{:S(2)}) collective-permute-start(bf16[128,1152]{1,0:T(8,128)(2,1)S(1)} %get-tuple-element.24.refs_4_.refs_1_), channel_id=1, source_target_pairs={{0,4},{1,5},{2,6},{3,7},{4,0},{5,1},{6,2},{7,3},{8,12},{9,13},{10,... | collective-permute-start | bytes 884744 | tf_op jit(solution)/shard_map/ppermute | solution.py:31
  22.5 4.7 %collective-permute-done.2.refs_4_ = bf16[512,256]{1,0:T(8,128)(2,1)S(1)} collective-permute-done((bf16[512,256]{1,0:T(8,128)(2,1)S(1)}, bf16[512,256]{1,0:T(8,128)(2,1)S(1)}, u32[]{:S(2)}, u32[]{:S(2)}) %collective-permute-start.2) | collective-permute-done | bytes 262176 | tf_op jit(solution)/shard_map/ppermute | solution.py:31
  27.2 0.0 collective-permute-start.4
  27.3 3.9 %projections.1 = (bf16[512,640]{1,0:T(8,128)(2,1)S(1)}, bf16[512,1152]{1,0:T(8,128)(2,1)S(1)}, f32[6,1152]{1,0:T(8,128)S(1)}, f32[4,1152]{1,0:T(4,128)S(1)}) custom-call(s32[1]{0:T(128)} %bitcast.slot_ref, s32[1]{0:T(128)S(6)} %copy.14.time_ref, s32[4]{0:T(128)S(1)} %copy-done.6, bf16[1728,1152]{1,0:T(8,128)(2,1)S(1)} %bitcast.7, f32[1,576]{1,0:T(1,128)S(1)} %copy-done.7, ...), custom_call_target="tpu_custom_call" | custom-call | flops 2038431744 | bytes 3981312 | tf_op jit(solution)/shard_map/projections/pallas_call | solution.py:207
  31.2 1.1 %collective-permute-done.5.refs_5_ = bf16[512,256]{1,0:T(8,128)(2,1)S(1)} collective-permute-done((bf16[512,256]{1,0:T(8,128)(2,1)S(1)}, bf16[512,256]{1,0:T(8,128)(2,1)S(1)}, u32[]{:S(2)}, u32[]{:S(2)}) %collective-permute-start.5) | collective-permute-done | bytes 262176 | tf_op jit(solution)/shard_map/ppermute | solution.py:31
  32.4 2.8 %collective-permute-start.10 = (bf16[128,1152]{1,0:T(8,128)(2,1)S(1)}, bf16[128,1152]{1,0:T(8,128)(2,1)S(1)}, u32[]{:S(2)}, u32[]{:S(2)}) collective-permute-start(bf16[128,1152]{1,0:T(8,128)(2,1)S(1)} %get-tuple-element.25.refs_5_.refs_2_), channel_id=1, source_target_pairs={{0,8},{1,9},{2,10},{3,11},{4,12},{5,13},{6,14},{7,15},{8,0},{9,1},... | collective-permute-start | bytes 884744 | tf_op jit(solution)/shard_map/ppermute | solution.py:31
  35.2 1.5 %collective-permute-start.6 = (bf16[512,128]{1,0:T(8,128)(2,1)S(1)}, bf16[512,128]{1,0:T(8,128)(2,1)S(1)}, u32[]{:S(2)}, u32[]{:S(2)}) collective-permute-start(bf16[512,128]{1,0:T(8,128)(2,1)S(1)} %get-tuple-element.32), channel_id=1, source_target_pairs={{0,2},{1,3},{2,0},{3,1},{4,6},{5,7},{6,4},{7,5},{8,10},{9,11},{10,... | collective-permute-start | bytes 393224 | tf_op jit(solution)/shard_map/ppermute | solution.py:31
  36.7 3.5 %shard_map.109.refs_7_ = bf16[512,256]{1,0:T(8,128)(2,1)S(1)} custom-call(bf16[512,640]{1,0:T(8,128)(2,1)S(1)} %get-tuple-element.27.refs_0_, bf16[512,1152]{1,0:T(8,128)(2,1)S(1)} %get-tuple-element.28.refs_1_, bf16[512,1152]{1,0:T(8,128)(2,1)S(1)} %collective-permute-done.refs_2_, bf16[512,512]{1,0:T(8,128)(2,1)S(1)} %collective-permute-done.1.refs_3_, ...), custom_call_target="tpu_custom_call" | custom-call | flops 2147483648 | bytes 4063232 | tf_op jit(solution)/shard_map/pallas_call | solution.py:69
  40.3 1.4 %collective-permute-start.11 = (bf16[128,1152]{1,0:T(8,128)(2,1)S(1)}, bf16[128,1152]{1,0:T(8,128)(2,1)S(1)}, u32[]{:S(2)}, u32[]{:S(2)}) collective-permute-start(bf16[128,1152]{1,0:T(8,128)(2,1)S(1)} %get-tuple-element.26.refs_6_.refs_3_), channel_id=1, source_target_pairs={{0,12},{1,13},{2,14},{3,15},{4,8},{5,9},{6,10},{7,11},{8,4},{9,5},... | collective-permute-start | bytes 884744 | tf_op jit(solution)/shard_map/ppermute | solution.py:31
  41.7 0.0 collective-permute-done.4.refs_6_.refs_8_
  41.7 0.2 collective-permute-start.8
  41.9 3.5 %shard_map.110 = (bf16[256,128]{1,0:T(8,128)(2,1)S(1)}, bf16[256,128]{1,0:T(8,128)(2,1)S(1)}, bf16[256,128]{1,0:T(8,128)(2,1)S(1)}, bf16[256,128]{1,0:T(8,128)(2,1)S(1)}, bf16[512,128]{1,0:T(8,128)(2,1)S(1)}) custom-call(bf16[512,640]{1,0:T(8,128)(2,1)S(1)} %get-tuple-element.27.refs_0_, bf16[512,1152]{1,0:T(8,128)(2,1)S(1)} %get-tuple-element.28.refs_1_, ...), custom_call_target="tpu_custom_call" | custom-call | flops 2147483648 | bytes 4849664 | tf_op jit(solution)/shard_map/pallas_call | solution.py:69
  45.4 0.7 collective-permute-start.12
  46.1 2.3 %shard_map.112.refs_7_ = bf16[320,128]{1,0:T(8,128)(2,1)S(1)} custom-call(bf16[512,640]{1,0:T(8,128)(2,1)S(1)} %get-tuple-element.27.refs_0_, bf16[512,1152]{1,0:T(8,128)(2,1)S(1)} %get-tuple-element.28.refs_1_, bf16[512,1152]{1,0:T(8,128)(2,1)S(1)} %collective-permute-done.refs_2_, bf16[512,512]{1,0:T(8,128)(2,1)S(1)} %collective-permute-done.1.refs_3_, ...), custom_call_target="tpu_custom_call" | custom-call | flops 1073741824 | bytes 5505024 | tf_op jit(solution)/shard_map/pallas_call | solution.py:69
  48.4 1.5 %collective-permute-start.13 = (bf16[320,128]{1,0:T(8,128)(2,1)S(1)}, bf16[320,128]{1,0:T(8,128)(2,1)S(1)}, u32[]{:S(2)}, u32[]{:S(2)}) collective-permute-start(bf16[320,128]{1,0:T(8,128)(2,1)S(1)} %shard_map.112.refs_7_), channel_id=1, source_target_pairs={{0,4},{1,5},{2,6},{3,7},{4,0},{5,1},{6,2},{7,3},{8,12},{9,13},{10,... | collective-permute-start | bytes 245768 | tf_op jit(solution)/shard_map/ppermute | solution.py:31
  49.9 2.1 %shard_map.113.refs_9_ = bf16[320,128]{1,0:T(8,128)(2,1)S(1)} custom-call(bf16[512,640]{1,0:T(8,128)(2,1)S(1)} %get-tuple-element.27.refs_0_, bf16[512,1152]{1,0:T(8,128)(2,1)S(1)} %get-tuple-element.28.refs_1_, bf16[512,1152]{1,0:T(8,128)(2,1)S(1)} %collective-permute-done.refs_2_, bf16[512,512]{1,0:T(8,128)(2,1)S(1)} %collective-permute-done.1.refs_3_, ...), custom_call_target="tpu_custom_call" | custom-call | flops 1073741824 | bytes 5505024 | tf_op jit(solution)/shard_map/pallas_call | solution.py:69
  52.1 2.1 %shard_map.114.refs_11_ = bf16[320,128]{1,0:T(8,128)(2,1)S(1)} custom-call(bf16[512,640]{1,0:T(8,128)(2,1)S(1)} %get-tuple-element.27.refs_0_, bf16[512,1152]{1,0:T(8,128)(2,1)S(1)} %get-tuple-element.28.refs_1_, bf16[512,1152]{1,0:T(8,128)(2,1)S(1)} %collective-permute-done.refs_2_, bf16[512,512]{1,0:T(8,128)(2,1)S(1)} %collective-permute-done.1.refs_3_, ...), custom_call_target="tpu_custom_call" | custom-call | flops 1073741824 | bytes 5505024 | tf_op jit(solution)/shard_map/pallas_call | solution.py:69
  54.2 0.0 collective-permute-done.9.refs_1_
  54.2 1.8 %collective-permute-start.14 = (bf16[256,128]{1,0:T(8,128)(2,1)S(1)}, bf16[256,128]{1,0:T(8,128)(2,1)S(1)}, u32[]{:S(2)}, u32[]{:S(2)}) collective-permute-start(bf16[256,128]{1,0:T(8,128)(2,1)S(1)} %get-tuple-element.35.refs_8_), channel_id=1, source_target_pairs={{0,8},{1,9},{2,10},{3,11},{4,12},{5,13},{6,14},{7,15},{8,0},{9,1},... | collective-permute-start | bytes 196616 | tf_op jit(solution)/shard_map/ppermute | solution.py:31
  56.0 1.2 %collective-permute-start.15 = (bf16[320,128]{1,0:T(8,128)(2,1)S(1)}, bf16[320,128]{1,0:T(8,128)(2,1)S(1)}, u32[]{:S(2)}, u32[]{:S(2)}) collective-permute-start(bf16[320,128]{1,0:T(8,128)(2,1)S(1)} %shard_map.113.refs_9_), channel_id=1, source_target_pairs={{0,8},{1,9},{2,10},{3,11},{4,12},{5,13},{6,14},{7,15},{8,0},{9,1},... | collective-permute-start | bytes 245768 | tf_op jit(solution)/shard_map/ppermute | solution.py:31
  57.2 2.5 %collective-permute-start.16 = (bf16[256,128]{1,0:T(8,128)(2,1)S(1)}, bf16[256,128]{1,0:T(8,128)(2,1)S(1)}, u32[]{:S(2)}, u32[]{:S(2)}) collective-permute-start(bf16[256,128]{1,0:T(8,128)(2,1)S(1)} %get-tuple-element.36.refs_10_), channel_id=1, source_target_pairs={{0,12},{1,13},{2,14},{3,15},{4,8},{5,9},{6,10},{7,11},{8,4},{9,5},... | collective-permute-start | bytes 196616 | tf_op jit(solution)/shard_map/ppermute | solution.py:31
  59.7 1.3 %collective-permute-start.17 = (bf16[320,128]{1,0:T(8,128)(2,1)S(1)}, bf16[320,128]{1,0:T(8,128)(2,1)S(1)}, u32[]{:S(2)}, u32[]{:S(2)}) collective-permute-start(bf16[320,128]{1,0:T(8,128)(2,1)S(1)} %shard_map.114.refs_11_), channel_id=1, source_target_pairs={{0,12},{1,13},{2,14},{3,15},{4,8},{5,9},{6,10},{7,11},{8,4},{9,5},... | collective-permute-start | bytes 245768 | tf_op jit(solution)/shard_map/ppermute | solution.py:31
  61.1 2.1 %shard_map.111.refs_5_ = bf16[320,128]{1,0:T(8,128)(2,1)S(1)} custom-call(bf16[512,640]{1,0:T(8,128)(2,1)S(1)} %get-tuple-element.27.refs_0_, bf16[512,1152]{1,0:T(8,128)(2,1)S(1)} %get-tuple-element.28.refs_1_, bf16[512,1152]{1,0:T(8,128)(2,1)S(1)} %collective-permute-done.refs_2_, bf16[512,512]{1,0:T(8,128)(2,1)S(1)} %collective-permute-done.1.refs_3_, ...), custom_call_target="tpu_custom_call" | custom-call | flops 1073741824 | bytes 5505024 | tf_op jit(solution)/shard_map/pallas_call | solution.py:69
  63.2 6.4 %collective-permute-done.14.refs_8_ = bf16[256,128]{1,0:T(8,128)(2,1)S(1)} collective-permute-done((bf16[256,128]{1,0:T(8,128)(2,1)S(1)}, bf16[256,128]{1,0:T(8,128)(2,1)S(1)}, u32[]{:S(2)}, u32[]{:S(2)}) %collective-permute-start.14) | collective-permute-done | bytes 65568 | tf_op jit(solution)/shard_map/ppermute | solution.py:31
  69.6 0.9 collective-permute-done.15.refs_9_
  70.5 4.4 %shard_map.116 = (bf16[512,640]{1,0:T(8,128)(2,1)S(1)}, bf16[512,1152]{1,0:T(8,128)(2,1)S(1)}) custom-call(bf16[128,1152]{1,0:T(8,128)(2,1)S(1)} %get-tuple-element.23.refs_3_.refs_0_, bf16[128,1152]{1,0:T(8,128)(2,1)S(1)} %collective-permute-done.9.refs_1_, bf16[128,1152]{1,0:T(8,128)(2,1)S(1)} %collective-permute-done.10.refs_2_, ...), custom_call_target="tpu_custom_call" | custom-call | flops 2717908992 | bytes 7123968 | tf_op jit(solution)/shard_map/pallas_call | solution.py:69
  74.9 1.0 %shard_map.118 = bf16[576,128]{1,0:T(8,128)(2,1)S(1)} custom-call(bf16[512,640]{1,0:T(8,128)(2,1)S(1)} %get-tuple-element.39.query_ref, bf16[512,1152]{1,0:T(8,128)(2,1)S(1)} %get-tuple-element.40.kv_ref), custom_call_target="tpu_custom_call" | custom-call | flops 268435456 | bytes 1835008 | tf_op jit(solution)/shard_map/pallas_call | solution.py:69
  75.9 1.0 %shard_map.119 = bf16[576,128]{1,0:T(8,128)(2,1)S(1)} custom-call(bf16[512,640]{1,0:T(8,128)(2,1)S(1)} %get-tuple-element.39.query_ref, bf16[512,1152]{1,0:T(8,128)(2,1)S(1)} %get-tuple-element.40.kv_ref), custom_call_target="tpu_custom_call" | custom-call | flops 268435456 | bytes 1835008 | tf_op jit(solution)/shard_map/pallas_call | solution.py:69
  76.9 3.7 %collective-permute-start.19 = (bf16[576,128]{1,0:T(8,128)(2,1)S(1)}, bf16[576,128]{1,0:T(8,128)(2,1)S(1)}, u32[]{:S(2)}, u32[]{:S(2)}) collective-permute-start(bf16[576,128]{1,0:T(8,128)(2,1)S(1)} %shard_map.118), channel_id=1, source_target_pairs={{0,12},{1,13},{2,14},{3,15},{4,8},{5,9},{6,10},{7,11},{8,4},{9,5},... | collective-permute-start | bytes 442376 | tf_op jit(solution)/shard_map/ppermute | solution.py:31
  80.7 2.7 %collective-permute-start.20 = (bf16[576,128]{1,0:T(8,128)(2,1)S(1)}, bf16[576,128]{1,0:T(8,128)(2,1)S(1)}, u32[]{:S(2)}, u32[]{:S(2)}) collective-permute-start(bf16[576,128]{1,0:T(8,128)(2,1)S(1)} %shard_map.119), channel_id=1, source_target_pairs={{0,4},{1,5},{2,6},{3,7},{4,0},{5,1},{6,2},{7,3},{8,12},{9,13},{10,... | collective-permute-start | bytes 442376 | tf_op jit(solution)/shard_map/ppermute | solution.py:31
  83.4 1.2 %shard_map.117 = bf16[576,128]{1,0:T(8,128)(2,1)S(1)} custom-call(bf16[512,640]{1,0:T(8,128)(2,1)S(1)} %get-tuple-element.39.query_ref, bf16[512,1152]{1,0:T(8,128)(2,1)S(1)} %get-tuple-element.40.kv_ref), custom_call_target="tpu_custom_call" | custom-call | flops 268435456 | bytes 1835008 | tf_op jit(solution)/shard_map/pallas_call | solution.py:69
  84.6 0.1 collective-permute-start.18
  84.7 1.2 %shard_map.115.after_ref = f32[512,1152]{1,0:T(8,128)S(1)} custom-call(bf16[128,1152]{1,0:T(8,128)(2,1)S(1)} %get-tuple-element.23.refs_3_.refs_0_, bf16[128,1152]{1,0:T(8,128)(2,1)S(1)} %get-tuple-element.24.refs_4_.refs_1_, bf16[128,1152]{1,0:T(8,128)(2,1)S(1)} %get-tuple-element.25.refs_5_.refs_2_, ...), custom_call_target="tpu_custom_call" | custom-call | flops 679477248 | bytes 3124224 | tf_op jit(solution)/shard_map/pallas_call | solution.py:69
  85.9 0.0 copy-start
  85.9 1.0 %shard_map.120.refs_2_ = bf16[576,128]{1,0:T(8,128)(2,1)S(1)} custom-call(bf16[512,640]{1,0:T(8,128)(2,1)S(1)} %get-tuple-element.39.query_ref, bf16[512,1152]{1,0:T(8,128)(2,1)S(1)} %get-tuple-element.40.kv_ref), custom_call_target="tpu_custom_call" | custom-call | flops 268435456 | bytes 1835008 | tf_op jit(solution)/shard_map/pallas_call | solution.py:69
  86.9 1.2 %collective-permute-done.20.refs_1_ = bf16[576,128]{1,0:T(8,128)(2,1)S(1)} collective-permute-done((bf16[576,128]{1,0:T(8,128)(2,1)S(1)}, bf16[576,128]{1,0:T(8,128)(2,1)S(1)}, u32[]{:S(2)}, u32[]{:S(2)}) %collective-permute-start.20) | collective-permute-done | bytes 147488 | tf_op jit(solution)/shard_map/ppermute | solution.py:31
  88.1 2.2 %shard_map.121.refs_1_ = f32[512,1152]{1,0:T(8,128)} custom-call(s32[1]{0:T(128)} %bitcast.slot_ref, f32[512,1152]{1,0:T(8,128)S(1)} %shard_map.115.after_ref, bf16[576,1152]{1,0:T(8,128)(2,1)S(1)} %copy-done, f32[6,1152]{1,0:T(8,128)S(1)} %get-tuple-element.37.refs_13_.refs_14_.modulation_ref, bf16[576,128]{1,0:T(8,128)(2,1)S(1)} %collective-permute-done.19.refs_0_, ...), custom_call_target="tpu_custom_call" | custom-call | tf_op jit(solution)/shard_map/pallas_call | solution.py:726
  90.3 3.8 %collective-permute-done.18.refs_0_ = bf16[576,128]{1,0:T(8,128)(2,1)S(1)} collective-permute-done((bf16[576,128]{1,0:T(8,128)(2,1)S(1)}, bf16[576,128]{1,0:T(8,128)(2,1)S(1)}, u32[]{:S(2)}, u32[]{:S(2)}) %collective-permute-start.18) | collective-permute-done | bytes 147488 | tf_op jit(solution)/shard_map/ppermute | solution.py:31
  94.1 1.3 %shard_map.122 = f32[512,1152]{1,0:T(8,128)} custom-call(s32[1]{0:T(128)} %bitcast.slot_ref, f32[512,1152]{1,0:T(8,128)S(1)} %shard_map.115.after_ref, bf16[576,1152]{1,0:T(8,128)(2,1)S(1)} %copy-done, f32[6,1152]{1,0:T(8,128)S(1)} %get-tuple-element.37.refs_13_.refs_14_.modulation_ref, ...), custom_call_target="tpu_custom_call", output_to_operand_aliasing={{}: (5, {})} | custom-call | tf_op jit(solution)/shard_map/pallas_call | solution.py:726
  (29 shorter events, 0.1 us)
Async XLA Ops:
  0.0 4.3 %copy-start.8 = (bf16[512,1152]{1,0:T(8,128)(2,1)S(1)}, bf16[512,1152]{1,0:T(8,128)(2,1)}, u32[]{:S(2)}) copy-start(bf16[512,1152]{1,0:T(8,128)(2,1)} %kv_ref.3) | copy-start | bytes 3538948
  1.2 15.0 %collective-permute-start.1 = (bf16[512,512]{1,0:T(8,128)(2,1)S(1)}, bf16[512,512]{1,0:T(8,128)(2,1)S(1)}, u32[]{:S(2)}, u32[]{:S(2)}) collective-permute-start(bf16[512,512]{1,0:T(8,128)(2,1)S(1)} %first.1), channel_id=1, source_target_pairs={{0,2},{1,3},{2,0},{3,1},{4,6},{5,7},{6,4},{7,5},{8,10},{9,11},{10,... | collective-permute-start | bytes 1572872 | tf_op jit(solution)/shard_map/ppermute | solution.py:31
  4.3 32.4 %collective-permute-start = (bf16[512,1152]{1,0:T(8,128)(2,1)S(1)}, bf16[512,1152]{1,0:T(8,128)(2,1)S(1)}, u32[]{:S(2)}, u32[]{:S(2)}) collective-permute-start(bf16[512,1152]{1,0:T(8,128)(2,1)S(1)} %copy-done.8), channel_id=1, source_target_pairs={{0,1},{1,0},{2,3},{3,2},{4,5},{5,4},{6,7},{7,6},{8,9},{9,8},{10,11... | collective-permute-start | bytes 3538952 | tf_op jit(solution)/shard_map/ppermute | solution.py:31
  16.2 19.0 %collective-permute-start.3 = (bf16[512,512]{1,0:T(8,128)(2,1)S(1)}, bf16[512,512]{1,0:T(8,128)(2,1)S(1)}, u32[]{:S(2)}, u32[]{:S(2)}) collective-permute-start(bf16[512,512]{1,0:T(8,128)(2,1)S(1)} %collective-permute-done.1.refs_3_), channel_id=1, source_target_pairs={{0,1},{1,0},{2,3},{3,2},{4,5},{5,4},{6,7},{7,6},{8,9},{9,8},{10,11... | collective-permute-start | bytes 1572872 | tf_op jit(solution)/shard_map/ppermute | solution.py:31
  16.2 11.0 %copy-start.2 = (bf16[3,1152,576]{1,2,0:T(8,128)(2,1)S(1)}, bf16[3,1152,576]{1,2,0:T(8,128)(2,1)}, u32[]{:S(2)}) copy-start(bf16[3,1152,576]{1,2,0:T(8,128)(2,1)} %param.17) | copy-start | bytes 11943940
  16.2 11.0 %copy-start.4 = (f32[6,1152]{1,0:T(8,128)S(1)}, f32[6,1152]{1,0:T(8,128)}, u32[]{:S(2)}) copy-start(f32[6,1152]{1,0:T(8,128)} %refs_1_.1) | copy-start | bytes 82948
  16.2 11.0 %copy-start.5 = (f32[6,1152]{1,0:T(8,128)S(1)}, f32[6,1152]{1,0:T(8,128)}, u32[]{:S(2)}) copy-start(f32[6,1152]{1,0:T(8,128)} %refs_2_.1) | copy-start | bytes 82948
  16.2 11.0 %copy-start.6 = (s32[4]{0:T(128)S(1)}, s32[4]{0:T(128)}, u32[]{:S(2)}) copy-start(s32[4]{0:T(128)} %order_ref.1) | copy-start | bytes 52
  16.3 11.0 %copy-start.7 = (f32[1,576]{1,0:T(1,128)S(1)}, f32[1,576]{1,0:T(1,128)}, u32[]{:S(2)}) copy-start(f32[1,576]{1,0:T(1,128)} %constant.22.clone.refs_0_) | copy-start | bytes 6916
  18.0 9.2 %collective-permute-start.2 = (bf16[512,256]{1,0:T(8,128)(2,1)S(1)}, bf16[512,256]{1,0:T(8,128)(2,1)S(1)}, u32[]{:S(2)}, u32[]{:S(2)}) collective-permute-start(bf16[512,256]{1,0:T(8,128)(2,1)S(1)} %get-tuple-element.29), channel_id=1, source_target_pairs={{0,2},{1,3},{2,0},{3,1},{4,6},{5,7},{6,4},{7,5},{8,10},{9,11},{10,... | collective-permute-start | bytes 786440 | tf_op jit(solution)/shard_map/ppermute | solution.py:31
  19.8 12.6 %collective-permute-start.5 = (bf16[512,256]{1,0:T(8,128)(2,1)S(1)}, bf16[512,256]{1,0:T(8,128)(2,1)S(1)}, u32[]{:S(2)}, u32[]{:S(2)}) collective-permute-start(bf16[512,256]{1,0:T(8,128)(2,1)S(1)} %get-tuple-element.31), channel_id=1, source_target_pairs={{0,2},{1,3},{2,0},{3,1},{4,6},{5,7},{6,4},{7,5},{8,10},{9,11},{10,... | collective-permute-start | bytes 786440 | tf_op jit(solution)/shard_map/ppermute | solution.py:31
  20.1 34.1 %collective-permute-start.9 = (bf16[128,1152]{1,0:T(8,128)(2,1)S(1)}, bf16[128,1152]{1,0:T(8,128)(2,1)S(1)}, u32[]{:S(2)}, u32[]{:S(2)}) collective-permute-start(bf16[128,1152]{1,0:T(8,128)(2,1)S(1)} %get-tuple-element.24.refs_4_.refs_1_), channel_id=1, source_target_pairs={{0,4},{1,5},{2,6},{3,7},{4,0},{5,1},{6,2},{7,3},{8,12},{9,13},{10,... | collective-permute-start | bytes 884744 | tf_op jit(solution)/shard_map/ppermute | solution.py:31
  27.2 14.4 %collective-permute-start.4 = (bf16[512,256]{1,0:T(8,128)(2,1)S(1)}, bf16[512,256]{1,0:T(8,128)(2,1)S(1)}, u32[]{:S(2)}, u32[]{:S(2)}) collective-permute-start(bf16[512,256]{1,0:T(8,128)(2,1)S(1)} %collective-permute-done.2.refs_4_), channel_id=1, source_target_pairs={{0,1},{1,0},{2,3},{3,2},{4,5},{5,4},{6,7},{7,6},{8,9},{9,8},{10,11... | collective-permute-start | bytes 786440 | tf_op jit(solution)/shard_map/ppermute | solution.py:31
  32.4 23.6 %collective-permute-start.10 = (bf16[128,1152]{1,0:T(8,128)(2,1)S(1)}, bf16[128,1152]{1,0:T(8,128)(2,1)S(1)}, u32[]{:S(2)}, u32[]{:S(2)}) collective-permute-start(bf16[128,1152]{1,0:T(8,128)(2,1)S(1)} %get-tuple-element.25.refs_5_.refs_2_), channel_id=1, source_target_pairs={{0,8},{1,9},{2,10},{3,11},{4,12},{5,13},{6,14},{7,15},{8,0},{9,1},... | collective-permute-start | bytes 884744 | tf_op jit(solution)/shard_map/ppermute | solution.py:31
  35.2 5.0 %collective-permute-start.6 = (bf16[512,128]{1,0:T(8,128)(2,1)S(1)}, bf16[512,128]{1,0:T(8,128)(2,1)S(1)}, u32[]{:S(2)}, u32[]{:S(2)}) collective-permute-start(bf16[512,128]{1,0:T(8,128)(2,1)S(1)} %get-tuple-element.32), channel_id=1, source_target_pairs={{0,2},{1,3},{2,0},{3,1},{4,6},{5,7},{6,4},{7,5},{8,10},{9,11},{10,... | collective-permute-start | bytes 393224 | tf_op jit(solution)/shard_map/ppermute | solution.py:31
  36.7 9.4 %collective-permute-start.7 = (bf16[512,256]{1,0:T(8,128)(2,1)S(1)}, bf16[512,256]{1,0:T(8,128)(2,1)S(1)}, u32[]{:S(2)}, u32[]{:S(2)}) collective-permute-start(bf16[512,256]{1,0:T(8,128)(2,1)S(1)} %collective-permute-done.5.refs_5_), channel_id=1, source_target_pairs={{0,1},{1,0},{2,3},{3,2},{4,5},{5,4},{6,7},{7,6},{8,9},{9,8},{10,11... | collective-permute-start | bytes 786440 | tf_op jit(solution)/shard_map/ppermute | solution.py:31
  40.3 17.0 %collective-permute-start.11 = (bf16[128,1152]{1,0:T(8,128)(2,1)S(1)}, bf16[128,1152]{1,0:T(8,128)(2,1)S(1)}, u32[]{:S(2)}, u32[]{:S(2)}) collective-permute-start(bf16[128,1152]{1,0:T(8,128)(2,1)S(1)} %get-tuple-element.26.refs_6_.refs_3_), channel_id=1, source_target_pairs={{0,12},{1,13},{2,14},{3,15},{4,8},{5,9},{6,10},{7,11},{8,4},{9,5},... | collective-permute-start | bytes 884744 | tf_op jit(solution)/shard_map/ppermute | solution.py:31
  41.7 3.8 %collective-permute-start.8 = (bf16[512,128]{1,0:T(8,128)(2,1)S(1)}, bf16[512,128]{1,0:T(8,128)(2,1)S(1)}, u32[]{:S(2)}, u32[]{:S(2)}) collective-permute-start(bf16[512,128]{1,0:T(8,128)(2,1)S(1)} %collective-permute-done.6.refs_6_), channel_id=1, source_target_pairs={{0,1},{1,0},{2,3},{3,2},{4,5},{5,4},{6,7},{7,6},{8,9},{9,8},{10,11... | collective-permute-start | bytes 393224 | tf_op jit(solution)/shard_map/ppermute | solution.py:31
  45.4 14.3 %collective-permute-start.12 = (bf16[256,128]{1,0:T(8,128)(2,1)S(1)}, bf16[256,128]{1,0:T(8,128)(2,1)S(1)}, u32[]{:S(2)}, u32[]{:S(2)}) collective-permute-start(bf16[256,128]{1,0:T(8,128)(2,1)S(1)} %get-tuple-element.34.refs_6_), channel_id=1, source_target_pairs={{0,4},{1,5},{2,6},{3,7},{4,0},{5,1},{6,2},{7,3},{8,12},{9,13},{10,... | collective-permute-start | bytes 196616 | tf_op jit(solution)/shard_map/ppermute | solution.py:31
  48.4 21.2 %collective-permute-start.13 = (bf16[320,128]{1,0:T(8,128)(2,1)S(1)}, bf16[320,128]{1,0:T(8,128)(2,1)S(1)}, u32[]{:S(2)}, u32[]{:S(2)}) collective-permute-start(bf16[320,128]{1,0:T(8,128)(2,1)S(1)} %shard_map.112.refs_7_), channel_id=1, source_target_pairs={{0,4},{1,5},{2,6},{3,7},{4,0},{5,1},{6,2},{7,3},{8,12},{9,13},{10,... | collective-permute-start | bytes 245768 | tf_op jit(solution)/shard_map/ppermute | solution.py:31
  54.2 15.4 %collective-permute-start.14 = (bf16[256,128]{1,0:T(8,128)(2,1)S(1)}, bf16[256,128]{1,0:T(8,128)(2,1)S(1)}, u32[]{:S(2)}, u32[]{:S(2)}) collective-permute-start(bf16[256,128]{1,0:T(8,128)(2,1)S(1)} %get-tuple-element.35.refs_8_), channel_id=1, source_target_pairs={{0,8},{1,9},{2,10},{3,11},{4,12},{5,13},{6,14},{7,15},{8,0},{9,1},... | collective-permute-start | bytes 196616 | tf_op jit(solution)/shard_map/ppermute | solution.py:31
  56.0 14.5 %collective-permute-start.15 = (bf16[320,128]{1,0:T(8,128)(2,1)S(1)}, bf16[320,128]{1,0:T(8,128)(2,1)S(1)}, u32[]{:S(2)}, u32[]{:S(2)}) collective-permute-start(bf16[320,128]{1,0:T(8,128)(2,1)S(1)} %shard_map.113.refs_9_), channel_id=1, source_target_pairs={{0,8},{1,9},{2,10},{3,11},{4,12},{5,13},{6,14},{7,15},{8,0},{9,1},... | collective-permute-start | bytes 245768 | tf_op jit(solution)/shard_map/ppermute | solution.py:31
  57.2 13.2 %copy-start.1 = (bf16[576,1152]{1,0:T(8,128)(2,1)S(1)}, bf16[576,1152]{1,0:T(8,128)(2,1)}, u32[]{:S(2)}) copy-start(bf16[576,1152]{1,0:T(8,128)(2,1)} %refs_12_.3) | copy-start | bytes 3981316
  57.2 13.2 %copy-start.3 = (bf16[3,1152,576]{1,2,0:T(8,128)(2,1)S(1)}, bf16[3,1152,576]{1,2,0:T(8,128)(2,1)}, u32[]{:S(2)}) copy-start(bf16[3,1152,576]{1,2,0:T(8,128)(2,1)} %param.19) | copy-start | bytes 11943940
  57.2 12.4 %collective-permute-start.16 = (bf16[256,128]{1,0:T(8,128)(2,1)S(1)}, bf16[256,128]{1,0:T(8,128)(2,1)S(1)}, u32[]{:S(2)}, u32[]{:S(2)}) collective-permute-start(bf16[256,128]{1,0:T(8,128)(2,1)S(1)} %get-tuple-element.36.refs_10_), channel_id=1, source_target_pairs={{0,12},{1,13},{2,14},{3,15},{4,8},{5,9},{6,10},{7,11},{8,4},{9,5},... | collective-permute-start | bytes 196616 | tf_op jit(solution)/shard_map/ppermute | solution.py:31
  59.7 10.8 %collective-permute-start.17 = (bf16[320,128]{1,0:T(8,128)(2,1)S(1)}, bf16[320,128]{1,0:T(8,128)(2,1)S(1)}, u32[]{:S(2)}, u32[]{:S(2)}) collective-permute-start(bf16[320,128]{1,0:T(8,128)(2,1)S(1)} %shard_map.114.refs_11_), channel_id=1, source_target_pairs={{0,12},{1,13},{2,14},{3,15},{4,8},{5,9},{6,10},{7,11},{8,4},{9,5},... | collective-permute-start | bytes 245768 | tf_op jit(solution)/shard_map/ppermute | solution.py:31
  76.9 9.9 %collective-permute-start.19 = (bf16[576,128]{1,0:T(8,128)(2,1)S(1)}, bf16[576,128]{1,0:T(8,128)(2,1)S(1)}, u32[]{:S(2)}, u32[]{:S(2)}) collective-permute-start(bf16[576,128]{1,0:T(8,128)(2,1)S(1)} %shard_map.118), channel_id=1, source_target_pairs={{0,12},{1,13},{2,14},{3,15},{4,8},{5,9},{6,10},{7,11},{8,4},{9,5},... | collective-permute-start | bytes 442376 | tf_op jit(solution)/shard_map/ppermute | solution.py:31
  80.7 7.4 %collective-permute-start.20 = (bf16[576,128]{1,0:T(8,128)(2,1)S(1)}, bf16[576,128]{1,0:T(8,128)(2,1)S(1)}, u32[]{:S(2)}, u32[]{:S(2)}) collective-permute-start(bf16[576,128]{1,0:T(8,128)(2,1)S(1)} %shard_map.119), channel_id=1, source_target_pairs={{0,4},{1,5},{2,6},{3,7},{4,0},{5,1},{6,2},{7,3},{8,12},{9,13},{10,... | collective-permute-start | bytes 442376 | tf_op jit(solution)/shard_map/ppermute | solution.py:31
  84.6 9.5 %collective-permute-start.18 = (bf16[576,128]{1,0:T(8,128)(2,1)S(1)}, bf16[576,128]{1,0:T(8,128)(2,1)S(1)}, u32[]{:S(2)}, u32[]{:S(2)}) collective-permute-start(bf16[576,128]{1,0:T(8,128)(2,1)S(1)} %shard_map.117), channel_id=1, source_target_pairs={{0,8},{1,9},{2,10},{3,11},{4,12},{5,13},{6,14},{7,15},{8,0},{9,1},... | collective-permute-start | bytes 442376 | tf_op jit(solution)/shard_map/ppermute | solution.py:31
  85.9 2.2 %copy-start = (bf16[576,1152]{1,0:T(8,128)(2,1)S(1)}, bf16[576,1152]{1,0:T(8,128)(2,1)}, u32[]{:S(2)}) copy-start(bf16[576,1152]{1,0:T(8,128)(2,1)} %weight_ref.3) | copy-start | bytes 3981316

commit v7 on v6

--- a/solution.py
+++ b/solution.py
@@ -440,11 +440,18 @@
     return row_parts(len(PAIR_GROUPS) - 1, rows)
 
 
+def input_halves(rows, piece):
+    parts = [part_pieces(chunks, piece) for chunks in target_parts(rows)]
+    if len(parts) < 3:
+        return [[s for part in parts for s in part]]
+    return [parts[-1] + parts[0], [s for part in parts[1:-1] for s in part]]
+
+
 def output_parts(rows, piece):
     parts = [part_pieces(chunks, piece) for chunks in target_parts(rows)]
-    if len(parts) < 2:
-        return parts
-    return [[s for part in parts[:1] + parts[2:] for s in part], parts[1]]
+    if len(parts) < 3:
+        return [[s for part in parts for s in part]]
+    return [[s for part in parts[2:] for s in part], parts[0] + parts[1]]
 
 
 def part_pieces(chunks, piece):
@@ -529,8 +536,8 @@
     return tokens, mixed
 
 
-def temporal_in_kernel(*refs, frames, columns):
-    groups = len(columns)
+def temporal_in_kernel(*refs, members, columns):
+    groups, frames = len(columns), len(members)
     tokens_refs = refs[:frames]
     mixed_refs = refs[frames : frames + frames * groups]
     out_weight, qkv_weight, modulation_ref, place_ref, query_ref, kv_ref = refs[
@@ -547,9 +554,9 @@
         [
             (
                 normal[frame * piece : (frame + 1) * piece]
-                + (modulation_ref[3:4, :] + place_ref[frame : frame + 1, :])
+                + (modulation_ref[3:4, :] + place_ref[member : member + 1, :])
             ).astype(bf16)
-            for frame in range(frames)
+            for frame, member in enumerate(members)
         ],
         axis=0,
     )
@@ -561,23 +568,31 @@
     ).astype(bf16)
 
 
-def temporal_in(tokens, mixed, columns, weights, modulation, places):
-    frames = len(tokens)
+def temporal_in(members, tokens, mixed, columns, weights, modulation, places):
     width, feature_width = weights[0].shape
     padded = -(-width // LANES) * LANES
-    rows = frames * tokens[0].shape[0]
+    rows = len(members) * tokens[0].shape[0]
     return on_chip_call(
-        functools.partial(temporal_in_kernel, frames=frames, columns=columns),
-        [*tokens, *[part for frame in mixed for part in frame], *weights, modulation, places],
+        functools.partial(temporal_in_kernel, members=members, columns=columns),
+        [
+            *[tokens[s] for s in members],
+            *[part for s in members for part in mixed[s]],
+            *weights,
+            modulation,
+            places,
+        ],
         [((rows, padded), bf16), ((rows, 2 * width), bf16)],
         2 * rows * feature_width * width * 4,
         8,
     )
 
 
-def temporal_kernel(query_ref, kv_ref, *out_refs, frames, head_dim, targets):
-    piece = query_ref.shape[0] // frames
-    width = kv_ref.shape[1] // 2
+def temporal_kernel(*refs, frames, head_dim, targets, halves):
+    query_refs, kv_refs = refs[: len(halves)], refs[len(halves) : 2 * len(halves)]
+    out_refs = refs[2 * len(halves) :]
+    piece = sum(ref.shape[0] for ref in query_refs) // frames
+    width = kv_refs[0].shape[1] // 2
+    where = {s: (h, at) for h, members in enumerate(halves) for at, s in enumerate(members)}
     scale = softmax_scale(head_dim)
     step = max(16, min(piece, LANES // frames))
     block = len(targets) * step
@@ -586,20 +601,16 @@
     same = row_at == column_at
     plan = pair_plan(width, head_dim)
 
-    def window(ref, members, start, tile):
-        return jnp.concatenate(
-            [
-                ref[
-                    frame * piece + start : frame * piece + start + step,
-                    tile * LANES : (tile + 2) * LANES,
-                ]
-                for frame in members
-            ],
-            axis=0,
-        )
+    def window(half_refs, members, start, tile):
+        rows = []
+        for s in members:
+            half, at = where[s]
+            first = at * piece + start
+            rows.append(half_refs[half][first : first + step, tile * LANES : (tile + 2) * LANES])
+        return jnp.concatenate(rows, axis=0)
 
     def score(start, tile, lane):
-        queries = window(query_ref, targets, start, tile)
+        queries = window(query_refs, targets, start, tile)
         stacked = jnp.concatenate(
             [
                 queries * column_mask(lane, head_dim, bf16),
@@ -608,7 +619,7 @@
             axis=0,
         )
         scores = lax.dot_general(
-            stacked, window(kv_ref, range(frames), start, tile), NT, preferred_element_type=f32
+            stacked, window(kv_refs, range(frames), start, tile), NT, preferred_element_type=f32
         )
         return jnp.where(same, scores * scale, -jnp.inf)
 
@@ -622,7 +633,7 @@
     weights = [weigh(value) for value in scores]
     mixed_pairs = [
         jnp.dot(
-            value, window(kv_ref, range(frames), start, value_tile), preferred_element_type=f32
+            value, window(kv_refs, range(frames), start, value_tile), preferred_element_type=f32
         )
         for value, (start, _, _, value_tile, _) in zip(weights, tasks)
     ]
@@ -647,13 +658,15 @@
         )
 
 
-def temporal(query, kv, frames, head_dim, targets):
-    width = kv.shape[1] // 2
-    rows = query.shape[0]
+def temporal(queries, kvs, halves, frames, head_dim, targets):
+    width = kvs[0].shape[1] // 2
+    rows = sum(query.shape[0] for query in queries)
     shape = (stack_rows(rows // frames, width), LANES)
     return on_chip_call(
-        functools.partial(temporal_kernel, frames=frames, head_dim=head_dim, targets=targets),
-        [query, kv],
+        functools.partial(
+            temporal_kernel, frames=frames, head_dim=head_dim, targets=targets, halves=halves
+        ),
+        [*queries, *kvs],
         [(shape, bf16) for _ in targets],
         2 * rows * 128 * 256 * 8,
         4,
@@ -811,11 +824,16 @@
     columns = group_columns(width, head_dim)
     after = after_spatial(pieces, local, columns, spatial_out, modulation)
     weights = (spatial_out, jnp.swapaxes(temporal_qkv, 1, 2).reshape(3 * width, feature_width))
-    temporal_query, temporal_kv = temporal_in(there, sent, columns, weights, modulation, places)
+    halves = input_halves(rows, piece)
+    inputs = [
+        temporal_in(members, there, sent, columns, weights, modulation, places)
+        for members in halves
+    ]
+    queries, kvs = [query for query, _ in inputs], [kv for _, kv in inputs]
     back = {}
     for chunks in target_parts(rows):
         targets = part_pieces(chunks, piece)
-        outs = temporal(temporal_query, temporal_kv, frames, head_dim, targets)
+        outs = temporal(queries, kvs, halves, frames, head_dim, targets)
         for s, out in zip(targets, outs):
             back[s] = out if s == 0 else permute(out, behind(s))
     result = None

time: 95.7 us -> 92.5 us (0.967)
  waiting for transfers between devices: 30 us -> 26.7 us
    ppermute x21, waiting for transfers between devices: 30 us -> 26.7 us  [permute(): lax.ppermute(value, 'patch', [(source, target(source)) for source in rang...]
    pallas_call x12 -> x13, Pallas kernels: 25.6 us -> 26.3 us  [on_chip_call(): pl.pallas_call(kernel, out_shape=[pltpu.VMEM(shape, dtype) for shape, dty...]
  transfers between devices with their start and end apart: 21 -> 21, of which waited for: 7 -> 8; matrix products, arithmetic and copies ran while one was open for 0% -> 0% of each run, Pallas kernels for 28% -> 31%
where the time goes in v7:
time: 92.5 us; the launch traced here: 92.4 us
  Pallas kernels  36.6 us (40%)
  starting transfers between devices  27.7 us (30%)
  waiting for transfers between devices  26.7 us (29%)
  between operations  1.11 us (1%)
    ppermute x21, starting transfers between devices, permute(): lax.ppermute(value, 'patch', [(source, target(source)) for source in rang...  27.7 us
    ppermute x21, waiting for transfers between devices, permute(): lax.ppermute(value, 'patch', [(source, target(source)) for source in rang...  26.7 us
    pallas_call x13, Pallas kernels, on_chip_call(): pl.pallas_call(kernel, out_shape=[pltpu.VMEM(shape, dtype) for shape, dty...  26.3 us
    pallas_call x1, Pallas kernels, projections(): pl.pallas_call(functools.partial(projection_kernel, frames=frames, width=...  3.95 us
    pallas_call x2, Pallas kernels, output(): pl.pallas_call(functools.partial(output_kernel, frames=frames, members=me...  3.45 us
  transfers between devices with their start and end apart: 21, of which 8 were waited for; matrix products, arithmetic and copies ran while one was open for 0% of the time, Pallas kernels for 31%

profile of v7, /device:TPU:0, one launch (start us, length us, event | category | flops | bytes accessed | tf_op | source)
XLA Modules:
  0.0 92.4 jit_solution(15966323654750284470)
XLA Ops:
  0.0 1.2 %first.1 = bf16[512,512]{1,0:T(8,128)(2,1)S(1)} custom-call(bf16[512,1152]{1,0:T(8,128)(2,1)} %kv_ref.3), custom_call_target="tpu_custom_call" | custom-call | tf_op jit(solution)/shard_map/first/pallas_call | solution.py:107
  1.2 3.1 %collective-permute-start.1 = (bf16[512,512]{1,0:T(8,128)(2,1)S(1)}, bf16[512,512]{1,0:T(8,128)(2,1)S(1)}, u32[]{:S(2)}, u32[]{:S(2)}) collective-permute-start(bf16[512,512]{1,0:T(8,128)(2,1)S(1)} %first.1), channel_id=1, source_target_pairs={{0,2},{1,3},{2,0},{3,1},{4,6},{5,7},{6,4},{7,5},{8,10},{9,11},{10,... | collective-permute-start | bytes 1572872 | tf_op jit(solution)/shard_map/ppermute | solution.py:31
  4.3 11.9 %collective-permute-done.1.refs_3_ = bf16[512,512]{1,0:T(8,128)(2,1)S(1)} collective-permute-done((bf16[512,512]{1,0:T(8,128)(2,1)S(1)}, bf16[512,512]{1,0:T(8,128)(2,1)S(1)}, u32[]{:S(2)}, u32[]{:S(2)}) %collective-permute-start.1) | collective-permute-done | bytes 524320 | tf_op jit(solution)/shard_map/ppermute | solution.py:31
  16.2 0.0 copy-start.6
  16.3 0.0 copy-start.7
  16.3 1.7 %pieces.1 = (bf16[128,1152]{1,0:T(8,128)(2,1)S(1)}, bf16[128,1152]{1,0:T(8,128)(2,1)S(1)}, bf16[128,1152]{1,0:T(8,128)(2,1)S(1)}, bf16[128,1152]{1,0:T(8,128)(2,...) custom-call(s32[1]{0:T(128)} %bitcast.slot_ref, ...), custom_call_target="tpu_custom_call" | custom-call | flops 4000000000 | bytes 2359296 | tf_op jit(solution)/shard_map/pieces/pallas_call | solution.py:140
  18.0 1.8 %collective-permute-start.2 = (bf16[512,256]{1,0:T(8,128)(2,1)S(1)}, bf16[512,256]{1,0:T(8,128)(2,1)S(1)}, u32[]{:S(2)}, u32[]{:S(2)}) collective-permute-start(bf16[512,256]{1,0:T(8,128)(2,1)S(1)} %get-tuple-element.31), channel_id=1, source_target_pairs={{0,2},{1,3},{2,0},{3,1},{4,6},{5,7},{6,4},{7,5},{8,10},{9,11},{10,... | collective-permute-start | bytes 786440 | tf_op jit(solution)/shard_map/ppermute | solution.py:31
  19.8 0.3 collective-permute-start.5
  20.1 3.8 %collective-permute-start.9 = (bf16[128,1152]{1,0:T(8,128)(2,1)S(1)}, bf16[128,1152]{1,0:T(8,128)(2,1)S(1)}, u32[]{:S(2)}, u32[]{:S(2)}) collective-permute-start(bf16[128,1152]{1,0:T(8,128)(2,1)S(1)} %get-tuple-element.28.refs_6_.refs_3_), channel_id=1, source_target_pairs={{0,12},{1,13},{2,14},{3,15},{4,8},{5,9},{6,10},{7,11},{8,4},{9,5},... | collective-permute-start | bytes 884744 | tf_op jit(solution)/shard_map/ppermute | solution.py:31
  24.6 2.7 %collective-permute-done.2.refs_4_ = bf16[512,256]{1,0:T(8,128)(2,1)S(1)} collective-permute-done((bf16[512,256]{1,0:T(8,128)(2,1)S(1)}, bf16[512,256]{1,0:T(8,128)(2,1)S(1)}, u32[]{:S(2)}, u32[]{:S(2)}) %collective-permute-start.2) | collective-permute-done | bytes 262176 | tf_op jit(solution)/shard_map/ppermute | solution.py:31
  27.3 3.9 %projections.1 = (bf16[512,640]{1,0:T(8,128)(2,1)S(1)}, bf16[512,1152]{1,0:T(8,128)(2,1)S(1)}, f32[6,1152]{1,0:T(8,128)S(1)}, f32[4,1152]{1,0:T(4,128)S(1)}) custom-call(s32[1]{0:T(128)} %bitcast.slot_ref, s32[1]{0:T(128)S(6)} %copy.14.time_ref, s32[4]{0:T(128)S(1)} %copy-done.6, bf16[1728,1152]{1,0:T(8,128)(2,1)S(1)} %bitcast.9, f32[1,576]{1,0:T(1,128)S(1)} %copy-done.7, ...), custom_call_target="tpu_custom_call" | custom-call | flops 2038431744 | bytes 3981312 | tf_op jit(solution)/shard_map/projections/pallas_call | solution.py:207
  31.2 1.2 %collective-permute-done.5.refs_5_ = bf16[512,256]{1,0:T(8,128)(2,1)S(1)} collective-permute-done((bf16[512,256]{1,0:T(8,128)(2,1)S(1)}, bf16[512,256]{1,0:T(8,128)(2,1)S(1)}, u32[]{:S(2)}, u32[]{:S(2)}) %collective-permute-start.5) | collective-permute-done | bytes 262176 | tf_op jit(solution)/shard_map/ppermute | solution.py:31
  32.4 2.8 %collective-permute-start.12 = (bf16[128,1152]{1,0:T(8,128)(2,1)S(1)}, bf16[128,1152]{1,0:T(8,128)(2,1)S(1)}, u32[]{:S(2)}, u32[]{:S(2)}) collective-permute-start(bf16[128,1152]{1,0:T(8,128)(2,1)S(1)} %get-tuple-element.27.refs_5_.refs_2_), channel_id=1, source_target_pairs={{0,8},{1,9},{2,10},{3,11},{4,12},{5,13},{6,14},{7,15},{8,0},{9,1},... | collective-permute-start | bytes 884744 | tf_op jit(solution)/shard_map/ppermute | solution.py:31
  35.2 1.5 %collective-permute-start.6 = (bf16[512,128]{1,0:T(8,128)(2,1)S(1)}, bf16[512,128]{1,0:T(8,128)(2,1)S(1)}, u32[]{:S(2)}, u32[]{:S(2)}) collective-permute-start(bf16[512,128]{1,0:T(8,128)(2,1)S(1)} %get-tuple-element.34), channel_id=1, source_target_pairs={{0,2},{1,3},{2,0},{3,1},{4,6},{5,7},{6,4},{7,5},{8,10},{9,11},{10,... | collective-permute-start | bytes 393224 | tf_op jit(solution)/shard_map/ppermute | solution.py:31
  36.7 3.5 %shard_map.109.refs_7_ = bf16[512,256]{1,0:T(8,128)(2,1)S(1)} custom-call(bf16[512,640]{1,0:T(8,128)(2,1)S(1)} %get-tuple-element.29.refs_0_, bf16[512,1152]{1,0:T(8,128)(2,1)S(1)} %get-tuple-element.30.refs_1_, bf16[512,1152]{1,0:T(8,128)(2,1)S(1)} %collective-permute-done.refs_2_, bf16[512,512]{1,0:T(8,128)(2,1)S(1)} %collective-permute-done.1.refs_3_, ...), custom_call_target="tpu_custom_call" | custom-call | flops 2147483648 | bytes 4063232 | tf_op jit(solution)/shard_map/pallas_call | solution.py:69
  40.3 1.6 %collective-permute-start.13 = (bf16[128,1152]{1,0:T(8,128)(2,1)S(1)}, bf16[128,1152]{1,0:T(8,128)(2,1)S(1)}, u32[]{:S(2)}, u32[]{:S(2)}) collective-permute-start(bf16[128,1152]{1,0:T(8,128)(2,1)S(1)} %get-tuple-element.26.refs_4_.refs_1_), channel_id=1, source_target_pairs={{0,4},{1,5},{2,6},{3,7},{4,0},{5,1},{6,2},{7,3},{8,12},{9,13},{10,... | collective-permute-start | bytes 884744 | tf_op jit(solution)/shard_map/ppermute | solution.py:31
  41.9 0.2 collective-permute-start.8
  42.1 3.5 %shard_map.110 = (bf16[256,128]{1,0:T(8,128)(2,1)S(1)}, bf16[256,128]{1,0:T(8,128)(2,1)S(1)}, bf16[256,128]{1,0:T(8,128)(2,1)S(1)}, bf16[256,128]{1,0:T(8,128)(2,1)S(1)}, bf16[512,128]{1,0:T(8,128)(2,1)S(1)}) custom-call(bf16[512,640]{1,0:T(8,128)(2,1)S(1)} %get-tuple-element.29.refs_0_, bf16[512,1152]{1,0:T(8,128)(2,1)S(1)} %get-tuple-element.30.refs_1_, ...), custom_call_target="tpu_custom_call" | custom-call | flops 2147483648 | bytes 4849664 | tf_op jit(solution)/shard_map/pallas_call | solution.py:69
  45.7 0.3 collective-permute-start.10
  46.0 2.3 %shard_map.114.refs_11_ = bf16[320,128]{1,0:T(8,128)(2,1)S(1)} custom-call(bf16[512,640]{1,0:T(8,128)(2,1)S(1)} %get-tuple-element.29.refs_0_, bf16[512,1152]{1,0:T(8,128)(2,1)S(1)} %get-tuple-element.30.refs_1_, bf16[512,1152]{1,0:T(8,128)(2,1)S(1)} %collective-permute-done.refs_2_, bf16[512,512]{1,0:T(8,128)(2,1)S(1)} %collective-permute-done.1.refs_3_, ...), custom_call_target="tpu_custom_call" | custom-call | flops 1073741824 | bytes 5505024 | tf_op jit(solution)/shard_map/pallas_call | solution.py:69
  48.3 3.7 %collective-permute-start.11 = (bf16[320,128]{1,0:T(8,128)(2,1)S(1)}, bf16[320,128]{1,0:T(8,128)(2,1)S(1)}, u32[]{:S(2)}, u32[]{:S(2)}) collective-permute-start(bf16[320,128]{1,0:T(8,128)(2,1)S(1)} %shard_map.114.refs_11_), channel_id=1, source_target_pairs={{0,12},{1,13},{2,14},{3,15},{4,8},{5,9},{6,10},{7,11},{8,4},{9,5},... | collective-permute-start | bytes 245768 | tf_op jit(solution)/shard_map/ppermute | solution.py:31
  51.9 2.1 %shard_map.111.refs_5_.refs_3_ = bf16[320,128]{1,0:T(8,128)(2,1)S(1)} custom-call(bf16[512,640]{1,0:T(8,128)(2,1)S(1)} %get-tuple-element.29.refs_0_, bf16[512,1152]{1,0:T(8,128)(2,1)S(1)} %get-tuple-element.30.refs_1_, bf16[512,1152]{1,0:T(8,128)(2,1)S(1)} %collective-permute-done.refs_2_, bf16[512,512]{1,0:T(8,128)(2,1)S(1)} %collective-permute-done.1.refs_3_, ...), custom_call_target="tpu_custom_call" | custom-call | flops 1073741824 | bytes 5505024 | tf_op jit(solution)/shard_map/pallas_call | solution.py:69
  54.1 2.1 %shard_map.112.refs_7_ = bf16[320,128]{1,0:T(8,128)(2,1)S(1)} custom-call(bf16[512,640]{1,0:T(8,128)(2,1)S(1)} %get-tuple-element.29.refs_0_, bf16[512,1152]{1,0:T(8,128)(2,1)S(1)} %get-tuple-element.30.refs_1_, bf16[512,1152]{1,0:T(8,128)(2,1)S(1)} %collective-permute-done.refs_2_, bf16[512,512]{1,0:T(8,128)(2,1)S(1)} %collective-permute-done.1.refs_3_, ...), custom_call_target="tpu_custom_call" | custom-call | flops 1073741824 | bytes 5505024 | tf_op jit(solution)/shard_map/pallas_call | solution.py:69
  56.2 0.0 copy-start
  56.2 0.0 copy-start.1
  56.3 2.1 %shard_map.113.refs_9_ = bf16[320,128]{1,0:T(8,128)(2,1)S(1)} custom-call(bf16[512,640]{1,0:T(8,128)(2,1)S(1)} %get-tuple-element.29.refs_0_, bf16[512,1152]{1,0:T(8,128)(2,1)S(1)} %get-tuple-element.30.refs_1_, bf16[512,1152]{1,0:T(8,128)(2,1)S(1)} %collective-permute-done.refs_2_, bf16[512,512]{1,0:T(8,128)(2,1)S(1)} %collective-permute-done.1.refs_3_, ...), custom_call_target="tpu_custom_call" | custom-call | flops 1073741824 | bytes 5505024 | tf_op jit(solution)/shard_map/pallas_call | solution.py:69
  58.4 0.1 collective-permute-start.14
  58.5 2.9 %collective-permute-start.15 = (bf16[320,128]{1,0:T(8,128)(2,1)S(1)}, bf16[320,128]{1,0:T(8,128)(2,1)S(1)}, u32[]{:S(2)}, u32[]{:S(2)}) collective-permute-start(bf16[320,128]{1,0:T(8,128)(2,1)S(1)} %shard_map.113.refs_9_), channel_id=1, source_target_pairs={{0,8},{1,9},{2,10},{3,11},{4,12},{5,13},{6,14},{7,15},{8,0},{9,1},... | collective-permute-start | bytes 245768 | tf_op jit(solution)/shard_map/ppermute | solution.py:31
  61.4 2.0 %collective-permute-start.17 = (bf16[320,128]{1,0:T(8,128)(2,1)S(1)}, bf16[320,128]{1,0:T(8,128)(2,1)S(1)}, u32[]{:S(2)}, u32[]{:S(2)}) collective-permute-start(bf16[320,128]{1,0:T(8,128)(2,1)S(1)} %shard_map.112.refs_7_), channel_id=1, source_target_pairs={{0,4},{1,5},{2,6},{3,7},{4,0},{5,1},{6,2},{7,3},{8,12},{9,13},{10,... | collective-permute-start | bytes 245768 | tf_op jit(solution)/shard_map/ppermute | solution.py:31
  63.5 2.5 %shard_map.116 = (bf16[256,640]{1,0:T(8,128)(2,1)S(1)}, bf16[256,1152]{1,0:T(8,128)(2,1)S(1)}) custom-call(bf16[128,1152]{1,0:T(8,128)(2,1)S(1)} %get-tuple-element.25.refs_3_.refs_0_, bf16[128,1152]{1,0:T(8,128)(2,1)S(1)} %collective-permute-done.9.refs_1_, bf16[256,128]{1,0:T(8,128)(2,1)S(1)} %get-tuple-element.32.refs_4_.refs_2_, ...), custom_call_target="tpu_custom_call" | custom-call | flops 1358954496 | bytes 6239232 | tf_op jit(solution)/shard_map/pallas_call | solution.py:69
  66.0 2.0 %collective-permute-done.16.refs_4_ = bf16[256,128]{1,0:T(8,128)(2,1)S(1)} collective-permute-done((bf16[256,128]{1,0:T(8,128)(2,1)S(1)}, bf16[256,128]{1,0:T(8,128)(2,1)S(1)}, u32[]{:S(2)}, u32[]{:S(2)}) %collective-permute-start.16) | collective-permute-done | bytes 65568 | tf_op jit(solution)/shard_map/ppermute | solution.py:31
  68.1 0.9 collective-permute-done.17.refs_5_
  68.9 2.5 %shard_map.117 = (bf16[256,640]{1,0:T(8,128)(2,1)S(1)}, bf16[256,1152]{1,0:T(8,128)(2,1)S(1)}) custom-call(bf16[128,1152]{1,0:T(8,128)(2,1)S(1)} %collective-permute-done.12.refs_0_, bf16[128,1152]{1,0:T(8,128)(2,1)S(1)} %collective-permute-done.13.refs_1_, bf16[256,128]{1,0:T(8,128)(2,1)S(1)} %collective-permute-done.14.refs_2_, ...), custom_call_target="tpu_custom_call" | custom-call | flops 1358954496 | bytes 6239232 | tf_op jit(solution)/shard_map/pallas_call | solution.py:69
  71.5 1.0 %shard_map.118 = bf16[576,128]{1,0:T(8,128)(2,1)S(1)} custom-call(bf16[256,640]{1,0:T(8,128)(2,1)S(1)} %get-tuple-element.41.refs_0_, bf16[256,640]{1,0:T(8,128)(2,1)S(1)} %get-tuple-element.42.refs_1_, bf16[256,1152]{1,0:T(8,128)(2,1)S(1)} %get-tuple-element.43.refs_2_, bf16[256,1152]{1,0:T(8,128)(2,1)S(1)} %get-tuple-element.44.refs_3_), custom_call_target="tpu_custom_call" | custom-call | flops 268435456 | bytes 1835008 | tf_op jit(solution)/shard_map/pallas_call | solution.py:69
  72.5 1.2 %shard_map.120 = bf16[576,128]{1,0:T(8,128)(2,1)S(1)} custom-call(bf16[256,640]{1,0:T(8,128)(2,1)S(1)} %get-tuple-element.41.refs_0_, bf16[256,640]{1,0:T(8,128)(2,1)S(1)} %get-tuple-element.42.refs_1_, bf16[256,1152]{1,0:T(8,128)(2,1)S(1)} %get-tuple-element.43.refs_2_, bf16[256,1152]{1,0:T(8,128)(2,1)S(1)} %get-tuple-element.44.refs_3_), custom_call_target="tpu_custom_call" | custom-call | flops 268435456 | bytes 1835008 | tf_op jit(solution)/shard_map/pallas_call | solution.py:69
  73.7 0.1 collective-permute-start.20
  73.8 1.0 %shard_map.119 = bf16[576,128]{1,0:T(8,128)(2,1)S(1)} custom-call(bf16[256,640]{1,0:T(8,128)(2,1)S(1)} %get-tuple-element.41.refs_0_, bf16[256,640]{1,0:T(8,128)(2,1)S(1)} %get-tuple-element.42.refs_1_, bf16[256,1152]{1,0:T(8,128)(2,1)S(1)} %get-tuple-element.43.refs_2_, bf16[256,1152]{1,0:T(8,128)(2,1)S(1)} %get-tuple-element.44.refs_3_), custom_call_target="tpu_custom_call" | custom-call | flops 268435456 | bytes 1835008 | tf_op jit(solution)/shard_map/pallas_call | solution.py:69
  74.8 0.2 collective-permute-start.18
  75.0 3.3 %collective-permute-start.19 = (bf16[576,128]{1,0:T(8,128)(2,1)S(1)}, bf16[576,128]{1,0:T(8,128)(2,1)S(1)}, u32[]{:S(2)}, u32[]{:S(2)}) collective-permute-start(bf16[576,128]{1,0:T(8,128)(2,1)S(1)} %shard_map.119), channel_id=1, source_target_pairs={{0,8},{1,9},{2,10},{3,11},{4,12},{5,13},{6,14},{7,15},{8,0},{9,1},... | collective-permute-start | bytes 442376 | tf_op jit(solution)/shard_map/ppermute | solution.py:31
  78.3 1.2 %shard_map.115.after_ref = f32[512,1152]{1,0:T(8,128)S(1)} custom-call(bf16[128,1152]{1,0:T(8,128)(2,1)S(1)} %get-tuple-element.25.refs_3_.refs_0_, bf16[128,1152]{1,0:T(8,128)(2,1)S(1)} %get-tuple-element.26.refs_4_.refs_1_, bf16[128,1152]{1,0:T(8,128)(2,1)S(1)} %get-tuple-element.27.refs_5_.refs_2_, ...), custom_call_target="tpu_custom_call" | custom-call | flops 679477248 | bytes 3124224 | tf_op jit(solution)/shard_map/pallas_call | solution.py:69
  79.5 0.0 copy-start.2
  79.5 1.0 %shard_map.121.refs_1_ = bf16[576,128]{1,0:T(8,128)(2,1)S(1)} custom-call(bf16[256,640]{1,0:T(8,128)(2,1)S(1)} %get-tuple-element.41.refs_0_, bf16[256,640]{1,0:T(8,128)(2,1)S(1)} %get-tuple-element.42.refs_1_, bf16[256,1152]{1,0:T(8,128)(2,1)S(1)} %get-tuple-element.43.refs_2_, bf16[256,1152]{1,0:T(8,128)(2,1)S(1)} %get-tuple-element.44.refs_3_), custom_call_target="tpu_custom_call" | custom-call | flops 268435456 | bytes 1835008 | tf_op jit(solution)/shard_map/pallas_call | solution.py:69
  80.6 0.1 collective-permute-done.20.refs_0_
  80.7 0.2 copy-done.2
  80.9 1.7 %shard_map.122.refs_2_ = f32[512,1152]{1,0:T(8,128)} custom-call(s32[1]{0:T(128)} %bitcast.slot_ref, f32[512,1152]{1,0:T(8,128)S(1)} %shard_map.115.after_ref, bf16[576,1152]{1,0:T(8,128)(2,1)S(1)} %copy-done.2, f32[6,1152]{1,0:T(8,128)S(1)} %get-tuple-element.39.refs_13_.refs_8_.modulation_ref, bf16[576,128]{1,0:T(8,128)(2,1)S(1)} %collective-permute-done.20.refs_0_, ...), custom_call_target="tpu_custom_call" | custom-call | tf_op jit(solution)/shard_map/pallas_call | solution.py:739
  82.6 0.7 collective-permute-done.18.refs_0_
  83.3 7.2 %collective-permute-done.19.refs_1_ = bf16[576,128]{1,0:T(8,128)(2,1)S(1)} collective-permute-done((bf16[576,128]{1,0:T(8,128)(2,1)S(1)}, bf16[576,128]{1,0:T(8,128)(2,1)S(1)}, u32[]{:S(2)}, u32[]{:S(2)}) %collective-permute-start.19) | collective-permute-done | bytes 147488 | tf_op jit(solution)/shard_map/ppermute | solution.py:31
  90.5 1.7 %shard_map.123 = f32[512,1152]{1,0:T(8,128)} custom-call(s32[1]{0:T(128)} %bitcast.slot_ref, f32[512,1152]{1,0:T(8,128)S(1)} %shard_map.115.after_ref, bf16[576,1152]{1,0:T(8,128)(2,1)S(1)} %copy-done.2, f32[6,1152]{1,0:T(8,128)S(1)} %get-tuple-element.39.refs_13_.refs_8_.modulation_ref, ...), custom_call_target="tpu_custom_call", output_to_operand_aliasing={{}: (6, {})} | custom-call | tf_op jit(solution)/shard_map/pallas_call | solution.py:739
  (30 shorter events, 0.1 us)
Async XLA Ops:
  0.0 4.3 %copy-start.8 = (bf16[512,1152]{1,0:T(8,128)(2,1)S(1)}, bf16[512,1152]{1,0:T(8,128)(2,1)}, u32[]{:S(2)}) copy-start(bf16[512,1152]{1,0:T(8,128)(2,1)} %kv_ref.3) | copy-start | bytes 3538948
  1.2 15.0 %collective-permute-start.1 = (bf16[512,512]{1,0:T(8,128)(2,1)S(1)}, bf16[512,512]{1,0:T(8,128)(2,1)S(1)}, u32[]{:S(2)}, u32[]{:S(2)}) collective-permute-start(bf16[512,512]{1,0:T(8,128)(2,1)S(1)} %first.1), channel_id=1, source_target_pairs={{0,2},{1,3},{2,0},{3,1},{4,6},{5,7},{6,4},{7,5},{8,10},{9,11},{10,... | collective-permute-start | bytes 1572872 | tf_op jit(solution)/shard_map/ppermute | solution.py:31
  4.3 32.4 %collective-permute-start = (bf16[512,1152]{1,0:T(8,128)(2,1)S(1)}, bf16[512,1152]{1,0:T(8,128)(2,1)S(1)}, u32[]{:S(2)}, u32[]{:S(2)}) collective-permute-start(bf16[512,1152]{1,0:T(8,128)(2,1)S(1)} %copy-done.8), channel_id=1, source_target_pairs={{0,1},{1,0},{2,3},{3,2},{4,5},{5,4},{6,7},{7,6},{8,9},{9,8},{10,11... | collective-permute-start | bytes 3538952 | tf_op jit(solution)/shard_map/ppermute | solution.py:31
  16.2 19.0 %collective-permute-start.3 = (bf16[512,512]{1,0:T(8,128)(2,1)S(1)}, bf16[512,512]{1,0:T(8,128)(2,1)S(1)}, u32[]{:S(2)}, u32[]{:S(2)}) collective-permute-start(bf16[512,512]{1,0:T(8,128)(2,1)S(1)} %collective-permute-done.1.refs_3_), channel_id=1, source_target_pairs={{0,1},{1,0},{2,3},{3,2},{4,5},{5,4},{6,7},{7,6},{8,9},{9,8},{10,11... | collective-permute-start | bytes 1572872 | tf_op jit(solution)/shard_map/ppermute | solution.py:31
  16.2 11.0 %copy-start.3 = (bf16[3,1152,576]{1,2,0:T(8,128)(2,1)S(1)}, bf16[3,1152,576]{1,2,0:T(8,128)(2,1)}, u32[]{:S(2)}) copy-start(bf16[3,1152,576]{1,2,0:T(8,128)(2,1)} %param.17) | copy-start | bytes 11943940
  16.2 11.0 %copy-start.4 = (f32[6,1152]{1,0:T(8,128)S(1)}, f32[6,1152]{1,0:T(8,128)}, u32[]{:S(2)}) copy-start(f32[6,1152]{1,0:T(8,128)} %refs_1_.1) | copy-start | bytes 82948
  16.2 11.0 %copy-start.5 = (f32[6,1152]{1,0:T(8,128)S(1)}, f32[6,1152]{1,0:T(8,128)}, u32[]{:S(2)}) copy-start(f32[6,1152]{1,0:T(8,128)} %refs_2_.1) | copy-start | bytes 82948
  16.2 11.0 %copy-start.6 = (s32[4]{0:T(128)S(1)}, s32[4]{0:T(128)}, u32[]{:S(2)}) copy-start(s32[4]{0:T(128)} %order_ref.1) | copy-start | bytes 52
  16.3 11.0 %copy-start.7 = (f32[1,576]{1,0:T(1,128)S(1)}, f32[1,576]{1,0:T(1,128)}, u32[]{:S(2)}) copy-start(f32[1,576]{1,0:T(1,128)} %constant.22.clone.refs_0_) | copy-start | bytes 6916
  18.0 9.2 %collective-permute-start.2 = (bf16[512,256]{1,0:T(8,128)(2,1)S(1)}, bf16[512,256]{1,0:T(8,128)(2,1)S(1)}, u32[]{:S(2)}, u32[]{:S(2)}) collective-permute-start(bf16[512,256]{1,0:T(8,128)(2,1)S(1)} %get-tuple-element.31), channel_id=1, source_target_pairs={{0,2},{1,3},{2,0},{3,1},{4,6},{5,7},{6,4},{7,5},{8,10},{9,11},{10,... | collective-permute-start | bytes 786440 | tf_op jit(solution)/shard_map/ppermute | solution.py:31
  19.8 12.6 %collective-permute-start.5 = (bf16[512,256]{1,0:T(8,128)(2,1)S(1)}, bf16[512,256]{1,0:T(8,128)(2,1)S(1)}, u32[]{:S(2)}, u32[]{:S(2)}) collective-permute-start(bf16[512,256]{1,0:T(8,128)(2,1)S(1)} %get-tuple-element.33), channel_id=1, source_target_pairs={{0,2},{1,3},{2,0},{3,1},{4,6},{5,7},{6,4},{7,5},{8,10},{9,11},{10,... | collective-permute-start | bytes 786440 | tf_op jit(solution)/shard_map/ppermute | solution.py:31
  20.1 38.3 %collective-permute-start.9 = (bf16[128,1152]{1,0:T(8,128)(2,1)S(1)}, bf16[128,1152]{1,0:T(8,128)(2,1)S(1)}, u32[]{:S(2)}, u32[]{:S(2)}) collective-permute-start(bf16[128,1152]{1,0:T(8,128)(2,1)S(1)} %get-tuple-element.28.refs_6_.refs_3_), channel_id=1, source_target_pairs={{0,12},{1,13},{2,14},{3,15},{4,8},{5,9},{6,10},{7,11},{8,4},{9,5},... | collective-permute-start | bytes 884744 | tf_op jit(solution)/shard_map/ppermute | solution.py:31
  27.2 14.7 %collective-permute-start.4 = (bf16[512,256]{1,0:T(8,128)(2,1)S(1)}, bf16[512,256]{1,0:T(8,128)(2,1)S(1)}, u32[]{:S(2)}, u32[]{:S(2)}) collective-permute-start(bf16[512,256]{1,0:T(8,128)(2,1)S(1)} %collective-permute-done.2.refs_4_), channel_id=1, source_target_pairs={{0,1},{1,0},{2,3},{3,2},{4,5},{5,4},{6,7},{7,6},{8,9},{9,8},{10,11... | collective-permute-start | bytes 786440 | tf_op jit(solution)/shard_map/ppermute | solution.py:31
  32.4 26.1 %collective-permute-start.12 = (bf16[128,1152]{1,0:T(8,128)(2,1)S(1)}, bf16[128,1152]{1,0:T(8,128)(2,1)S(1)}, u32[]{:S(2)}, u32[]{:S(2)}) collective-permute-start(bf16[128,1152]{1,0:T(8,128)(2,1)S(1)} %get-tuple-element.27.refs_5_.refs_2_), channel_id=1, source_target_pairs={{0,8},{1,9},{2,10},{3,11},{4,12},{5,13},{6,14},{7,15},{8,0},{9,1},... | collective-permute-start | bytes 884744 | tf_op jit(solution)/shard_map/ppermute | solution.py:31
  35.2 5.0 %collective-permute-start.6 = (bf16[512,128]{1,0:T(8,128)(2,1)S(1)}, bf16[512,128]{1,0:T(8,128)(2,1)S(1)}, u32[]{:S(2)}, u32[]{:S(2)}) collective-permute-start(bf16[512,128]{1,0:T(8,128)(2,1)S(1)} %get-tuple-element.34), channel_id=1, source_target_pairs={{0,2},{1,3},{2,0},{3,1},{4,6},{5,7},{6,4},{7,5},{8,10},{9,11},{10,... | collective-permute-start | bytes 393224 | tf_op jit(solution)/shard_map/ppermute | solution.py:31
  36.7 9.2 %collective-permute-start.7 = (bf16[512,256]{1,0:T(8,128)(2,1)S(1)}, bf16[512,256]{1,0:T(8,128)(2,1)S(1)}, u32[]{:S(2)}, u32[]{:S(2)}) collective-permute-start(bf16[512,256]{1,0:T(8,128)(2,1)S(1)} %collective-permute-done.5.refs_5_), channel_id=1, source_target_pairs={{0,1},{1,0},{2,3},{3,2},{4,5},{5,4},{6,7},{7,6},{8,9},{9,8},{10,11... | collective-permute-start | bytes 786440 | tf_op jit(solution)/shard_map/ppermute | solution.py:31
  40.3 25.7 %collective-permute-start.13 = (bf16[128,1152]{1,0:T(8,128)(2,1)S(1)}, bf16[128,1152]{1,0:T(8,128)(2,1)S(1)}, u32[]{:S(2)}, u32[]{:S(2)}) collective-permute-start(bf16[128,1152]{1,0:T(8,128)(2,1)S(1)} %get-tuple-element.26.refs_4_.refs_1_), channel_id=1, source_target_pairs={{0,4},{1,5},{2,6},{3,7},{4,0},{5,1},{6,2},{7,3},{8,12},{9,13},{10,... | collective-permute-start | bytes 884744 | tf_op jit(solution)/shard_map/ppermute | solution.py:31
  41.9 3.8 %collective-permute-start.8 = (bf16[512,128]{1,0:T(8,128)(2,1)S(1)}, bf16[512,128]{1,0:T(8,128)(2,1)S(1)}, u32[]{:S(2)}, u32[]{:S(2)}) collective-permute-start(bf16[512,128]{1,0:T(8,128)(2,1)S(1)} %collective-permute-done.6.refs_6_), channel_id=1, source_target_pairs={{0,1},{1,0},{2,3},{3,2},{4,5},{5,4},{6,7},{7,6},{8,9},{9,8},{10,11... | collective-permute-start | bytes 393224 | tf_op jit(solution)/shard_map/ppermute | solution.py:31
  45.7 15.8 %collective-permute-start.10 = (bf16[256,128]{1,0:T(8,128)(2,1)S(1)}, bf16[256,128]{1,0:T(8,128)(2,1)S(1)}, u32[]{:S(2)}, u32[]{:S(2)}) collective-permute-start(bf16[256,128]{1,0:T(8,128)(2,1)S(1)} %get-tuple-element.38.refs_10_), channel_id=1, source_target_pairs={{0,12},{1,13},{2,14},{3,15},{4,8},{5,9},{6,10},{7,11},{8,4},{9,5},... | collective-permute-start | bytes 196616 | tf_op jit(solution)/shard_map/ppermute | solution.py:31
  48.3 13.1 %collective-permute-start.11 = (bf16[320,128]{1,0:T(8,128)(2,1)S(1)}, bf16[320,128]{1,0:T(8,128)(2,1)S(1)}, u32[]{:S(2)}, u32[]{:S(2)}) collective-permute-start(bf16[320,128]{1,0:T(8,128)(2,1)S(1)} %shard_map.114.refs_11_), channel_id=1, source_target_pairs={{0,12},{1,13},{2,14},{3,15},{4,8},{5,9},{6,10},{7,11},{8,4},{9,5},... | collective-permute-start | bytes 245768 | tf_op jit(solution)/shard_map/ppermute | solution.py:31
  56.2 7.2 %copy-start = (bf16[3,1152,576]{1,2,0:T(8,128)(2,1)S(1)}, bf16[3,1152,576]{1,2,0:T(8,128)(2,1)}, u32[]{:S(2)}) copy-start(bf16[3,1152,576]{1,2,0:T(8,128)(2,1)} %param.19) | copy-start | bytes 11943940
  56.2 7.2 %copy-start.1 = (bf16[576,1152]{1,0:T(8,128)(2,1)S(1)}, bf16[576,1152]{1,0:T(8,128)(2,1)}, u32[]{:S(2)}) copy-start(bf16[576,1152]{1,0:T(8,128)(2,1)} %refs_6_.3) | copy-start | bytes 3981316
  58.4 7.6 %collective-permute-start.14 = (bf16[256,128]{1,0:T(8,128)(2,1)S(1)}, bf16[256,128]{1,0:T(8,128)(2,1)S(1)}, u32[]{:S(2)}, u32[]{:S(2)}) collective-permute-start(bf16[256,128]{1,0:T(8,128)(2,1)S(1)} %get-tuple-element.37.refs_8_), channel_id=1, source_target_pairs={{0,8},{1,9},{2,10},{3,11},{4,12},{5,13},{6,14},{7,15},{8,0},{9,1},... | collective-permute-start | bytes 196616 | tf_op jit(solution)/shard_map/ppermute | solution.py:31
  58.5 9.5 %collective-permute-start.15 = (bf16[320,128]{1,0:T(8,128)(2,1)S(1)}, bf16[320,128]{1,0:T(8,128)(2,1)S(1)}, u32[]{:S(2)}, u32[]{:S(2)}) collective-permute-start(bf16[320,128]{1,0:T(8,128)(2,1)S(1)} %shard_map.113.refs_9_), channel_id=1, source_target_pairs={{0,8},{1,9},{2,10},{3,11},{4,12},{5,13},{6,14},{7,15},{8,0},{9,1},... | collective-permute-start | bytes 245768 | tf_op jit(solution)/shard_map/ppermute | solution.py:31
  61.4 6.6 %collective-permute-start.16 = (bf16[256,128]{1,0:T(8,128)(2,1)S(1)}, bf16[256,128]{1,0:T(8,128)(2,1)S(1)}, u32[]{:S(2)}, u32[]{:S(2)}) collective-permute-start(bf16[256,128]{1,0:T(8,128)(2,1)S(1)} %get-tuple-element.36.refs_6_), channel_id=1, source_target_pairs={{0,4},{1,5},{2,6},{3,7},{4,0},{5,1},{6,2},{7,3},{8,12},{9,13},{10,... | collective-permute-start | bytes 196616 | tf_op jit(solution)/shard_map/ppermute | solution.py:31
  61.4 7.5 %collective-permute-start.17 = (bf16[320,128]{1,0:T(8,128)(2,1)S(1)}, bf16[320,128]{1,0:T(8,128)(2,1)S(1)}, u32[]{:S(2)}, u32[]{:S(2)}) collective-permute-start(bf16[320,128]{1,0:T(8,128)(2,1)S(1)} %shard_map.112.refs_7_), channel_id=1, source_target_pairs={{0,4},{1,5},{2,6},{3,7},{4,0},{5,1},{6,2},{7,3},{8,12},{9,13},{10,... | collective-permute-start | bytes 245768 | tf_op jit(solution)/shard_map/ppermute | solution.py:31
  73.7 7.0 %collective-permute-start.20 = (bf16[576,128]{1,0:T(8,128)(2,1)S(1)}, bf16[576,128]{1,0:T(8,128)(2,1)S(1)}, u32[]{:S(2)}, u32[]{:S(2)}) collective-permute-start(bf16[576,128]{1,0:T(8,128)(2,1)S(1)} %shard_map.120), channel_id=1, source_target_pairs={{0,4},{1,5},{2,6},{3,7},{4,0},{5,1},{6,2},{7,3},{8,12},{9,13},{10,... | collective-permute-start | bytes 442376 | tf_op jit(solution)/shard_map/ppermute | solution.py:31
  74.8 8.5 %collective-permute-start.18 = (bf16[576,128]{1,0:T(8,128)(2,1)S(1)}, bf16[576,128]{1,0:T(8,128)(2,1)S(1)}, u32[]{:S(2)}, u32[]{:S(2)}) collective-permute-start(bf16[576,128]{1,0:T(8,128)(2,1)S(1)} %shard_map.118), channel_id=1, source_target_pairs={{0,12},{1,13},{2,14},{3,15},{4,8},{5,9},{6,10},{7,11},{8,4},{9,5},... | collective-permute-start | bytes 442376 | tf_op jit(solution)/shard_map/ppermute | solution.py:31
  75.0 15.4 %collective-permute-start.19 = (bf16[576,128]{1,0:T(8,128)(2,1)S(1)}, bf16[576,128]{1,0:T(8,128)(2,1)S(1)}, u32[]{:S(2)}, u32[]{:S(2)}) collective-permute-start(bf16[576,128]{1,0:T(8,128)(2,1)S(1)} %shard_map.119), channel_id=1, source_target_pairs={{0,8},{1,9},{2,10},{3,11},{4,12},{5,13},{6,14},{7,15},{8,0},{9,1},... | collective-permute-start | bytes 442376 | tf_op jit(solution)/shard_map/ppermute | solution.py:31
  79.5 1.3 %copy-start.2 = (bf16[576,1152]{1,0:T(8,128)(2,1)S(1)}, bf16[576,1152]{1,0:T(8,128)(2,1)}, u32[]{:S(2)}) copy-start(bf16[576,1152]{1,0:T(8,128)(2,1)} %weight_ref.3) | copy-start | bytes 3981316

commit v8 on v7

--- a/solution.py
+++ b/solution.py
@@ -285,7 +285,7 @@
     return groups
 
 
-def spatial_kernel(*refs, group, frames, head_dim, width, tiles, held, emitted, kept, columns, chunks):
+def spatial_kernel(*refs, group, frames, head_dim, width, tiles, held, emitted, kept, columns, chunks, merged):
     plan = pair_plan(width, head_dim)
     count = len(tiles)
     position = 0
@@ -301,6 +301,8 @@
     rows = query_ref.shape[0]
     piece = rows // frames
     covered = part_pieces(chunks, piece)
+    earlier = dict(zip(covered, refs[position : position + len(covered)])) if merged else {}
+    position += len(earlier)
     out_count = len(covered) if emitted else 0
     out_refs = dict(zip(covered, refs[position : position + out_count]))
     kept_ref = refs[position + out_count] if kept else None
@@ -392,9 +394,11 @@
         if emitted:
             for sub in range(QUERY_ROWS // piece):
                 cut = slice(sub * piece, (sub + 1) * piece)
-                out_refs[(at + sub * piece) // piece][...] = stack(
-                    [parts[tile][cut] for tile in emitted], columns
-                )
+                target = (at + sub * piece) // piece
+                value = stack([parts[tile][cut] for tile in emitted], columns)
+                if merged:
+                    value = jnp.concatenate([earlier[target][...], value], axis=0)
+                out_refs[target][...] = value
         parts.clear()
 
     score(0)
@@ -440,6 +444,11 @@
     return row_parts(len(PAIR_GROUPS) - 1, rows)
 
 
+def merged_pieces(rows, piece):
+    parts = target_parts(rows)
+    return part_pieces(parts[-2], piece) if len(parts) > 2 else []
+
+
 def input_halves(rows, piece):
     parts = [part_pieces(chunks, piece) for chunks in target_parts(rows)]
     if len(parts) < 3:
@@ -451,7 +460,12 @@
     parts = [part_pieces(chunks, piece) for chunks in target_parts(rows)]
     if len(parts) < 3:
         return [[s for part in parts for s in part]]
-    return [[s for part in parts[2:] for s in part], parts[0] + parts[1]]
+    return [[s for part in parts[:1] + parts[2:] for s in part], parts[1]]
+
+
+def back_parts(rows):
+    parts = target_parts(rows)
+    return parts[:1] + parts[2:-1] + parts[1:2] + parts[-1:] if len(parts) > 2 else parts
 
 
 def part_pieces(chunks, piece):
@@ -467,7 +481,7 @@
 
 
 def spatial_group(
-    number, part, query, own_kv, peer_kv, near, far, carry, frames, head_dim, width
+    number, part, query, own_kv, peer_kv, near, far, carry, earlier, frames, head_dim, width
 ):
     group = PAIR_GROUPS[number]
     held, emitted, kept = tile_flow(width, head_dim)[number]
@@ -479,12 +493,14 @@
     columns = emitted_columns(emitted, width)
     if emitted:
         count = len(chunks) * QUERY_ROWS // (rows // frames)
-        shapes += [((stack_rows(rows // frames, columns), LANES), bf16) for _ in range(count)]
+        length = stack_rows(rows // frames, columns) + (earlier[0].shape[0] if earlier else 0)
+        shapes += [((length, LANES), bf16) for _ in range(count)]
     if kept:
         shapes.append(((rows, len(kept) * LANES), bf16))
     operands = [query, own_kv, peer_kv, *near[:arrived], *far[:arrived]]
     if held:
         operands.append(carry)
+    operands += earlier
     keys = 4 * rows
     results = on_chip_call(
         functools.partial(
@@ -499,6 +515,7 @@
             kept=kept,
             columns=columns,
             chunks=chunks,
+            merged=bool(earlier),
         ),
         operands,
         shapes,
@@ -515,37 +532,36 @@
     return results, carry
 
 
-def joined_rows(tokens_refs, mixed_refs, columns, first, count):
-    groups = len(columns)
+def joined_rows(tokens_refs, mixed_refs, columns, counts):
     piece = tokens_refs[0].shape[0]
-    cut = slice(first, first + count)
-    tokens = jnp.concatenate([ref[cut, :] for ref in tokens_refs], axis=0).astype(f32)
-    mixed = jnp.concatenate(
-        [
+    tokens = jnp.concatenate([ref[...] for ref in tokens_refs], axis=0).astype(f32)
+    sizes = [stack_rows(piece, width) for width in columns]
+    rows, position = [], 0
+    for count in counts:
+        refs = mixed_refs[position : position + count]
+        position += count
+        if count == 1:
+            starts = [sum(sizes[:g]) for g in range(len(sizes))]
+            stacks = [refs[0][at : at + size, :] for at, size in zip(starts, sizes)]
+        else:
+            stacks = [ref[...] for ref in refs]
+        rows.append(
             jnp.concatenate(
-                [
-                    unstack(mixed_refs[frame * groups + g][...], piece, columns[g], first, count)
-                    for g in range(groups)
-                ],
-                axis=1,
+                [unstack(x, piece, width, 0, piece) for x, width in zip(stacks, columns)], axis=1
             )
-            for frame in range(len(tokens_refs))
-        ],
-        axis=0,
-    )
-    return tokens, mixed
-
-
-def temporal_in_kernel(*refs, members, columns):
-    groups, frames = len(columns), len(members)
+        )
+    return tokens, jnp.concatenate(rows, axis=0)
+
+
+def temporal_in_kernel(*refs, members, columns, counts):
+    frames = len(members)
+    mixed_end = frames + sum(counts)
     tokens_refs = refs[:frames]
-    mixed_refs = refs[frames : frames + frames * groups]
-    out_weight, qkv_weight, modulation_ref, place_ref, query_ref, kv_ref = refs[
-        frames + frames * groups :
-    ]
+    mixed_refs = refs[frames:mixed_end]
+    out_weight, qkv_weight, modulation_ref, place_ref, query_ref, kv_ref = refs[mixed_end:]
     width = out_weight.shape[0]
     piece = tokens_refs[0].shape[0]
-    tokens, mixed = joined_rows(tokens_refs, mixed_refs, columns, 0, piece)
+    tokens, mixed = joined_rows(tokens_refs, mixed_refs, columns, counts)
     after = tokens + modulation_ref[2:3, :] * jnp.dot(
         mixed, out_weight[...], preferred_element_type=f32
     )
@@ -573,7 +589,12 @@
     padded = -(-width // LANES) * LANES
     rows = len(members) * tokens[0].shape[0]
     return on_chip_call(
-        functools.partial(temporal_in_kernel, members=members, columns=columns),
+        functools.partial(
+            temporal_in_kernel,
+            members=members,
+            columns=columns,
+            counts=[len(mixed[s]) for s in members],
+        ),
         [
             *[tokens[s] for s in members],
             *[part for s in members for part in mixed[s]],
@@ -674,11 +695,10 @@
     )
 
 
-def after_kernel(*refs, frames, columns):
-    mixed_end = frames * (1 + len(columns))
+def after_kernel(*refs, frames, columns, counts):
+    mixed_end = frames + sum(counts)
     weight_ref, modulation_ref, out_ref = refs[mixed_end:]
-    piece = refs[0].shape[0]
-    tokens, mixed = joined_rows(refs[:frames], refs[frames:mixed_end], columns, 0, piece)
+    tokens, mixed = joined_rows(refs[:frames], refs[frames:mixed_end], columns, counts)
     out_ref[...] = tokens + modulation_ref[2:3, :] * jnp.dot(
         mixed, weight_ref[...], preferred_element_type=f32
     )
@@ -689,7 +709,9 @@
     width, feature_width = weight.shape
     rows = frames * tokens[0].shape[0]
     return on_chip_call(
-        functools.partial(after_kernel, frames=frames, columns=columns),
+        functools.partial(
+            after_kernel, frames=frames, columns=columns, counts=[len(part) for part in mixed]
+        ),
         [*tokens, *[part for frame in mixed for part in frame], weight, modulation],
         [((rows, feature_width), f32)],
         2 * rows * feature_width * width,
@@ -807,19 +829,35 @@
         width,
     )
 
+    merged = merged_pieces(rows, piece)
     carry = None
     local = [[] for _ in range(frames)]
     sent = [[] for _ in range(frames)]
     for number in range(len(PAIR_GROUPS)):
         handed = carry
         for part, chunks in enumerate(row_parts(number, rows)):
+            covered = part_pieces(chunks, piece)
+            held_back = number == len(PAIR_GROUPS) - 1 and covered == merged
             outs, carry = spatial_group(
-                number, part, query, own_kv, peer_kv, near, far, handed, frames, head_dim, width
+                number,
+                part,
+                query,
+                own_kv,
+                peer_kv,
+                near,
+                far,
+                handed,
+                [local[s].pop() for s in covered] if held_back else [],
+                frames,
+                head_dim,
+                width,
             )
-            covered = part_pieces(chunks, piece)
             for s, out in zip(covered, outs):
                 local[s].append(out)
-                sent[s].append(out if s == 0 else permute(out, ahead(s)))
+                if s == 0:
+                    sent[s].append(out)
+                elif s not in merged or held_back:
+                    sent[s].append(permute(out, ahead(s)))
 
     columns = group_columns(width, head_dim)
     after = after_spatial(pieces, local, columns, spatial_out, modulation)
@@ -831,7 +869,7 @@
     ]
     queries, kvs = [query for query, _ in inputs], [kv for _, kv in inputs]
     back = {}
-    for chunks in target_parts(rows):
+    for chunks in back_parts(rows):
         targets = part_pieces(chunks, piece)
         outs = temporal(queries, kvs, halves, frames, head_dim, targets)
         for s, out in zip(targets, outs):

time: 92.5 us -> 89.2 us (0.964)
  waiting for transfers between devices: 26.7 us -> 24.6 us
  starting transfers between devices: 27.7 us -> 26.7 us
    ppermute x21 -> x20, waiting for transfers between devices: 26.7 us -> 24.6 us  [permute(): lax.ppermute(value, 'patch', [(source, target(source)) for source in rang...]
    ppermute x21 -> x20, starting transfers between devices: 27.7 us -> 26.7 us  [permute(): lax.ppermute(value, 'patch', [(source, target(source)) for source in rang...]
  transfers between devices with their start and end apart: 21 -> 20, of which waited for: 8 -> 7; matrix products, arithmetic and copies ran while one was open for 0% -> 0% of each run, Pallas kernels for 31% -> 33%
where the time goes in v8:
time: 89.2 us; the launch traced here: 89.1 us
  Pallas kernels  36.6 us (41%)
  starting transfers between devices  26.7 us (30%)
  waiting for transfers between devices  24.6 us (28%)
  between operations  1.1 us (1%)
    ppermute x20, starting transfers between devices, permute(): lax.ppermute(value, 'patch', [(source, target(source)) for source in rang...  26.7 us
    pallas_call x13, Pallas kernels, on_chip_call(): pl.pallas_call(kernel, out_shape=[pltpu.VMEM(shape, dtype) for shape, dty...  26.3 us
    ppermute x20, waiting for transfers between devices, permute(): lax.ppermute(value, 'patch', [(source, target(source)) for source in rang...  24.6 us
    pallas_call x1, Pallas kernels, projections(): pl.pallas_call(functools.partial(projection_kernel, frames=frames, width=...  3.95 us
    pallas_call x2, Pallas kernels, output(): pl.pallas_call(functools.partial(output_kernel, frames=frames, members=me...  3.45 us
  transfers between devices with their start and end apart: 20, of which 7 were waited for; matrix products, arithmetic and copies ran while one was open for 0% of the time, Pallas kernels for 33%

profile of v8, /device:TPU:0, one launch (start us, length us, event | category | flops | bytes accessed | tf_op | source)
XLA Modules:
  0.0 89.1 jit_solution(11646601507126966336)
XLA Ops:
  0.0 1.2 %first.1 = bf16[512,512]{1,0:T(8,128)(2,1)S(1)} custom-call(bf16[512,1152]{1,0:T(8,128)(2,1)} %kv_ref.3), custom_call_target="tpu_custom_call" | custom-call | tf_op jit(solution)/shard_map/first/pallas_call | solution.py:107
  1.2 3.1 %collective-permute-start.1 = (bf16[512,512]{1,0:T(8,128)(2,1)S(1)}, bf16[512,512]{1,0:T(8,128)(2,1)S(1)}, u32[]{:S(2)}, u32[]{:S(2)}) collective-permute-start(bf16[512,512]{1,0:T(8,128)(2,1)S(1)} %first.1), channel_id=1, source_target_pairs={{0,2},{1,3},{2,0},{3,1},{4,6},{5,7},{6,4},{7,5},{8,10},{9,11},{10,... | collective-permute-start | bytes 1572872 | tf_op jit(solution)/shard_map/ppermute | solution.py:31
  4.3 0.0 collective-permute-start
  4.3 11.9 %collective-permute-done.1.refs_3_ = bf16[512,512]{1,0:T(8,128)(2,1)S(1)} collective-permute-done((bf16[512,512]{1,0:T(8,128)(2,1)S(1)}, bf16[512,512]{1,0:T(8,128)(2,1)S(1)}, u32[]{:S(2)}, u32[]{:S(2)}) %collective-permute-start.1) | collective-permute-done | bytes 524320 | tf_op jit(solution)/shard_map/ppermute | solution.py:31
  16.2 0.0 copy-start.6
  16.3 0.0 copy-start.7
  16.3 1.7 %pieces.1 = (bf16[128,1152]{1,0:T(8,128)(2,1)S(1)}, bf16[128,1152]{1,0:T(8,128)(2,1)S(1)}, bf16[128,1152]{1,0:T(8,128)(2,1)S(1)}, bf16[128,1152]{1,0:T(8,128)(2,...) custom-call(s32[1]{0:T(128)} %bitcast.slot_ref, ...), custom_call_target="tpu_custom_call" | custom-call | flops 4000000000 | bytes 2359296 | tf_op jit(solution)/shard_map/pieces/pallas_call | solution.py:140
  18.0 1.8 %collective-permute-start.2 = (bf16[512,256]{1,0:T(8,128)(2,1)S(1)}, bf16[512,256]{1,0:T(8,128)(2,1)S(1)}, u32[]{:S(2)}, u32[]{:S(2)}) collective-permute-start(bf16[512,256]{1,0:T(8,128)(2,1)S(1)} %get-tuple-element.31), channel_id=1, source_target_pairs={{0,2},{1,3},{2,0},{3,1},{4,6},{5,7},{6,4},{7,5},{8,10},{9,11},{10,... | collective-permute-start | bytes 786440 | tf_op jit(solution)/shard_map/ppermute | solution.py:31
  19.8 0.3 collective-permute-start.5
  20.1 3.8 %collective-permute-start.9 = (bf16[128,1152]{1,0:T(8,128)(2,1)S(1)}, bf16[128,1152]{1,0:T(8,128)(2,1)S(1)}, u32[]{:S(2)}, u32[]{:S(2)}) collective-permute-start(bf16[128,1152]{1,0:T(8,128)(2,1)S(1)} %get-tuple-element.28.refs_6_.refs_3_), channel_id=1, source_target_pairs={{0,12},{1,13},{2,14},{3,15},{4,8},{5,9},{6,10},{7,11},{8,4},{9,5},... | collective-permute-start | bytes 884744 | tf_op jit(solution)/shard_map/ppermute | solution.py:31
  24.6 2.7 %collective-permute-done.2.refs_4_ = bf16[512,256]{1,0:T(8,128)(2,1)S(1)} collective-permute-done((bf16[512,256]{1,0:T(8,128)(2,1)S(1)}, bf16[512,256]{1,0:T(8,128)(2,1)S(1)}, u32[]{:S(2)}, u32[]{:S(2)}) %collective-permute-start.2) | collective-permute-done | bytes 262176 | tf_op jit(solution)/shard_map/ppermute | solution.py:31
  27.2 0.0 collective-permute-start.4
  27.3 3.9 %projections.1 = (bf16[512,640]{1,0:T(8,128)(2,1)S(1)}, bf16[512,1152]{1,0:T(8,128)(2,1)S(1)}, f32[6,1152]{1,0:T(8,128)S(1)}, f32[4,1152]{1,0:T(4,128)S(1)}) custom-call(s32[1]{0:T(128)} %bitcast.slot_ref, s32[1]{0:T(128)S(6)} %copy.14.time_ref, s32[4]{0:T(128)S(1)} %copy-done.6, bf16[1728,1152]{1,0:T(8,128)(2,1)S(1)} %bitcast.9, f32[1,576]{1,0:T(1,128)S(1)} %copy-done.7, ...), custom_call_target="tpu_custom_call" | custom-call | flops 2038431744 | bytes 3981312 | tf_op jit(solution)/shard_map/projections/pallas_call | solution.py:207
  31.2 1.1 %collective-permute-done.5.refs_5_ = bf16[512,256]{1,0:T(8,128)(2,1)S(1)} collective-permute-done((bf16[512,256]{1,0:T(8,128)(2,1)S(1)}, bf16[512,256]{1,0:T(8,128)(2,1)S(1)}, u32[]{:S(2)}, u32[]{:S(2)}) %collective-permute-start.5) | collective-permute-done | bytes 262176 | tf_op jit(solution)/shard_map/ppermute | solution.py:31
  32.4 2.8 %collective-permute-start.12 = (bf16[128,1152]{1,0:T(8,128)(2,1)S(1)}, bf16[128,1152]{1,0:T(8,128)(2,1)S(1)}, u32[]{:S(2)}, u32[]{:S(2)}) collective-permute-start(bf16[128,1152]{1,0:T(8,128)(2,1)S(1)} %get-tuple-element.27.refs_5_.refs_2_), channel_id=1, source_target_pairs={{0,8},{1,9},{2,10},{3,11},{4,12},{5,13},{6,14},{7,15},{8,0},{9,1},... | collective-permute-start | bytes 884744 | tf_op jit(solution)/shard_map/ppermute | solution.py:31
  35.2 1.5 %collective-permute-start.6 = (bf16[512,128]{1,0:T(8,128)(2,1)S(1)}, bf16[512,128]{1,0:T(8,128)(2,1)S(1)}, u32[]{:S(2)}, u32[]{:S(2)}) collective-permute-start(bf16[512,128]{1,0:T(8,128)(2,1)S(1)} %get-tuple-element.34), channel_id=1, source_target_pairs={{0,2},{1,3},{2,0},{3,1},{4,6},{5,7},{6,4},{7,5},{8,10},{9,11},{10,... | collective-permute-start | bytes 393224 | tf_op jit(solution)/shard_map/ppermute | solution.py:31
  36.7 3.5 %shard_map.109.refs_7_ = bf16[512,256]{1,0:T(8,128)(2,1)S(1)} custom-call(bf16[512,640]{1,0:T(8,128)(2,1)S(1)} %get-tuple-element.29.refs_0_, bf16[512,1152]{1,0:T(8,128)(2,1)S(1)} %get-tuple-element.30.refs_1_, bf16[512,1152]{1,0:T(8,128)(2,1)S(1)} %collective-permute-done.refs_2_, bf16[512,512]{1,0:T(8,128)(2,1)S(1)} %collective-permute-done.1.refs_3_, ...), custom_call_target="tpu_custom_call" | custom-call | flops 2147483648 | bytes 4063232 | tf_op jit(solution)/shard_map/pallas_call | solution.py:69
  40.3 1.6 %collective-permute-start.13 = (bf16[128,1152]{1,0:T(8,128)(2,1)S(1)}, bf16[128,1152]{1,0:T(8,128)(2,1)S(1)}, u32[]{:S(2)}, u32[]{:S(2)}) collective-permute-start(bf16[128,1152]{1,0:T(8,128)(2,1)S(1)} %get-tuple-element.26.refs_4_.refs_1_), channel_id=1, source_target_pairs={{0,4},{1,5},{2,6},{3,7},{4,0},{5,1},{6,2},{7,3},{8,12},{9,13},{10,... | collective-permute-start | bytes 884744 | tf_op jit(solution)/shard_map/ppermute | solution.py:31
  41.9 0.0 collective-permute-done.4.refs_6_.refs_8_
  41.9 0.2 collective-permute-start.8
  42.1 3.5 %shard_map.110 = (bf16[256,128]{1,0:T(8,128)(2,1)S(1)}, bf16[256,128]{1,0:T(8,128)(2,1)S(1)}, bf16[256,128]{1,0:T(8,128)(2,1)S(1)}, bf16[256,128]{1,0:T(8,128)(2,1)S(1)}, bf16[512,128]{1,0:T(8,128)(2,1)S(1)}) custom-call(bf16[512,640]{1,0:T(8,128)(2,1)S(1)} %get-tuple-element.29.refs_0_, bf16[512,1152]{1,0:T(8,128)(2,1)S(1)} %get-tuple-element.30.refs_1_, ...), custom_call_target="tpu_custom_call" | custom-call | flops 2147483648 | bytes 4849664 | tf_op jit(solution)/shard_map/pallas_call | solution.py:69
  45.7 0.3 collective-permute-start.10
  46.0 2.3 %shard_map.114.refs_10_ = bf16[320,128]{1,0:T(8,128)(2,1)S(1)} custom-call(bf16[512,640]{1,0:T(8,128)(2,1)S(1)} %get-tuple-element.29.refs_0_, bf16[512,1152]{1,0:T(8,128)(2,1)S(1)} %get-tuple-element.30.refs_1_, bf16[512,1152]{1,0:T(8,128)(2,1)S(1)} %collective-permute-done.refs_2_, bf16[512,512]{1,0:T(8,128)(2,1)S(1)} %collective-permute-done.1.refs_3_, ...), custom_call_target="tpu_custom_call" | custom-call | flops 1073741824 | bytes 5505024 | tf_op jit(solution)/shard_map/pallas_call | solution.py:69
  48.3 3.7 %collective-permute-start.11 = (bf16[320,128]{1,0:T(8,128)(2,1)S(1)}, bf16[320,128]{1,0:T(8,128)(2,1)S(1)}, u32[]{:S(2)}, u32[]{:S(2)}) collective-permute-start(bf16[320,128]{1,0:T(8,128)(2,1)S(1)} %shard_map.114.refs_10_), channel_id=1, source_target_pairs={{0,12},{1,13},{2,14},{3,15},{4,8},{5,9},{6,10},{7,11},{8,4},{9,5},... | collective-permute-start | bytes 245768 | tf_op jit(solution)/shard_map/ppermute | solution.py:31
  52.0 2.1 %shard_map.111.refs_5_.refs_3_ = bf16[320,128]{1,0:T(8,128)(2,1)S(1)} custom-call(bf16[512,640]{1,0:T(8,128)(2,1)S(1)} %get-tuple-element.29.refs_0_, bf16[512,1152]{1,0:T(8,128)(2,1)S(1)} %get-tuple-element.30.refs_1_, bf16[512,1152]{1,0:T(8,128)(2,1)S(1)} %collective-permute-done.refs_2_, bf16[512,512]{1,0:T(8,128)(2,1)S(1)} %collective-permute-done.1.refs_3_, ...), custom_call_target="tpu_custom_call" | custom-call | flops 1073741824 | bytes 5505024 | tf_op jit(solution)/shard_map/pallas_call | solution.py:69
  54.1 2.1 %shard_map.112.refs_6_ = bf16[576,128]{1,0:T(8,128)(2,1)S(1)} custom-call(bf16[512,640]{1,0:T(8,128)(2,1)S(1)} %get-tuple-element.29.refs_0_, bf16[512,1152]{1,0:T(8,128)(2,1)S(1)} %get-tuple-element.30.refs_1_, bf16[512,1152]{1,0:T(8,128)(2,1)S(1)} %collective-permute-done.refs_2_, bf16[512,512]{1,0:T(8,128)(2,1)S(1)} %collective-permute-done.1.refs_3_, ...), custom_call_target="tpu_custom_call" | custom-call | flops 1073741824 | bytes 5570560 | tf_op jit(solution)/shard_map/pallas_call | solution.py:69
  56.2 0.0 copy-start
  56.3 0.0 copy-start.1
  56.3 0.1 collective-permute-start.16
  56.4 2.1 %shard_map.113.refs_8_ = bf16[320,128]{1,0:T(8,128)(2,1)S(1)} custom-call(bf16[512,640]{1,0:T(8,128)(2,1)S(1)} %get-tuple-element.29.refs_0_, bf16[512,1152]{1,0:T(8,128)(2,1)S(1)} %get-tuple-element.30.refs_1_, bf16[512,1152]{1,0:T(8,128)(2,1)S(1)} %collective-permute-done.refs_2_, bf16[512,512]{1,0:T(8,128)(2,1)S(1)} %collective-permute-done.1.refs_3_, ...), custom_call_target="tpu_custom_call" | custom-call | flops 1073741824 | bytes 5505024 | tf_op jit(solution)/shard_map/pallas_call | solution.py:69
  58.5 0.8 collective-permute-start.14
  59.4 2.2 %collective-permute-start.15 = (bf16[320,128]{1,0:T(8,128)(2,1)S(1)}, bf16[320,128]{1,0:T(8,128)(2,1)S(1)}, u32[]{:S(2)}, u32[]{:S(2)}) collective-permute-start(bf16[320,128]{1,0:T(8,128)(2,1)S(1)} %shard_map.113.refs_8_), channel_id=1, source_target_pairs={{0,8},{1,9},{2,10},{3,11},{4,12},{5,13},{6,14},{7,15},{8,0},{9,1},... | collective-permute-start | bytes 245768 | tf_op jit(solution)/shard_map/ppermute | solution.py:31
  61.5 2.5 %shard_map.116 = (bf16[256,640]{1,0:T(8,128)(2,1)S(1)}, bf16[256,1152]{1,0:T(8,128)(2,1)S(1)}) custom-call(bf16[128,1152]{1,0:T(8,128)(2,1)S(1)} %get-tuple-element.25.refs_3_.refs_0_, bf16[128,1152]{1,0:T(8,128)(2,1)S(1)} %collective-permute-done.9.refs_1_, bf16[256,128]{1,0:T(8,128)(2,1)S(1)} %get-tuple-element.32.refs_4_.refs_2_, ...), custom_call_target="tpu_custom_call" | custom-call | flops 1358954496 | bytes 6239232 | tf_op jit(solution)/shard_map/pallas_call | solution.py:69
  64.1 3.2 %collective-permute-done.14.refs_2_ = bf16[256,128]{1,0:T(8,128)(2,1)S(1)} collective-permute-done((bf16[256,128]{1,0:T(8,128)(2,1)S(1)}, bf16[256,128]{1,0:T(8,128)(2,1)S(1)}, u32[]{:S(2)}, u32[]{:S(2)}) %collective-permute-start.14) | collective-permute-done | bytes 65568 | tf_op jit(solution)/shard_map/ppermute | solution.py:31
  67.2 0.9 collective-permute-done.15.refs_3_
  68.1 2.5 %shard_map.117 = (bf16[256,640]{1,0:T(8,128)(2,1)S(1)}, bf16[256,1152]{1,0:T(8,128)(2,1)S(1)}) custom-call(bf16[128,1152]{1,0:T(8,128)(2,1)S(1)} %collective-permute-done.12.refs_0_, bf16[128,1152]{1,0:T(8,128)(2,1)S(1)} %collective-permute-done.13.refs_1_, bf16[256,128]{1,0:T(8,128)(2,1)S(1)} %collective-permute-done.14.refs_2_, ...), custom_call_target="tpu_custom_call" | custom-call | flops 1358954496 | bytes 6239232 | tf_op jit(solution)/shard_map/pallas_call | solution.py:69
  70.6 1.0 %shard_map.119 = bf16[576,128]{1,0:T(8,128)(2,1)S(1)} custom-call(bf16[256,640]{1,0:T(8,128)(2,1)S(1)} %get-tuple-element.41.refs_0_, bf16[256,640]{1,0:T(8,128)(2,1)S(1)} %get-tuple-element.42.refs_1_, bf16[256,1152]{1,0:T(8,128)(2,1)S(1)} %get-tuple-element.43.refs_2_, bf16[256,1152]{1,0:T(8,128)(2,1)S(1)} %get-tuple-element.44.refs_3_), custom_call_target="tpu_custom_call" | custom-call | flops 268435456 | bytes 1835008 | tf_op jit(solution)/shard_map/pallas_call | solution.py:69
  71.7 1.2 %shard_map.120 = bf16[576,128]{1,0:T(8,128)(2,1)S(1)} custom-call(bf16[256,640]{1,0:T(8,128)(2,1)S(1)} %get-tuple-element.41.refs_0_, bf16[256,640]{1,0:T(8,128)(2,1)S(1)} %get-tuple-element.42.refs_1_, bf16[256,1152]{1,0:T(8,128)(2,1)S(1)} %get-tuple-element.43.refs_2_, bf16[256,1152]{1,0:T(8,128)(2,1)S(1)} %get-tuple-element.44.refs_3_), custom_call_target="tpu_custom_call" | custom-call | flops 268435456 | bytes 1835008 | tf_op jit(solution)/shard_map/pallas_call | solution.py:69
  72.9 1.5 %collective-permute-start.18 = (bf16[576,128]{1,0:T(8,128)(2,1)S(1)}, bf16[576,128]{1,0:T(8,128)(2,1)S(1)}, u32[]{:S(2)}, u32[]{:S(2)}) collective-permute-start(bf16[576,128]{1,0:T(8,128)(2,1)S(1)} %shard_map.119), channel_id=1, source_target_pairs={{0,12},{1,13},{2,14},{3,15},{4,8},{5,9},{6,10},{7,11},{8,4},{9,5},... | collective-permute-start | bytes 442376 | tf_op jit(solution)/shard_map/ppermute | solution.py:31
  74.4 1.0 %shard_map.118 = bf16[576,128]{1,0:T(8,128)(2,1)S(1)} custom-call(bf16[256,640]{1,0:T(8,128)(2,1)S(1)} %get-tuple-element.41.refs_0_, bf16[256,640]{1,0:T(8,128)(2,1)S(1)} %get-tuple-element.42.refs_1_, bf16[256,1152]{1,0:T(8,128)(2,1)S(1)} %get-tuple-element.43.refs_2_, bf16[256,1152]{1,0:T(8,128)(2,1)S(1)} %get-tuple-element.44.refs_3_), custom_call_target="tpu_custom_call" | custom-call | flops 268435456 | bytes 1835008 | tf_op jit(solution)/shard_map/pallas_call | solution.py:69
  75.4 3.0 %collective-permute-start.17 = (bf16[576,128]{1,0:T(8,128)(2,1)S(1)}, bf16[576,128]{1,0:T(8,128)(2,1)S(1)}, u32[]{:S(2)}, u32[]{:S(2)}) collective-permute-start(bf16[576,128]{1,0:T(8,128)(2,1)S(1)} %shard_map.118), channel_id=1, source_target_pairs={{0,8},{1,9},{2,10},{3,11},{4,12},{5,13},{6,14},{7,15},{8,0},{9,1},... | collective-permute-start | bytes 442376 | tf_op jit(solution)/shard_map/ppermute | solution.py:31
  78.4 1.2 %shard_map.115.after_ref = f32[512,1152]{1,0:T(8,128)S(1)} custom-call(bf16[128,1152]{1,0:T(8,128)(2,1)S(1)} %get-tuple-element.25.refs_3_.refs_0_, bf16[128,1152]{1,0:T(8,128)(2,1)S(1)} %get-tuple-element.26.refs_4_.refs_1_, bf16[128,1152]{1,0:T(8,128)(2,1)S(1)} %get-tuple-element.27.refs_5_.refs_2_, ...), custom_call_target="tpu_custom_call" | custom-call | flops 679477248 | bytes 3124224 | tf_op jit(solution)/shard_map/pallas_call | solution.py:69
  79.6 0.0 copy-start.2
  79.6 1.0 %shard_map.121.refs_2_ = bf16[576,128]{1,0:T(8,128)(2,1)S(1)} custom-call(bf16[256,640]{1,0:T(8,128)(2,1)S(1)} %get-tuple-element.41.refs_0_, bf16[256,640]{1,0:T(8,128)(2,1)S(1)} %get-tuple-element.42.refs_1_, bf16[256,1152]{1,0:T(8,128)(2,1)S(1)} %get-tuple-element.43.refs_2_, bf16[256,1152]{1,0:T(8,128)(2,1)S(1)} %get-tuple-element.44.refs_3_), custom_call_target="tpu_custom_call" | custom-call | flops 268435456 | bytes 1835008 | tf_op jit(solution)/shard_map/pallas_call | solution.py:69
  80.6 0.9 %collective-permute-done.18.refs_0_ = bf16[576,128]{1,0:T(8,128)(2,1)S(1)} collective-permute-done((bf16[576,128]{1,0:T(8,128)(2,1)S(1)}, bf16[576,128]{1,0:T(8,128)(2,1)S(1)}, u32[]{:S(2)}, u32[]{:S(2)}) %collective-permute-start.18) | collective-permute-done | bytes 147488 | tf_op jit(solution)/shard_map/ppermute | solution.py:31
  81.6 3.9 %collective-permute-done.19.refs_1_ = bf16[576,128]{1,0:T(8,128)(2,1)S(1)} collective-permute-done((bf16[576,128]{1,0:T(8,128)(2,1)S(1)}, bf16[576,128]{1,0:T(8,128)(2,1)S(1)}, u32[]{:S(2)}, u32[]{:S(2)}) %collective-permute-start.19) | collective-permute-done | bytes 147488 | tf_op jit(solution)/shard_map/ppermute | solution.py:31
  85.4 2.2 %shard_map.122.refs_1_ = f32[512,1152]{1,0:T(8,128)} custom-call(s32[1]{0:T(128)} %bitcast.slot_ref, f32[512,1152]{1,0:T(8,128)S(1)} %shard_map.115.after_ref, bf16[576,1152]{1,0:T(8,128)(2,1)S(1)} %copy-done.2, f32[6,1152]{1,0:T(8,128)S(1)} %get-tuple-element.39.refs_12_.refs_8_.refs_7_.modulation_ref, ...), custom_call_target="tpu_custom_call" | custom-call | tf_op jit(solution)/shard_map/pallas_call | solution.py:761
  87.6 1.3 %shard_map.123 = f32[512,1152]{1,0:T(8,128)} custom-call(s32[1]{0:T(128)} %bitcast.slot_ref, f32[512,1152]{1,0:T(8,128)S(1)} %shard_map.115.after_ref, bf16[576,1152]{1,0:T(8,128)(2,1)S(1)} %copy-done.2, f32[6,1152]{1,0:T(8,128)S(1)} %get-tuple-element.39.refs_12_.refs_8_.refs_7_.modulation_ref, ...), custom_call_target="tpu_custom_call", output_to_operand_aliasing={{}: (5, {})} | custom-call | tf_op jit(solution)/shard_map/pallas_call | solution.py:761
  (28 shorter events, 0.1 us)
Async XLA Ops:
  0.0 4.3 %copy-start.8 = (bf16[512,1152]{1,0:T(8,128)(2,1)S(1)}, bf16[512,1152]{1,0:T(8,128)(2,1)}, u32[]{:S(2)}) copy-start(bf16[512,1152]{1,0:T(8,128)(2,1)} %kv_ref.3) | copy-start | bytes 3538948
  1.2 15.0 %collective-permute-start.1 = (bf16[512,512]{1,0:T(8,128)(2,1)S(1)}, bf16[512,512]{1,0:T(8,128)(2,1)S(1)}, u32[]{:S(2)}, u32[]{:S(2)}) collective-permute-start(bf16[512,512]{1,0:T(8,128)(2,1)S(1)} %first.1), channel_id=1, source_target_pairs={{0,2},{1,3},{2,0},{3,1},{4,6},{5,7},{6,4},{7,5},{8,10},{9,11},{10,... | collective-permute-start | bytes 1572872 | tf_op jit(solution)/shard_map/ppermute | solution.py:31
  4.3 32.4 %collective-permute-start = (bf16[512,1152]{1,0:T(8,128)(2,1)S(1)}, bf16[512,1152]{1,0:T(8,128)(2,1)S(1)}, u32[]{:S(2)}, u32[]{:S(2)}) collective-permute-start(bf16[512,1152]{1,0:T(8,128)(2,1)S(1)} %copy-done.8), channel_id=1, source_target_pairs={{0,1},{1,0},{2,3},{3,2},{4,5},{5,4},{6,7},{7,6},{8,9},{9,8},{10,11... | collective-permute-start | bytes 3538952 | tf_op jit(solution)/shard_map/ppermute | solution.py:31
  16.2 19.0 %collective-permute-start.3 = (bf16[512,512]{1,0:T(8,128)(2,1)S(1)}, bf16[512,512]{1,0:T(8,128)(2,1)S(1)}, u32[]{:S(2)}, u32[]{:S(2)}) collective-permute-start(bf16[512,512]{1,0:T(8,128)(2,1)S(1)} %collective-permute-done.1.refs_3_), channel_id=1, source_target_pairs={{0,1},{1,0},{2,3},{3,2},{4,5},{5,4},{6,7},{7,6},{8,9},{9,8},{10,11... | collective-permute-start | bytes 1572872 | tf_op jit(solution)/shard_map/ppermute | solution.py:31
  16.2 11.0 %copy-start.3 = (bf16[3,1152,576]{1,2,0:T(8,128)(2,1)S(1)}, bf16[3,1152,576]{1,2,0:T(8,128)(2,1)}, u32[]{:S(2)}) copy-start(bf16[3,1152,576]{1,2,0:T(8,128)(2,1)} %param.17) | copy-start | bytes 11943940
  16.2 11.0 %copy-start.4 = (f32[6,1152]{1,0:T(8,128)S(1)}, f32[6,1152]{1,0:T(8,128)}, u32[]{:S(2)}) copy-start(f32[6,1152]{1,0:T(8,128)} %refs_1_.1) | copy-start | bytes 82948
  16.2 11.0 %copy-start.5 = (f32[6,1152]{1,0:T(8,128)S(1)}, f32[6,1152]{1,0:T(8,128)}, u32[]{:S(2)}) copy-start(f32[6,1152]{1,0:T(8,128)} %refs_2_.1) | copy-start | bytes 82948
  16.2 11.0 %copy-start.6 = (s32[4]{0:T(128)S(1)}, s32[4]{0:T(128)}, u32[]{:S(2)}) copy-start(s32[4]{0:T(128)} %order_ref.1) | copy-start | bytes 52
  16.3 11.0 %copy-start.7 = (f32[1,576]{1,0:T(1,128)S(1)}, f32[1,576]{1,0:T(1,128)}, u32[]{:S(2)}) copy-start(f32[1,576]{1,0:T(1,128)} %constant.22.clone.refs_0_) | copy-start | bytes 6916
  18.0 9.2 %collective-permute-start.2 = (bf16[512,256]{1,0:T(8,128)(2,1)S(1)}, bf16[512,256]{1,0:T(8,128)(2,1)S(1)}, u32[]{:S(2)}, u32[]{:S(2)}) collective-permute-start(bf16[512,256]{1,0:T(8,128)(2,1)S(1)} %get-tuple-element.31), channel_id=1, source_target_pairs={{0,2},{1,3},{2,0},{3,1},{4,6},{5,7},{6,4},{7,5},{8,10},{9,11},{10,... | collective-permute-start | bytes 786440 | tf_op jit(solution)/shard_map/ppermute | solution.py:31
  19.8 12.6 %collective-permute-start.5 = (bf16[512,256]{1,0:T(8,128)(2,1)S(1)}, bf16[512,256]{1,0:T(8,128)(2,1)S(1)}, u32[]{:S(2)}, u32[]{:S(2)}) collective-permute-start(bf16[512,256]{1,0:T(8,128)(2,1)S(1)} %get-tuple-element.33), channel_id=1, source_target_pairs={{0,2},{1,3},{2,0},{3,1},{4,6},{5,7},{6,4},{7,5},{8,10},{9,11},{10,... | collective-permute-start | bytes 786440 | tf_op jit(solution)/shard_map/ppermute | solution.py:31
  20.1 36.2 %collective-permute-start.9 = (bf16[128,1152]{1,0:T(8,128)(2,1)S(1)}, bf16[128,1152]{1,0:T(8,128)(2,1)S(1)}, u32[]{:S(2)}, u32[]{:S(2)}) collective-permute-start(bf16[128,1152]{1,0:T(8,128)(2,1)S(1)} %get-tuple-element.28.refs_6_.refs_3_), channel_id=1, source_target_pairs={{0,12},{1,13},{2,14},{3,15},{4,8},{5,9},{6,10},{7,11},{8,4},{9,5},... | collective-permute-start | bytes 884744 | tf_op jit(solution)/shard_map/ppermute | solution.py:31
  27.2 14.7 %collective-permute-start.4 = (bf16[512,256]{1,0:T(8,128)(2,1)S(1)}, bf16[512,256]{1,0:T(8,128)(2,1)S(1)}, u32[]{:S(2)}, u32[]{:S(2)}) collective-permute-start(bf16[512,256]{1,0:T(8,128)(2,1)S(1)} %collective-permute-done.2.refs_4_), channel_id=1, source_target_pairs={{0,1},{1,0},{2,3},{3,2},{4,5},{5,4},{6,7},{7,6},{8,9},{9,8},{10,11... | collective-permute-start | bytes 786440 | tf_op jit(solution)/shard_map/ppermute | solution.py:31
  32.4 31.7 %collective-permute-start.12 = (bf16[128,1152]{1,0:T(8,128)(2,1)S(1)}, bf16[128,1152]{1,0:T(8,128)(2,1)S(1)}, u32[]{:S(2)}, u32[]{:S(2)}) collective-permute-start(bf16[128,1152]{1,0:T(8,128)(2,1)S(1)} %get-tuple-element.27.refs_5_.refs_2_), channel_id=1, source_target_pairs={{0,8},{1,9},{2,10},{3,11},{4,12},{5,13},{6,14},{7,15},{8,0},{9,1},... | collective-permute-start | bytes 884744 | tf_op jit(solution)/shard_map/ppermute | solution.py:31
  35.2 5.0 %collective-permute-start.6 = (bf16[512,128]{1,0:T(8,128)(2,1)S(1)}, bf16[512,128]{1,0:T(8,128)(2,1)S(1)}, u32[]{:S(2)}, u32[]{:S(2)}) collective-permute-start(bf16[512,128]{1,0:T(8,128)(2,1)S(1)} %get-tuple-element.34), channel_id=1, source_target_pairs={{0,2},{1,3},{2,0},{3,1},{4,6},{5,7},{6,4},{7,5},{8,10},{9,11},{10,... | collective-permute-start | bytes 393224 | tf_op jit(solution)/shard_map/ppermute | solution.py:31
  36.7 9.2 %collective-permute-start.7 = (bf16[512,256]{1,0:T(8,128)(2,1)S(1)}, bf16[512,256]{1,0:T(8,128)(2,1)S(1)}, u32[]{:S(2)}, u32[]{:S(2)}) collective-permute-start(bf16[512,256]{1,0:T(8,128)(2,1)S(1)} %collective-permute-done.5.refs_5_), channel_id=1, source_target_pairs={{0,1},{1,0},{2,3},{3,2},{4,5},{5,4},{6,7},{7,6},{8,9},{9,8},{10,11... | collective-permute-start | bytes 786440 | tf_op jit(solution)/shard_map/ppermute | solution.py:31
  40.3 23.8 %collective-permute-start.13 = (bf16[128,1152]{1,0:T(8,128)(2,1)S(1)}, bf16[128,1152]{1,0:T(8,128)(2,1)S(1)}, u32[]{:S(2)}, u32[]{:S(2)}) collective-permute-start(bf16[128,1152]{1,0:T(8,128)(2,1)S(1)} %get-tuple-element.26.refs_4_.refs_1_), channel_id=1, source_target_pairs={{0,4},{1,5},{2,6},{3,7},{4,0},{5,1},{6,2},{7,3},{8,12},{9,13},{10,... | collective-permute-start | bytes 884744 | tf_op jit(solution)/shard_map/ppermute | solution.py:31
  41.9 3.8 %collective-permute-start.8 = (bf16[512,128]{1,0:T(8,128)(2,1)S(1)}, bf16[512,128]{1,0:T(8,128)(2,1)S(1)}, u32[]{:S(2)}, u32[]{:S(2)}) collective-permute-start(bf16[512,128]{1,0:T(8,128)(2,1)S(1)} %collective-permute-done.6.refs_6_), channel_id=1, source_target_pairs={{0,1},{1,0},{2,3},{3,2},{4,5},{5,4},{6,7},{7,6},{8,9},{9,8},{10,11... | collective-permute-start | bytes 393224 | tf_op jit(solution)/shard_map/ppermute | solution.py:31
  45.7 12.8 %collective-permute-start.10 = (bf16[256,128]{1,0:T(8,128)(2,1)S(1)}, bf16[256,128]{1,0:T(8,128)(2,1)S(1)}, u32[]{:S(2)}, u32[]{:S(2)}) collective-permute-start(bf16[256,128]{1,0:T(8,128)(2,1)S(1)} %get-tuple-element.38.refs_9_), channel_id=1, source_target_pairs={{0,12},{1,13},{2,14},{3,15},{4,8},{5,9},{6,10},{7,11},{8,4},{9,5},... | collective-permute-start | bytes 196616 | tf_op jit(solution)/shard_map/ppermute | solution.py:31
  48.3 11.1 %collective-permute-start.11 = (bf16[320,128]{1,0:T(8,128)(2,1)S(1)}, bf16[320,128]{1,0:T(8,128)(2,1)S(1)}, u32[]{:S(2)}, u32[]{:S(2)}) collective-permute-start(bf16[320,128]{1,0:T(8,128)(2,1)S(1)} %shard_map.114.refs_10_), channel_id=1, source_target_pairs={{0,12},{1,13},{2,14},{3,15},{4,8},{5,9},{6,10},{7,11},{8,4},{9,5},... | collective-permute-start | bytes 245768 | tf_op jit(solution)/shard_map/ppermute | solution.py:31
  56.2 5.3 %copy-start = (bf16[3,1152,576]{1,2,0:T(8,128)(2,1)S(1)}, bf16[3,1152,576]{1,2,0:T(8,128)(2,1)}, u32[]{:S(2)}) copy-start(bf16[3,1152,576]{1,2,0:T(8,128)(2,1)} %param.19) | copy-start | bytes 11943940
  56.3 5.3 %copy-start.1 = (bf16[576,1152]{1,0:T(8,128)(2,1)S(1)}, bf16[576,1152]{1,0:T(8,128)(2,1)}, u32[]{:S(2)}) copy-start(bf16[576,1152]{1,0:T(8,128)(2,1)} %refs_5_.1) | copy-start | bytes 3981316
  56.3 11.8 %collective-permute-start.16 = (bf16[576,128]{1,0:T(8,128)(2,1)S(1)}, bf16[576,128]{1,0:T(8,128)(2,1)S(1)}, u32[]{:S(2)}, u32[]{:S(2)}) collective-permute-start(bf16[576,128]{1,0:T(8,128)(2,1)S(1)} %shard_map.112.refs_6_), channel_id=1, source_target_pairs={{0,4},{1,5},{2,6},{3,7},{4,0},{5,1},{6,2},{7,3},{8,12},{9,13},{10,... | collective-permute-start | bytes 442376 | tf_op jit(solution)/shard_map/ppermute | solution.py:31
  58.5 8.7 %collective-permute-start.14 = (bf16[256,128]{1,0:T(8,128)(2,1)S(1)}, bf16[256,128]{1,0:T(8,128)(2,1)S(1)}, u32[]{:S(2)}, u32[]{:S(2)}) collective-permute-start(bf16[256,128]{1,0:T(8,128)(2,1)S(1)} %get-tuple-element.37.refs_7_), channel_id=1, source_target_pairs={{0,8},{1,9},{2,10},{3,11},{4,12},{5,13},{6,14},{7,15},{8,0},{9,1},... | collective-permute-start | bytes 196616 | tf_op jit(solution)/shard_map/ppermute | solution.py:31
  59.4 8.8 %collective-permute-start.15 = (bf16[320,128]{1,0:T(8,128)(2,1)S(1)}, bf16[320,128]{1,0:T(8,128)(2,1)S(1)}, u32[]{:S(2)}, u32[]{:S(2)}) collective-permute-start(bf16[320,128]{1,0:T(8,128)(2,1)S(1)} %shard_map.113.refs_8_), channel_id=1, source_target_pairs={{0,8},{1,9},{2,10},{3,11},{4,12},{5,13},{6,14},{7,15},{8,0},{9,1},... | collective-permute-start | bytes 245768 | tf_op jit(solution)/shard_map/ppermute | solution.py:31
  72.9 8.7 %collective-permute-start.18 = (bf16[576,128]{1,0:T(8,128)(2,1)S(1)}, bf16[576,128]{1,0:T(8,128)(2,1)S(1)}, u32[]{:S(2)}, u32[]{:S(2)}) collective-permute-start(bf16[576,128]{1,0:T(8,128)(2,1)S(1)} %shard_map.119), channel_id=1, source_target_pairs={{0,12},{1,13},{2,14},{3,15},{4,8},{5,9},{6,10},{7,11},{8,4},{9,5},... | collective-permute-start | bytes 442376 | tf_op jit(solution)/shard_map/ppermute | solution.py:31
  74.4 11.0 %collective-permute-start.19 = (bf16[576,128]{1,0:T(8,128)(2,1)S(1)}, bf16[576,128]{1,0:T(8,128)(2,1)S(1)}, u32[]{:S(2)}, u32[]{:S(2)}) collective-permute-start(bf16[576,128]{1,0:T(8,128)(2,1)S(1)} %shard_map.120), channel_id=1, source_target_pairs={{0,4},{1,5},{2,6},{3,7},{4,0},{5,1},{6,2},{7,3},{8,12},{9,13},{10,... | collective-permute-start | bytes 442376 | tf_op jit(solution)/shard_map/ppermute | solution.py:31
  75.4 12.2 %collective-permute-start.17 = (bf16[576,128]{1,0:T(8,128)(2,1)S(1)}, bf16[576,128]{1,0:T(8,128)(2,1)S(1)}, u32[]{:S(2)}, u32[]{:S(2)}) collective-permute-start(bf16[576,128]{1,0:T(8,128)(2,1)S(1)} %shard_map.118), channel_id=1, source_target_pairs={{0,8},{1,9},{2,10},{3,11},{4,12},{5,13},{6,14},{7,15},{8,0},{9,1},... | collective-permute-start | bytes 442376 | tf_op jit(solution)/shard_map/ppermute | solution.py:31
  79.6 5.8 %copy-start.2 = (bf16[576,1152]{1,0:T(8,128)(2,1)S(1)}, bf16[576,1152]{1,0:T(8,128)(2,1)}, u32[]{:S(2)}) copy-start(bf16[576,1152]{1,0:T(8,128)(2,1)} %weight_ref.3) | copy-start | bytes 3981316

commit v9 on v8

--- a/solution.py
+++ b/solution.py
@@ -465,7 +465,10 @@
 
 def back_parts(rows):
     parts = target_parts(rows)
-    return parts[:1] + parts[2:-1] + parts[1:2] + parts[-1:] if len(parts) > 2 else parts
+    if len(parts) < 3:
+        return parts
+    between = [chunk for part in parts[1:-1] for chunk in part]
+    return [parts[0], between, parts[-1]]
 
 
 def part_pieces(chunks, piece):

time: 89.2 us -> 89.8 us (level)
  waiting for transfers between devices: 24.6 us -> 25.9 us
    ppermute x20, waiting for transfers between devices: 24.6 us -> 25.9 us  [permute(): lax.ppermute(value, 'patch', [(source, target(source)) for source in rang...]
    pallas_call x13 -> x12, Pallas kernels: 26.3 us -> 25.6 us  [on_chip_call(): pl.pallas_call(kernel, out_shape=[pltpu.VMEM(shape, dtype) for shape, dty...]
  transfers between devices with their start and end apart: 20 -> 20, of which waited for: 7 -> 7; matrix products, arithmetic and copies ran while one was open for 0% -> 0% of each run, Pallas kernels for 33% -> 32%
where the time goes in v9:
time: 89.8 us; the launch traced here: 89.6 us
  Pallas kernels  35.9 us (40%)
  starting transfers between devices  26.6 us (30%)
  waiting for transfers between devices  25.9 us (29%)
  between operations  1.1 us (1%)
    ppermute x20, starting transfers between devices, permute(): lax.ppermute(value, 'patch', [(source, target(source)) for source in rang...  26.6 us
    ppermute x20, waiting for transfers between devices, permute(): lax.ppermute(value, 'patch', [(source, target(source)) for source in rang...  25.9 us
    pallas_call x12, Pallas kernels, on_chip_call(): pl.pallas_call(kernel, out_shape=[pltpu.VMEM(shape, dtype) for shape, dty...  25.6 us
    pallas_call x1, Pallas kernels, projections(): pl.pallas_call(functools.partial(projection_kernel, frames=frames, width=...  3.95 us
    pallas_call x2, Pallas kernels, output(): pl.pallas_call(functools.partial(output_kernel, frames=frames, members=me...  3.45 us
  transfers between devices with their start and end apart: 20, of which 7 were waited for; matrix products, arithmetic and copies ran while one was open for 0% of the time, Pallas kernels for 32%

profile of v9, /device:TPU:0, one launch (start us, length us, event | category | flops | bytes accessed | tf_op | source)
XLA Modules:
  0.0 89.6 jit_solution(18013960239767577838)
XLA Ops:
  0.0 1.2 %first.1 = bf16[512,512]{1,0:T(8,128)(2,1)S(1)} custom-call(bf16[512,1152]{1,0:T(8,128)(2,1)} %kv_ref.3), custom_call_target="tpu_custom_call" | custom-call | tf_op jit(solution)/shard_map/first/pallas_call | solution.py:107
  1.2 3.1 %collective-permute-start.1 = (bf16[512,512]{1,0:T(8,128)(2,1)S(1)}, bf16[512,512]{1,0:T(8,128)(2,1)S(1)}, u32[]{:S(2)}, u32[]{:S(2)}) collective-permute-start(bf16[512,512]{1,0:T(8,128)(2,1)S(1)} %first.1), channel_id=1, source_target_pairs={{0,2},{1,3},{2,0},{3,1},{4,6},{5,7},{6,4},{7,5},{8,10},{9,11},{10,... | collective-permute-start | bytes 1572872 | tf_op jit(solution)/shard_map/ppermute | solution.py:31
  4.3 0.0 collective-permute-start
  4.3 11.9 %collective-permute-done.1.refs_3_ = bf16[512,512]{1,0:T(8,128)(2,1)S(1)} collective-permute-done((bf16[512,512]{1,0:T(8,128)(2,1)S(1)}, bf16[512,512]{1,0:T(8,128)(2,1)S(1)}, u32[]{:S(2)}, u32[]{:S(2)}) %collective-permute-start.1) | collective-permute-done | bytes 524320 | tf_op jit(solution)/shard_map/ppermute | solution.py:31
  16.2 0.0 copy-start.6
  16.3 0.0 copy-start.7
  16.3 1.7 %pieces.1 = (bf16[128,1152]{1,0:T(8,128)(2,1)S(1)}, bf16[128,1152]{1,0:T(8,128)(2,1)S(1)}, bf16[128,1152]{1,0:T(8,128)(2,1)S(1)}, bf16[128,1152]{1,0:T(8,128)(2,...) custom-call(s32[1]{0:T(128)} %bitcast.slot_ref, ...), custom_call_target="tpu_custom_call" | custom-call | flops 4000000000 | bytes 2359296 | tf_op jit(solution)/shard_map/pieces/pallas_call | solution.py:140
  18.0 1.8 %collective-permute-start.2 = (bf16[512,256]{1,0:T(8,128)(2,1)S(1)}, bf16[512,256]{1,0:T(8,128)(2,1)S(1)}, u32[]{:S(2)}, u32[]{:S(2)}) collective-permute-start(bf16[512,256]{1,0:T(8,128)(2,1)S(1)} %get-tuple-element.33), channel_id=1, source_target_pairs={{0,2},{1,3},{2,0},{3,1},{4,6},{5,7},{6,4},{7,5},{8,10},{9,11},{10,... | collective-permute-start | bytes 786440 | tf_op jit(solution)/shard_map/ppermute | solution.py:31
  19.8 0.3 collective-permute-start.5
  20.1 3.8 %collective-permute-start.9 = (bf16[128,1152]{1,0:T(8,128)(2,1)S(1)}, bf16[128,1152]{1,0:T(8,128)(2,1)S(1)}, u32[]{:S(2)}, u32[]{:S(2)}) collective-permute-start(bf16[128,1152]{1,0:T(8,128)(2,1)S(1)} %get-tuple-element.30.refs_6_.refs_3_), channel_id=1, source_target_pairs={{0,12},{1,13},{2,14},{3,15},{4,8},{5,9},{6,10},{7,11},{8,4},{9,5},... | collective-permute-start | bytes 884744 | tf_op jit(solution)/shard_map/ppermute | solution.py:31
  24.6 2.7 %collective-permute-done.2.refs_4_ = bf16[512,256]{1,0:T(8,128)(2,1)S(1)} collective-permute-done((bf16[512,256]{1,0:T(8,128)(2,1)S(1)}, bf16[512,256]{1,0:T(8,128)(2,1)S(1)}, u32[]{:S(2)}, u32[]{:S(2)}) %collective-permute-start.2) | collective-permute-done | bytes 262176 | tf_op jit(solution)/shard_map/ppermute | solution.py:31
  27.2 0.0 collective-permute-start.4
  27.3 3.9 %projections.1 = (bf16[512,640]{1,0:T(8,128)(2,1)S(1)}, bf16[512,1152]{1,0:T(8,128)(2,1)S(1)}, f32[6,1152]{1,0:T(8,128)S(1)}, f32[4,1152]{1,0:T(4,128)S(1)}) custom-call(s32[1]{0:T(128)} %bitcast.slot_ref, s32[1]{0:T(128)S(6)} %copy.14.time_ref, s32[4]{0:T(128)S(1)} %copy-done.6, bf16[1728,1152]{1,0:T(8,128)(2,1)S(1)} %bitcast.9, f32[1,576]{1,0:T(1,128)S(1)} %copy-done.7, ...), custom_call_target="tpu_custom_call" | custom-call | flops 2038431744 | bytes 3981312 | tf_op jit(solution)/shard_map/projections/pallas_call | solution.py:207
  31.2 1.1 %collective-permute-done.5.refs_5_ = bf16[512,256]{1,0:T(8,128)(2,1)S(1)} collective-permute-done((bf16[512,256]{1,0:T(8,128)(2,1)S(1)}, bf16[512,256]{1,0:T(8,128)(2,1)S(1)}, u32[]{:S(2)}, u32[]{:S(2)}) %collective-permute-start.5) | collective-permute-done | bytes 262176 | tf_op jit(solution)/shard_map/ppermute | solution.py:31
  32.4 2.8 %collective-permute-start.12 = (bf16[128,1152]{1,0:T(8,128)(2,1)S(1)}, bf16[128,1152]{1,0:T(8,128)(2,1)S(1)}, u32[]{:S(2)}, u32[]{:S(2)}) collective-permute-start(bf16[128,1152]{1,0:T(8,128)(2,1)S(1)} %get-tuple-element.29.refs_5_.refs_2_), channel_id=1, source_target_pairs={{0,8},{1,9},{2,10},{3,11},{4,12},{5,13},{6,14},{7,15},{8,0},{9,1},... | collective-permute-start | bytes 884744 | tf_op jit(solution)/shard_map/ppermute | solution.py:31
  35.2 1.5 %collective-permute-start.6 = (bf16[512,128]{1,0:T(8,128)(2,1)S(1)}, bf16[512,128]{1,0:T(8,128)(2,1)S(1)}, u32[]{:S(2)}, u32[]{:S(2)}) collective-permute-start(bf16[512,128]{1,0:T(8,128)(2,1)S(1)} %get-tuple-element.36), channel_id=1, source_target_pairs={{0,2},{1,3},{2,0},{3,1},{4,6},{5,7},{6,4},{7,5},{8,10},{9,11},{10,... | collective-permute-start | bytes 393224 | tf_op jit(solution)/shard_map/ppermute | solution.py:31
  36.7 3.5 %shard_map.109.refs_7_ = bf16[512,256]{1,0:T(8,128)(2,1)S(1)} custom-call(bf16[512,640]{1,0:T(8,128)(2,1)S(1)} %get-tuple-element.31.refs_0_, bf16[512,1152]{1,0:T(8,128)(2,1)S(1)} %get-tuple-element.32.refs_1_, bf16[512,1152]{1,0:T(8,128)(2,1)S(1)} %collective-permute-done.refs_2_, bf16[512,512]{1,0:T(8,128)(2,1)S(1)} %collective-permute-done.1.refs_3_, ...), custom_call_target="tpu_custom_call" | custom-call | flops 2147483648 | bytes 4063232 | tf_op jit(solution)/shard_map/pallas_call | solution.py:69
  40.3 1.6 %collective-permute-start.13 = (bf16[128,1152]{1,0:T(8,128)(2,1)S(1)}, bf16[128,1152]{1,0:T(8,128)(2,1)S(1)}, u32[]{:S(2)}, u32[]{:S(2)}) collective-permute-start(bf16[128,1152]{1,0:T(8,128)(2,1)S(1)} %get-tuple-element.28.refs_4_.refs_1_), channel_id=1, source_target_pairs={{0,4},{1,5},{2,6},{3,7},{4,0},{5,1},{6,2},{7,3},{8,12},{9,13},{10,... | collective-permute-start | bytes 884744 | tf_op jit(solution)/shard_map/ppermute | solution.py:31
  41.9 0.0 collective-permute-done.4.refs_6_.refs_8_
  41.9 0.2 collective-permute-start.8
  42.1 3.5 %shard_map.110 = (bf16[256,128]{1,0:T(8,128)(2,1)S(1)}, bf16[256,128]{1,0:T(8,128)(2,1)S(1)}, bf16[256,128]{1,0:T(8,128)(2,1)S(1)}, bf16[256,128]{1,0:T(8,128)(2,1)S(1)}, bf16[512,128]{1,0:T(8,128)(2,1)S(1)}) custom-call(bf16[512,640]{1,0:T(8,128)(2,1)S(1)} %get-tuple-element.31.refs_0_, bf16[512,1152]{1,0:T(8,128)(2,1)S(1)} %get-tuple-element.32.refs_1_, ...), custom_call_target="tpu_custom_call" | custom-call | flops 2147483648 | bytes 4849664 | tf_op jit(solution)/shard_map/pallas_call | solution.py:69
  45.7 0.0 collective-permute-done.8.refs_10_
  45.7 0.3 collective-permute-start.10
  46.0 2.3 %shard_map.114.refs_10_ = bf16[320,128]{1,0:T(8,128)(2,1)S(1)} custom-call(bf16[512,640]{1,0:T(8,128)(2,1)S(1)} %get-tuple-element.31.refs_0_, bf16[512,1152]{1,0:T(8,128)(2,1)S(1)} %get-tuple-element.32.refs_1_, bf16[512,1152]{1,0:T(8,128)(2,1)S(1)} %collective-permute-done.refs_2_, bf16[512,512]{1,0:T(8,128)(2,1)S(1)} %collective-permute-done.1.refs_3_, ...), custom_call_target="tpu_custom_call" | custom-call | flops 1073741824 | bytes 5505024 | tf_op jit(solution)/shard_map/pallas_call | solution.py:69
  48.3 3.7 %collective-permute-start.11 = (bf16[320,128]{1,0:T(8,128)(2,1)S(1)}, bf16[320,128]{1,0:T(8,128)(2,1)S(1)}, u32[]{:S(2)}, u32[]{:S(2)}) collective-permute-start(bf16[320,128]{1,0:T(8,128)(2,1)S(1)} %shard_map.114.refs_10_), channel_id=1, source_target_pairs={{0,12},{1,13},{2,14},{3,15},{4,8},{5,9},{6,10},{7,11},{8,4},{9,5},... | collective-permute-start | bytes 245768 | tf_op jit(solution)/shard_map/ppermute | solution.py:31
  52.0 2.1 %shard_map.111.refs_5_.refs_3_ = bf16[320,128]{1,0:T(8,128)(2,1)S(1)} custom-call(bf16[512,640]{1,0:T(8,128)(2,1)S(1)} %get-tuple-element.31.refs_0_, bf16[512,1152]{1,0:T(8,128)(2,1)S(1)} %get-tuple-element.32.refs_1_, bf16[512,1152]{1,0:T(8,128)(2,1)S(1)} %collective-permute-done.refs_2_, bf16[512,512]{1,0:T(8,128)(2,1)S(1)} %collective-permute-done.1.refs_3_, ...), custom_call_target="tpu_custom_call" | custom-call | flops 1073741824 | bytes 5505024 | tf_op jit(solution)/shard_map/pallas_call | solution.py:69
  54.1 2.1 %shard_map.112.refs_6_ = bf16[576,128]{1,0:T(8,128)(2,1)S(1)} custom-call(bf16[512,640]{1,0:T(8,128)(2,1)S(1)} %get-tuple-element.31.refs_0_, bf16[512,1152]{1,0:T(8,128)(2,1)S(1)} %get-tuple-element.32.refs_1_, bf16[512,1152]{1,0:T(8,128)(2,1)S(1)} %collective-permute-done.refs_2_, bf16[512,512]{1,0:T(8,128)(2,1)S(1)} %collective-permute-done.1.refs_3_, ...), custom_call_target="tpu_custom_call" | custom-call | flops 1073741824 | bytes 5570560 | tf_op jit(solution)/shard_map/pallas_call | solution.py:69
  56.2 0.0 copy-start
  56.3 0.0 copy-start.1
  56.3 0.1 collective-permute-start.16
  56.4 2.1 %shard_map.113.refs_8_ = bf16[320,128]{1,0:T(8,128)(2,1)S(1)} custom-call(bf16[512,640]{1,0:T(8,128)(2,1)S(1)} %get-tuple-element.31.refs_0_, bf16[512,1152]{1,0:T(8,128)(2,1)S(1)} %get-tuple-element.32.refs_1_, bf16[512,1152]{1,0:T(8,128)(2,1)S(1)} %collective-permute-done.refs_2_, bf16[512,512]{1,0:T(8,128)(2,1)S(1)} %collective-permute-done.1.refs_3_, ...), custom_call_target="tpu_custom_call" | custom-call | flops 1073741824 | bytes 5505024 | tf_op jit(solution)/shard_map/pallas_call | solution.py:69
  58.5 0.8 collective-permute-start.14
  59.4 2.2 %collective-permute-start.15 = (bf16[320,128]{1,0:T(8,128)(2,1)S(1)}, bf16[320,128]{1,0:T(8,128)(2,1)S(1)}, u32[]{:S(2)}, u32[]{:S(2)}) collective-permute-start(bf16[320,128]{1,0:T(8,128)(2,1)S(1)} %shard_map.113.refs_8_), channel_id=1, source_target_pairs={{0,8},{1,9},{2,10},{3,11},{4,12},{5,13},{6,14},{7,15},{8,0},{9,1},... | collective-permute-start | bytes 245768 | tf_op jit(solution)/shard_map/ppermute | solution.py:31
  61.5 2.5 %shard_map.116 = (bf16[256,640]{1,0:T(8,128)(2,1)S(1)}, bf16[256,1152]{1,0:T(8,128)(2,1)S(1)}) custom-call(bf16[128,1152]{1,0:T(8,128)(2,1)S(1)} %get-tuple-element.27.refs_3_.refs_0_, bf16[128,1152]{1,0:T(8,128)(2,1)S(1)} %collective-permute-done.9.refs_1_, bf16[256,128]{1,0:T(8,128)(2,1)S(1)} %get-tuple-element.34.refs_4_.refs_2_, ...), custom_call_target="tpu_custom_call" | custom-call | flops 1358954496 | bytes 6239232 | tf_op jit(solution)/shard_map/pallas_call | solution.py:69
  64.1 3.2 %collective-permute-done.14.refs_2_ = bf16[256,128]{1,0:T(8,128)(2,1)S(1)} collective-permute-done((bf16[256,128]{1,0:T(8,128)(2,1)S(1)}, bf16[256,128]{1,0:T(8,128)(2,1)S(1)}, u32[]{:S(2)}, u32[]{:S(2)}) %collective-permute-start.14) | collective-permute-done | bytes 65568 | tf_op jit(solution)/shard_map/ppermute | solution.py:31
  67.2 0.9 collective-permute-done.15.refs_3_
  68.1 2.5 %shard_map.117 = (bf16[256,640]{1,0:T(8,128)(2,1)S(1)}, bf16[256,1152]{1,0:T(8,128)(2,1)S(1)}) custom-call(bf16[128,1152]{1,0:T(8,128)(2,1)S(1)} %collective-permute-done.12.refs_0_, bf16[128,1152]{1,0:T(8,128)(2,1)S(1)} %collective-permute-done.13.refs_1_, bf16[256,128]{1,0:T(8,128)(2,1)S(1)} %collective-permute-done.14.refs_2_, ...), custom_call_target="tpu_custom_call" | custom-call | flops 1358954496 | bytes 6239232 | tf_op jit(solution)/shard_map/pallas_call | solution.py:69
  70.6 1.3 %shard_map.118 = (bf16[576,128]{1,0:T(8,128)(2,1)S(1)}, bf16[576,128]{1,0:T(8,128)(2,1)S(1)}) custom-call(bf16[256,640]{1,0:T(8,128)(2,1)S(1)} %get-tuple-element.43.refs_0_, bf16[256,640]{1,0:T(8,128)(2,1)S(1)} %get-tuple-element.44.refs_1_, bf16[256,1152]{1,0:T(8,128)(2,1)S(1)} %get-tuple-element.45.refs_2_, bf16[256,1152]{1,0:T(8,128)(2,1)S(1)} %get-tuple-element.46.refs_3_), custom_call_target="tpu_custom_call" | custom-call | flops 268435456 | bytes 1835008 | tf_op jit(solution)/shard_map/pallas_call | solution.py:69
  72.0 1.2 %shard_map.119 = bf16[576,128]{1,0:T(8,128)(2,1)S(1)} custom-call(bf16[256,640]{1,0:T(8,128)(2,1)S(1)} %get-tuple-element.43.refs_0_, bf16[256,640]{1,0:T(8,128)(2,1)S(1)} %get-tuple-element.44.refs_1_, bf16[256,1152]{1,0:T(8,128)(2,1)S(1)} %get-tuple-element.45.refs_2_, bf16[256,1152]{1,0:T(8,128)(2,1)S(1)} %get-tuple-element.46.refs_3_), custom_call_target="tpu_custom_call" | custom-call | flops 268435456 | bytes 1835008 | tf_op jit(solution)/shard_map/pallas_call | solution.py:69
  73.2 1.5 %collective-permute-start.18 = (bf16[576,128]{1,0:T(8,128)(2,1)S(1)}, bf16[576,128]{1,0:T(8,128)(2,1)S(1)}, u32[]{:S(2)}, u32[]{:S(2)}) collective-permute-start(bf16[576,128]{1,0:T(8,128)(2,1)S(1)} %shard_map.119), channel_id=1, source_target_pairs={{0,12},{1,13},{2,14},{3,15},{4,8},{5,9},{6,10},{7,11},{8,4},{9,5},... | collective-permute-start | bytes 442376 | tf_op jit(solution)/shard_map/ppermute | solution.py:31
  74.7 2.9 %collective-permute-start.17 = (bf16[576,128]{1,0:T(8,128)(2,1)S(1)}, bf16[576,128]{1,0:T(8,128)(2,1)S(1)}, u32[]{:S(2)}, u32[]{:S(2)}) collective-permute-start(bf16[576,128]{1,0:T(8,128)(2,1)S(1)} %get-tuple-element.47), channel_id=1, source_target_pairs={{0,8},{1,9},{2,10},{3,11},{4,12},{5,13},{6,14},{7,15},{8,0},{9,1},... | collective-permute-start | bytes 442376 | tf_op jit(solution)/shard_map/ppermute | solution.py:31
  77.7 1.2 %shard_map.115.after_ref = f32[512,1152]{1,0:T(8,128)S(1)} custom-call(bf16[128,1152]{1,0:T(8,128)(2,1)S(1)} %get-tuple-element.27.refs_3_.refs_0_, bf16[128,1152]{1,0:T(8,128)(2,1)S(1)} %get-tuple-element.28.refs_4_.refs_1_, bf16[128,1152]{1,0:T(8,128)(2,1)S(1)} %get-tuple-element.29.refs_5_.refs_2_, ...), custom_call_target="tpu_custom_call" | custom-call | flops 679477248 | bytes 3124224 | tf_op jit(solution)/shard_map/pallas_call | solution.py:69
  78.8 0.0 copy-start.2
  78.9 1.0 %shard_map.120.refs_2_ = bf16[576,128]{1,0:T(8,128)(2,1)S(1)} custom-call(bf16[256,640]{1,0:T(8,128)(2,1)S(1)} %get-tuple-element.43.refs_0_, bf16[256,640]{1,0:T(8,128)(2,1)S(1)} %get-tuple-element.44.refs_1_, bf16[256,1152]{1,0:T(8,128)(2,1)S(1)} %get-tuple-element.45.refs_2_, bf16[256,1152]{1,0:T(8,128)(2,1)S(1)} %get-tuple-element.46.refs_3_), custom_call_target="tpu_custom_call" | custom-call | flops 268435456 | bytes 1835008 | tf_op jit(solution)/shard_map/pallas_call | solution.py:69
  79.9 1.9 %collective-permute-done.18.refs_0_ = bf16[576,128]{1,0:T(8,128)(2,1)S(1)} collective-permute-done((bf16[576,128]{1,0:T(8,128)(2,1)S(1)}, bf16[576,128]{1,0:T(8,128)(2,1)S(1)}, u32[]{:S(2)}, u32[]{:S(2)}) %collective-permute-start.18) | collective-permute-done | bytes 147488 | tf_op jit(solution)/shard_map/ppermute | solution.py:31
  81.8 4.2 %collective-permute-done.19.refs_1_ = bf16[576,128]{1,0:T(8,128)(2,1)S(1)} collective-permute-done((bf16[576,128]{1,0:T(8,128)(2,1)S(1)}, bf16[576,128]{1,0:T(8,128)(2,1)S(1)}, u32[]{:S(2)}, u32[]{:S(2)}) %collective-permute-start.19) | collective-permute-done | bytes 147488 | tf_op jit(solution)/shard_map/ppermute | solution.py:31
  86.0 2.2 %shard_map.121.refs_1_ = f32[512,1152]{1,0:T(8,128)} custom-call(s32[1]{0:T(128)} %bitcast.slot_ref, f32[512,1152]{1,0:T(8,128)S(1)} %shard_map.115.after_ref, bf16[576,1152]{1,0:T(8,128)(2,1)S(1)} %copy-done.2, f32[6,1152]{1,0:T(8,128)S(1)} %get-tuple-element.41.refs_12_.refs_8_.refs_7_.modulation_ref, ...), custom_call_target="tpu_custom_call" | custom-call | tf_op jit(solution)/shard_map/pallas_call | solution.py:764
  88.2 1.3 %shard_map.122 = f32[512,1152]{1,0:T(8,128)} custom-call(s32[1]{0:T(128)} %bitcast.slot_ref, f32[512,1152]{1,0:T(8,128)S(1)} %shard_map.115.after_ref, bf16[576,1152]{1,0:T(8,128)(2,1)S(1)} %copy-done.2, f32[6,1152]{1,0:T(8,128)S(1)} %get-tuple-element.41.refs_12_.refs_8_.refs_7_.modulation_ref, ...), custom_call_target="tpu_custom_call", output_to_operand_aliasing={{}: (5, {})} | custom-call | tf_op jit(solution)/shard_map/pallas_call | solution.py:764
  (27 shorter events, 0.1 us)
Async XLA Ops:
  0.0 4.3 %copy-start.8 = (bf16[512,1152]{1,0:T(8,128)(2,1)S(1)}, bf16[512,1152]{1,0:T(8,128)(2,1)}, u32[]{:S(2)}) copy-start(bf16[512,1152]{1,0:T(8,128)(2,1)} %kv_ref.3) | copy-start | bytes 3538948
  1.2 15.0 %collective-permute-start.1 = (bf16[512,512]{1,0:T(8,128)(2,1)S(1)}, bf16[512,512]{1,0:T(8,128)(2,1)S(1)}, u32[]{:S(2)}, u32[]{:S(2)}) collective-permute-start(bf16[512,512]{1,0:T(8,128)(2,1)S(1)} %first.1), channel_id=1, source_target_pairs={{0,2},{1,3},{2,0},{3,1},{4,6},{5,7},{6,4},{7,5},{8,10},{9,11},{10,... | collective-permute-start | bytes 1572872 | tf_op jit(solution)/shard_map/ppermute | solution.py:31
  4.3 32.4 %collective-permute-start = (bf16[512,1152]{1,0:T(8,128)(2,1)S(1)}, bf16[512,1152]{1,0:T(8,128)(2,1)S(1)}, u32[]{:S(2)}, u32[]{:S(2)}) collective-permute-start(bf16[512,1152]{1,0:T(8,128)(2,1)S(1)} %copy-done.8), channel_id=1, source_target_pairs={{0,1},{1,0},{2,3},{3,2},{4,5},{5,4},{6,7},{7,6},{8,9},{9,8},{10,11... | collective-permute-start | bytes 3538952 | tf_op jit(solution)/shard_map/ppermute | solution.py:31
  16.2 19.0 %collective-permute-start.3 = (bf16[512,512]{1,0:T(8,128)(2,1)S(1)}, bf16[512,512]{1,0:T(8,128)(2,1)S(1)}, u32[]{:S(2)}, u32[]{:S(2)}) collective-permute-start(bf16[512,512]{1,0:T(8,128)(2,1)S(1)} %collective-permute-done.1.refs_3_), channel_id=1, source_target_pairs={{0,1},{1,0},{2,3},{3,2},{4,5},{5,4},{6,7},{7,6},{8,9},{9,8},{10,11... | collective-permute-start | bytes 1572872 | tf_op jit(solution)/shard_map/ppermute | solution.py:31
  16.2 11.0 %copy-start.3 = (bf16[3,1152,576]{1,2,0:T(8,128)(2,1)S(1)}, bf16[3,1152,576]{1,2,0:T(8,128)(2,1)}, u32[]{:S(2)}) copy-start(bf16[3,1152,576]{1,2,0:T(8,128)(2,1)} %param.17) | copy-start | bytes 11943940
  16.2 11.0 %copy-start.4 = (f32[6,1152]{1,0:T(8,128)S(1)}, f32[6,1152]{1,0:T(8,128)}, u32[]{:S(2)}) copy-start(f32[6,1152]{1,0:T(8,128)} %refs_1_.1) | copy-start | bytes 82948
  16.2 11.0 %copy-start.5 = (f32[6,1152]{1,0:T(8,128)S(1)}, f32[6,1152]{1,0:T(8,128)}, u32[]{:S(2)}) copy-start(f32[6,1152]{1,0:T(8,128)} %refs_2_.1) | copy-start | bytes 82948
  16.2 11.0 %copy-start.6 = (s32[4]{0:T(128)S(1)}, s32[4]{0:T(128)}, u32[]{:S(2)}) copy-start(s32[4]{0:T(128)} %order_ref.1) | copy-start | bytes 52
  16.3 11.0 %copy-start.7 = (f32[1,576]{1,0:T(1,128)S(1)}, f32[1,576]{1,0:T(1,128)}, u32[]{:S(2)}) copy-start(f32[1,576]{1,0:T(1,128)} %constant.22.clone.refs_0_) | copy-start | bytes 6916
  18.0 9.2 %collective-permute-start.2 = (bf16[512,256]{1,0:T(8,128)(2,1)S(1)}, bf16[512,256]{1,0:T(8,128)(2,1)S(1)}, u32[]{:S(2)}, u32[]{:S(2)}) collective-permute-start(bf16[512,256]{1,0:T(8,128)(2,1)S(1)} %get-tuple-element.33), channel_id=1, source_target_pairs={{0,2},{1,3},{2,0},{3,1},{4,6},{5,7},{6,4},{7,5},{8,10},{9,11},{10,... | collective-permute-start | bytes 786440 | tf_op jit(solution)/shard_map/ppermute | solution.py:31
  19.8 12.6 %collective-permute-start.5 = (bf16[512,256]{1,0:T(8,128)(2,1)S(1)}, bf16[512,256]{1,0:T(8,128)(2,1)S(1)}, u32[]{:S(2)}, u32[]{:S(2)}) collective-permute-start(bf16[512,256]{1,0:T(8,128)(2,1)S(1)} %get-tuple-element.35), channel_id=1, source_target_pairs={{0,2},{1,3},{2,0},{3,1},{4,6},{5,7},{6,4},{7,5},{8,10},{9,11},{10,... | collective-permute-start | bytes 786440 | tf_op jit(solution)/shard_map/ppermute | solution.py:31
  20.1 36.2 %collective-permute-start.9 = (bf16[128,1152]{1,0:T(8,128)(2,1)S(1)}, bf16[128,1152]{1,0:T(8,128)(2,1)S(1)}, u32[]{:S(2)}, u32[]{:S(2)}) collective-permute-start(bf16[128,1152]{1,0:T(8,128)(2,1)S(1)} %get-tuple-element.30.refs_6_.refs_3_), channel_id=1, source_target_pairs={{0,12},{1,13},{2,14},{3,15},{4,8},{5,9},{6,10},{7,11},{8,4},{9,5},... | collective-permute-start | bytes 884744 | tf_op jit(solution)/shard_map/ppermute | solution.py:31
  27.2 14.7 %collective-permute-start.4 = (bf16[512,256]{1,0:T(8,128)(2,1)S(1)}, bf16[512,256]{1,0:T(8,128)(2,1)S(1)}, u32[]{:S(2)}, u32[]{:S(2)}) collective-permute-start(bf16[512,256]{1,0:T(8,128)(2,1)S(1)} %collective-permute-done.2.refs_4_), channel_id=1, source_target_pairs={{0,1},{1,0},{2,3},{3,2},{4,5},{5,4},{6,7},{7,6},{8,9},{9,8},{10,11... | collective-permute-start | bytes 786440 | tf_op jit(solution)/shard_map/ppermute | solution.py:31
  32.4 31.7 %collective-permute-start.12 = (bf16[128,1152]{1,0:T(8,128)(2,1)S(1)}, bf16[128,1152]{1,0:T(8,128)(2,1)S(1)}, u32[]{:S(2)}, u32[]{:S(2)}) collective-permute-start(bf16[128,1152]{1,0:T(8,128)(2,1)S(1)} %get-tuple-element.29.refs_5_.refs_2_), channel_id=1, source_target_pairs={{0,8},{1,9},{2,10},{3,11},{4,12},{5,13},{6,14},{7,15},{8,0},{9,1},... | collective-permute-start | bytes 884744 | tf_op jit(solution)/shard_map/ppermute | solution.py:31
  35.2 5.0 %collective-permute-start.6 = (bf16[512,128]{1,0:T(8,128)(2,1)S(1)}, bf16[512,128]{1,0:T(8,128)(2,1)S(1)}, u32[]{:S(2)}, u32[]{:S(2)}) collective-permute-start(bf16[512,128]{1,0:T(8,128)(2,1)S(1)} %get-tuple-element.36), channel_id=1, source_target_pairs={{0,2},{1,3},{2,0},{3,1},{4,6},{5,7},{6,4},{7,5},{8,10},{9,11},{10,... | collective-permute-start | bytes 393224 | tf_op jit(solution)/shard_map/ppermute | solution.py:31
  36.7 9.2 %collective-permute-start.7 = (bf16[512,256]{1,0:T(8,128)(2,1)S(1)}, bf16[512,256]{1,0:T(8,128)(2,1)S(1)}, u32[]{:S(2)}, u32[]{:S(2)}) collective-permute-start(bf16[512,256]{1,0:T(8,128)(2,1)S(1)} %collective-permute-done.5.refs_5_), channel_id=1, source_target_pairs={{0,1},{1,0},{2,3},{3,2},{4,5},{5,4},{6,7},{7,6},{8,9},{9,8},{10,11... | collective-permute-start | bytes 786440 | tf_op jit(solution)/shard_map/ppermute | solution.py:31
  40.3 23.8 %collective-permute-start.13 = (bf16[128,1152]{1,0:T(8,128)(2,1)S(1)}, bf16[128,1152]{1,0:T(8,128)(2,1)S(1)}, u32[]{:S(2)}, u32[]{:S(2)}) collective-permute-start(bf16[128,1152]{1,0:T(8,128)(2,1)S(1)} %get-tuple-element.28.refs_4_.refs_1_), channel_id=1, source_target_pairs={{0,4},{1,5},{2,6},{3,7},{4,0},{5,1},{6,2},{7,3},{8,12},{9,13},{10,... | collective-permute-start | bytes 884744 | tf_op jit(solution)/shard_map/ppermute | solution.py:31
  41.9 3.8 %collective-permute-start.8 = (bf16[512,128]{1,0:T(8,128)(2,1)S(1)}, bf16[512,128]{1,0:T(8,128)(2,1)S(1)}, u32[]{:S(2)}, u32[]{:S(2)}) collective-permute-start(bf16[512,128]{1,0:T(8,128)(2,1)S(1)} %collective-permute-done.6.refs_6_), channel_id=1, source_target_pairs={{0,1},{1,0},{2,3},{3,2},{4,5},{5,4},{6,7},{7,6},{8,9},{9,8},{10,11... | collective-permute-start | bytes 393224 | tf_op jit(solution)/shard_map/ppermute | solution.py:31
  45.7 12.8 %collective-permute-start.10 = (bf16[256,128]{1,0:T(8,128)(2,1)S(1)}, bf16[256,128]{1,0:T(8,128)(2,1)S(1)}, u32[]{:S(2)}, u32[]{:S(2)}) collective-permute-start(bf16[256,128]{1,0:T(8,128)(2,1)S(1)} %get-tuple-element.40.refs_9_), channel_id=1, source_target_pairs={{0,12},{1,13},{2,14},{3,15},{4,8},{5,9},{6,10},{7,11},{8,4},{9,5},... | collective-permute-start | bytes 196616 | tf_op jit(solution)/shard_map/ppermute | solution.py:31
  48.3 11.1 %collective-permute-start.11 = (bf16[320,128]{1,0:T(8,128)(2,1)S(1)}, bf16[320,128]{1,0:T(8,128)(2,1)S(1)}, u32[]{:S(2)}, u32[]{:S(2)}) collective-permute-start(bf16[320,128]{1,0:T(8,128)(2,1)S(1)} %shard_map.114.refs_10_), channel_id=1, source_target_pairs={{0,12},{1,13},{2,14},{3,15},{4,8},{5,9},{6,10},{7,11},{8,4},{9,5},... | collective-permute-start | bytes 245768 | tf_op jit(solution)/shard_map/ppermute | solution.py:31
  56.2 5.3 %copy-start = (bf16[3,1152,576]{1,2,0:T(8,128)(2,1)S(1)}, bf16[3,1152,576]{1,2,0:T(8,128)(2,1)}, u32[]{:S(2)}) copy-start(bf16[3,1152,576]{1,2,0:T(8,128)(2,1)} %param.19) | copy-start | bytes 11943940
  56.3 5.3 %copy-start.1 = (bf16[576,1152]{1,0:T(8,128)(2,1)S(1)}, bf16[576,1152]{1,0:T(8,128)(2,1)}, u32[]{:S(2)}) copy-start(bf16[576,1152]{1,0:T(8,128)(2,1)} %refs_5_.1) | copy-start | bytes 3981316
  56.3 11.8 %collective-permute-start.16 = (bf16[576,128]{1,0:T(8,128)(2,1)S(1)}, bf16[576,128]{1,0:T(8,128)(2,1)S(1)}, u32[]{:S(2)}, u32[]{:S(2)}) collective-permute-start(bf16[576,128]{1,0:T(8,128)(2,1)S(1)} %shard_map.112.refs_6_), channel_id=1, source_target_pairs={{0,4},{1,5},{2,6},{3,7},{4,0},{5,1},{6,2},{7,3},{8,12},{9,13},{10,... | collective-permute-start | bytes 442376 | tf_op jit(solution)/shard_map/ppermute | solution.py:31
  58.5 8.7 %collective-permute-start.14 = (bf16[256,128]{1,0:T(8,128)(2,1)S(1)}, bf16[256,128]{1,0:T(8,128)(2,1)S(1)}, u32[]{:S(2)}, u32[]{:S(2)}) collective-permute-start(bf16[256,128]{1,0:T(8,128)(2,1)S(1)} %get-tuple-element.39.refs_7_), channel_id=1, source_target_pairs={{0,8},{1,9},{2,10},{3,11},{4,12},{5,13},{6,14},{7,15},{8,0},{9,1},... | collective-permute-start | bytes 196616 | tf_op jit(solution)/shard_map/ppermute | solution.py:31
  59.4 8.8 %collective-permute-start.15 = (bf16[320,128]{1,0:T(8,128)(2,1)S(1)}, bf16[320,128]{1,0:T(8,128)(2,1)S(1)}, u32[]{:S(2)}, u32[]{:S(2)}) collective-permute-start(bf16[320,128]{1,0:T(8,128)(2,1)S(1)} %shard_map.113.refs_8_), channel_id=1, source_target_pairs={{0,8},{1,9},{2,10},{3,11},{4,12},{5,13},{6,14},{7,15},{8,0},{9,1},... | collective-permute-start | bytes 245768 | tf_op jit(solution)/shard_map/ppermute | solution.py:31
  73.2 8.6 %collective-permute-start.18 = (bf16[576,128]{1,0:T(8,128)(2,1)S(1)}, bf16[576,128]{1,0:T(8,128)(2,1)S(1)}, u32[]{:S(2)}, u32[]{:S(2)}) collective-permute-start(bf16[576,128]{1,0:T(8,128)(2,1)S(1)} %shard_map.119), channel_id=1, source_target_pairs={{0,12},{1,13},{2,14},{3,15},{4,8},{5,9},{6,10},{7,11},{8,4},{9,5},... | collective-permute-start | bytes 442376 | tf_op jit(solution)/shard_map/ppermute | solution.py:31
  74.7 11.3 %collective-permute-start.19 = (bf16[576,128]{1,0:T(8,128)(2,1)S(1)}, bf16[576,128]{1,0:T(8,128)(2,1)S(1)}, u32[]{:S(2)}, u32[]{:S(2)}) collective-permute-start(bf16[576,128]{1,0:T(8,128)(2,1)S(1)} %get-tuple-element.48), channel_id=1, source_target_pairs={{0,4},{1,5},{2,6},{3,7},{4,0},{5,1},{6,2},{7,3},{8,12},{9,13},{10,... | collective-permute-start | bytes 442376 | tf_op jit(solution)/shard_map/ppermute | solution.py:31
  74.7 13.5 %collective-permute-start.17 = (bf16[576,128]{1,0:T(8,128)(2,1)S(1)}, bf16[576,128]{1,0:T(8,128)(2,1)S(1)}, u32[]{:S(2)}, u32[]{:S(2)}) collective-permute-start(bf16[576,128]{1,0:T(8,128)(2,1)S(1)} %get-tuple-element.47), channel_id=1, source_target_pairs={{0,8},{1,9},{2,10},{3,11},{4,12},{5,13},{6,14},{7,15},{8,0},{9,1},... | collective-permute-start | bytes 442376 | tf_op jit(solution)/shard_map/ppermute | solution.py:31
  78.8 7.1 %copy-start.2 = (bf16[576,1152]{1,0:T(8,128)(2,1)S(1)}, bf16[576,1152]{1,0:T(8,128)(2,1)}, u32[]{:S(2)}) copy-start(bf16[576,1152]{1,0:T(8,128)(2,1)} %weight_ref.3) | copy-start | bytes 3981316
